TPU v7x, 32 devices: a whole 2x2x4 slice. The times are simulated.
32 devices in a mesh: section: 4 (over y, x), dp: 8 (over z, core).
Axes of the slice: x: 2, y: 2, z: 4, core: 2. Of those that a mesh axis runs over, the one named last changes fastest.
Arguments:
- saved_inputs: bfloat16 [4, 2, 1024, 320], P('section', None, 'dp'), may hold values from -6 to 6
- timesteps: int32 [2, 1024], P(None, 'dp'), may hold values from 0 to 999
- time_table: bfloat16 [1000, 320], replicated, may hold values from -6 to 6
- skip_weight: bfloat16 [4, 320, 320], P('section'), may hold values from -0.3125 to 0.3125
- ff_in: bfloat16 [4, 1280, 320], P('section'), may hold values from -0.3125 to 0.3125
- ff_out: bfloat16 [4, 1280, 320], P('section'), may hold values from -0.15625 to 0.15625
- output_cotangent: bfloat16 [2, 1024, 320], P(None, 'dp'), may hold values from -6 to 6
Outputs:
- input_grads: bfloat16 [4, 2, 1024, 320], P('section', None, 'dp')
- skip_weight_grad: float32 [4, 102400], P('section', 'dp')
- ff_in_grad: float32 [4, 1280, 320], P('section', 'dp')
- ff_out_grad: float32 [4, 1280, 320], P('section', 'dp')
All inputs are finite; a program needn't handle non-finite values.
Results may differ from a plain program's by a relative error of at most 0.01.
Values may be sent and summed in bfloat16 or wider, within the bound.
No kernel may reach another device: no remote copies, remote signals or barrier semaphores. Data moves between devices by JAX's collectives and lax.ppermute only.
A program may use at most 128 MiB of HBM per device.

v0:
```python
import jax
import jax.numpy as jnp
from jax import lax
from jax.sharding import PartitionSpec as P

EPS = 1e-06


def from_partner(shard, axis, stride):
    return lax.ppermute(shard, axis, [(i, i ^ 1 << stride) for i in range(lax.axis_size(axis))])


def passed_along(value, axis, steps):
    count = lax.axis_size(axis)
    first, last = (max(0, -steps), min(count, count - steps))
    return lax.ppermute(value, axis, [(source, source + steps) for source in range(first, last)])


def contract(left, right, dims):
    return lax.dot_general(
        left, right, ((dims[0], dims[1]), ((), ())), preferred_element_type=jnp.float32
    )


def forward(inputs, source, w_skip, w_in, w_out):
    united = inputs.astype(jnp.float32) + jnp.dot(
        source, w_skip, preferred_element_type=jnp.float32
    )
    recip = lax.rsqrt(jnp.mean(united * united, axis=-1, keepdims=True) + EPS)
    normed = (united * recip).astype(jnp.bfloat16)
    preact = contract(normed, w_in, ((1,), (1,)))
    active = jax.nn.silu(preact).astype(jnp.bfloat16)
    output = united + jnp.dot(active, w_out, preferred_element_type=jnp.float32)
    return (united, recip, normed, preact, active, output)


def put_micro(buffer, value, index, valid):
    updated = lax.dynamic_update_index_in_dim(buffer, value, index, 0)
    return jnp.where(valid, updated, buffer)


def shards(saved_inputs, timesteps, time_table, skip_weight, ff_in, ff_out, output_cotangent):
    section = lax.axis_index("section")
    n_micro = saved_inputs.shape[1]
    rows = saved_inputs.shape[2]
    width = saved_inputs.shape[3]
    hidden = ff_in.shape[1]
    inputs = saved_inputs[0]
    w_skip = skip_weight[0]
    w_in = ff_in[0]
    w_out = ff_out[0]
    bit_order = (0, 1)
    levels = lax.broadcasted_iota(jnp.int32, (1, time_table.shape[0]), 1)
    embed_list = []
    value_list = []
    for micro in range(n_micro):
        onehot = (timesteps[micro][:, None] == levels).astype(jnp.bfloat16)
        embed = jnp.dot(onehot, time_table, preferred_element_type=jnp.float32).astype(jnp.bfloat16)
        embed_list.append(embed)
        value_list.append(
            forward(inputs[micro], embed, w_skip, w_in, w_out)[5].astype(jnp.bfloat16)
        )
    embeds = jnp.stack(embed_list)
    values = jnp.stack(value_list)
    received = values
    for bit in bit_order:
        received = from_partner(received, "section", bit)
    sources = jnp.where(section >= 2, received, embeds)

    def active_path(operands):
        grad_out, own_input, source = operands
        united, recip, normed, preact, active, output = forward(
            own_input, source, w_skip, w_in, w_out
        )
        grad_low = grad_out.astype(jnp.bfloat16)
        grad_act = contract(grad_low, w_out, ((1,), (1,)))
        sigma = jax.nn.sigmoid(preact)
        grad_pre = (grad_act * sigma * (1.0 + preact * (1.0 - sigma))).astype(jnp.bfloat16)
        grad_norm = jnp.dot(grad_pre, w_in, preferred_element_type=jnp.float32)
        grad_united = (
            grad_out
            + recip * grad_norm
            - united * recip**3 * jnp.mean(grad_norm * united, axis=-1, keepdims=True)
        )
        united_low = grad_united.astype(jnp.bfloat16)
        d_skip = contract(source, united_low, ((0,), (0,)))
        grad_source = contract(united_low, w_skip, ((1,), (1,))).astype(jnp.bfloat16)
        extra = (contract(grad_pre, normed, ((0,), (0,))), contract(active, grad_low, ((0,), (0,))))
        return (united_low, grad_source, d_skip) + extra

    def resting_path(operands):
        low_rows = jnp.zeros((rows, width), jnp.bfloat16)
        base = (low_rows, low_rows, jnp.zeros((width, width), jnp.float32))
        extra = (jnp.zeros((hidden, width), jnp.float32), jnp.zeros((hidden, width), jnp.float32))
        return base + extra

    chain = jnp.zeros((rows, width), jnp.bfloat16)
    skip_store = jnp.zeros((n_micro, rows, width), jnp.bfloat16)
    grad_store = jnp.zeros((n_micro, rows, width), jnp.bfloat16)
    total_skip = jnp.zeros((width, width), jnp.float32)
    total_in = jnp.zeros((hidden, width), jnp.float32)
    total_out = jnp.zeros((hidden, width), jnp.float32)
    for tick in range(n_micro + 3):
        micro = tick - (3 - section)
        valid = (micro >= 0) & (micro < n_micro)
        index = jnp.clip(micro, 0, n_micro - 1)
        own_input = lax.dynamic_index_in_dim(inputs, index, 0, keepdims=False)
        source = lax.dynamic_index_in_dim(sources, index, 0, keepdims=False)
        carried = lax.dynamic_index_in_dim(skip_store, index, 0, keepdims=False).astype(jnp.float32)
        upstream = chain.astype(jnp.float32) + jnp.where(section < 2, carried, 0.0)
        top = lax.dynamic_index_in_dim(output_cotangent, index, 0, keepdims=False).astype(
            jnp.float32
        )
        grad_out = jnp.where(section == 3, top, upstream)
        parts = lax.cond(valid, active_path, resting_path, (grad_out, own_input, source))
        united_low = parts[0]
        grad_store = put_micro(grad_store, united_low, index, valid)
        total_skip = total_skip + parts[2]
        total_in = total_in + parts[3]
        total_out = total_out + parts[4]
        chain = passed_along(united_low, "section", -1)
        back = parts[1]
        for bit in bit_order:
            back = from_partner(back, "section", bit)
        sender = tick - section
        receive = (section < 2) & (sender >= 0) & (sender < n_micro)
        skip_store = put_micro(skip_store, back, jnp.clip(sender, 0, n_micro - 1), receive)
    grad_in, grad_out_w, grad_skip = (
        lax.psum_scatter(total_in, "dp", scatter_dimension=0, tiled=True),
        lax.psum_scatter(total_out, "dp", scatter_dimension=0, tiled=True),
        lax.psum_scatter(total_skip.reshape(-1), "dp", scatter_dimension=0, tiled=True),
    )
    return (grad_store[None], grad_skip[None], grad_in[None], grad_out_w[None])


def solution(mesh):
    in_specs = (
        P("section", None, "dp", None),
        P(None, "dp"),
        P(),
        P("section", None, None),
        P("section", None, None),
        P("section", None, None),
        P(None, "dp", None),
    )
    out_specs = (
        P("section", None, "dp", None),
        P("section", "dp"),
        P("section", "dp", None),
        P("section", "dp", None),
    )
    return jax.shard_map(shards, mesh=mesh, in_specs=in_specs, out_specs=out_specs, check_vma=False)
```

profile of v0, /device:TPU:0, one launch (start us, length us, event | category | flops | bytes accessed | tf_op | source)
XLA Modules:
  0.0 272.1 jit_solution(12050596302691011541)
XLA Ops:
  8.7 1.3 multiply_reduce_fusion.10
  12.4 3.0 %collective-permute-start = (bf16[2,128,320]{1,2,0:T(8,128)(2,1)S(1)}, bf16[2,128,320]{1,2,0:T(8,128)(2,1)S(1)}, u32[]{:S(2)}, u32[]{:S(2)}) collective-permute-start(bf16[2,128,320]{1,2,0:T(8,128)(2,1)S(1)} %pad_maximum_fusion), channel_id=1, source_target_pairs={{0,8},{8,0},{16,24},{24,16},{1,9},{9,1},{17,25},{25,17},{2,10},{10... | collective-permute-start | bytes 491528 | tf_op jit(solution)/shard_map/ppermute | solution.py:10
  15.4 4.2 %collective-permute-done = bf16[2,128,320]{1,2,0:T(8,128)(2,1)S(1)} collective-permute-done((bf16[2,128,320]{1,2,0:T(8,128)(2,1)S(1)}, bf16[2,128,320]{1,2,0:T(8,128)(2,1)S(1)}, u32[]{:S(2)}, u32[]{:S(2)}) %collective-permute-start) | collective-permute-done | bytes 163872 | tf_op jit(solution)/shard_map/ppermute | solution.py:10
  19.6 1.8 collective-permute-start.1
  21.4 1.3 copy.55
  23.3 1.7 collective-permute-done.1
  26.3 3.5 %conditional.5 = (bf16[128,320]{0,1:T(8,128)(2,1)}, bf16[128,320]{0,1:T(8,128)(2,1)S(1)}, f32[320,320]{1,0:T(8,128)}, f32[1280,320]{0,1:T(8,128)S(1)}, f32[1280,...) conditional(s32[]{:T(128)} %convert_element_type.325, () %tuple.76, (bf16[2,128,320]{1,2,0:T(8,128)(2,1)}, s32[]{:T(128)}, ...), branch_computations={%region_2.3_spmd, %region_3.6_spmd} | conditional | flops 606249344 | bytes 17243340 | solution.py:115
  27.9 1.3 broadcast.295.clone
  29.8 1.7 collective-permute-start.2
  31.5 1.3 collective-permute-start.4
  32.8 2.1 collective-permute-done.2
  34.9 8.5 %collective-permute-start.3 = (bf16[128,320]{0,1:T(8,128)(2,1)}, bf16[128,320]{0,1:T(8,128)(2,1)}, u32[]{:S(2)}, u32[]{:S(2)}) collective-permute-start(bf16[128,320]{0,1:T(8,128)(2,1)} %collective-permute-done.2), channel_id=1, source_target_pairs={{0,16},{8,24},{16,0},{24,8},{1,17},{9,25},{17,1},{25,9},{2,18},{10... | collective-permute-start | bytes 245768 | tf_op jit(solution)/shard_map/ppermute | solution.py:10
  43.4 1.6 convert_element_type.339
  45.0 1.2 collective-permute-done.3
  46.8 1.5 bitcast_dynamic-update-slice_fusion.1
  49.7 4.8 %conditional.6 = (bf16[128,320]{0,1:T(8,128)(2,1)}, bf16[128,320]{0,1:T(8,128)(2,1)S(1)}, f32[320,320]{1,0:T(8,128)}, f32[1280,320]{0,1:T(8,128)}, f32[1280,320]{0,1:T(8,128)}, /*index=5*/bf16[1,128,320]{1,2,0:T(8,128)(2,1)}) conditional(s32[]{:T(128)} %convert_element_type.338, () %tuple.78, (bf16[2,128,320]{1,2,0:T(8,128)(2,1)}, s32[]{:T(128)}, ...), branch_computations={%region_6.7_spmd, %region_7.10_spmd} | conditional | flops 606208384 | bytes 16301140 | solution.py:115
  51.2 1.3 broadcast.301
  52.5 1.3 broadcast.301.clone
  54.5 1.3 collective-permute-start.5
  55.8 1.3 collective-permute-start.7
  57.1 1.8 collective-permute-done.5
  58.9 10.6 %collective-permute-start.6 = (bf16[128,320]{0,1:T(8,128)(2,1)S(1)}, bf16[128,320]{0,1:T(8,128)(2,1)S(1)}, u32[]{:S(2)}, u32[]{:S(2)}) collective-permute-start(bf16[128,320]{0,1:T(8,128)(2,1)S(1)} %collective-permute-done.5), channel_id=1, source_target_pairs={{0,16},{8,24},{16,0},{24,8},{1,17},{9,25},{17,1},{25,9},{2,18},{10... | collective-permute-start | bytes 245768 | tf_op jit(solution)/shard_map/ppermute | solution.py:10
  70.2 1.7 collective-permute-done.6
  71.9 1.5 fusion.120
  73.5 3.6 %conditional.7 = (bf16[128,320]{0,1:T(8,128)(2,1)}, bf16[128,320]{0,1:T(8,128)(2,1)S(1)}, f32[320,320]{1,0:T(8,128)}, f32[1280,320]{0,1:T(8,128)S(1)}, f32[1280,...) conditional(s32[]{:T(128)} %convert_element_type.340, () %tuple.80, (bf16[2,128,320]{1,2,0:T(8,128)(2,1)}, s32[]{:T(128)}, ...), branch_computations={%region_10.11_spmd, %region_11.14_spmd} | conditional | flops 606208384 | bytes 16301140 | solution.py:115
  75.1 1.4 broadcast.307.clone
  77.1 9.8 %collective-permute-start.8 = (bf16[128,320]{0,1:T(8,128)(2,1)S(1)}, bf16[128,320]{0,1:T(8,128)(2,1)}, u32[]{:S(2)}, u32[]{:S(2)}) collective-permute-start(bf16[128,320]{0,1:T(8,128)(2,1)S(1)} %get-tuple-element.599), channel_id=1, source_target_pairs={{0,8},{8,0},{16,24},{24,16},{1,9},{9,1},{17,25},{25,17},{2,10},{10... | collective-permute-start | bytes 245768 | tf_op jit(solution)/shard_map/ppermute | solution.py:10
  86.9 1.3 collective-permute-start.10
  88.2 1.2 collective-permute-done.8
  89.4 2.9 %collective-permute-start.9 = (bf16[128,320]{0,1:T(8,128)(2,1)}, bf16[128,320]{0,1:T(8,128)(2,1)}, u32[]{:S(2)}, u32[]{:S(2)}) collective-permute-start(bf16[128,320]{0,1:T(8,128)(2,1)} %collective-permute-done.8), channel_id=1, source_target_pairs={{0,16},{8,24},{16,0},{24,8},{1,17},{9,25},{17,1},{25,9},{2,18},{10... | collective-permute-start | bytes 245768 | tf_op jit(solution)/shard_map/ppermute | solution.py:10
  92.4 1.2 collective-permute-done.10
  93.6 1.6 convert_element_type.343
  95.1 1.6 fusion.119
  96.7 13.5 %conditional.8 = (bf16[128,320]{0,1:T(8,128)(2,1)}, bf16[128,320]{0,1:T(8,128)(2,1)S(1)}, f32[320,320]{1,0:T(8,128)}, f32[1280,320]{0,1:T(8,128)}, f32[1280,320]{0,1:T(8,128)}, /*index=5*/bf16[1,128,320]{1,2,0:T(8,128)(2,1)}) conditional(s32[]{:T(128)} %convert_element_type.342, () %tuple.82, (bf16[2,128,320]{1,2,0:T(8,128)(2,1)}, s32[]{:T(128)}, ...), branch_computations={%region_14.15_spmd, %region_15.18_spmd} | conditional | flops 606208384 | bytes 16301140 | solution.py:115
  96.7 1.1 copy.59
  97.8 1.3 multiply_reduce_fusion.7
  99.1 1.2 fusion.65
  102.4 1.1 convolution_convert_fusion.3
  103.5 1.9 fusion.66
  105.4 1.6 fusion.73
  107.0 1.6 fusion.62
  108.7 1.5 copy.121
  110.2 1.1 collective-permute-start.11
  111.3 1.3 collective-permute-start.13
  112.6 2.1 collective-permute-done.11
  115.7 2.2 collective-permute-done.13
  119.1 11.4 %conditional.9 = (f32[320,320]{1,0:T(8,128)S(1)}, f32[1280,320]{0,1:T(8,128)S(1)}, f32[1280,320]{0,1:T(8,128)}, bf16[1,128,320]{1,2,0:T(8,128)(2,1)}) conditional(s32[]{:T(128)} %convert_element_type.344, () %tuple.84, (bf16[2,128,320]{1,2,0:T(8,128)(2,1)}, s32[]{:T(128)}, bf16[2,128,320]{1,2,0:T(8,128)(2,1)}, s32[]{:T(128)}, pred[]{:T(512)}, ...), branch_computations={%region_18.19_spmd, %region_19.22_spmd.clone} | conditional | flops 579993984 | bytes 16997552 | solution.py:115
  119.1 1.1 copy.60
  120.2 1.3 multiply_reduce_fusion.9
  121.5 1.6 fusion.89
  123.1 1.2 fusion.83
  126.4 1.1 fusion.84
  127.6 1.3 fusion.92
  128.8 1.6 fusion.80
  131.2 1.7 add_add_fusion.2
  134.1 3.9 %add_add_fusion.1 = f32[1280,320]{0,1:T(8,128)S(1)} fusion(f32[1280,320]{0,1:T(8,128)} %copy-done.4, f32[1280,320]{0,1:T(8,128)} %get-tuple-element.613, f32[1280,320]{0,1:T(8,128)} %copy-done.3, f32[1280,320]{0,1:T(8,128)} %copy-done.2, f32[1280,320]{0,1:T(8,128)} %get-tuple-element.611), kind=kLoop, calls=%fused_computation.160 | loop fusion | flops 1638400 | bytes 9830400 | tf_op jit(solution)/shard_map/add | solution.py:119
  137.9 1.8 copy.63
  139.8 3.9 %add_add_fusion = f32[1280,320]{0,1:T(8,128)S(1)} fusion(f32[1280,320]{0,1:T(8,128)} %get-tuple-element.619, f32[1280,320]{0,1:T(8,128)} %get-tuple-element.618, f32[1280,320]{0,1:T(8,128)} %get-tuple-element.617, f32[1280,320]{0,1:T(8,128)} %get-tuple-element.615, f32[1280,320]{0,1:T(8,128)} %get-tuple-element.616), kind=kLoop, calls=%fused_computation.159 | loop fusion | flops 1638400 | bytes 9830400 | tf_op jit(solution)/shard_map/add | solution.py:120
  143.7 1.8 copy.65
  149.4 37.9 %all-reduce.3.cloned.1.call-done = f32[102400]{0:T(1024)} async-done(((f32[102400]{0:T(1024)}), f32[102400]{0:T(1024)}) %all-reduce.3.cloned.1.call-update) | async-done | bytes 409616
  188.9 38.1 %reduce-scatter.7.cloned.1.call-done = f32[160,320]{1,0:T(8,128)} async-done(((f32[1280,320]{1,0:T(8,128)}), f32[160,320]{1,0:T(8,128)}) %reduce-scatter.7.cloned.1.call-update) | async-done | bytes 204816
  227.0 1.1 copy.64
  228.9 34.7 %reduce-scatter.9.cloned.1.call-done = f32[160,320]{1,0:T(8,128)} async-done(((f32[1280,320]{1,0:T(8,128)}), f32[160,320]{1,0:T(8,128)}) %reduce-scatter.9.cloned.1.call-update) | async-done | bytes 204816
  263.6 1.1 copy.66
  (97 shorter events, 29.9 us)
Async XLA Ops:
  7.2 1.1 copy-start
  7.2 3.3 %copy-start.6 = (bf16[1,2,128,320]{2,3,1,0:T(8,128)(2,1)S(1)}, bf16[1,2,128,320]{2,3,1,0:T(8,128)(2,1)}, u32[]{:S(2)}) copy-start(bf16[1,2,128,320]{2,3,1,0:T(8,128)(2,1)} %param.17) | copy-start | bytes 491524
  7.2 3.3 %copy-start.1 = (bf16[1,320,320]{2,1,0:T(8,128)(2,1)S(1)}, bf16[1,320,320]{2,1,0:T(8,128)(2,1)}, u32[]{:S(2)}) copy-start(bf16[1,320,320]{2,1,0:T(8,128)(2,1)} %param.20) | copy-start | bytes 614404
  7.2 3.6 %copy-start.17 = (bf16[1,1280,320]{1,2,0:T(8,128)(2,1)S(1)}, bf16[1,1280,320]{1,2,0:T(8,128)(2,1)}, u32[]{:S(2)}) copy-start(bf16[1,1280,320]{1,2,0:T(8,128)(2,1)} %param.22) | copy-start | bytes 2457604
  7.2 3.6 %copy-start.18 = (bf16[1,1280,320]{1,2,0:T(8,128)(2,1)S(1)}, bf16[1,1280,320]{1,2,0:T(8,128)(2,1)}, u32[]{:S(2)}) copy-start(bf16[1,1280,320]{1,2,0:T(8,128)(2,1)} %param.21) | copy-start | bytes 2457604
  7.2 180.1 %all-reduce.3.cloned.1.call-start = ((), (), s32[]{:S(2)}) async-start(), calls=%async_computation.4 | async-start | bytes 819200
  12.4 7.2 %collective-permute-start = (bf16[2,128,320]{1,2,0:T(8,128)(2,1)S(1)}, bf16[2,128,320]{1,2,0:T(8,128)(2,1)S(1)}, u32[]{:S(2)}, u32[]{:S(2)}) collective-permute-start(bf16[2,128,320]{1,2,0:T(8,128)(2,1)S(1)} %pad_maximum_fusion), channel_id=1, source_target_pairs={{0,8},{8,0},{16,24},{24,16},{1,9},{9,1},{17,25},{25,17},{2,10},{10... | collective-permute-start | bytes 491528 | tf_op jit(solution)/shard_map/ppermute | solution.py:10
  19.6 5.4 %collective-permute-start.1 = (bf16[2,128,320]{1,2,0:T(8,128)(2,1)S(1)}, bf16[2,128,320]{1,2,0:T(8,128)(2,1)S(1)}, u32[]{:S(2)}, u32[]{:S(2)}) collective-permute-start(bf16[2,128,320]{1,2,0:T(8,128)(2,1)S(1)} %collective-permute-done), channel_id=1, source_target_pairs={{0,16},{8,24},{16,0},{24,8},{1,17},{9,25},{17,1},{25,9},{2,18},{10... | collective-permute-start | bytes 491528 | tf_op jit(solution)/shard_map/ppermute | solution.py:10
  29.8 19.8 %copy-start.2 = (f32[1280,320]{0,1:T(8,128)}, f32[1280,320]{0,1:T(8,128)S(1)}, u32[]{:S(2)}) copy-start(f32[1280,320]{0,1:T(8,128)S(1)} %get-tuple-element.610) | copy-start | bytes 4915204
  29.8 5.1 %collective-permute-start.2 = (bf16[128,320]{0,1:T(8,128)(2,1)S(1)}, bf16[128,320]{0,1:T(8,128)(2,1)}, u32[]{:S(2)}, u32[]{:S(2)}) collective-permute-start(bf16[128,320]{0,1:T(8,128)(2,1)S(1)} %get-tuple-element.593), channel_id=1, source_target_pairs={{0,8},{8,0},{16,24},{24,16},{1,9},{9,1},{17,25},{25,17},{2,10},{10... | collective-permute-start | bytes 245768 | tf_op jit(solution)/shard_map/ppermute | solution.py:10
  31.5 11.9 %collective-permute-start.4 = (bf16[128,320]{0,1:T(8,128)(2,1)}, bf16[128,320]{0,1:T(8,128)(2,1)}, u32[]{:S(2)}, u32[]{:S(2)}) collective-permute-start(bf16[128,320]{0,1:T(8,128)(2,1)} %get-tuple-element.594), channel_id=1, source_target_pairs={{8,0},{16,8},{24,16},{9,1},{17,9},{25,17},{10,2},{18,10},{26,18},{... | collective-permute-start | bytes 245768 | tf_op jit(solution)/shard_map/ppermute | solution.py:16
  34.9 11.3 %collective-permute-start.3 = (bf16[128,320]{0,1:T(8,128)(2,1)}, bf16[128,320]{0,1:T(8,128)(2,1)}, u32[]{:S(2)}, u32[]{:S(2)}) collective-permute-start(bf16[128,320]{0,1:T(8,128)(2,1)} %collective-permute-done.2), channel_id=1, source_target_pairs={{0,16},{8,24},{16,0},{24,8},{1,17},{9,25},{17,1},{25,9},{2,18},{10... | collective-permute-start | bytes 245768 | tf_op jit(solution)/shard_map/ppermute | solution.py:10
  54.5 4.4 %collective-permute-start.5 = (bf16[128,320]{0,1:T(8,128)(2,1)S(1)}, bf16[128,320]{0,1:T(8,128)(2,1)S(1)}, u32[]{:S(2)}, u32[]{:S(2)}) collective-permute-start(bf16[128,320]{0,1:T(8,128)(2,1)S(1)} %get-tuple-element.596), channel_id=1, source_target_pairs={{0,8},{8,0},{16,24},{24,16},{1,9},{9,1},{17,25},{25,17},{2,10},{10... | collective-permute-start | bytes 245768 | tf_op jit(solution)/shard_map/ppermute | solution.py:10
  55.8 13.7 %collective-permute-start.7 = (bf16[128,320]{0,1:T(8,128)(2,1)}, bf16[128,320]{0,1:T(8,128)(2,1)S(1)}, u32[]{:S(2)}, u32[]{:S(2)}) collective-permute-start(bf16[128,320]{0,1:T(8,128)(2,1)} %get-tuple-element.597), channel_id=1, source_target_pairs={{8,0},{16,8},{24,16},{9,1},{17,9},{25,17},{10,2},{18,10},{26,18},{... | collective-permute-start | bytes 245768 | tf_op jit(solution)/shard_map/ppermute | solution.py:16
  58.9 13.0 %collective-permute-start.6 = (bf16[128,320]{0,1:T(8,128)(2,1)S(1)}, bf16[128,320]{0,1:T(8,128)(2,1)S(1)}, u32[]{:S(2)}, u32[]{:S(2)}) collective-permute-start(bf16[128,320]{0,1:T(8,128)(2,1)S(1)} %collective-permute-done.5), channel_id=1, source_target_pairs={{0,16},{8,24},{16,0},{24,8},{1,17},{9,25},{17,1},{25,9},{2,18},{10... | collective-permute-start | bytes 245768 | tf_op jit(solution)/shard_map/ppermute | solution.py:10
  77.1 19.6 %copy-start.3 = (f32[1280,320]{0,1:T(8,128)}, f32[1280,320]{0,1:T(8,128)S(1)}, u32[]{:S(2)}) copy-start(f32[1280,320]{0,1:T(8,128)S(1)} %get-tuple-element.612) | copy-start | bytes 4915204
  77.1 12.3 %collective-permute-start.8 = (bf16[128,320]{0,1:T(8,128)(2,1)S(1)}, bf16[128,320]{0,1:T(8,128)(2,1)}, u32[]{:S(2)}, u32[]{:S(2)}) collective-permute-start(bf16[128,320]{0,1:T(8,128)(2,1)S(1)} %get-tuple-element.599), channel_id=1, source_target_pairs={{0,8},{8,0},{16,24},{24,16},{1,9},{9,1},{17,25},{25,17},{2,10},{10... | collective-permute-start | bytes 245768 | tf_op jit(solution)/shard_map/ppermute | solution.py:10
  86.9 6.6 %collective-permute-start.10 = (bf16[128,320]{0,1:T(8,128)(2,1)}, bf16[128,320]{0,1:T(8,128)(2,1)}, u32[]{:S(2)}, u32[]{:S(2)}) collective-permute-start(bf16[128,320]{0,1:T(8,128)(2,1)} %get-tuple-element.600), channel_id=1, source_target_pairs={{8,0},{16,8},{24,16},{9,1},{17,9},{25,17},{10,2},{18,10},{26,18},{... | collective-permute-start | bytes 245768 | tf_op jit(solution)/shard_map/ppermute | solution.py:16
  89.4 5.7 %collective-permute-start.9 = (bf16[128,320]{0,1:T(8,128)(2,1)}, bf16[128,320]{0,1:T(8,128)(2,1)}, u32[]{:S(2)}, u32[]{:S(2)}) collective-permute-start(bf16[128,320]{0,1:T(8,128)(2,1)} %collective-permute-done.8), channel_id=1, source_target_pairs={{0,16},{8,24},{16,0},{24,8},{1,17},{9,25},{17,1},{25,9},{2,18},{10... | collective-permute-start | bytes 245768 | tf_op jit(solution)/shard_map/ppermute | solution.py:10
  97.8 2.9 %copy-start.15 = (bf16[1280,320]{1,0:T(8,128)(2,1)S(1)}, bf16[1280,320]{1,0:T(8,128)(2,1)}, u32[]{:S(2)}) copy-start(bf16[1280,320]{1,0:T(8,128)(2,1)} %get-tuple-element.542) | copy-start | bytes 2457604 | tf_op jit(solution)/shard_map/cond
  110.2 4.4 %collective-permute-start.11 = (bf16[128,320]{0,1:T(8,128)(2,1)S(1)}, bf16[128,320]{0,1:T(8,128)(2,1)S(1)}, u32[]{:S(2)}, u32[]{:S(2)}) collective-permute-start(bf16[128,320]{0,1:T(8,128)(2,1)S(1)} %get-tuple-element.602), channel_id=1, source_target_pairs={{0,8},{8,0},{16,24},{24,16},{1,9},{9,1},{17,25},{25,17},{2,10},{10... | collective-permute-start | bytes 245768 | tf_op jit(solution)/shard_map/ppermute | solution.py:10
  111.3 6.5 %collective-permute-start.13 = (bf16[128,320]{0,1:T(8,128)(2,1)}, bf16[128,320]{0,1:T(8,128)(2,1)S(1)}, u32[]{:S(2)}, u32[]{:S(2)}) collective-permute-start(bf16[128,320]{0,1:T(8,128)(2,1)} %get-tuple-element.603), channel_id=1, source_target_pairs={{8,0},{16,8},{24,16},{9,1},{17,9},{25,17},{10,2},{18,10},{26,18},{... | collective-permute-start | bytes 245768 | tf_op jit(solution)/shard_map/ppermute | solution.py:16
  114.6 4.4 %collective-permute-start.12 = (bf16[128,320]{0,1:T(8,128)(2,1)S(1)}, bf16[128,320]{0,1:T(8,128)(2,1)S(1)}, u32[]{:S(2)}, u32[]{:S(2)}) collective-permute-start(bf16[128,320]{0,1:T(8,128)(2,1)S(1)} %collective-permute-done.11), channel_id=1, source_target_pairs={{0,16},{8,24},{16,0},{24,8},{1,17},{9,25},{17,1},{25,9},{2,18},{10... | collective-permute-start | bytes 245768 | tf_op jit(solution)/shard_map/ppermute | solution.py:10
  119.1 1.1 copy-start.20
  120.2 4.6 %copy-start.16 = (bf16[1280,320]{1,0:T(8,128)(2,1)S(1)}, bf16[1280,320]{1,0:T(8,128)(2,1)}, u32[]{:S(2)}) copy-start(bf16[1280,320]{1,0:T(8,128)(2,1)} %get-tuple-element.637) | copy-start | bytes 2457604 | tf_op jit(solution)/shard_map/cond
  121.5 4.3 %copy-start.5 = (f32[128,320]{0,1:T(8,128)}, f32[128,320]{0,1:T(8,128)S(1)}, u32[]{:S(2)}) copy-start(f32[128,320]{0,1:T(8,128)S(1)} %get-tuple-element.938) | copy-start | bytes 491524 | tf_op jit(solution)/shard_map/cond
  130.5 0.8 copy-start.7
  130.5 3.5 %copy-start.4 = (f32[1280,320]{0,1:T(8,128)}, f32[1280,320]{0,1:T(8,128)S(1)}, u32[]{:S(2)}) copy-start(f32[1280,320]{0,1:T(8,128)S(1)} %get-tuple-element.614) | copy-start | bytes 4915204
  134.0 92.9 %reduce-scatter.7.cloned.1.call-start = ((), (), s32[]{:S(2)}) async-start(), calls=%async_computation.2 | async-start | bytes 2211840
  139.7 123.8 %reduce-scatter.9.cloned.1.call-start = ((), (), s32[]{:S(2)}) async-start(), calls=%async_computation.3 | async-start | bytes 2211840
  145.5 0.7 copy-start.21
  149.4 116.1 %copy-start.19 = (bf16[1,2,128,320]{2,3,1,0:T(8,128)(2,1)}, bf16[1,2,128,320]{2,3,1,0:T(8,128)(2,1)S(1)}, u32[]{:S(2)}) copy-start(bf16[1,2,128,320]{2,3,1,0:T(8,128)(2,1)S(1)} %bitcast_dynamic-update-slice_fusion) | copy-start | bytes 491524
Sparse Core Ops, SparseCore 0:
  134.1 53.1 all-reduce.2
  189.6 37.2 reduce-scatter.6
  229.3 34.2 reduce-scatter.8
where the time goes:
time: 273 us; the launch traced here: 272 us
  waiting for transfers between devices  131 us (48%)
  starting transfers between devices  47.1 us (17%)
  local copies, waits for them, and re-layouts  33.2 us (12%)
  other arithmetic  26.8 us (10%)
  matrix products  19.7 us (7%)
  between operations  14.6 us (5%)
    unnamed x6, waiting for transfers between devices  111 us
    ppermute x10, starting transfers between devices, from_partner(): lax.ppermute(shard, axis, [(i, i ^ 1 << stride) for i in range(lax.axis_s...  41.8 us
    ppermute x10, waiting for transfers between devices, from_partner(): lax.ppermute(shard, axis, [(i, i ^ 1 << stride) for i in range(lax.axis_s...  16.5 us
    another operation x19, local copies, waits for them, and re-layouts  12.8 us
    unnamed x33, local copies, waits for them, and re-layouts  12.4 us
    dot_general x11, matrix products, contract(): lax.dot_general(left, right, ((dims[0], dims[1]), ((), ())), preferred_el...  12.1 us
    select_n x9, other arithmetic, put_micro(): return jnp.where(valid, updated, buffer)  8.34 us
  transfers between devices with their start and end apart: 17, of which 14 were waited for; matrix products, arithmetic and copies ran while one was open for 9% of the time, Pallas kernels for 0%

commit v1 on v0

v1 whole, which is shorter than its diff:
```python
import jax
import jax.numpy as jnp
from jax import lax
from jax.sharding import PartitionSpec as P

EPS = 1e-06
LOW = jnp.bfloat16


def contract(left, right, dims):
    return lax.dot_general(
        left, right, ((dims[0], dims[1]), ((), ())), preferred_element_type=jnp.float32
    )


def forward_norm(inputs, source, w_skip, w_in):
    united = inputs.astype(jnp.float32) + jnp.dot(
        source, w_skip, preferred_element_type=jnp.float32
    )
    recip = lax.rsqrt(jnp.mean(united * united, axis=-1, keepdims=True) + EPS)
    normed = (united * recip).astype(LOW)
    preact = contract(normed, w_in, ((1,), (1,)))
    return united, recip, normed, preact


def slope_of(preact):
    sigma = jax.nn.sigmoid(preact)
    return sigma * (1.0 + preact * (1.0 - sigma))


def stage(grad_out, united, recip, slope, w_in, w_out):
    grad_low = grad_out.astype(LOW)
    grad_act = contract(grad_low, w_out, ((1,), (1,)))
    grad_pre = (grad_act * slope).astype(LOW)
    grad_norm = jnp.dot(grad_pre, w_in, preferred_element_type=jnp.float32)
    grad_united = (
        grad_out
        + recip * grad_norm
        - united * recip**3 * jnp.mean(grad_norm * united, axis=-1, keepdims=True)
    )
    return grad_low, grad_pre, grad_united.astype(LOW)


def exchange(value, count, mask):
    return lax.ppermute(value, "dp", [(i, i ^ mask) for i in range(count)])


def gather_blocks(value, count):
    blocks = [value]
    masks = [k for k in range(2, count, 2)]
    blocks = blocks + [exchange(value, count, mask) for mask in masks]
    other = [exchange(block, count, 1) for block in blocks]
    return jnp.concatenate(blocks + other, axis=0)


def scatter_sum(partial, count):
    place = lax.axis_index("dp")
    core = place % 2
    pairs = partial.reshape(count // 2, 2, -1)
    give = lax.dynamic_index_in_dim(pairs, 1 - core, 1, keepdims=False).astype(LOW)
    keep = lax.dynamic_index_in_dim(pairs, core, 1, keepdims=False)
    joined = keep + exchange(give, count, 1).astype(jnp.float32)
    chip = place // 2
    total = lax.dynamic_index_in_dim(joined, chip, 0, keepdims=False)
    for mask in range(1, count // 2):
        piece = lax.dynamic_index_in_dim(joined, chip ^ mask, 0, keepdims=False)
        total = total + exchange(piece.astype(LOW), count, 2 * mask).astype(jnp.float32)
    return total


def shards(saved_inputs, timesteps, time_table, skip_weight, ff_in, ff_out, output_cotangent):
    section = lax.axis_index("section")
    count = lax.axis_size("dp")
    n_micro = saved_inputs.shape[1]
    width = saved_inputs.shape[3]
    rows = n_micro * saved_inputs.shape[2]
    hidden = ff_in.shape[1]
    inputs = saved_inputs.reshape(rows, width)
    w_skip = skip_weight[0]
    w_in = ff_in[0]
    w_out = ff_out[0]
    levels = lax.broadcasted_iota(jnp.int32, (1, time_table.shape[0]), 1)
    onehot = (timesteps.reshape(rows)[:, None] == levels).astype(LOW)
    embed = jnp.dot(onehot, time_table, preferred_element_type=jnp.float32).astype(LOW)

    united, recip, normed, preact = forward_norm(inputs, embed, w_skip, w_in)
    active = jax.nn.silu(preact).astype(LOW)
    value = (united + jnp.dot(active, w_out, preferred_element_type=jnp.float32)).astype(LOW)
    received = lax.ppermute(value, "section", [(0, 3), (1, 2)])
    w_mirror = lax.ppermute(w_skip, "section", [(2, 1)])
    source = jnp.where(section >= 2, received, embed)
    united, recip, normed, preact = forward_norm(inputs, source, w_skip, w_in)
    slope = slope_of(preact)

    grad_out = output_cotangent.reshape(rows, width).astype(jnp.float32)
    grad_low = None
    for tick in range(4):
        owner = 3 - tick
        low, pre, chain = stage(grad_out, united, recip, slope, w_in, w_out)
        if tick == 0:
            grad_low, grad_pre, kept = low, pre, chain
            back = contract(chain, w_skip, ((1,), (1,))).astype(LOW)
            skip_far = lax.ppermute(back, "section", [(3, 0)])
        else:
            mine = section == owner
            grad_low = jnp.where(mine, low, grad_low)
            grad_pre = jnp.where(mine, pre, grad_pre)
            kept = jnp.where(mine, chain, kept)
        if tick < 3:
            chain = lax.ppermute(chain, "section", [(owner, owner - 1)])
            grad_out = chain.astype(jnp.float32)
            if tick == 1:
                back = contract(chain, w_mirror, ((1,), (1,))).astype(LOW)
                grad_out = grad_out + back.astype(jnp.float32)
            if tick == 2:
                grad_out = grad_out + skip_far.astype(jnp.float32)

    skip_part = contract(source, kept, ((0,), (0,)))
    if count * rows <= 4096:
        part = hidden // count
        start = lax.axis_index("dp") * part
        own_in = lax.dynamic_slice_in_dim(w_in, start, part, 0)
        own_out = lax.dynamic_slice_in_dim(w_out, start, part, 0)
        normed_all = gather_blocks(normed, count)
        pre_all = contract(normed_all, own_in, ((1,), (1,)))
        act_all = jax.nn.silu(pre_all).astype(LOW)
        slope_all = slope_of(pre_all)
        low_all = gather_blocks(grad_low, count)
        grad_pre_all = (contract(low_all, own_out, ((1,), (1,))) * slope_all).astype(LOW)
        grad_in = contract(grad_pre_all, normed_all, ((0,), (0,)))
        grad_out_w = contract(act_all, low_all, ((0,), (0,)))
        grad_skip = scatter_sum(skip_part.reshape(count, -1), count)
    else:
        active = jax.nn.silu(preact).astype(LOW)
        grad_in, grad_out_w, grad_skip = (
            lax.psum_scatter(value, "dp", scatter_dimension=0, tiled=True)
            for value in (
                contract(grad_pre, normed, ((0,), (0,))),
                contract(active, grad_low, ((0,), (0,))),
                skip_part.reshape(-1),
            )
        )
    return (kept.reshape(saved_inputs.shape), grad_skip[None], grad_in[None], grad_out_w[None])


def solution(mesh):
    in_specs = (
        P("section", None, "dp", None),
        P(None, "dp"),
        P(),
        P("section", None, None),
        P("section", None, None),
        P("section", None, None),
        P(None, "dp", None),
    )
    out_specs = (
        P("section", None, "dp", None),
        P("section", "dp"),
        P("section", "dp", None),
        P("section", "dp", None),
    )
    return jax.shard_map(shards, mesh=mesh, in_specs=in_specs, out_specs=out_specs, check_vma=False)
```

time: 273 us -> 105 us (0.38)
  waiting for transfers between devices: 131 us -> 19.8 us
  starting transfers between devices: 47.1 us -> 25.8 us
  other arithmetic: 26.8 us -> 7.33 us
  between operations: 14.6 us -> 0.94 us
  local copies, waits for them, and re-layouts: 33.2 us -> 20.9 us
  matrix products: 19.7 us -> 29.1 us
    unnamed x6 -> x0, waiting for transfers between devices: 111 us -> none
    ppermute x14 -> x24, starting transfers between devices: 47 us -> 25.8 us  [the longest x18 14.5 us: exchange(): return lax.ppermute(value, 'dp', [(i, i ^ mask) for i in range(count)])]
    another operation x19 -> x1, local copies, waits for them, and re-layouts: 12.8 us -> 0.39 us  [scatter_sum(): pairs = partial.reshape(count // 2, 2, -1)]
    select_n x12 -> x0, other arithmetic: 11.4 us -> none  [the longest x9 8.34 us: put_micro(): return jnp.where(valid, updated, buffer)]
    add x3 -> x2, other arithmetic: 9.48 us -> 0.94 us  [the longest x1 0.86 us: scatter_sum(): total + exchange(piece.astype(LOW), count, 2 * mask).astype(jnp.float32)]
    dot_general x10 -> x8, matrix products: 7.54 us -> 14 us  [the longest x4 8.77 us: stage(): grad_norm = jnp.dot(grad_pre, w_in, preferred_element_type=jnp.float32)]
    unnamed x0 -> x2, other arithmetic: none -> 3.1 us
    unnamed x33 -> x38, local copies, waits for them, and re-layouts: 12.4 us -> 15.3 us
  transfers between devices with their start and end apart: 17 -> 24, of which waited for: 14 -> 6; matrix products, arithmetic and copies ran while one was open for 9% -> 37% of each run, Pallas kernels for 0% -> 0%
where the time goes in v1:
time: 105 us; the launch traced here: 104 us
  matrix products  29.1 us (28%)
  starting transfers between devices  25.8 us (25%)
  local copies, waits for them, and re-layouts  20.9 us (20%)
  waiting for transfers between devices  19.8 us (19%)
  other arithmetic  7.33 us (7%)
    unnamed x38, local copies, waits for them, and re-layouts  15.3 us
    dot_general x7, matrix products, contract(): lax.dot_general(left, right, ((dims[0], dims[1]), ((), ())), preferred_el...  15 us
    ppermute x18, starting transfers between devices, exchange(): return lax.ppermute(value, 'dp', [(i, i ^ mask) for i in range(count)])  14.5 us
    ppermute x18, waiting for transfers between devices, exchange(): return lax.ppermute(value, 'dp', [(i, i ^ mask) for i in range(count)])  10.7 us
    dot_general x4, matrix products, stage(): grad_norm = jnp.dot(grad_pre, w_in, preferred_element_type=jnp.float32)  8.77 us
    ppermute x3, waiting for transfers between devices, shards(): chain = lax.ppermute(chain, 'section', [(owner, owner - 1)])  7.05 us
    ppermute x1, starting transfers between devices, shards(): received = lax.ppermute(value, 'section', [(0, 3), (1, 2)])  5.84 us
    convert_element_type x3, other arithmetic, stage(): return (grad_low, grad_pre, grad_united.astype(LOW))  3.25 us
  transfers between devices with their start and end apart: 24, of which 6 were waited for; matrix products, arithmetic and copies ran while one was open for 37% of the time, Pallas kernels for 0%

profile of v1, /device:TPU:0, one launch (start us, length us, event | category | flops | bytes accessed | tf_op | source)
XLA Modules:
  0.0 103.8 jit_solution(12582676339448031306)
XLA Ops:
  0.6 1.2 %copy.15 = f32[1,2,128,320]{2,1,3,0:T(2,128)S(1)} copy(bf16[1,2,128,320]{2,3,1,0:T(8,128)(2,1)} %param.7) | data formatting | bytes 491520 | tf_op jit(solution)/shard_map/convert_element_type | solution.py:17
  1.8 1.7 %convolution_convert_fusion.2 = bf16[256,320]{0,1:T(8,128)(2,1)S(1)} fusion(bf16[1000,320]{0,1:T(8,128)(2,1)} %param.9, s32[256]{0:T(256)} %bitcast.124), kind=kOutput, calls=%fused_computation.24 | convolution fusion | flops 164177920 | bytes 804864 | tf_op jit(solution)/shard_map/dot_general | solution.py:84
  3.5 1.3 %multiply_reduce_fusion.5 = (f32[256]{0:T(256)S(1)}, f32[256,320]{0,1:T(8,128)S(1)}) fusion(bf16[256,320]{0,1:T(8,128)(2,1)S(1)} %convolution_convert_fusion.2, bf16[1,320,320]{2,1,0:T(8,128)(2,1)} %param.10, f32[40,8,2,128]{3,2,1,0:T(2,128)S(1)} %bitcast.121), kind=kOutput, calls=%fused_computation.58 | convolution fusion | flops 52674304 | bytes 1025024 | tf_op jit(solution)/shard_map/dot_general | solution.py:17
  4.8 1.0 fusion.10
  5.8 5.8 %collective-permute-start = (bf16[256,320]{0,1:T(8,128)(2,1)S(1)}, bf16[256,320]{0,1:T(8,128)(2,1)S(1)}, u32[]{:S(2)}, u32[]{:S(2)}) collective-permute-start(bf16[256,320]{0,1:T(8,128)(2,1)S(1)} %fusion.10), channel_id=1, source_target_pairs={{0,24},{8,16},{1,25},{9,17},{2,26},{10,18},{3,27},{11,19},{4,28},{... | collective-permute-start | bytes 491528 | tf_op jit(solution)/shard_map/ppermute | solution.py:89
  11.7 1.4 %collective-permute-start.3 = (bf16[320,320]{1,0:T(8,128)(2,1)}, bf16[320,320]{1,0:T(8,128)(2,1)}, u32[]{:S(2)}, u32[]{:S(2)}) collective-permute-start(bf16[320,320]{1,0:T(8,128)(2,1)} %bitcast.1), channel_id=1, source_target_pairs={{16,8},{17,9},{18,10},{19,11},{20,12},{21,13},{22,14},{23,15}} | collective-permute-start | bytes 614408 | tf_op jit(solution)/shard_map/ppermute | solution.py:90
  13.0 2.1 %collective-permute-done = bf16[256,320]{0,1:T(8,128)(2,1)S(1)} collective-permute-done((bf16[256,320]{0,1:T(8,128)(2,1)S(1)}, bf16[256,320]{0,1:T(8,128)(2,1)S(1)}, u32[]{:S(2)}, u32[]{:S(2)}) %collective-permute-start) | collective-permute-done | bytes 163872 | tf_op jit(solution)/shard_map/ppermute | solution.py:89
  15.1 1.3 %multiply_reduce_fusion.4 = (f32[256]{0:T(256)S(1)}, f32[256,320]{0,1:T(8,128)S(1)}) fusion(bf16[1,320,320]{2,1,0:T(8,128)(2,1)} %param.10, bf16[256,320]{0,1:T(8,128)(2,1)S(1)} %collective-permute-done, bf16[256,320]{0,1:T(8,128)(2,1)S(1)} %convolution_convert_fusion.2, pred[]{:T(512)S(6)} %ge.3, f32[40,8,2,128]{3,2,1,0:T(2,128)S(1)} %bitcast.122), kind=kOutput, calls=%fused_computation.56 | convolution fusion | flops 52756224 | bytes 1188865 | tf_op jit(solution)/shard_map/dot_general | solution.py:17
  16.4 0.8 constant_dynamic-update-slice_fusion.15
  17.2 1.7 %add_multiply_fusion = f32[256,1280]{1,0:T(8,128)S(1)} fusion(bf16[256,320]{0,1:T(8,128)(2,1)} %get-tuple-element.18, bf16[1,1280,320]{1,2,0:T(8,128)(2,1)S(1)} %copy-done), kind=kOutput, calls=%fused_computation.12 | convolution fusion | flops 212008960 | bytes 2293760 | tf_op jit(solution)/shard_map/dot_general | solution.py:11
  18.9 1.6 %collective-permute-start.17 = (bf16[256,320]{0,1:T(8,128)(2,1)}, bf16[256,320]{0,1:T(8,128)(2,1)}, u32[]{:S(2)}, u32[]{:S(2)}) collective-permute-start(bf16[256,320]{0,1:T(8,128)(2,1)} %get-tuple-element.18), channel_id=1, source_target_pairs={{0,2},{1,3},{2,0},{3,1},{4,6},{5,7},{6,4},{7,5},{8,10},{9,11},{10,... | collective-permute-start | bytes 491528 | tf_op jit(solution)/shard_map/ppermute | solution.py:45
  20.5 2.6 %collective-permute-start.18 = (bf16[256,320]{0,1:T(8,128)(2,1)}, bf16[256,320]{0,1:T(8,128)(2,1)}, u32[]{:S(2)}, u32[]{:S(2)}) collective-permute-start(bf16[256,320]{0,1:T(8,128)(2,1)} %get-tuple-element.18), channel_id=1, source_target_pairs={{0,4},{1,5},{2,6},{3,7},{4,0},{5,1},{6,2},{7,3},{8,12},{9,13},{10,... | collective-permute-start | bytes 491528 | tf_op jit(solution)/shard_map/ppermute | solution.py:45
  23.1 0.2 collective-permute-start.19
  23.4 1.7 %multiply_reduce_fusion.3 = (f32[256]{0:T(256)S(1)}, f32[256,320]{0,1:T(8,128)}) fusion(f32[256,320]{0,1:T(8,128)S(1)} %get-tuple-element.25, bf16[1,1280,320]{1,2,0:T(8,128)(2,1)S(1)} %copy-done, f32[256,1280]{1,0:T(8,128)S(1)} %add_multiply_fusion, bf16[1,1280,320]{1,2,0:T(8,128)(2,1)S(1)} %copy-done.1, bf16[2,128,320]{1,2,0:T(8,128)(2,1)S(1)} %copy-done.2), kind=kOutput, calls=%fused_computation.54 | convolution fusion | flops 420249344 | bytes 3769344 | tf_op jit(solution)/shard_map/dot_general | solution.py:35
  25.1 1.0 %subtract_convert_fusion.3 = bf16[256,320]{0,1:T(8,128)(2,1)S(1)} fusion(f32[256,320]{0,1:T(8,128)} %get-tuple-element.27, f32[256,320]{0,1:T(8,128)S(1)} %get-tuple-element.25, f32[256]{0:T(256)S(1)} %broadcast_multiply_fusion.3, f32[256]{0:T(256)S(1)} %get-tuple-element.20, f32[256]{0:T(256)S(1)} %get-tuple-element.21, bf16[2,128,320]{1,2,0:T(8,128)(2,1)S(1)} %copy-done.2), kind=kLoop, calls=%fused_computation.53 | loop fusion | flops 573440 | bytes 986112 | tf_op jit(solution)/shard_map/convert_element_type | solution.py:41
  26.1 0.7 collective-permute-start.1
  26.8 1.9 %convolution_convert_fusion = bf16[256,320]{0,1:T(8,128)(2,1)} fusion(bf16[256,320]{0,1:T(8,128)(2,1)S(1)} %subtract_convert_fusion.3, bf16[1,320,320]{2,1,0:T(8,128)(2,1)} %param.10), kind=kOutput, calls=%fused_computation.21 | convolution fusion | flops 52510720 | bytes 532480 | tf_op jit(solution)/shard_map/dot_general | solution.py:11
  28.8 1.7 %multiply_reduce_fusion.2 = (f32[256]{0:T(256)S(1)}, f32[256,320]{0,1:T(8,128)}) fusion(f32[256,320]{0,1:T(8,128)S(1)} %get-tuple-element.25, bf16[1,1280,320]{1,2,0:T(8,128)(2,1)S(1)} %copy-done, f32[256,1280]{1,0:T(8,128)S(1)} %add_multiply_fusion, bf16[256,320]{0,1:T(8,128)(2,1)S(1)} %collective-permute-done.1, bf16[1,1280,320]{1,2,0:T(8,128)(2,1)S(1)} %copy-done.1), kind=kOutput, calls=%fused_computation.52 | convolution fusion | flops 420249344 | bytes 3769344 | tf_op jit(solution)/shard_map/dot_general | solution.py:35
  30.5 1.0 %subtract_convert_fusion.2 = bf16[256,320]{0,1:T(8,128)(2,1)S(1)} fusion(f32[256,320]{0,1:T(8,128)} %get-tuple-element.29, bf16[256,320]{0,1:T(8,128)(2,1)S(1)} %collective-permute-done.1, f32[256,320]{0,1:T(8,128)S(1)} %get-tuple-element.25, f32[256]{0:T(256)S(1)} %broadcast_multiply_fusion.2, f32[256]{0:T(256)S(1)} %get-tuple-element.20, ...), kind=kLoop, calls=%fused_computation.51 | loop fusion | flops 573440 | bytes 986112 | tf_op jit(solution)/shard_map/convert_element_type | solution.py:41
  31.5 1.3 %collective-permute-start.5 = (bf16[256,320]{0,1:T(8,128)(2,1)}, bf16[256,320]{0,1:T(8,128)(2,1)}, u32[]{:S(2)}, u32[]{:S(2)}) collective-permute-start(bf16[256,320]{0,1:T(8,128)(2,1)} %convolution_convert_fusion), channel_id=1, source_target_pairs={{24,0},{25,1},{26,2},{27,3},{28,4},{29,5},{30,6},{31,7}} | collective-permute-start | bytes 491528 | tf_op jit(solution)/shard_map/ppermute | solution.py:103
  32.8 1.6 %constant_dynamic-update-slice_fusion.14 = bf16[2048,320]{0,1:T(8,128)(2,1)} fusion(bf16[2048,320]{0,1:T(8,128)(2,1)} %get-tuple-element.17, bf16[256,320]{0,1:T(8,128)(2,1)} %collective-permute-done.17), kind=kLoop, calls=%fused_computation.97 | loop fusion | bytes 327680
  34.4 0.9 collective-permute-done.18
  35.4 0.7 collective-permute-start.2
  36.1 1.6 %constant_dynamic-update-slice_fusion.13 = bf16[2048,320]{0,1:T(8,128)(2,1)} fusion(bf16[2048,320]{0,1:T(8,128)(2,1)} %constant_dynamic-update-slice_fusion.14, bf16[256,320]{0,1:T(8,128)(2,1)} %collective-permute-done.18), kind=kLoop, calls=%fused_computation.96 | loop fusion | bytes 327680
  37.7 1.6 %constant_dynamic-update-slice_fusion.12 = bf16[2048,320]{0,1:T(8,128)(2,1)} fusion(bf16[2048,320]{0,1:T(8,128)(2,1)} %constant_dynamic-update-slice_fusion.13, bf16[256,320]{0,1:T(8,128)(2,1)} %collective-permute-done.19), kind=kLoop, calls=%fused_computation.95 | loop fusion | bytes 327680
  39.3 0.5 collective-permute-start.22
  39.8 1.6 %constant_dynamic-update-slice_fusion.11 = bf16[2048,320]{0,1:T(8,128)(2,1)} fusion(bf16[2048,320]{0,1:T(8,128)(2,1)} %constant_dynamic-update-slice_fusion.12, bf16[256,320]{0,1:T(8,128)(2,1)} %collective-permute-done.20), kind=kLoop, calls=%fused_computation.94 | loop fusion | bytes 327680
  41.4 1.9 %fusion.9 = f32[256,320]{0,1:T(8,128)} fusion(bf16[320,320]{1,0:T(8,128)(2,1)} %collective-permute-done.3, bf16[256,320]{0,1:T(8,128)(2,1)S(1)} %collective-permute-done.2), kind=kOutput, calls=%fused_computation.23 | convolution fusion | flops 52592640 | bytes 696320 | tf_op jit(solution)/shard_map/dot_general | solution.py:11
  43.3 2.7 %multiply_reduce_fusion.1 = (f32[256]{0:T(256)S(1)}, f32[256,320]{0,1:T(8,128)}) fusion(f32[256,320]{0,1:T(8,128)S(1)} %get-tuple-element.25, bf16[1,1280,320]{1,2,0:T(8,128)(2,1)S(1)} %copy-done, f32[256,1280]{1,0:T(8,128)S(1)} %add_multiply_fusion, bf16[1,1280,320]{1,2,0:T(8,128)(2,1)S(1)} %copy-done.1, f32[256,320]{0,1:T(8,128)} %fusion.9, ...), kind=kOutput, calls=%fused_computation.49 | convolution fusion | flops 420495104 | bytes 4097024 | tf_op jit(solution)/shard_map/dot_general | solution.py:35
  46.0 1.2 %subtract_convert_fusion.1 = bf16[256,320]{0,1:T(8,128)(2,1)S(1)} fusion(f32[256,320]{0,1:T(8,128)} %get-tuple-element.31, f32[256,320]{0,1:T(8,128)S(1)} %get-tuple-element.25, f32[256,320]{0,1:T(8,128)} %fusion.9, bf16[256,320]{0,1:T(8,128)(2,1)S(1)} %collective-permute-done.2, f32[256]{0:T(256)S(1)} %broadcast_multiply_fusion.1, ...), kind=kLoop, calls=%fused_computation.48 | loop fusion | flops 655360 | bytes 1313792 | tf_op jit(solution)/shard_map/convert_element_type | solution.py:41
  47.2 0.7 copy-done.8
  47.8 1.5 %collective-permute-start.4 = (bf16[256,320]{0,1:T(8,128)(2,1)S(1)}, bf16[256,320]{0,1:T(8,128)(2,1)}, u32[]{:S(2)}, u32[]{:S(2)}) collective-permute-start(bf16[256,320]{0,1:T(8,128)(2,1)S(1)} %subtract_convert_fusion.1), channel_id=1, source_target_pairs={{8,0},{9,1},{10,2},{11,3},{12,4},{13,5},{14,6},{15,7}} | collective-permute-start | bytes 491528 | tf_op jit(solution)/shard_map/ppermute | solution.py:110
  49.3 1.6 %constant_dynamic-update-slice_fusion.10 = bf16[2048,320]{0,1:T(8,128)(2,1)} fusion(bf16[2048,320]{0,1:T(8,128)(2,1)} %constant_dynamic-update-slice_fusion.11, bf16[256,320]{0,1:T(8,128)(2,1)} %collective-permute-done.21), kind=kLoop, calls=%fused_computation.93 | loop fusion | bytes 327680
  51.0 1.6 %constant_dynamic-update-slice_fusion.9 = bf16[2048,320]{0,1:T(8,128)(2,1)} fusion(bf16[2048,320]{0,1:T(8,128)(2,1)} %constant_dynamic-update-slice_fusion.10, bf16[256,320]{0,1:T(8,128)(2,1)} %collective-permute-done.22), kind=kLoop, calls=%fused_computation.92 | loop fusion | bytes 327680
  52.6 1.6 %constant_dynamic-update-slice_fusion.8 = bf16[2048,320]{0,1:T(8,128)(2,1)} fusion(bf16[2048,320]{0,1:T(8,128)(2,1)} %constant_dynamic-update-slice_fusion.9, bf16[256,320]{0,1:T(8,128)(2,1)} %collective-permute-done.23), kind=kLoop, calls=%fused_computation.91 | loop fusion | bytes 327680 | tf_op jit(solution)/shard_map/concatenate | solution.py:53
  54.2 7.0 %collective-permute-done.4 = bf16[256,320]{0,1:T(8,128)(2,1)} collective-permute-done((bf16[256,320]{0,1:T(8,128)(2,1)S(1)}, bf16[256,320]{0,1:T(8,128)(2,1)}, u32[]{:S(2)}, u32[]{:S(2)}) %collective-permute-start.4) | collective-permute-done | bytes 163872 | tf_op jit(solution)/shard_map/ppermute | solution.py:110
  61.2 2.7 %multiply_reduce_fusion = (f32[256]{0:T(256)S(1)}, f32[256,320]{0,1:T(8,128)}) fusion(f32[256,320]{0,1:T(8,128)S(1)} %get-tuple-element.25, bf16[1,1280,320]{1,2,0:T(8,128)(2,1)S(1)} %copy-done, f32[256,1280]{1,0:T(8,128)S(1)} %add_multiply_fusion, bf16[1,1280,320]{1,2,0:T(8,128)(2,1)S(1)} %copy-done.1, bf16[256,320]{0,1:T(8,128)(2,1)} %collective-permute-done.5, ...), kind=kOutput, calls=%fused_computation.46 | convolution fusion | flops 420577024 | bytes 3933184 | tf_op jit(solution)/shard_map/dot_general | solution.py:35
  63.9 2.3 %constant_dynamic-update-slice_fusion.7 = (bf16[2048,320]{0,1:T(8,128)(2,1)}, bf16[256,320]{0,1:T(8,128)(2,1)S(1)}, bf16[256,320]{0,1:T(8,128)(2,1)S(1)}) fusion(bf16[256,320]{0,1:T(8,128)(2,1)} %copy-done.3, pred[]{:T(512)S(6)} %eq.32, f32[256,320]{0,1:T(8,128)} %fusion.9, bf16[256,320]{0,1:T(8,128)(2,1)S(1)} %collective-permute-done.2, pred[]{:T(512)S(6)} %eq.31, ...), kind=kLoop, calls=%fused_computation.90 | loop fusion | flops 1556479 | bytes 2788355
  66.3 0.3 fusion.58
  66.5 0.4 reshape_reshape.3
  67.4 1.1 %collective-permute-done.6 = bf16[4,12800]{1,0:T(4,128)(2,1)S(1)} collective-permute-done((bf16[4,12800]{1,0:T(4,128)(2,1)S(1)}, bf16[4,12800]{1,0:T(4,128)(2,1)S(1)}, u32[]{:S(2)}, u32[]{:S(2)}) %collective-permute-start.6) | collective-permute-done | bytes 102432 | tf_op jit(solution)/shard_map/ppermute | solution.py:45
  68.6 0.4 convert_reduce_fusion.2
  69.1 0.7 collective-permute-start.7
  69.8 3.5 %collective-permute-start.8 = (bf16[12800]{0:T(1024)(128)(2,1)S(1)}, bf16[12800]{0:T(1024)(128)(2,1)}, u32[]{:S(2)}, u32[]{:S(2)}) collective-permute-start(bf16[12800]{0:T(1024)(128)(2,1)S(1)} %get-tuple-element.14), channel_id=1, source_target_pairs={{0,4},{1,5},{2,6},{3,7},{4,0},{5,1},{6,2},{7,3},{8,12},{9,13},{10,... | collective-permute-start | bytes 76808 | tf_op jit(solution)/shard_map/ppermute | solution.py:45
  73.3 0.2 collective-permute-start.9
  73.5 3.0 %fusion.44 = f32[2048,160]{0,1:T(8,128)} fusion(bf16[2048,320]{0,1:T(8,128)(2,1)} %constant_dynamic-update-slice_fusion.8, bf16[1,1280,320]{1,2,0:T(8,128)(2,1)S(1)} %copy-done, s32[]{:T(128)S(6)} %select_n.92), kind=kOutput, calls=%fused_computation.68 | convolution fusion | flops 209715200 | bytes 2785284 | tf_op jit(solution)/shard_map/dot_general | solution.py:11
  76.5 0.4 collective-permute-start.10
  76.9 3.8 %collective-permute-start.11 = (bf16[256,320]{0,1:T(8,128)(2,1)S(1)}, bf16[256,320]{0,1:T(8,128)(2,1)S(1)}, u32[]{:S(2)}, u32[]{:S(2)}) collective-permute-start(bf16[256,320]{0,1:T(8,128)(2,1)S(1)} %get-tuple-element.16), channel_id=1, source_target_pairs={{0,4},{1,5},{2,6},{3,7},{4,0},{5,1},{6,2},{7,3},{8,12},{9,13},{10,... | collective-permute-start | bytes 491528 | tf_op jit(solution)/shard_map/ppermute | solution.py:45
  80.8 0.7 copy.17
  81.6 0.3 collective-permute-start.12
  81.9 0.9 convert_add_fusion.2
  82.8 0.7 broadcast_in_dim.6
  83.4 1.3 %collective-permute-done.10 = bf16[256,320]{0,1:T(8,128)(2,1)S(1)} collective-permute-done((bf16[256,320]{0,1:T(8,128)(2,1)S(1)}, bf16[256,320]{0,1:T(8,128)(2,1)S(1)}, u32[]{:S(2)}, u32[]{:S(2)}) %collective-permute-start.10) | collective-permute-done | bytes 163872 | tf_op jit(solution)/shard_map/ppermute | solution.py:45
  84.8 0.7 constant_dynamic-update-slice_fusion.6
  85.5 7.3 %collective-permute-done.11 = bf16[256,320]{0,1:T(8,128)(2,1)S(1)} collective-permute-done((bf16[256,320]{0,1:T(8,128)(2,1)S(1)}, bf16[256,320]{0,1:T(8,128)(2,1)S(1)}, u32[]{:S(2)}, u32[]{:S(2)}) %collective-permute-start.11) | collective-permute-done | bytes 163872 | tf_op jit(solution)/shard_map/ppermute | solution.py:45
  92.7 0.7 constant_dynamic-update-slice_fusion.5
  93.4 0.5 collective-permute-start.16
  93.9 0.7 constant_dynamic-update-slice_fusion.4
  94.7 0.7 constant_dynamic-update-slice_fusion.3
  95.4 0.7 constant_dynamic-update-slice_fusion.2
  96.1 0.7 constant_dynamic-update-slice_fusion.1
  96.8 0.7 constant_dynamic-update-slice_fusion
  97.5 2.6 %convolution_bitcast_fusion = f32[1,160,320]{2,1,0:T(8,128)} fusion(bf16[2048,320]{0,1:T(8,128)(2,1)} %constant_dynamic-update-slice_fusion, f32[2048,160]{0,1:T(8,128)S(1)} %copy-done.7), kind=kOutput, calls=%fused_computation.26 | convolution fusion | flops 211353600 | bytes 2826240 | tf_op jit(solution)/shard_map/dot_general | solution.py:11
  100.1 3.7 %convolution_bitcast_fusion.1 = f32[1,160,320]{2,1,0:T(8,128)} fusion(bf16[2048,320]{0,1:T(8,128)(2,1)} %constant_dynamic-update-slice_fusion.8, bf16[2048,320]{0,1:T(8,128)(2,1)} %constant_dynamic-update-slice_fusion, f32[2048,160]{0,1:T(8,128)S(1)} %copy-done.7, bf16[1,1280,320]{1,2,0:T(8,128)(2,1)S(1)} %copy-done.1, s32[]{:T(128)S(6)} %select_n.92), kind=kOutput, calls=%fused_computation.27 | convolution fusion | flops 422379520 | bytes 4300804 | tf_op jit(solution)/shard_map/dot_general | solution.py:11
  (60 shorter events, 1.0 us)
Async XLA Ops:
  0.6 4.2 %copy-start = (bf16[1,1280,320]{1,2,0:T(8,128)(2,1)S(1)}, bf16[1,1280,320]{1,2,0:T(8,128)(2,1)}, u32[]{:S(2)}) copy-start(bf16[1,1280,320]{1,2,0:T(8,128)(2,1)} %param.11) | copy-start | bytes 2457604
  1.8 3.0 %copy-start.1 = (bf16[1,1280,320]{1,2,0:T(8,128)(2,1)S(1)}, bf16[1,1280,320]{1,2,0:T(8,128)(2,1)}, u32[]{:S(2)}) copy-start(bf16[1,1280,320]{1,2,0:T(8,128)(2,1)} %param.12) | copy-start | bytes 2457604
  3.5 11.6 %copy-start.5 = (bf16[256,320]{0,1:T(8,128)(2,1)}, bf16[256,320]{0,1:T(8,128)(2,1)S(1)}, u32[]{:S(2)}) copy-start(bf16[256,320]{0,1:T(8,128)(2,1)S(1)} %convolution_convert_fusion.2) | copy-start | bytes 491524
  5.8 9.3 %collective-permute-start = (bf16[256,320]{0,1:T(8,128)(2,1)S(1)}, bf16[256,320]{0,1:T(8,128)(2,1)S(1)}, u32[]{:S(2)}, u32[]{:S(2)}) collective-permute-start(bf16[256,320]{0,1:T(8,128)(2,1)S(1)} %fusion.10), channel_id=1, source_target_pairs={{0,24},{8,16},{1,25},{9,17},{2,26},{10,18},{3,27},{11,19},{4,28},{... | collective-permute-start | bytes 491528 | tf_op jit(solution)/shard_map/ppermute | solution.py:89
  11.7 29.7 %collective-permute-start.3 = (bf16[320,320]{1,0:T(8,128)(2,1)}, bf16[320,320]{1,0:T(8,128)(2,1)}, u32[]{:S(2)}, u32[]{:S(2)}) collective-permute-start(bf16[320,320]{1,0:T(8,128)(2,1)} %bitcast.1), channel_id=1, source_target_pairs={{16,8},{17,9},{18,10},{19,11},{20,12},{21,13},{22,14},{23,15}} | collective-permute-start | bytes 614408 | tf_op jit(solution)/shard_map/ppermute | solution.py:90
  15.1 2.1 %copy-start.10 = (bf16[256,320]{0,1:T(8,128)(2,1)}, bf16[256,320]{0,1:T(8,128)(2,1)S(1)}, u32[]{:S(2)}) copy-start(bf16[256,320]{0,1:T(8,128)(2,1)S(1)} %collective-permute-done) | copy-start | bytes 491524
  17.2 6.1 %copy-start.2 = (bf16[2,128,320]{1,2,0:T(8,128)(2,1)S(1)}, bf16[2,128,320]{1,2,0:T(8,128)(2,1)}, u32[]{:S(2)}) copy-start(bf16[2,128,320]{1,2,0:T(8,128)(2,1)} %param.13) | copy-start | bytes 491524
  18.9 12.6 %collective-permute-start.17 = (bf16[256,320]{0,1:T(8,128)(2,1)}, bf16[256,320]{0,1:T(8,128)(2,1)}, u32[]{:S(2)}, u32[]{:S(2)}) collective-permute-start(bf16[256,320]{0,1:T(8,128)(2,1)} %get-tuple-element.18), channel_id=1, source_target_pairs={{0,2},{1,3},{2,0},{3,1},{4,6},{5,7},{6,4},{7,5},{8,10},{9,11},{10,... | collective-permute-start | bytes 491528 | tf_op jit(solution)/shard_map/ppermute | solution.py:45
  20.5 14.8 %collective-permute-start.18 = (bf16[256,320]{0,1:T(8,128)(2,1)}, bf16[256,320]{0,1:T(8,128)(2,1)}, u32[]{:S(2)}, u32[]{:S(2)}) collective-permute-start(bf16[256,320]{0,1:T(8,128)(2,1)} %get-tuple-element.18), channel_id=1, source_target_pairs={{0,4},{1,5},{2,6},{3,7},{4,0},{5,1},{6,2},{7,3},{8,12},{9,13},{10,... | collective-permute-start | bytes 491528 | tf_op jit(solution)/shard_map/ppermute | solution.py:45
  23.1 14.5 %collective-permute-start.19 = (bf16[256,320]{0,1:T(8,128)(2,1)}, bf16[256,320]{0,1:T(8,128)(2,1)}, u32[]{:S(2)}, u32[]{:S(2)}) collective-permute-start(bf16[256,320]{0,1:T(8,128)(2,1)} %get-tuple-element.18), channel_id=1, source_target_pairs={{0,6},{1,7},{2,4},{3,5},{4,2},{5,3},{6,0},{7,1},{8,14},{9,15},{10,... | collective-permute-start | bytes 491528 | tf_op jit(solution)/shard_map/ppermute | solution.py:45
  26.1 2.6 %copy-start.4 = (bf16[256,320]{0,1:T(8,128)(2,1)}, bf16[256,320]{0,1:T(8,128)(2,1)S(1)}, u32[]{:S(2)}) copy-start(bf16[256,320]{0,1:T(8,128)(2,1)S(1)} %subtract_convert_fusion.3) | copy-start | bytes 491524
  26.1 2.5 %collective-permute-start.1 = (bf16[256,320]{0,1:T(8,128)(2,1)S(1)}, bf16[256,320]{0,1:T(8,128)(2,1)S(1)}, u32[]{:S(2)}, u32[]{:S(2)}) collective-permute-start(bf16[256,320]{0,1:T(8,128)(2,1)S(1)} %subtract_convert_fusion.3), channel_id=1, source_target_pairs={{24,16},{25,17},{26,18},{27,19},{28,20},{29,21},{30,22},{31,23}} | collective-permute-start | bytes 491528 | tf_op jit(solution)/shard_map/ppermute | solution.py:110
  28.7 5.8 %copy-start.3 = (bf16[256,320]{0,1:T(8,128)(2,1)}, bf16[256,320]{0,1:T(8,128)(2,1)S(1)}, u32[]{:S(2)}) copy-start(bf16[256,320]{0,1:T(8,128)(2,1)S(1)} %collective-permute-done.1) | copy-start | bytes 491524
  28.7 10.6 %collective-permute-start.20 = (bf16[256,320]{0,1:T(8,128)(2,1)}, bf16[256,320]{0,1:T(8,128)(2,1)}, u32[]{:S(2)}, u32[]{:S(2)}) collective-permute-start(bf16[256,320]{0,1:T(8,128)(2,1)} %get-tuple-element.18), channel_id=1, source_target_pairs={{0,1},{1,0},{2,3},{3,2},{4,5},{5,4},{6,7},{7,6},{8,9},{9,8},{10,11... | collective-permute-start | bytes 491528 | tf_op jit(solution)/shard_map/ppermute | solution.py:45
  31.5 9.9 %copy-start.9 = (bf16[256,320]{0,1:T(8,128)(2,1)}, bf16[256,320]{0,1:T(8,128)(2,1)S(1)}, u32[]{:S(2)}) copy-start(bf16[256,320]{0,1:T(8,128)(2,1)S(1)} %subtract_convert_fusion.2) | copy-start | bytes 491524
  31.5 22.6 %collective-permute-start.5 = (bf16[256,320]{0,1:T(8,128)(2,1)}, bf16[256,320]{0,1:T(8,128)(2,1)}, u32[]{:S(2)}, u32[]{:S(2)}) collective-permute-start(bf16[256,320]{0,1:T(8,128)(2,1)} %convolution_convert_fusion), channel_id=1, source_target_pairs={{24,0},{25,1},{26,2},{27,3},{28,4},{29,5},{30,6},{31,7}} | collective-permute-start | bytes 491528 | tf_op jit(solution)/shard_map/ppermute | solution.py:103
  35.4 6.0 %collective-permute-start.2 = (bf16[256,320]{0,1:T(8,128)(2,1)S(1)}, bf16[256,320]{0,1:T(8,128)(2,1)S(1)}, u32[]{:S(2)}, u32[]{:S(2)}) collective-permute-start(bf16[256,320]{0,1:T(8,128)(2,1)S(1)} %subtract_convert_fusion.2), channel_id=1, source_target_pairs={{16,8},{17,9},{18,10},{19,11},{20,12},{21,13},{22,14},{23,15}} | collective-permute-start | bytes 491528 | tf_op jit(solution)/shard_map/ppermute | solution.py:110
  37.7 11.6 %collective-permute-start.21 = (bf16[256,320]{0,1:T(8,128)(2,1)}, bf16[256,320]{0,1:T(8,128)(2,1)}, u32[]{:S(2)}, u32[]{:S(2)}) collective-permute-start(bf16[256,320]{0,1:T(8,128)(2,1)} %collective-permute-done.17), channel_id=1, source_target_pairs={{0,1},{1,0},{2,3},{3,2},{4,5},{5,4},{6,7},{7,6},{8,9},{9,8},{10,11... | collective-permute-start | bytes 491528 | tf_op jit(solution)/shard_map/ppermute | solution.py:45
  39.3 11.7 %collective-permute-start.22 = (bf16[256,320]{0,1:T(8,128)(2,1)}, bf16[256,320]{0,1:T(8,128)(2,1)}, u32[]{:S(2)}, u32[]{:S(2)}) collective-permute-start(bf16[256,320]{0,1:T(8,128)(2,1)} %collective-permute-done.18), channel_id=1, source_target_pairs={{0,1},{1,0},{2,3},{3,2},{4,5},{5,4},{6,7},{7,6},{8,9},{9,8},{10,11... | collective-permute-start | bytes 491528 | tf_op jit(solution)/shard_map/ppermute | solution.py:45
  41.4 11.2 %collective-permute-start.23 = (bf16[256,320]{0,1:T(8,128)(2,1)}, bf16[256,320]{0,1:T(8,128)(2,1)}, u32[]{:S(2)}, u32[]{:S(2)}) collective-permute-start(bf16[256,320]{0,1:T(8,128)(2,1)} %collective-permute-done.19), channel_id=1, source_target_pairs={{0,1},{1,0},{2,3},{3,2},{4,5},{5,4},{6,7},{7,6},{8,9},{9,8},{10,11... | collective-permute-start | bytes 491528 | tf_op jit(solution)/shard_map/ppermute | solution.py:45
  47.2 0.7 copy-start.8
  47.8 13.4 %collective-permute-start.4 = (bf16[256,320]{0,1:T(8,128)(2,1)S(1)}, bf16[256,320]{0,1:T(8,128)(2,1)}, u32[]{:S(2)}, u32[]{:S(2)}) collective-permute-start(bf16[256,320]{0,1:T(8,128)(2,1)S(1)} %subtract_convert_fusion.1), channel_id=1, source_target_pairs={{8,0},{9,1},{10,2},{11,3},{12,4},{13,5},{14,6},{15,7}} | collective-permute-start | bytes 491528 | tf_op jit(solution)/shard_map/ppermute | solution.py:110
  63.9 2.3 %copy-start.6 = (bf16[256,320]{0,1:T(8,128)(2,1)S(1)}, bf16[256,320]{0,1:T(8,128)(2,1)}, u32[]{:S(2)}) copy-start(bf16[256,320]{0,1:T(8,128)(2,1)} %copy-done.5) | copy-start | bytes 491524
  63.9 2.3 %copy-start.11 = (bf16[256,320]{0,1:T(8,128)(2,1)S(1)}, bf16[256,320]{0,1:T(8,128)(2,1)}, u32[]{:S(2)}) copy-start(bf16[256,320]{0,1:T(8,128)(2,1)} %copy-done.10) | copy-start | bytes 491524
  67.2 1.4 %collective-permute-start.6 = (bf16[4,12800]{1,0:T(4,128)(2,1)S(1)}, bf16[4,12800]{1,0:T(4,128)(2,1)S(1)}, u32[]{:S(2)}, u32[]{:S(2)}) collective-permute-start(bf16[4,12800]{1,0:T(4,128)(2,1)S(1)} %bitcast.123), channel_id=1, source_target_pairs={{0,1},{1,0},{2,3},{3,2},{4,5},{5,4},{6,7},{7,6},{8,9},{9,8},{10,11... | collective-permute-start | bytes 307208 | tf_op jit(solution)/shard_map/ppermute | solution.py:45
  69.1 12.5 %collective-permute-start.7 = (bf16[12800]{0:T(1024)(128)(2,1)S(1)}, bf16[12800]{0:T(1024)(128)(2,1)S(1)}, u32[]{:S(2)}, u32[]{:S(2)}) collective-permute-start(bf16[12800]{0:T(1024)(128)(2,1)S(1)} %get-tuple-element.12), channel_id=1, source_target_pairs={{0,2},{1,3},{2,0},{3,1},{4,6},{5,7},{6,4},{7,5},{8,10},{9,11},{10,... | collective-permute-start | bytes 76808 | tf_op jit(solution)/shard_map/ppermute | solution.py:45
  69.8 12.1 %collective-permute-start.8 = (bf16[12800]{0:T(1024)(128)(2,1)S(1)}, bf16[12800]{0:T(1024)(128)(2,1)}, u32[]{:S(2)}, u32[]{:S(2)}) collective-permute-start(bf16[12800]{0:T(1024)(128)(2,1)S(1)} %get-tuple-element.14), channel_id=1, source_target_pairs={{0,4},{1,5},{2,6},{3,7},{4,0},{5,1},{6,2},{7,3},{8,12},{9,13},{10,... | collective-permute-start | bytes 76808 | tf_op jit(solution)/shard_map/ppermute | solution.py:45
  73.3 8.6 %collective-permute-start.9 = (bf16[12800]{0:T(1024)(128)(2,1)S(1)}, bf16[12800]{0:T(1024)(128)(2,1)}, u32[]{:S(2)}, u32[]{:S(2)}) collective-permute-start(bf16[12800]{0:T(1024)(128)(2,1)S(1)} %get-tuple-element.13), channel_id=1, source_target_pairs={{0,6},{1,7},{2,4},{3,5},{4,2},{5,3},{6,0},{7,1},{8,14},{9,15},{10,... | collective-permute-start | bytes 76808 | tf_op jit(solution)/shard_map/ppermute | solution.py:45
  76.5 8.2 %collective-permute-start.10 = (bf16[256,320]{0,1:T(8,128)(2,1)S(1)}, bf16[256,320]{0,1:T(8,128)(2,1)S(1)}, u32[]{:S(2)}, u32[]{:S(2)}) collective-permute-start(bf16[256,320]{0,1:T(8,128)(2,1)S(1)} %get-tuple-element.16), channel_id=1, source_target_pairs={{0,2},{1,3},{2,0},{3,1},{4,6},{5,7},{6,4},{7,5},{8,10},{9,11},{10,... | collective-permute-start | bytes 491528 | tf_op jit(solution)/shard_map/ppermute | solution.py:45
  76.9 15.8 %collective-permute-start.11 = (bf16[256,320]{0,1:T(8,128)(2,1)S(1)}, bf16[256,320]{0,1:T(8,128)(2,1)S(1)}, u32[]{:S(2)}, u32[]{:S(2)}) collective-permute-start(bf16[256,320]{0,1:T(8,128)(2,1)S(1)} %get-tuple-element.16), channel_id=1, source_target_pairs={{0,4},{1,5},{2,6},{3,7},{4,0},{5,1},{6,2},{7,3},{8,12},{9,13},{10,... | collective-permute-start | bytes 491528 | tf_op jit(solution)/shard_map/ppermute | solution.py:45
  81.6 15.9 %copy-start.7 = (f32[2048,160]{0,1:T(8,128)S(1)}, f32[2048,160]{0,1:T(8,128)}, u32[]{:S(2)}) copy-start(f32[2048,160]{0,1:T(8,128)} %fusion.44) | copy-start | bytes 3932164
  81.6 11.8 %collective-permute-start.12 = (bf16[256,320]{0,1:T(8,128)(2,1)S(1)}, bf16[256,320]{0,1:T(8,128)(2,1)S(1)}, u32[]{:S(2)}, u32[]{:S(2)}) collective-permute-start(bf16[256,320]{0,1:T(8,128)(2,1)S(1)} %get-tuple-element.16), channel_id=1, source_target_pairs={{0,6},{1,7},{2,4},{3,5},{4,2},{5,3},{6,0},{7,1},{8,14},{9,15},{10,... | collective-permute-start | bytes 491528 | tf_op jit(solution)/shard_map/ppermute | solution.py:45
  81.9 12.8 %collective-permute-start.13 = (bf16[256,320]{0,1:T(8,128)(2,1)S(1)}, bf16[256,320]{0,1:T(8,128)(2,1)S(1)}, u32[]{:S(2)}, u32[]{:S(2)}) collective-permute-start(bf16[256,320]{0,1:T(8,128)(2,1)S(1)} %get-tuple-element.16), channel_id=1, source_target_pairs={{0,1},{1,0},{2,3},{3,2},{4,5},{5,4},{6,7},{7,6},{8,9},{9,8},{10,11... | collective-permute-start | bytes 491528 | tf_op jit(solution)/shard_map/ppermute | solution.py:45
  84.8 10.6 %collective-permute-start.14 = (bf16[256,320]{0,1:T(8,128)(2,1)S(1)}, bf16[256,320]{0,1:T(8,128)(2,1)S(1)}, u32[]{:S(2)}, u32[]{:S(2)}) collective-permute-start(bf16[256,320]{0,1:T(8,128)(2,1)S(1)} %collective-permute-done.10), channel_id=1, source_target_pairs={{0,1},{1,0},{2,3},{3,2},{4,5},{5,4},{6,7},{7,6},{8,9},{9,8},{10,11... | collective-permute-start | bytes 491528 | tf_op jit(solution)/shard_map/ppermute | solution.py:45
  92.7 3.3 %collective-permute-start.15 = (bf16[256,320]{0,1:T(8,128)(2,1)S(1)}, bf16[256,320]{0,1:T(8,128)(2,1)S(1)}, u32[]{:S(2)}, u32[]{:S(2)}) collective-permute-start(bf16[256,320]{0,1:T(8,128)(2,1)S(1)} %collective-permute-done.11), channel_id=1, source_target_pairs={{0,1},{1,0},{2,3},{3,2},{4,5},{5,4},{6,7},{7,6},{8,9},{9,8},{10,11... | collective-permute-start | bytes 491528 | tf_op jit(solution)/shard_map/ppermute | solution.py:45
  93.4 3.3 %collective-permute-start.16 = (bf16[256,320]{0,1:T(8,128)(2,1)S(1)}, bf16[256,320]{0,1:T(8,128)(2,1)S(1)}, u32[]{:S(2)}, u32[]{:S(2)}) collective-permute-start(bf16[256,320]{0,1:T(8,128)(2,1)S(1)} %collective-permute-done.12), channel_id=1, source_target_pairs={{0,1},{1,0},{2,3},{3,2},{4,5},{5,4},{6,7},{7,6},{8,9},{9,8},{10,11... | collective-permute-start | bytes 491528 | tf_op jit(solution)/shard_map/ppermute | solution.py:45

commit v2 on v1

v2 whole, which is shorter than its diff:
```python
import jax
import jax.numpy as jnp
from jax import lax
from jax.experimental import pallas as pl
from jax.experimental.pallas import tpu as pltpu
from jax.sharding import PartitionSpec as P

EPS = 1e-06
LOW = jnp.bfloat16
F32 = jnp.float32
VMEM_BYTES = 20 * 1024 * 1024


def contract(left, right, dims):
    return lax.dot_general(left, right, ((dims[0], dims[1]), ((), ())), preferred_element_type=F32)


def dot(left, right, on_left, on_right):
    return contract(left, right, ((on_left,), (on_right,)))


def call(body, outs, *args):
    specs = [
        pl.BlockSpec(memory_space=pltpu.SMEM if arg.ndim == 1 else pltpu.VMEM) for arg in args
    ]
    return pl.pallas_call(
        body,
        out_shape=[jax.ShapeDtypeStruct(shape, kind) for shape, kind in outs],
        in_specs=specs,
        out_specs=[pl.BlockSpec(memory_space=pltpu.VMEM) for _ in outs],
        compiler_params=pltpu.CompilerParams(vmem_limit_bytes=VMEM_BYTES),
    )(*args)


def side_by_side(ref):
    return jnp.concatenate([ref[m] for m in range(ref.shape[0])], axis=1)


def norm_of(united):
    return lax.rsqrt(jnp.mean(united * united, axis=0, keepdims=True) + EPS)


def sigmoid(value):
    return 1.0 / (1.0 + jnp.exp(-value))


def encode_body(times, table, inputs, w_skip, w_in, w_out, embed_out, value_out):
    levels = lax.broadcasted_iota(jnp.int32, (table.shape[1], times.shape[1]), 0)
    hot = [
        jnp.where(levels == times[m : m + 1, :], 1.0, 0.0).astype(LOW)
        for m in range(times.shape[0])
    ]
    embed = dot(table[...], jnp.concatenate(hot, axis=1), 1, 0).astype(LOW)
    embed_out[...] = embed
    united = side_by_side(inputs).astype(F32) + dot(w_skip[...], embed, 0, 0)
    normed = (united * norm_of(united)).astype(LOW)
    preact = dot(w_in[...], normed, 0, 0)
    active = (preact * sigmoid(preact)).astype(LOW)
    value_out[...] = (united + dot(w_out[...], active, 1, 0)).astype(LOW)


def back_through(grad_out, grad_low, united, slope, w_in, w_out):
    grad_pre = (dot(w_out[...], grad_low, 0, 0) * slope).astype(LOW)
    grad_norm = dot(w_in[...], grad_pre, 1, 0)
    recip = norm_of(united)
    along = jnp.mean(grad_norm * united, axis=0, keepdims=True)
    return (grad_out + recip * grad_norm - united * (recip * recip * recip * along)).astype(LOW)


def decode_body(
    flags, received, embed, inputs, upstream, w_skip, w_in, w_out,
    source_out, normed_out, united_out, slope_out, chain_out,
):
    source = jnp.where(flags[0] >= 2, received[...], embed[...])
    source_out[...] = source
    united = side_by_side(inputs).astype(F32) + dot(w_skip[...], source, 0, 0)
    united_out[...] = united
    normed = (united * norm_of(united)).astype(LOW)
    normed_out[...] = normed
    preact = dot(w_in[...], normed, 0, 0)
    sigma = sigmoid(preact)
    slope = sigma * (1.0 + preact * (1.0 - sigma))
    slope_out[...] = slope
    low = side_by_side(upstream)
    chain_out[...] = back_through(low.astype(F32), low, united, slope, w_in, w_out)


def back_body(chain, w_skip, back_out):
    back_out[...] = dot(w_skip[...], chain[...], 1, 0).astype(LOW)


def tick_body(received, united, slope, w_in, w_out, chain_out):
    low = received[...]
    chain_out[...] = back_through(low.astype(F32), low, united[...], slope[...], w_in, w_out)


def mirror_tick_body(received, w_mirror, united, slope, w_in, w_out, chain_out, low_out):
    back = dot(w_mirror[...], received[...], 1, 0).astype(LOW)
    grad_out = received[...].astype(F32) + back.astype(F32)
    low = grad_out.astype(LOW)
    low_out[...] = low
    chain_out[...] = back_through(grad_out, low, united[...], slope[...], w_in, w_out)


def pick_body(flags, received, skip_far, low_1, low_2, upstream, grad_low_out):
    own = (received[...].astype(F32) + skip_far[...].astype(F32)).astype(LOW)
    section = flags[0]
    own = jnp.where(section == 1, low_1[...], own)
    own = jnp.where(section == 2, low_2[...], own)
    grad_low_out[...] = jnp.where(section == 3, side_by_side(upstream), own)


def last_body(
    flags, received, skip_far, united, slope, w_in, w_out, source, chain_1, chain_2, chain_3,
    kept_out, keep_out, give_out, parts,
):
    grad_out = received[...].astype(F32) + skip_far[...].astype(F32)
    low = grad_out.astype(LOW)
    section = flags[0]
    kept = back_through(grad_out, low, united[...], slope[...], w_in, w_out)
    kept = jnp.where(section == 1, chain_1[...], kept)
    kept = jnp.where(section == 2, chain_2[...], kept)
    kept = jnp.where(section == 3, chain_3[...], kept)
    span = kept_out.shape[2]
    for m in range(kept_out.shape[0]):
        kept_out[m] = kept[:, m * span : (m + 1) * span]
    partial = dot(source[...], kept, 1, 1)
    size = parts.shape[2]
    for block in range(parts.shape[0]):
        for core in range(2):
            first = (2 * block + core) * size
            parts[block, core] = partial[first : first + size, :]
    core = flags[1]
    for block in range(parts.shape[0]):
        keep_out[block] = parts[block, core]
        give_out[block] = parts[block, 1 - core].astype(LOW)


def join_body(flags, keep, given, own_out, *piece_outs):
    chip = flags[2]
    own_out[...] = keep[chip] + given[chip].astype(F32)
    for mask, piece_out in enumerate(piece_outs, 1):
        far = chip ^ mask
        piece_out[...] = (keep[far] + given[far].astype(F32)).astype(LOW)


def slice_forward_body(own_in, *refs):
    count = len(refs) // 3
    for block in range(count):
        preact = dot(own_in[...], refs[block][...], 0, 0)
        sigma = sigmoid(preact)
        refs[count + block][...] = (preact * sigma).astype(LOW)
        refs[2 * count + block][...] = sigma * (1.0 + preact * (1.0 - sigma))


def slice_grad_body(own_out, *refs):
    count = (len(refs) - 2) // 4
    total_in = total_out = None
    for block in range(count):
        normed, active, slope, low = (refs[block + part * count][...] for part in range(4))
        grad_pre = (dot(own_out[...], low, 0, 0) * slope).astype(LOW)
        part_in = dot(grad_pre, normed, 1, 1)
        part_out = dot(active, low, 1, 1)
        total_in = part_in if total_in is None else total_in + part_in
        total_out = part_out if total_out is None else total_out + part_out
    refs[-2][...] = total_in
    refs[-1][...] = total_out


def exchange(value, count, mask):
    return lax.ppermute(value, "dp", [(i, i ^ mask) for i in range(count)])


def gather_blocks(value, count):
    blocks = [value] + [exchange(value, count, mask) for mask in range(2, count, 2)]
    return blocks + [exchange(block, count, 1) for block in blocks]


def shards(saved_inputs, timesteps, time_table, skip_weight, ff_in, ff_out, output_cotangent):
    section = lax.axis_index("section")
    place = lax.axis_index("dp")
    count = lax.axis_size("dp")
    n_micro = saved_inputs.shape[1]
    width = saved_inputs.shape[3]
    span = saved_inputs.shape[2]
    rows = n_micro * span
    hidden = ff_in.shape[1]
    flags = jnp.stack([section, place % 2, place // 2]).astype(jnp.int32)
    inputs = jnp.swapaxes(saved_inputs[0], 1, 2)
    upstream = jnp.swapaxes(output_cotangent, 1, 2)
    table = time_table.T
    w_skip = skip_weight[0]
    w_in = ff_in[0].T
    w_out = ff_out[0].T
    low = ((width, rows), LOW)
    wide = ((hidden, rows), F32)

    embed, value = call(encode_body, [low, low], timesteps, table, inputs, w_skip, w_in, w_out)
    received = lax.ppermute(value, "section", [(0, 3), (1, 2)])
    source, normed, united, slope, chain_3 = call(
        decode_body, [low, low, ((width, rows), F32), wide, low],
        flags, received, embed, inputs, upstream, w_skip, w_in, w_out,
    )
    chain = lax.ppermute(chain_3, "section", [(3, 2)])
    w_mirror = lax.ppermute(w_skip, "section", [(2, 1)])
    (back,) = call(back_body, [low], chain_3, w_skip)
    skip_far = lax.ppermute(back, "section", [(3, 0)])
    low_2 = chain
    (chain_2,) = call(tick_body, [low], chain, united, slope, w_in, w_out)
    chain = lax.ppermute(chain_2, "section", [(2, 1)])
    chain_1, low_1 = call(
        mirror_tick_body, [low, low], chain, w_mirror, united, slope, w_in, w_out
    )
    chain = lax.ppermute(chain_1, "section", [(1, 0)])
    (grad_low,) = call(pick_body, [low], flags, chain, skip_far, low_1, low_2, upstream)

    sliced = count * rows <= 4096 and count % 2 == 0 and width % count == 0
    if not sliced:
        return by_reduction(
            section, flags, chain, skip_far, united, slope, w_in, w_out, source, normed, grad_low,
            (chain_1, chain_2, chain_3), saved_inputs.shape,
        )

    part = hidden // count
    own_in = lax.dynamic_slice_in_dim(w_in, place * part, part, 1)
    own_out = lax.dynamic_slice_in_dim(w_out, place * part, part, 1)
    normed_all = gather_blocks(normed, count)
    forward_all = call(
        slice_forward_body, [((part, rows), LOW)] * count + [((part, rows), F32)] * count,
        own_in, *normed_all,
    )
    low_all = gather_blocks(grad_low, count)

    block = ((count // 2, width // count, width), F32)
    kept, keep, give = pl.pallas_call(
        last_body,
        out_shape=[
            jax.ShapeDtypeStruct((n_micro, width, span), LOW),
            jax.ShapeDtypeStruct(*block),
            jax.ShapeDtypeStruct(block[0], LOW),
        ],
        in_specs=[pl.BlockSpec(memory_space=pltpu.SMEM)]
        + [pl.BlockSpec(memory_space=pltpu.VMEM)] * 10,
        out_specs=[pl.BlockSpec(memory_space=pltpu.VMEM)] * 3,
        scratch_shapes=[pltpu.VMEM((count // 2, 2, width // count, width), F32)],
        compiler_params=pltpu.CompilerParams(vmem_limit_bytes=VMEM_BYTES),
    )(flags, chain, skip_far, united, slope, w_in, w_out, source, chain_1, chain_2, chain_3)
    given = exchange(give, count, 1)
    piece = block[0][1:]
    pieces = call(
        join_body, [(piece, F32)] + [(piece, LOW)] * (count // 2 - 1), flags, keep, given
    )
    grad_skip = pieces[0]
    for mask in range(1, count // 2):
        grad_skip = grad_skip + exchange(pieces[mask], count, 2 * mask).astype(F32)
    grad_in, grad_out_w = call(
        slice_grad_body, [((part, width), F32)] * 2, own_out, *normed_all, *forward_all, *low_all
    )
    kept = jnp.swapaxes(kept, 1, 2)
    return (kept[None], grad_skip.reshape(1, -1), grad_in[None], grad_out_w[None])


def by_reduction(
    section, flags, chain, skip_far, united, slope, w_in, w_out, source, normed, grad_low, chains,
    shape,
):
    grad_out = chain.astype(F32) + skip_far.astype(F32)
    grad_pre = (dot(w_out, grad_low, 0, 0) * slope).astype(LOW)
    preact = dot(w_in, normed, 0, 0)
    active = (preact * jax.nn.sigmoid(preact)).astype(LOW)
    own_pre = (dot(w_out, grad_out.astype(LOW), 0, 0) * slope).astype(LOW)
    grad_norm = dot(w_in, own_pre, 1, 0)
    recip = norm_of(united)
    along = jnp.mean(grad_norm * united, axis=0, keepdims=True)
    kept = (grad_out + recip * grad_norm - united * (recip * recip * recip * along)).astype(LOW)
    for owner, other in enumerate(chains, 1):
        kept = jnp.where(section == owner, other, kept)
    grad_in, grad_out_w, grad_skip = (
        lax.psum_scatter(value, "dp", scatter_dimension=0, tiled=True)
        for value in (
            dot(grad_pre, normed, 1, 1),
            dot(active, grad_low, 1, 1),
            dot(source, kept, 1, 1).reshape(-1),
        )
    )
    kept = kept.reshape(shape[3], shape[1], shape[2]).transpose(1, 2, 0)
    return (kept[None], grad_skip[None], grad_in[None], grad_out_w[None])


def solution(mesh):
    in_specs = (
        P("section", None, "dp", None),
        P(None, "dp"),
        P(),
        P("section", None, None),
        P("section", None, None),
        P("section", None, None),
        P(None, "dp", None),
    )
    out_specs = (
        P("section", None, "dp", None),
        P("section", "dp"),
        P("section", "dp", None),
        P("section", "dp", None),
    )
    return jax.shard_map(shards, mesh=mesh, in_specs=in_specs, out_specs=out_specs, check_vma=False)
```

time: 105 us -> 91.6 us (0.87)
  the two profiles are of different devices: /device:TPU:0 before, /device:TPU:5 now
where the time goes in v2:
time: 91.6 us; the launch traced here: 90.8 us
  starting transfers between devices  29.7 us (32%)
  waiting for transfers between devices  21.2 us (23%)
  local copies, waits for them, and re-layouts  20.9 us (23%)
  Pallas kernels  17.3 us (19%)
  between operations  0.93 us (1%)
    ppermute x18, starting transfers between devices, exchange(): return lax.ppermute(value, 'dp', [(i, i ^ mask) for i in range(count)])  23.2 us
    unnamed x58, local copies, waits for them, and re-layouts  19.1 us
    pallas_call x9, Pallas kernels, call(): pl.pallas_call(body, out_shape=[jax.ShapeDtypeStruct(shape, kind) for sha...  14.5 us
    ppermute x18, waiting for transfers between devices, exchange(): return lax.ppermute(value, 'dp', [(i, i ^ mask) for i in range(count)])  11.2 us
    ppermute x1, waiting for transfers between devices, shards(): received = lax.ppermute(value, 'section', [(0, 3), (1, 2)])  6.48 us
    ppermute x1, waiting for transfers between devices, shards(): chain = lax.ppermute(chain_3, 'section', [(3, 2)])  3.45 us
    pallas_call x1, Pallas kernels, shards(): pl.pallas_call(last_body, out_shape=[jax.ShapeDtypeStruct((n_micro, width...  2.79 us
  transfers between devices with their start and end apart: 24, of which 4 were waited for; matrix products, arithmetic and copies ran while one was open for 3% of the time, Pallas kernels for 10%

profile of v2, /device:TPU:5, one launch (start us, length us, event | category | flops | bytes accessed | tf_op | source)
XLA Modules:
  0.0 90.8 jit_solution(13506478873705985794)
XLA Ops:
  0.6 1.1 %copy-done = bf16[1,1280,320]{1,2,0:T(8,128)(2,1)S(1)} copy-done((bf16[1,1280,320]{1,2,0:T(8,128)(2,1)S(1)}, bf16[1,1280,320]{1,2,0:T(8,128)(2,1)}, u32[]{:S(2)}) %copy-start) | copy-done | bytes 819224
  1.8 1.1 %copy-done.2 = bf16[1,1280,320]{1,2,0:T(8,128)(2,1)S(1)} copy-done((bf16[1,1280,320]{1,2,0:T(8,128)(2,1)S(1)}, bf16[1,1280,320]{1,2,0:T(8,128)(2,1)}, u32[]{:S(2)}) %copy-start.2) | copy-done | bytes 819224
  2.9 0.9 %copy-done.4 = bf16[1,320,320]{2,1,0:T(8,128)(2,1)S(1)} copy-done((bf16[1,320,320]{2,1,0:T(8,128)(2,1)S(1)}, bf16[1,320,320]{2,1,0:T(8,128)(2,1)}, u32[]{:S(2)}) %copy-start.4) | copy-done | bytes 204824
  3.9 0.9 %copy-done.6 = bf16[1,2,128,320]{2,3,1,0:T(8,128)(2,1)S(1)} copy-done((bf16[1,2,128,320]{2,3,1,0:T(8,128)(2,1)S(1)}, bf16[1,2,128,320]{2,3,1,0:T(8,128)(2,1)}, u32[]{:S(2)}) %copy-start.6) | copy-done | bytes 163864
  4.8 1.1 %copy-done.9 = bf16[1000,320]{0,1:T(8,128)(2,1)S(1)} copy-done((bf16[1000,320]{0,1:T(8,128)(2,1)S(1)}, bf16[1000,320]{0,1:T(8,128)(2,1)}, u32[]{:S(2)}) %copy-start.9) | copy-done | bytes 640024
  5.9 0.7 copy-done.28
  6.6 1.9 %shard_map.102 = (bf16[320,256]{1,0:T(8,128)(2,1)S(1)}, bf16[320,256]{1,0:T(8,128)(2,1)S(1)}) custom-call(s32[2,128]{1,0:T(2,128)S(1)} %copy-done.28, bf16[320,1000]{1,0:T(8,128)(2,1)S(1)} %bitcast.46, bf16[2,320,128]{2,1,0:T(8,128)(2,1)S(1)} %bitcast.42, bf16[320,320]{1,0:T(8,128)(2,1)S(1)} %bitcast.38, bf16[320,1280]{1,0:T(8,128)(2,1)S(1)} %bitcast.28, ...), custom_call_target="tpu_custom_call" | custom-call | tf_op jit(solution)/shard_map/pallas_call | solution.py:26
  8.5 1.3 %collective-permute-start = (bf16[320,256]{1,0:T(8,128)(2,1)S(1)}, bf16[320,256]{1,0:T(8,128)(2,1)S(1)}, u32[]{:S(2)}, u32[]{:S(2)}) collective-permute-start(bf16[320,256]{1,0:T(8,128)(2,1)S(1)} %get-tuple-element.38), channel_id=1, source_target_pairs={{0,24},{8,16},{1,25},{9,17},{2,26},{10,18},{3,27},{11,19},{4,28},{... | collective-permute-start | bytes 491528 | tf_op jit(solution)/shard_map/ppermute | solution.py:199
  9.8 0.1 pad_add_fusion.flags
  9.8 6.5 %collective-permute-done.received = bf16[320,256]{1,0:T(8,128)(2,1)S(1)} collective-permute-done((bf16[320,256]{1,0:T(8,128)(2,1)S(1)}, bf16[320,256]{1,0:T(8,128)(2,1)S(1)}, u32[]{:S(2)}, u32[]{:S(2)}) %collective-permute-start) | collective-permute-done | bytes 163872 | tf_op jit(solution)/shard_map/ppermute | solution.py:199
  16.4 2.3 %shard_map.103 = (bf16[320,256]{1,0:T(8,128)(2,1)S(1)}, bf16[320,256]{1,0:T(8,128)(2,1)S(1)}, f32[320,256]{1,0:T(8,128)S(1)}, f32[1280,256]{1,0:T(8,128)S(1)}, bf16[320,256]{1,0:T(8,128)(2,1)S(1)}) custom-call(s32[3]{0:T(128)S(1)} %pad_add_fusion.flags, bf16[320,256]{1,0:T(8,128)(2,1)S(1)} %collective-permute-done.received, ...), custom_call_target="tpu_custom_call" | custom-call | tf_op jit(solution)/shard_map/pallas_call | solution.py:26
  18.7 1.3 %collective-permute-start.1 = (bf16[320,256]{1,0:T(8,128)(2,1)S(1)}, bf16[320,256]{1,0:T(8,128)(2,1)S(1)}, u32[]{:S(2)}, u32[]{:S(2)}) collective-permute-start(bf16[320,256]{1,0:T(8,128)(2,1)S(1)} %get-tuple-element.40.chain.chain_3), channel_id=1, source_target_pairs={{24,16},{25,17},{26,18},{27,19},{28,20},{29,21},{30,22},{31,23}} | collective-permute-start | bytes 491528 | tf_op jit(solution)/shard_map/ppermute | solution.py:204
  20.0 1.3 %collective-permute-start.3 = (bf16[320,320]{1,0:T(8,128)(2,1)S(1)}, bf16[320,320]{1,0:T(8,128)(2,1)S(1)}, u32[]{:S(2)}, u32[]{:S(2)}) collective-permute-start(bf16[320,320]{1,0:T(8,128)(2,1)S(1)} %bitcast.40), channel_id=1, source_target_pairs={{16,8},{17,9},{18,10},{19,11},{20,12},{21,13},{22,14},{23,15}} | collective-permute-start | bytes 614408 | tf_op jit(solution)/shard_map/ppermute | solution.py:205
  21.3 3.5 %collective-permute-done.1.received.low_2 = bf16[320,256]{1,0:T(8,128)(2,1)S(1)} collective-permute-done((bf16[320,256]{1,0:T(8,128)(2,1)S(1)}, bf16[320,256]{1,0:T(8,128)(2,1)S(1)}, u32[]{:S(2)}, u32[]{:S(2)}) %collective-permute-start.1) | collective-permute-done | bytes 163872 | tf_op jit(solution)/shard_map/ppermute | solution.py:204
  24.7 1.2 %shard_map.104.chain_2 = bf16[320,256]{1,0:T(8,128)(2,1)S(1)} custom-call(bf16[320,256]{1,0:T(8,128)(2,1)S(1)} %collective-permute-done.1.received.low_2, f32[320,256]{1,0:T(8,128)S(1)} %get-tuple-element.41.united, f32[1280,256]{1,0:T(8,128)S(1)} %get-tuple-element.42.slope, bf16[320,1280]{1,0:T(8,128)(2,1)S(1)} %bitcast.30, bf16[320,1280]{1,0:T(8,128)(2,1)S(1)} %bitcast.35), custom_call_target="tpu_custom_call" | custom-call | tf_op jit(solution)/shard_map/pallas_call | solution.py:26
  25.9 1.3 %collective-permute-start.2 = (bf16[320,256]{1,0:T(8,128)(2,1)S(1)}, bf16[320,256]{1,0:T(8,128)(2,1)S(1)}, u32[]{:S(2)}, u32[]{:S(2)}) collective-permute-start(bf16[320,256]{1,0:T(8,128)(2,1)S(1)} %shard_map.104.chain_2), channel_id=1, source_target_pairs={{16,8},{17,9},{18,10},{19,11},{20,12},{21,13},{22,14},{23,15}} | collective-permute-start | bytes 491528 | tf_op jit(solution)/shard_map/ppermute | solution.py:210
  27.3 0.2 shard_map.106
  27.5 0.7 collective-permute-start.5
  28.2 3.4 %collective-permute-start.12 = (bf16[320,256]{1,0:T(8,128)(2,1)S(1)}, bf16[320,256]{1,0:T(8,128)(2,1)S(1)}, u32[]{:S(2)}, u32[]{:S(2)}) collective-permute-start(bf16[320,256]{1,0:T(8,128)(2,1)S(1)} %get-tuple-element.52.refs_0_), channel_id=1, source_target_pairs={{0,6},{1,7},{2,4},{3,5},{4,2},{5,3},{6,0},{7,1},{8,14},{9,15},{10,... | collective-permute-start | bytes 491528 | tf_op jit(solution)/shard_map/ppermute | solution.py:171
  31.6 1.4 %shard_map.105 = (bf16[320,256]{1,0:T(8,128)(2,1)S(1)}, bf16[320,256]{1,0:T(8,128)(2,1)S(1)}) custom-call(bf16[320,256]{1,0:T(8,128)(2,1)S(1)} %collective-permute-done.2.received, bf16[320,320]{1,0:T(8,128)(2,1)S(1)} %collective-permute-done.3.w_mirror, f32[320,256]{1,0:T(8,128)S(1)} %get-tuple-element.41.united, f32[1280,256]{1,0:T(8,128)S(1)} %get-tuple-element.42.slope, ...), custom_call_target="tpu_custom_call" | custom-call | tf_op jit(solution)/shard_map/pallas_call | solution.py:26
  33.0 0.7 collective-permute-start.4
  33.7 0.4 collective-permute-start.10
  34.1 3.4 %collective-permute-start.13 = (bf16[320,256]{1,0:T(8,128)(2,1)S(1)}, bf16[320,256]{1,0:T(8,128)(2,1)S(1)}, u32[]{:S(2)}, u32[]{:S(2)}) collective-permute-start(bf16[320,256]{1,0:T(8,128)(2,1)S(1)} %get-tuple-element.52.refs_0_), channel_id=1, source_target_pairs={{0,1},{1,0},{2,3},{3,2},{4,5},{5,4},{6,7},{7,6},{8,9},{9,8},{10,11... | collective-permute-start | bytes 491528 | tf_op jit(solution)/shard_map/ppermute | solution.py:171
  37.5 1.6 %collective-permute-start.16 = (bf16[320,256]{1,0:T(8,128)(2,1)S(1)}, bf16[320,256]{1,0:T(8,128)(2,1)S(1)}, u32[]{:S(2)}, u32[]{:S(2)}) collective-permute-start(bf16[320,256]{1,0:T(8,128)(2,1)S(1)} %collective-permute-done.12.refs_3_), channel_id=1, source_target_pairs={{0,1},{1,0},{2,3},{3,2},{4,5},{5,4},{6,7},{7,6},{8,9},{9,8},{10,11... | collective-permute-start | bytes 491528 | tf_op jit(solution)/shard_map/ppermute | solution.py:171
  39.1 5.9 %collective-permute-done.11.refs_2_ = bf16[320,256]{1,0:T(8,128)(2,1)S(1)} collective-permute-done((bf16[320,256]{1,0:T(8,128)(2,1)S(1)}, bf16[320,256]{1,0:T(8,128)(2,1)S(1)}, u32[]{:S(2)}, u32[]{:S(2)}) %collective-permute-start.11) | collective-permute-done | bytes 163872 | tf_op jit(solution)/shard_map/ppermute | solution.py:171
  45.0 1.4 %collective-permute-start.15 = (bf16[320,256]{1,0:T(8,128)(2,1)S(1)}, bf16[320,256]{1,0:T(8,128)(2,1)}, u32[]{:S(2)}, u32[]{:S(2)}) collective-permute-start(bf16[320,256]{1,0:T(8,128)(2,1)S(1)} %collective-permute-done.11.refs_2_), channel_id=1, source_target_pairs={{0,1},{1,0},{2,3},{3,2},{4,5},{5,4},{6,7},{7,6},{8,9},{9,8},{10,11... | collective-permute-start | bytes 491528 | tf_op jit(solution)/shard_map/ppermute | solution.py:171
  46.4 2.8 %shard_map.107 = (bf16[2,320,128]{2,1,0:T(8,128)(2,1)}, f32[4,40,320]{2,1,0:T(8,128)S(1)}, bf16[4,40,320]{2,1,0:T(8,128)(2,1)}) custom-call(s32[3]{0:T(128)S(1)} %pad_add_fusion.flags, bf16[320,256]{1,0:T(8,128)(2,1)S(1)} %collective-permute-done.4.received, bf16[320,256]{1,0:T(8,128)(2,1)S(1)} %collective-permute-done.5.skip_far, ...), custom_call_target="tpu_custom_call" | custom-call | tf_op jit(solution)/shard_map/pallas_call | solution.py:235
  49.2 0.7 copy-done.10
  49.9 0.5 collective-permute-start.14
  50.4 0.9 %copy-done.13 = bf16[320,256]{1,0:T(8,128)(2,1)S(1)} copy-done((bf16[320,256]{1,0:T(8,128)(2,1)S(1)}, bf16[320,256]{1,0:T(8,128)(2,1)}, u32[]{:S(2)}) %copy-start.13) | copy-done | bytes 163864
  51.3 0.6 shard_map.110.refs_24_
  51.9 2.3 %collective-permute-start.19 = (bf16[320,256]{1,0:T(8,128)(2,1)S(1)}, bf16[320,256]{1,0:T(8,128)(2,1)S(1)}, u32[]{:S(2)}, u32[]{:S(2)}) collective-permute-start(bf16[320,256]{1,0:T(8,128)(2,1)S(1)} %shard_map.110.refs_24_), channel_id=1, source_target_pairs={{0,6},{1,7},{2,4},{3,5},{4,2},{5,3},{6,0},{7,1},{8,14},{9,15},{10,... | collective-permute-start | bytes 491528 | tf_op jit(solution)/shard_map/ppermute | solution.py:171
  54.2 0.9 %copy-done.11 = f32[4,40,320]{2,1,0:T(8,128)S(1)} copy-done((f32[4,40,320]{2,1,0:T(8,128)S(1)}, f32[4,40,320]{2,1,0:T(8,128)}, u32[]{:S(2)}) %copy-start.11) | copy-done | bytes 204824
  55.1 0.9 %shard_map.108 = (f32[40,320]{1,0:T(8,128)S(1)}, bf16[40,320]{1,0:T(8,128)(2,1)S(1)}, bf16[40,320]{1,0:T(8,128)(2,1)S(1)}, bf16[40,320]{1,0:T(8,128)(2,1)S(1)}) custom-call(s32[3]{0:T(128)S(1)} %pad_add_fusion.flags, f32[4,40,320]{2,1,0:T(8,128)S(1)} %copy-done.11, bf16[4,40,320]{2,1,0:T(8,128)(2,1)} %collective-permute-done.6.given), custom_call_target="tpu_custom_call" | custom-call | tf_op jit(solution)/shard_map/pallas_call | solution.py:26
  56.1 0.1 collective-permute-start.18
  56.2 1.3 %collective-permute-start.17 = (bf16[320,256]{1,0:T(8,128)(2,1)S(1)}, bf16[320,256]{1,0:T(8,128)(2,1)S(1)}, u32[]{:S(2)}, u32[]{:S(2)}) collective-permute-start(bf16[320,256]{1,0:T(8,128)(2,1)S(1)} %shard_map.110.refs_24_), channel_id=1, source_target_pairs={{0,2},{1,3},{2,0},{3,1},{4,6},{5,7},{6,4},{7,5},{8,10},{9,11},{10,... | collective-permute-start | bytes 491528 | tf_op jit(solution)/shard_map/ppermute | solution.py:171
  57.5 0.2 collective-permute-start.7
  57.7 0.1 dynamic-slice_bitcast_fusion.own_in
  57.9 2.3 %collective-permute-start.8 = (bf16[40,320]{1,0:T(8,128)(2,1)S(1)}, bf16[40,320]{1,0:T(8,128)(2,1)S(1)}, u32[]{:S(2)}, u32[]{:S(2)}) collective-permute-start(bf16[40,320]{1,0:T(8,128)(2,1)S(1)} %get-tuple-element.50), channel_id=1, source_target_pairs={{0,4},{1,5},{2,6},{3,7},{4,0},{5,1},{6,2},{7,3},{8,12},{9,13},{10,... | collective-permute-start | bytes 76808 | tf_op jit(solution)/shard_map/ppermute | solution.py:171
  60.2 5.3 %collective-permute-done.7 = bf16[40,320]{1,0:T(8,128)(2,1)S(1)} collective-permute-done((bf16[40,320]{1,0:T(8,128)(2,1)S(1)}, bf16[40,320]{1,0:T(8,128)(2,1)S(1)}, u32[]{:S(2)}, u32[]{:S(2)}) %collective-permute-start.7) | collective-permute-done | bytes 25632 | tf_op jit(solution)/shard_map/ppermute | solution.py:171
  65.5 5.0 %collective-permute-start.9 = (bf16[40,320]{1,0:T(8,128)(2,1)S(1)}, bf16[40,320]{1,0:T(8,128)(2,1)S(1)}, u32[]{:S(2)}, u32[]{:S(2)}) collective-permute-start(bf16[40,320]{1,0:T(8,128)(2,1)S(1)} %get-tuple-element.51), channel_id=1, source_target_pairs={{0,6},{1,7},{2,4},{3,5},{4,2},{5,3},{6,0},{7,1},{8,14},{9,15},{10,... | collective-permute-start | bytes 76808 | tf_op jit(solution)/shard_map/ppermute | solution.py:171
  70.5 0.1 dynamic-slice_bitcast_fusion.1.own_out
  70.6 1.8 %shard_map.109 = (bf16[160,256]{1,0:T(8,128)(2,1)S(1)}, bf16[160,256]{1,0:T(8,128)(2,1)S(1)}, bf16[160,256]{1,0:T(8,128)(2,1)S(1)}, bf16[160,256]{1,0:T(8,128)(2...) custom-call(bf16[320,160]{1,0:T(8,128)(2,1)S(1)} %dynamic-slice_bitc, ...), custom_call_target="tpu_custom_call" | custom-call | tf_op jit(solution)/shard_map/pallas_call | solution.py:26
  72.5 0.6 copy-done.14
  73.1 0.6 copy-done.16
  73.7 0.6 copy-done.18
  74.4 0.6 copy-done.20
  75.0 0.6 copy-done.22
  75.6 0.6 copy-done.24
  76.3 0.6 copy-done.26
  76.9 0.7 collective-permute-start.20
  77.6 0.1 collective-permute-start.23
  77.7 0.4 collective-permute-start.22
  78.2 0.1 collective-permute-start.21
  78.2 0.6 convert_add_fusion
  78.9 1.6 %reshape.17 = f32[1,12800]{1,0:T(1,128)} reshape(f32[40,320]{1,0:T(8,128)} %convert_add_fusion) | data formatting | bytes 102400 | tf_op jit(solution)/shard_map/reshape | solution.py:260
  80.5 0.9 copy-done.15
  81.3 0.9 copy-done.17
  82.2 0.9 copy-done.19
  83.1 0.9 copy-done.21
  84.0 0.9 copy-done.23
  84.9 0.9 copy-done.25
  85.8 0.9 copy-done.27
  86.7 4.1 %shard_map.111 = (f32[160,320]{1,0:T(8,128)}, f32[160,320]{1,0:T(8,128)}) custom-call(bf16[320,160]{1,0:T(8,128)(2,1)S(1)} %dynamic-slice_bitcast_fusion.1.own_out, bf16[320,256]{1,0:T(8,128)(2,1)S(1)} %get-tuple-element.52.refs_0_, bf16[320,256]{1,0:T(8,128)(2,1)S(1)} %collective-permute-done.10.refs_1_, ...), custom_call_target="tpu_custom_call" | custom-call | tf_op jit(solution)/shard_map/pallas_call | solution.py:26
  (57 shorter events, 0.1 us)
Async XLA Ops:
  0.6 1.1 %copy-start = (bf16[1,1280,320]{1,2,0:T(8,128)(2,1)S(1)}, bf16[1,1280,320]{1,2,0:T(8,128)(2,1)}, u32[]{:S(2)}) copy-start(bf16[1,1280,320]{1,2,0:T(8,128)(2,1)} %param.11) | copy-start | bytes 2457604
  1.8 1.1 %copy-start.2 = (bf16[1,1280,320]{1,2,0:T(8,128)(2,1)S(1)}, bf16[1,1280,320]{1,2,0:T(8,128)(2,1)}, u32[]{:S(2)}) copy-start(bf16[1,1280,320]{1,2,0:T(8,128)(2,1)} %param.12) | copy-start | bytes 2457604
  2.9 0.9 %copy-start.4 = (bf16[1,320,320]{2,1,0:T(8,128)(2,1)S(1)}, bf16[1,320,320]{2,1,0:T(8,128)(2,1)}, u32[]{:S(2)}) copy-start(bf16[1,320,320]{2,1,0:T(8,128)(2,1)} %param.10) | copy-start | bytes 614404
  3.9 0.9 %copy-start.6 = (bf16[1,2,128,320]{2,3,1,0:T(8,128)(2,1)S(1)}, bf16[1,2,128,320]{2,3,1,0:T(8,128)(2,1)}, u32[]{:S(2)}) copy-start(bf16[1,2,128,320]{2,3,1,0:T(8,128)(2,1)} %param.7) | copy-start | bytes 491524
  4.8 1.1 %copy-start.9 = (bf16[1000,320]{0,1:T(8,128)(2,1)S(1)}, bf16[1000,320]{0,1:T(8,128)(2,1)}, u32[]{:S(2)}) copy-start(bf16[1000,320]{0,1:T(8,128)(2,1)} %param.9) | copy-start | bytes 1920004
  5.9 0.7 copy-start.28
  6.6 9.8 %copy-start.1 = (bf16[1,1280,320]{1,2,0:T(8,128)(2,1)S(1)}, bf16[1,1280,320]{1,2,0:T(8,128)(2,1)}, u32[]{:S(2)}) copy-start(bf16[1,1280,320]{1,2,0:T(8,128)(2,1)} %param.11) | copy-start | bytes 2457604
  6.6 9.8 %copy-start.3 = (bf16[1,1280,320]{1,2,0:T(8,128)(2,1)S(1)}, bf16[1,1280,320]{1,2,0:T(8,128)(2,1)}, u32[]{:S(2)}) copy-start(bf16[1,1280,320]{1,2,0:T(8,128)(2,1)} %param.12) | copy-start | bytes 2457604
  6.6 9.8 %copy-start.5 = (bf16[1,320,320]{2,1,0:T(8,128)(2,1)S(1)}, bf16[1,320,320]{2,1,0:T(8,128)(2,1)}, u32[]{:S(2)}) copy-start(bf16[1,320,320]{2,1,0:T(8,128)(2,1)} %param.10) | copy-start | bytes 614404
  6.6 9.8 %copy-start.7 = (bf16[1,2,128,320]{2,3,1,0:T(8,128)(2,1)S(1)}, bf16[1,2,128,320]{2,3,1,0:T(8,128)(2,1)}, u32[]{:S(2)}) copy-start(bf16[1,2,128,320]{2,3,1,0:T(8,128)(2,1)} %param.7) | copy-start | bytes 491524
  6.6 9.8 %copy-start.8 = (bf16[2,128,320]{1,2,0:T(8,128)(2,1)S(1)}, bf16[2,128,320]{1,2,0:T(8,128)(2,1)}, u32[]{:S(2)}) copy-start(bf16[2,128,320]{1,2,0:T(8,128)(2,1)} %param.13) | copy-start | bytes 491524
  8.5 7.9 %collective-permute-start = (bf16[320,256]{1,0:T(8,128)(2,1)S(1)}, bf16[320,256]{1,0:T(8,128)(2,1)S(1)}, u32[]{:S(2)}, u32[]{:S(2)}) collective-permute-start(bf16[320,256]{1,0:T(8,128)(2,1)S(1)} %get-tuple-element.38), channel_id=1, source_target_pairs={{0,24},{8,16},{1,25},{9,17},{2,26},{10,18},{3,27},{11,19},{4,28},{... | collective-permute-start | bytes 491528 | tf_op jit(solution)/shard_map/ppermute | solution.py:199
  18.7 6.1 %collective-permute-start.1 = (bf16[320,256]{1,0:T(8,128)(2,1)S(1)}, bf16[320,256]{1,0:T(8,128)(2,1)S(1)}, u32[]{:S(2)}, u32[]{:S(2)}) collective-permute-start(bf16[320,256]{1,0:T(8,128)(2,1)S(1)} %get-tuple-element.40.chain.chain_3), channel_id=1, source_target_pairs={{24,16},{25,17},{26,18},{27,19},{28,20},{29,21},{30,22},{31,23}} | collective-permute-start | bytes 491528 | tf_op jit(solution)/shard_map/ppermute | solution.py:204
  20.0 11.6 %collective-permute-start.3 = (bf16[320,320]{1,0:T(8,128)(2,1)S(1)}, bf16[320,320]{1,0:T(8,128)(2,1)S(1)}, u32[]{:S(2)}, u32[]{:S(2)}) collective-permute-start(bf16[320,320]{1,0:T(8,128)(2,1)S(1)} %bitcast.40), channel_id=1, source_target_pairs={{16,8},{17,9},{18,10},{19,11},{20,12},{21,13},{22,14},{23,15}} | collective-permute-start | bytes 614408 | tf_op jit(solution)/shard_map/ppermute | solution.py:205
  25.9 5.6 %collective-permute-start.2 = (bf16[320,256]{1,0:T(8,128)(2,1)S(1)}, bf16[320,256]{1,0:T(8,128)(2,1)S(1)}, u32[]{:S(2)}, u32[]{:S(2)}) collective-permute-start(bf16[320,256]{1,0:T(8,128)(2,1)S(1)} %shard_map.104.chain_2), channel_id=1, source_target_pairs={{16,8},{17,9},{18,10},{19,11},{20,12},{21,13},{22,14},{23,15}} | collective-permute-start | bytes 491528 | tf_op jit(solution)/shard_map/ppermute | solution.py:210
  27.5 6.6 %collective-permute-start.5 = (bf16[320,256]{1,0:T(8,128)(2,1)S(1)}, bf16[320,256]{1,0:T(8,128)(2,1)S(1)}, u32[]{:S(2)}, u32[]{:S(2)}) collective-permute-start(bf16[320,256]{1,0:T(8,128)(2,1)S(1)} %shard_map.106), channel_id=1, source_target_pairs={{24,0},{25,1},{26,2},{27,3},{28,4},{29,5},{30,6},{31,7}} | collective-permute-start | bytes 491528 | tf_op jit(solution)/shard_map/ppermute | solution.py:207
  28.2 9.3 %collective-permute-start.12 = (bf16[320,256]{1,0:T(8,128)(2,1)S(1)}, bf16[320,256]{1,0:T(8,128)(2,1)S(1)}, u32[]{:S(2)}, u32[]{:S(2)}) collective-permute-start(bf16[320,256]{1,0:T(8,128)(2,1)S(1)} %get-tuple-element.52.refs_0_), channel_id=1, source_target_pairs={{0,6},{1,7},{2,4},{3,5},{4,2},{5,3},{6,0},{7,1},{8,14},{9,15},{10,... | collective-permute-start | bytes 491528 | tf_op jit(solution)/shard_map/ppermute | solution.py:171
  31.6 13.5 %collective-permute-start.11 = (bf16[320,256]{1,0:T(8,128)(2,1)S(1)}, bf16[320,256]{1,0:T(8,128)(2,1)S(1)}, u32[]{:S(2)}, u32[]{:S(2)}) collective-permute-start(bf16[320,256]{1,0:T(8,128)(2,1)S(1)} %get-tuple-element.52.refs_0_), channel_id=1, source_target_pairs={{0,4},{1,5},{2,6},{3,7},{4,0},{5,1},{6,2},{7,3},{8,12},{9,13},{10,... | collective-permute-start | bytes 491528 | tf_op jit(solution)/shard_map/ppermute | solution.py:171
  33.0 16.2 %copy-start.12 = (bf16[320,256]{1,0:T(8,128)(2,1)}, bf16[320,256]{1,0:T(8,128)(2,1)S(1)}, u32[]{:S(2)}) copy-start(bf16[320,256]{1,0:T(8,128)(2,1)S(1)} %get-tuple-element.69.low_1) | copy-start | bytes 491524
  33.0 13.4 %collective-permute-start.4 = (bf16[320,256]{1,0:T(8,128)(2,1)S(1)}, bf16[320,256]{1,0:T(8,128)(2,1)S(1)}, u32[]{:S(2)}, u32[]{:S(2)}) collective-permute-start(bf16[320,256]{1,0:T(8,128)(2,1)S(1)} %get-tuple-element.43.chain_1), channel_id=1, source_target_pairs={{8,0},{9,1},{10,2},{11,3},{12,4},{13,5},{14,6},{15,7}} | collective-permute-start | bytes 491528 | tf_op jit(solution)/shard_map/ppermute | solution.py:214
  33.7 16.2 %collective-permute-start.10 = (bf16[320,256]{1,0:T(8,128)(2,1)S(1)}, bf16[320,256]{1,0:T(8,128)(2,1)S(1)}, u32[]{:S(2)}, u32[]{:S(2)}) collective-permute-start(bf16[320,256]{1,0:T(8,128)(2,1)S(1)} %get-tuple-element.52.refs_0_), channel_id=1, source_target_pairs={{0,2},{1,3},{2,0},{3,1},{4,6},{5,7},{6,4},{7,5},{8,10},{9,11},{10,... | collective-permute-start | bytes 491528 | tf_op jit(solution)/shard_map/ppermute | solution.py:171
  34.1 22.0 %collective-permute-start.13 = (bf16[320,256]{1,0:T(8,128)(2,1)S(1)}, bf16[320,256]{1,0:T(8,128)(2,1)S(1)}, u32[]{:S(2)}, u32[]{:S(2)}) collective-permute-start(bf16[320,256]{1,0:T(8,128)(2,1)S(1)} %get-tuple-element.52.refs_0_), channel_id=1, source_target_pairs={{0,1},{1,0},{2,3},{3,2},{4,5},{5,4},{6,7},{7,6},{8,9},{9,8},{10,11... | collective-permute-start | bytes 491528 | tf_op jit(solution)/shard_map/ppermute | solution.py:171
  37.5 18.7 %collective-permute-start.16 = (bf16[320,256]{1,0:T(8,128)(2,1)S(1)}, bf16[320,256]{1,0:T(8,128)(2,1)S(1)}, u32[]{:S(2)}, u32[]{:S(2)}) collective-permute-start(bf16[320,256]{1,0:T(8,128)(2,1)S(1)} %collective-permute-done.12.refs_3_), channel_id=1, source_target_pairs={{0,1},{1,0},{2,3},{3,2},{4,5},{5,4},{6,7},{7,6},{8,9},{9,8},{10,11... | collective-permute-start | bytes 491528 | tf_op jit(solution)/shard_map/ppermute | solution.py:171
  45.0 12.5 %collective-permute-start.15 = (bf16[320,256]{1,0:T(8,128)(2,1)S(1)}, bf16[320,256]{1,0:T(8,128)(2,1)}, u32[]{:S(2)}, u32[]{:S(2)}) collective-permute-start(bf16[320,256]{1,0:T(8,128)(2,1)S(1)} %collective-permute-done.11.refs_2_), channel_id=1, source_target_pairs={{0,1},{1,0},{2,3},{3,2},{4,5},{5,4},{6,7},{7,6},{8,9},{9,8},{10,11... | collective-permute-start | bytes 491528 | tf_op jit(solution)/shard_map/ppermute | solution.py:171
  49.2 0.7 copy-start.10
  49.9 2.0 %collective-permute-start.6 = (bf16[4,40,320]{2,1,0:T(8,128)(2,1)}, bf16[4,40,320]{2,1,0:T(8,128)(2,1)}, u32[]{:S(2)}, u32[]{:S(2)}) collective-permute-start(bf16[4,40,320]{2,1,0:T(8,128)(2,1)} %get-tuple-element.47), channel_id=1, source_target_pairs={{0,1},{1,0},{2,3},{3,2},{4,5},{5,4},{6,7},{7,6},{8,9},{9,8},{10,11... | collective-permute-start | bytes 307208 | tf_op jit(solution)/shard_map/ppermute | solution.py:171
  49.9 8.0 %collective-permute-start.14 = (bf16[320,256]{1,0:T(8,128)(2,1)S(1)}, bf16[320,256]{1,0:T(8,128)(2,1)}, u32[]{:S(2)}, u32[]{:S(2)}) collective-permute-start(bf16[320,256]{1,0:T(8,128)(2,1)S(1)} %collective-permute-done.10.refs_1_), channel_id=1, source_target_pairs={{0,1},{1,0},{2,3},{3,2},{4,5},{5,4},{6,7},{7,6},{8,9},{9,8},{10,11... | collective-permute-start | bytes 491528 | tf_op jit(solution)/shard_map/ppermute | solution.py:171
  50.4 0.9 %copy-start.13 = (bf16[320,256]{1,0:T(8,128)(2,1)S(1)}, bf16[320,256]{1,0:T(8,128)(2,1)}, u32[]{:S(2)}) copy-start(bf16[320,256]{1,0:T(8,128)(2,1)} %copy-done.12) | copy-start | bytes 491524
  51.9 25.7 %collective-permute-start.19 = (bf16[320,256]{1,0:T(8,128)(2,1)S(1)}, bf16[320,256]{1,0:T(8,128)(2,1)S(1)}, u32[]{:S(2)}, u32[]{:S(2)}) collective-permute-start(bf16[320,256]{1,0:T(8,128)(2,1)S(1)} %shard_map.110.refs_24_), channel_id=1, source_target_pairs={{0,6},{1,7},{2,4},{3,5},{4,2},{5,3},{6,0},{7,1},{8,14},{9,15},{10,... | collective-permute-start | bytes 491528 | tf_op jit(solution)/shard_map/ppermute | solution.py:171
  54.2 0.9 %copy-start.11 = (f32[4,40,320]{2,1,0:T(8,128)S(1)}, f32[4,40,320]{2,1,0:T(8,128)}, u32[]{:S(2)}) copy-start(f32[4,40,320]{2,1,0:T(8,128)} %copy-done.10) | copy-start | bytes 614404
  56.1 21.6 %collective-permute-start.18 = (bf16[320,256]{1,0:T(8,128)(2,1)S(1)}, bf16[320,256]{1,0:T(8,128)(2,1)S(1)}, u32[]{:S(2)}, u32[]{:S(2)}) collective-permute-start(bf16[320,256]{1,0:T(8,128)(2,1)S(1)} %shard_map.110.refs_24_), channel_id=1, source_target_pairs={{0,4},{1,5},{2,6},{3,7},{4,0},{5,1},{6,2},{7,3},{8,12},{9,13},{10,... | collective-permute-start | bytes 491528 | tf_op jit(solution)/shard_map/ppermute | solution.py:171
  56.2 22.0 %collective-permute-start.17 = (bf16[320,256]{1,0:T(8,128)(2,1)S(1)}, bf16[320,256]{1,0:T(8,128)(2,1)S(1)}, u32[]{:S(2)}, u32[]{:S(2)}) collective-permute-start(bf16[320,256]{1,0:T(8,128)(2,1)S(1)} %shard_map.110.refs_24_), channel_id=1, source_target_pairs={{0,2},{1,3},{2,0},{3,1},{4,6},{5,7},{6,4},{7,5},{8,10},{9,11},{10,... | collective-permute-start | bytes 491528 | tf_op jit(solution)/shard_map/ppermute | solution.py:171
  57.5 8.0 %collective-permute-start.7 = (bf16[40,320]{1,0:T(8,128)(2,1)S(1)}, bf16[40,320]{1,0:T(8,128)(2,1)S(1)}, u32[]{:S(2)}, u32[]{:S(2)}) collective-permute-start(bf16[40,320]{1,0:T(8,128)(2,1)S(1)} %get-tuple-element.49), channel_id=1, source_target_pairs={{0,2},{1,3},{2,0},{3,1},{4,6},{5,7},{6,4},{7,5},{8,10},{9,11},{10,... | collective-permute-start | bytes 76808 | tf_op jit(solution)/shard_map/ppermute | solution.py:171
  57.9 19.0 %collective-permute-start.8 = (bf16[40,320]{1,0:T(8,128)(2,1)S(1)}, bf16[40,320]{1,0:T(8,128)(2,1)S(1)}, u32[]{:S(2)}, u32[]{:S(2)}) collective-permute-start(bf16[40,320]{1,0:T(8,128)(2,1)S(1)} %get-tuple-element.50), channel_id=1, source_target_pairs={{0,4},{1,5},{2,6},{3,7},{4,0},{5,1},{6,2},{7,3},{8,12},{9,13},{10,... | collective-permute-start | bytes 76808 | tf_op jit(solution)/shard_map/ppermute | solution.py:171
  65.5 12.7 %collective-permute-start.9 = (bf16[40,320]{1,0:T(8,128)(2,1)S(1)}, bf16[40,320]{1,0:T(8,128)(2,1)S(1)}, u32[]{:S(2)}, u32[]{:S(2)}) collective-permute-start(bf16[40,320]{1,0:T(8,128)(2,1)S(1)} %get-tuple-element.51), channel_id=1, source_target_pairs={{0,6},{1,7},{2,4},{3,5},{4,2},{5,3},{6,0},{7,1},{8,14},{9,15},{10,... | collective-permute-start | bytes 76808 | tf_op jit(solution)/shard_map/ppermute | solution.py:171
  72.5 0.6 copy-start.14
  73.1 0.6 copy-start.16
  73.7 0.6 copy-start.18
  74.4 0.6 copy-start.20
  75.0 0.6 copy-start.22
  75.6 0.6 copy-start.24
  76.3 0.6 copy-start.26
  76.9 3.5 %collective-permute-start.20 = (bf16[320,256]{1,0:T(8,128)(2,1)S(1)}, bf16[320,256]{1,0:T(8,128)(2,1)S(1)}, u32[]{:S(2)}, u32[]{:S(2)}) collective-permute-start(bf16[320,256]{1,0:T(8,128)(2,1)S(1)} %shard_map.110.refs_24_), channel_id=1, source_target_pairs={{0,1},{1,0},{2,3},{3,2},{4,5},{5,4},{6,7},{7,6},{8,9},{9,8},{10,11... | collective-permute-start | bytes 491528 | tf_op jit(solution)/shard_map/ppermute | solution.py:171
  77.6 2.8 %collective-permute-start.23 = (bf16[320,256]{1,0:T(8,128)(2,1)S(1)}, bf16[320,256]{1,0:T(8,128)(2,1)S(1)}, u32[]{:S(2)}, u32[]{:S(2)}) collective-permute-start(bf16[320,256]{1,0:T(8,128)(2,1)S(1)} %collective-permute-done.19.refs_27_), channel_id=1, source_target_pairs={{0,1},{1,0},{2,3},{3,2},{4,5},{5,4},{6,7},{7,6},{8,9},{9,8},{10,11... | collective-permute-start | bytes 491528 | tf_op jit(solution)/shard_map/ppermute | solution.py:171
  77.7 2.7 %collective-permute-start.22 = (bf16[320,256]{1,0:T(8,128)(2,1)S(1)}, bf16[320,256]{1,0:T(8,128)(2,1)}, u32[]{:S(2)}, u32[]{:S(2)}) collective-permute-start(bf16[320,256]{1,0:T(8,128)(2,1)S(1)} %collective-permute-done.18.refs_26_), channel_id=1, source_target_pairs={{0,1},{1,0},{2,3},{3,2},{4,5},{5,4},{6,7},{7,6},{8,9},{9,8},{10,11... | collective-permute-start | bytes 491528 | tf_op jit(solution)/shard_map/ppermute | solution.py:171
  78.2 2.3 %collective-permute-start.21 = (bf16[320,256]{1,0:T(8,128)(2,1)S(1)}, bf16[320,256]{1,0:T(8,128)(2,1)}, u32[]{:S(2)}, u32[]{:S(2)}) collective-permute-start(bf16[320,256]{1,0:T(8,128)(2,1)S(1)} %collective-permute-done.17.refs_25_), channel_id=1, source_target_pairs={{0,1},{1,0},{2,3},{3,2},{4,5},{5,4},{6,7},{7,6},{8,9},{9,8},{10,11... | collective-permute-start | bytes 491528 | tf_op jit(solution)/shard_map/ppermute | solution.py:171
  80.4 0.9 copy-start.15
  81.3 0.9 copy-start.17
  82.2 0.9 copy-start.19
  83.1 0.9 copy-start.21
  84.0 0.9 copy-start.23
  84.9 0.9 copy-start.25
  85.8 0.9 copy-start.27

commit v3 on v2

v3 whole, which is shorter than its diff:
```python
import jax
import jax.numpy as jnp
from jax import lax
from jax.experimental import pallas as pl
from jax.experimental.pallas import tpu as pltpu
from jax.sharding import PartitionSpec as P


EPS = 1e-06
LOW = jnp.bfloat16
F32 = jnp.float32
VMEM_BYTES = 20 * 1024 * 1024


def contract(left, right, dims):
    return lax.dot_general(left, right, ((dims[0], dims[1]), ((), ())), preferred_element_type=F32)


def dot(left, right, on_left, on_right):
    return contract(left, right, ((on_left,), (on_right,)))


def call(body, outs, *args, scratch=(), far=()):
    places = [
        pltpu.SMEM if arg.ndim == 1 else pltpu.HBM if index in far else pltpu.VMEM
        for index, arg in enumerate(args)
    ]
    args = [
        pltpu.with_memory_space_constraint(arg, pltpu.HBM) if index in far else arg
        for index, arg in enumerate(args)
    ]
    return pl.pallas_call(
        body,
        out_shape=[jax.ShapeDtypeStruct(shape, kind) for shape, kind in outs],
        in_specs=[pl.BlockSpec(memory_space=place) for place in places],
        out_specs=[pl.BlockSpec(memory_space=pltpu.VMEM) for _ in outs],
        scratch_shapes=list(scratch),
        compiler_params=pltpu.CompilerParams(vmem_limit_bytes=VMEM_BYTES),
    )(*args)


def side_by_side(ref):
    return jnp.concatenate([ref[m] for m in range(ref.shape[0])], axis=1)


def norm_of(united):
    return lax.rsqrt(jnp.mean(united * united, axis=0, keepdims=True) + EPS)


def sigmoid(value):
    return 1.0 / (1.0 + jnp.exp(-value))


def encode_body(*refs):
    distant, (embed_out, value_out), local, sems = refs[:6], refs[6:8], refs[8:14], refs[14]
    copies = [
        pltpu.make_async_copy(source, target, sems.at[index])
        for index, (source, target) in enumerate(zip(distant, local))
    ]
    for copy in copies:
        copy.start()
    times, table, w_skip, inputs, w_in, w_out = local
    copies[0].wait()
    levels = lax.broadcasted_iota(jnp.int32, (table.shape[1], times.shape[1]), 0)
    hot = [
        jnp.where(levels == times[m : m + 1, :], 1.0, 0.0).astype(LOW)
        for m in range(times.shape[0])
    ]
    copies[1].wait()
    embed = dot(table[...], jnp.concatenate(hot, axis=1), 1, 0).astype(LOW)
    embed_out[...] = embed
    copies[2].wait()
    copies[3].wait()
    united = side_by_side(inputs).astype(F32) + dot(w_skip[...], embed, 0, 0)
    normed = (united * norm_of(united)).astype(LOW)
    copies[4].wait()
    preact = dot(w_in[...], normed, 0, 0)
    active = (preact * sigmoid(preact)).astype(LOW)
    copies[5].wait()
    value_out[...] = (united + dot(w_out[...], active, 1, 0)).astype(LOW)


def early_body(upstream, w_out, low_out, grad_act_out):
    low = side_by_side(upstream)
    low_out[...] = low
    grad_act_out[...] = dot(w_out[...], low, 0, 0)


def back_through(grad_out, grad_act, united, slope, w_in):
    grad_pre = (grad_act * slope).astype(LOW)
    grad_norm = dot(w_in[...], grad_pre, 1, 0)
    recip = norm_of(united)
    along = jnp.mean(grad_norm * united, axis=0, keepdims=True)
    return (grad_out + recip * grad_norm - united * (recip * recip * recip * along)).astype(LOW)


def decode_body(
    received, embed, inputs, top_low, grad_act, w_skip, w_in,
    source_out, normed_out, united_out, slope_out, chain_out,
):
    source = jnp.where(lax.axis_index("section") >= 2, received[...], embed[...])
    source_out[...] = source
    united = side_by_side(inputs).astype(F32) + dot(w_skip[...], source, 0, 0)
    united_out[...] = united
    normed = (united * norm_of(united)).astype(LOW)
    normed_out[...] = normed
    preact = dot(w_in[...], normed, 0, 0)
    sigma = sigmoid(preact)
    slope = sigma * (1.0 + preact * (1.0 - sigma))
    slope_out[...] = slope
    chain_out[...] = back_through(top_low[...].astype(F32), grad_act[...], united, slope, w_in)


def back_body(chain, w_skip, back_out):
    back_out[...] = dot(w_skip[...], chain[...], 1, 0).astype(LOW)


def tick_body(received, united, slope, w_in, w_out, chain_out):
    low = received[...]
    grad_act = dot(w_out[...], low, 0, 0)
    chain_out[...] = back_through(low.astype(F32), grad_act, united[...], slope[...], w_in)


def mirror_tick_body(
    received, w_mirror, united, slope, w_in, w_out, skip_far, back_2, chain_2, chain_3,
    top_low, chain_out, low_out, next_out,
):
    back = dot(w_mirror[...], received[...], 1, 0).astype(LOW)
    grad_out = received[...].astype(F32) + back.astype(F32)
    low = grad_out.astype(LOW)
    low_out[...] = low
    grad_act = dot(w_out[...], low, 0, 0)
    chain = back_through(grad_out, grad_act, united[...], slope[...], w_in)
    chain_out[...] = chain
    section = lax.axis_index("section")
    ahead = (chain.astype(F32) + skip_far[...].astype(F32)).astype(LOW)
    ahead = jnp.where(
        section == 2, (chain_2[...].astype(F32) + back_2[...].astype(F32)).astype(LOW), ahead
    )
    ahead = jnp.where(section == 3, chain_3[...], ahead)
    next_out[...] = jnp.where(section == 0, top_low[...], ahead)


def pick_body(received, skip_far, low_1, low_2, top_low, grad_low_out):
    own = (received[...].astype(F32) + skip_far[...].astype(F32)).astype(LOW)
    section = lax.axis_index("section")
    own = jnp.where(section == 1, low_1[...], own)
    own = jnp.where(section == 2, low_2[...], own)
    grad_low_out[...] = jnp.where(section == 3, top_low[...], own)


def last_body(
    grad_low, received, skip_far, united, slope, w_in, w_out, source, chain_1, chain_2,
    chain_3, kept_out, keep_out, give_out,
):
    grad_out = received[...].astype(F32) + skip_far[...].astype(F32)
    grad_act = dot(w_out[...], grad_low[...], 0, 0)
    section = lax.axis_index("section")
    kept = back_through(grad_out, grad_act, united[...], slope[...], w_in)
    kept = jnp.where(section == 1, chain_1[...], kept)
    kept = jnp.where(section == 2, chain_2[...], kept)
    kept = jnp.where(section == 3, chain_3[...], kept)
    span = kept_out.shape[2]
    for m in range(kept_out.shape[0]):
        kept_out[m] = kept[:, m * span : (m + 1) * span]
    partial = dot(source[...], kept, 1, 1)
    size = keep_out.shape[1]
    first_core = lax.axis_index("dp") % 2 == 0
    for block in range(keep_out.shape[0]):
        start = 2 * block * size
        even = partial[start : start + size, :]
        odd = partial[start + size : start + 2 * size, :]
        keep_out[block] = jnp.where(first_core, even, odd)
        give_out[block] = jnp.where(first_core, odd, even).astype(LOW)


def join_body(keep, given, own_out, *piece_outs):
    chip = lax.axis_index("dp") // 2
    own_out[...] = keep[chip] + given[chip].astype(F32)
    for mask, piece_out in enumerate(piece_outs, 1):
        far = chip ^ mask
        piece_out[...] = (keep[far] + given[far].astype(F32)).astype(LOW)


def flat_body(own, *refs):
    pieces, out, lanes, square = refs[:-3], refs[-3], refs[-2], refs[-1]
    total = own[...]
    for piece in pieces:
        total = total + piece[...].astype(F32)
    lanes[0] = total[:, :128]
    lanes[1] = total[:, 128:256]
    lanes[2] = jnp.concatenate([total[:, 256:], total[:, 256:]], axis=1)
    half = total.shape[0] // 2
    even = [lanes[part, pl.ds(0, half, stride=2), :] for part in range(3)]
    odd = [lanes[part, pl.ds(1, half, stride=2), :] for part in range(3)]
    lines = [
        even[0],
        even[1],
        jnp.concatenate([even[2][:, :64], odd[0][:, :64]], axis=1),
        jnp.concatenate([odd[0][:, 64:], odd[1][:, :64]], axis=1),
        jnp.concatenate([odd[1][:, 64:], odd[2][:, :64]], axis=1),
    ]
    for place, line in enumerate(lines):
        square[pl.ds(place, half, stride=5), :] = line
    for row in range(square.shape[0]):
        out[:, row * 128 : (row + 1) * 128] = square[row : row + 1, :]


def cut_body(w_in, w_out, own_in, own_out):
    part = own_in.shape[1]
    place = lax.axis_index("dp")
    for index in range(w_in.shape[1] // part):

        @pl.when(place == index)
        def _():
            columns = slice(index * part, (index + 1) * part)
            own_in[...] = w_in[:, columns]
            own_out[...] = w_out[:, columns]


def slice_forward_body(own_in, *refs):
    blocks, active_out, slope_out = refs[:-2], refs[-2], refs[-1]
    rows = blocks[0].shape[1]
    for place, block in enumerate(blocks):
        columns = slice(place * rows, (place + 1) * rows)
        preact = dot(own_in[...], block[...], 0, 0)
        sigma = sigmoid(preact)
        active_out[:, columns] = (preact * sigma).astype(LOW)
        slope_out[:, columns] = sigma * (1.0 + preact * (1.0 - sigma))


def slice_grad(own_out, active, slope, normed, low, first):
    rows = low[0].shape[1]
    columns = slice(first * rows, (first + len(low)) * rows)
    lows = jnp.concatenate([block[...] for block in low], axis=1)
    grad_pre = (dot(own_out[...], lows, 0, 0) * slope[:, columns]).astype(LOW)
    normeds = jnp.concatenate([block[...] for block in normed], axis=1)
    return dot(grad_pre, normeds, 1, 1), dot(active[:, columns], lows, 1, 1)


def half_grad_body(own_out, active, slope, *refs):
    half = (len(refs) - 2) // 2
    refs[-2][...], refs[-1][...] = slice_grad(
        own_out, active, slope, refs[:half], refs[half : 2 * half], 0
    )


def rest_grad_body(own_out, active, slope, sum_in, sum_out, *refs):
    half = (len(refs) - 2) // 2
    part_in, part_out = slice_grad(
        own_out, active, slope, refs[:half], refs[half : 2 * half], half
    )
    refs[-2][...] = sum_in[...] + part_in
    refs[-1][...] = sum_out[...] + part_out


def hop(value, pairs):
    return lax.ppermute(value, "section", pairs)


def exchange(value, count, mask):
    return lax.ppermute(value, "dp", [(i, i ^ mask) for i in range(count)])


def from_next(value, count, mask):
    pairs = [
        (((section + 1) % 4) * count + i, section * count + (i ^ mask))
        for section in range(4)
        for i in range(count)
    ]
    return lax.ppermute(value, ("section", "dp"), pairs)


def program(saved_inputs, timesteps, time_table, skip_weight, ff_in, ff_out, output_cotangent):
    section = lax.axis_index("section")
    count = lax.axis_size("dp")
    n_micro = saved_inputs.shape[1]
    width = saved_inputs.shape[3]
    span = saved_inputs.shape[2]
    rows = n_micro * span
    hidden = ff_in.shape[1]
    inputs = jnp.swapaxes(saved_inputs[0], 1, 2)
    upstream = jnp.swapaxes(output_cotangent, 1, 2)
    table = time_table.T
    w_skip = skip_weight[0]
    w_in = ff_in[0].T
    w_out = ff_out[0].T
    low = ((width, rows), LOW)
    wide = ((hidden, rows), F32)

    distant = (timesteps, table, w_skip, inputs, w_in, w_out)
    embed, value = call(
        encode_body, [low, low], *distant,
        scratch=[pltpu.VMEM(arg.shape, arg.dtype) for arg in distant]
        + [pltpu.SemaphoreType.DMA((len(distant),))],
        far=range(len(distant)),
    )
    received = hop(value, [(0, 3), (1, 2)])
    top_low, grad_act = call(early_body, [low, wide], upstream, w_out)
    source, normed, united, slope, chain_3 = call(
        decode_body, [low, low, ((width, rows), F32), wide, low],
        received, embed, inputs, top_low, grad_act, w_skip, w_in,
    )
    chain = hop(chain_3, [(3, 2)])
    w_mirror = hop(w_skip, [(2, 1)])
    (back,) = call(back_body, [low], chain_3, w_skip)
    skip_far = hop(back, [(3, 0)])
    skip_next = hop(back, [(3, 1)])
    low_2 = chain
    (chain_2,) = call(tick_body, [low], chain, united, slope, w_in, w_out)
    chain = hop(chain_2, [(2, 1)])
    (back_2,) = call(back_body, [low], chain_2, w_skip)
    chain_1, low_1, ahead = call(
        mirror_tick_body, [low, low, low],
        chain, w_mirror, united, slope, w_in, w_out, skip_next, back_2, chain_2, chain_3,
        top_low,
    )
    chain = hop(chain_1, [(1, 0)])
    (grad_low,) = call(pick_body, [low], chain, skip_far, low_1, low_2, top_low)

    if not (count == 8 and count * rows <= 4096 and width % 128 == 64 and width // 128 == 2):
        return by_reduction(
            section, chain, skip_far, united, slope, w_in, w_out, source, normed, grad_low,
            (chain_1, chain_2, chain_3), saved_inputs.shape,
        )

    part = hidden // count
    own_in, own_out = call(cut_body, [((width, part), LOW)] * 2, w_in, w_out)
    normed_all = [normed] + [exchange(normed, count, mask) for mask in (2, 4, 6)]
    normed_all += [exchange(block, count, 1) for block in normed_all]
    active_all, slope_all = call(
        slice_forward_body,
        [((part, count * rows), LOW), ((part, count * rows), F32)], own_in, *normed_all,
    )
    low_all = [
        grad_low,
        from_next(ahead, count, 2),
        exchange(grad_low, count, 4),
        from_next(ahead, count, 6),
    ]
    low_all += [exchange(block, count, 1) for block in low_all]
    block = (count // 2, width // count, width)
    kept, keep, give = call(
        last_body, [((n_micro, width, span), LOW), (block, F32), (block, LOW)],
        grad_low, chain, skip_far, united, slope, w_in, w_out, source, chain_1, chain_2,
        chain_3,
    )
    given = exchange(give, count, 1)
    piece = block[1:]
    own, *pieces = call(
        join_body, [(piece, F32)] + [(piece, LOW)] * (count // 2 - 1),
        keep, given,
    )
    pieces = [exchange(value, count, 2 * i) for i, value in enumerate(pieces, 1)]
    (grad_skip,) = call(
        flat_body, [((1, piece[0] * piece[1]), F32)], own, *pieces,
        scratch=[
            pltpu.VMEM((3, piece[0], 128), F32),
            pltpu.VMEM((piece[0] * piece[1] // 128, 128), F32),
        ],
    )
    grads = ((part, width), F32)
    half = count // 2
    sums = call(
        half_grad_body, [grads] * 2,
        own_out, active_all, slope_all, *normed_all[:half], *low_all[:half],
    )
    grad_in, grad_out_w = call(
        rest_grad_body, [grads] * 2,
        own_out, active_all, slope_all, *sums, *normed_all[half:], *low_all[half:],
    )
    kept = jnp.swapaxes(kept, 1, 2)
    return (kept[None], grad_skip, grad_in[None], grad_out_w[None])


def by_reduction(
    section, chain, skip_far, united, slope, w_in, w_out, source, normed, grad_low, chains,
    shape,
):
    grad_out = chain.astype(F32) + skip_far.astype(F32)
    grad_pre = (dot(w_out, grad_low, 0, 0) * slope).astype(LOW)
    preact = dot(w_in, normed, 0, 0)
    active = (preact * jax.nn.sigmoid(preact)).astype(LOW)
    own_pre = (dot(w_out, grad_out.astype(LOW), 0, 0) * slope).astype(LOW)
    grad_norm = dot(w_in, own_pre, 1, 0)
    recip = norm_of(united)
    along = jnp.mean(grad_norm * united, axis=0, keepdims=True)
    kept = (grad_out + recip * grad_norm - united * (recip * recip * recip * along)).astype(LOW)
    for owner, other in enumerate(chains, 1):
        kept = jnp.where(section == owner, other, kept)
    grad_in, grad_out_w, grad_skip = (
        lax.psum_scatter(value, "dp", scatter_dimension=0, tiled=True)
        for value in (
            dot(grad_pre, normed, 1, 1),
            dot(active, grad_low, 1, 1),
            dot(source, kept, 1, 1).reshape(-1),
        )
    )
    kept = kept.reshape(shape[3], shape[1], shape[2]).transpose(1, 2, 0)
    return (kept[None], grad_skip[None], grad_in[None], grad_out_w[None])


def solution(mesh):
    in_specs = (
        P("section", None, "dp", None),
        P(None, "dp"),
        P(),
        P("section", None, None),
        P("section", None, None),
        P("section", None, None),
        P(None, "dp", None),
    )
    out_specs = (
        P("section", None, "dp", None),
        P("section", "dp"),
        P("section", "dp", None),
        P("section", "dp", None),
    )
    return jax.shard_map(program, mesh=mesh, in_specs=in_specs, out_specs=out_specs, check_vma=False)
```

time: 91.6 us -> 79.5 us (0.87)
  the two profiles are of different devices: /device:TPU:5 before, /device:TPU:0 now
where the time goes in v3:
time: 79.5 us; the launch traced here: 79.3 us
  starting transfers between devices  32.3 us (41%)
  waiting for transfers between devices  31.1 us (39%)
  Pallas kernels  14.9 us (19%)
  between operations  0.92 us (1%)
    ppermute x16, waiting for transfers between devices, exchange(): return lax.ppermute(value, 'dp', [(i, i ^ mask) for i in range(count)])  22.8 us
    pallas_call x15, Pallas kernels, call(): pl.pallas_call(body, out_shape=[jax.ShapeDtypeStruct(shape, kind) for sha...  14.9 us
    ppermute x2, starting transfers between devices, from_next(): return lax.ppermute(value, ('section', 'dp'), pairs)  11.2 us
    ppermute x7, starting transfers between devices, hop(): return lax.ppermute(value, 'section', pairs)  11.1 us
    ppermute x16, starting transfers between devices, exchange(): return lax.ppermute(value, 'dp', [(i, i ^ mask) for i in range(count)])  9.99 us
    ppermute x7, waiting for transfers between devices, hop(): return lax.ppermute(value, 'section', pairs)  5.04 us
    ppermute x2, waiting for transfers between devices, from_next(): return lax.ppermute(value, ('section', 'dp'), pairs)  3.28 us
  transfers between devices with their start and end apart: 25, of which 9 were waited for; matrix products, arithmetic and copies ran while one was open for 0% of the time, Pallas kernels for 10%

profile of v3, /device:TPU:0, one launch (start us, length us, event | category | flops | bytes accessed | tf_op | source)
XLA Modules:
  0.0 79.3 jit_solution(17015463691224927940)
XLA Ops:
  0.7 3.6 %shard_map.102 = (bf16[320,256]{1,0:T(8,128)(2,1)S(1)}, bf16[320,256]{1,0:T(8,128)(2,1)S(1)}) custom-call(s32[2,128]{1,0:T(2,128)} %refs_0_.1, bf16[320,1000]{1,0:T(8,128)(2,1)} %bitcast.37, bf16[320,320]{1,0:T(8,128)(2,1)} %bitcast.29, bf16[2,320,128]{2,1,0:T(8,128)(2,1)} %bitcast.34, bf16[320,1280]{1,0:T(8,128)(2,1)} %bitcast.17, bf16[320,1280]{1,0:T(8,128)(2,1)} %bitcast.23), custom_call_target="tpu_custom_call" | custom-call | tf_op jit(solution)/shard_map/pallas_call | solution.py:32
  4.2 5.8 %collective-permute-start = (bf16[320,256]{1,0:T(8,128)(2,1)S(1)}, bf16[320,256]{1,0:T(8,128)(2,1)S(1)}, u32[]{:S(2)}, u32[]{:S(2)}) collective-permute-start(bf16[320,256]{1,0:T(8,128)(2,1)S(1)} %get-tuple-element.31), channel_id=1, source_target_pairs={{0,24},{8,16},{1,25},{9,17},{2,26},{10,18},{3,27},{11,19},{4,28},{... | collective-permute-start | bytes 491528 | tf_op jit(solution)/shard_map/ppermute | solution.py:258
  10.1 0.5 shard_map.103
  10.7 2.9 %collective-permute-done.received = bf16[320,256]{1,0:T(8,128)(2,1)S(1)} collective-permute-done((bf16[320,256]{1,0:T(8,128)(2,1)S(1)}, bf16[320,256]{1,0:T(8,128)(2,1)S(1)}, u32[]{:S(2)}, u32[]{:S(2)}) %collective-permute-start) | collective-permute-done | bytes 163872 | tf_op jit(solution)/shard_map/ppermute | solution.py:258
  13.5 1.6 %shard_map.104 = (bf16[320,256]{1,0:T(8,128)(2,1)S(1)}, bf16[320,256]{1,0:T(8,128)(2,1)S(1)}, f32[320,256]{1,0:T(8,128)S(1)}, f32[1280,256]{1,0:T(8,128)S(1)}, bf16[320,256]{1,0:T(8,128)(2,1)S(1)}) custom-call(bf16[320,256]{1,0:T(8,128)(2,1)S(1)} %collective-permute-done.received, bf16[320,256]{1,0:T(8,128)(2,1)S(1)} %get-tuple-element.32.embed, ...), custom_call_target="tpu_custom_call" | custom-call | tf_op jit(solution)/shard_map/pallas_call | solution.py:32
  15.1 0.7 collective-permute-start.1
  15.8 0.7 collective-permute-start.3
  16.5 0.2 shard_map.106
  16.7 0.7 collective-permute-start.4
  17.4 0.0 collective-permute-done.1.received.low_2
  17.4 1.2 %shard_map.105.chain.chain_2 = bf16[320,256]{1,0:T(8,128)(2,1)S(1)} custom-call(bf16[320,256]{1,0:T(8,128)(2,1)S(1)} %collective-permute-done.1.received.low_2, f32[320,256]{1,0:T(8,128)S(1)} %get-tuple-element.36.united, f32[1280,256]{1,0:T(8,128)S(1)} %get-tuple-element.37.slope, bf16[320,1280]{1,0:T(8,128)(2,1)S(1)} %bitcast.19, ...), custom_call_target="tpu_custom_call" | custom-call | tf_op jit(solution)/shard_map/pallas_call | solution.py:32
  18.6 0.7 collective-permute-start.2
  19.3 1.3 %collective-permute-start.6 = (bf16[320,256]{1,0:T(8,128)(2,1)S(1)}, bf16[320,256]{1,0:T(8,128)(2,1)S(1)}, u32[]{:S(2)}, u32[]{:S(2)}) collective-permute-start(bf16[320,256]{1,0:T(8,128)(2,1)S(1)} %shard_map.106), channel_id=1, source_target_pairs={{24,0},{25,1},{26,2},{27,3},{28,4},{29,5},{30,6},{31,7}} | collective-permute-start | bytes 491528 | tf_op jit(solution)/shard_map/ppermute | solution.py:258
  20.6 1.7 %collective-permute-start.11 = (bf16[320,256]{1,0:T(8,128)(2,1)S(1)}, bf16[320,256]{1,0:T(8,128)(2,1)S(1)}, u32[]{:S(2)}, u32[]{:S(2)}) collective-permute-start(bf16[320,256]{1,0:T(8,128)(2,1)S(1)} %get-tuple-element.50.refs_0_), channel_id=1, source_target_pairs={{0,2},{1,3},{2,0},{3,1},{4,6},{5,7},{6,4},{7,5},{8,10},{9,11},{10,... | collective-permute-start | bytes 491528 | tf_op jit(solution)/shard_map/ppermute | solution.py:262
  22.2 0.0 collective-permute-done.3.w_mirror
  22.2 2.6 %collective-permute-start.12 = (bf16[320,256]{1,0:T(8,128)(2,1)S(1)}, bf16[320,256]{1,0:T(8,128)(2,1)S(1)}, u32[]{:S(2)}, u32[]{:S(2)}) collective-permute-start(bf16[320,256]{1,0:T(8,128)(2,1)S(1)} %get-tuple-element.50.refs_0_), channel_id=1, source_target_pairs={{0,4},{1,5},{2,6},{3,7},{4,0},{5,1},{6,2},{7,3},{8,12},{9,13},{10,... | collective-permute-start | bytes 491528 | tf_op jit(solution)/shard_map/ppermute | solution.py:262
  24.8 0.2 shard_map.107.back_2
  25.1 0.0 collective-permute-done.4.skip_far
  25.1 0.3 collective-permute-start.13
  25.4 0.0 collective-permute-done.2.received
  25.4 1.5 %shard_map.108 = (bf16[320,256]{1,0:T(8,128)(2,1)S(1)}, bf16[320,256]{1,0:T(8,128)(2,1)S(1)}, bf16[320,256]{1,0:T(8,128)(2,1)S(1)}) custom-call(bf16[320,256]{1,0:T(8,128)(2,1)S(1)} %collective-permute-done.2.received, bf16[320,320]{1,0:T(8,128)(2,1)S(1)} %collective-permute-done.3.w_mirror, f32[320,256]{1,0:T(8,128)S(1)} %get-tuple-element.36.united, ...), custom_call_target="tpu_custom_call" | custom-call | tf_op jit(solution)/shard_map/pallas_call | solution.py:32
  26.9 1.3 %collective-permute-start.5 = (bf16[320,256]{1,0:T(8,128)(2,1)S(1)}, bf16[320,256]{1,0:T(8,128)(2,1)S(1)}, u32[]{:S(2)}, u32[]{:S(2)}) collective-permute-start(bf16[320,256]{1,0:T(8,128)(2,1)S(1)} %get-tuple-element.38.chain_1), channel_id=1, source_target_pairs={{8,0},{9,1},{10,2},{11,3},{12,4},{13,5},{14,6},{15,7}} | collective-permute-start | bytes 491528 | tf_op jit(solution)/shard_map/ppermute | solution.py:258
  28.2 2.0 %collective-permute-done.6.skip_far = bf16[320,256]{1,0:T(8,128)(2,1)S(1)} collective-permute-done((bf16[320,256]{1,0:T(8,128)(2,1)S(1)}, bf16[320,256]{1,0:T(8,128)(2,1)S(1)}, u32[]{:S(2)}, u32[]{:S(2)}) %collective-permute-start.6) | collective-permute-done | bytes 163872 | tf_op jit(solution)/shard_map/ppermute | solution.py:258
  30.2 0.0 collective-permute-start.14
  30.2 0.0 collective-permute-done.11.refs_1_
  30.2 0.5 collective-permute-start.15
  30.7 6.0 %collective-permute-done.12.refs_2_ = bf16[320,256]{1,0:T(8,128)(2,1)S(1)} collective-permute-done((bf16[320,256]{1,0:T(8,128)(2,1)S(1)}, bf16[320,256]{1,0:T(8,128)(2,1)S(1)}, u32[]{:S(2)}, u32[]{:S(2)}) %collective-permute-start.12) | collective-permute-done | bytes 163872 | tf_op jit(solution)/shard_map/ppermute | solution.py:262
  36.8 0.0 collective-permute-start.16
  36.8 0.0 collective-permute-done.13.refs_3_
  36.8 7.3 %collective-permute-start.18 = (bf16[320,256]{1,0:T(8,128)(2,1)S(1)}, bf16[320,256]{1,0:T(8,128)(2,1)S(1)}, u32[]{:S(2)}, u32[]{:S(2)}) collective-permute-start(bf16[320,256]{1,0:T(8,128)(2,1)S(1)} %get-tuple-element.53), channel_id=1, source_target_pairs={{8,2},{9,3},{10,0},{11,1},{12,6},{13,7},{14,4},{15,5},{16,10},{17,... | collective-permute-start | bytes 491528 | tf_op jit(solution)/shard_map/ppermute | solution.py:271
  44.1 0.1 collective-permute-done.5.received
  44.2 3.9 %collective-permute-start.20 = (bf16[320,256]{1,0:T(8,128)(2,1)S(1)}, bf16[320,256]{1,0:T(8,128)(2,1)S(1)}, u32[]{:S(2)}, u32[]{:S(2)}) collective-permute-start(bf16[320,256]{1,0:T(8,128)(2,1)S(1)} %get-tuple-element.53), channel_id=1, source_target_pairs={{8,6},{9,7},{10,4},{11,5},{12,2},{13,3},{14,0},{15,1},{16,14},{17,... | collective-permute-start | bytes 491528 | tf_op jit(solution)/shard_map/ppermute | solution.py:271
  48.1 0.1 shard_map.109.grad_low.refs_4_
  48.2 0.0 collective-permute-done.14.refs_4_.refs_0_
  48.2 0.1 collective-permute-start.19
  48.3 2.0 %shard_map.110 = (bf16[2,320,128]{2,1,0:T(8,128)(2,1)}, f32[4,40,320]{2,1,0:T(8,128)S(1)}, bf16[4,40,320]{2,1,0:T(8,128)(2,1)S(1)}) custom-call(bf16[320,256]{1,0:T(8,128)(2,1)S(1)} %shard_map.109.grad_low.refs_4_, bf16[320,256]{1,0:T(8,128)(2,1)S(1)} %collective-permute-done.5.received, bf16[320,256]{1,0:T(8,128)(2,1)S(1)} %collective-permute-done.6.skip_far, ...), custom_call_target="tpu_custom_call" | custom-call | tf_op jit(solution)/shard_map/pallas_call | solution.py:32
  50.2 0.0 collective-permute-done.15.refs_5_.refs_1_
  50.2 0.0 collective-permute-start.7
  50.2 0.0 collective-permute-done.16.refs_6_.refs_2_
  50.2 0.5 collective-permute-start.17
  50.8 0.0 collective-permute-done.18.refs_5_
  50.8 0.1 collective-permute-start.21
  50.8 3.3 %collective-permute-done.20.refs_7_ = bf16[320,256]{1,0:T(8,128)(2,1)S(1)} collective-permute-done((bf16[320,256]{1,0:T(8,128)(2,1)S(1)}, bf16[320,256]{1,0:T(8,128)(2,1)S(1)}, u32[]{:S(2)}, u32[]{:S(2)}) %collective-permute-start.20) | collective-permute-done | bytes 163872 | tf_op jit(solution)/shard_map/ppermute | solution.py:271
  54.1 0.0 collective-permute-start.22
  54.1 0.0 collective-permute-done.7.given
  54.1 0.5 collective-permute-start.24
  54.6 7.0 %collective-permute-done.19.refs_6_ = bf16[320,256]{1,0:T(8,128)(2,1)S(1)} collective-permute-done((bf16[320,256]{1,0:T(8,128)(2,1)S(1)}, bf16[320,256]{1,0:T(8,128)(2,1)S(1)}, u32[]{:S(2)}, u32[]{:S(2)}) %collective-permute-start.19) | collective-permute-done | bytes 163872 | tf_op jit(solution)/shard_map/ppermute | solution.py:262
  61.6 0.0 collective-permute-start.23
  61.6 0.0 collective-permute-done.17.refs_7_.refs_3_
  61.7 0.1 collective-permute-start.8
  61.7 3.9 %collective-permute-done.8.refs_0_ = bf16[40,320]{1,0:T(8,128)(2,1)S(1)} collective-permute-done((bf16[40,320]{1,0:T(8,128)(2,1)S(1)}, bf16[40,320]{1,0:T(8,128)(2,1)S(1)}, u32[]{:S(2)}, u32[]{:S(2)}) %collective-permute-start.8) | collective-permute-done | bytes 25632 | tf_op jit(solution)/shard_map/ppermute | solution.py:262
  65.6 1.2 %collective-permute-start.9 = (bf16[40,320]{1,0:T(8,128)(2,1)S(1)}, bf16[40,320]{1,0:T(8,128)(2,1)S(1)}, u32[]{:S(2)}, u32[]{:S(2)}) collective-permute-start(bf16[40,320]{1,0:T(8,128)(2,1)S(1)} %get-tuple-element.46), channel_id=1, source_target_pairs={{0,4},{1,5},{2,6},{3,7},{4,0},{5,1},{6,2},{7,3},{8,12},{9,13},{10,... | collective-permute-start | bytes 76808 | tf_op jit(solution)/shard_map/ppermute | solution.py:262
  66.8 3.6 %collective-permute-done.9.refs_1_ = bf16[40,320]{1,0:T(8,128)(2,1)S(1)} collective-permute-done((bf16[40,320]{1,0:T(8,128)(2,1)S(1)}, bf16[40,320]{1,0:T(8,128)(2,1)S(1)}, u32[]{:S(2)}, u32[]{:S(2)}) %collective-permute-start.9) | collective-permute-done | bytes 25632 | tf_op jit(solution)/shard_map/ppermute | solution.py:262
  70.4 2.5 %collective-permute-start.10 = (bf16[40,320]{1,0:T(8,128)(2,1)S(1)}, bf16[40,320]{1,0:T(8,128)(2,1)S(1)}, u32[]{:S(2)}, u32[]{:S(2)}) collective-permute-start(bf16[40,320]{1,0:T(8,128)(2,1)S(1)} %get-tuple-element.47), channel_id=1, source_target_pairs={{0,6},{1,7},{2,4},{3,5},{4,2},{5,3},{6,0},{7,1},{8,14},{9,15},{10,... | collective-permute-start | bytes 76808 | tf_op jit(solution)/shard_map/ppermute | solution.py:262
  72.9 0.1 shard_map.113
  73.0 0.8 %shard_map.114 = (bf16[160,2048]{1,0:T(8,128)(2,1)S(1)}, f32[160,2048]{1,0:T(8,128)S(1)}) custom-call(bf16[320,160]{1,0:T(8,128)(2,1)S(1)} %get-tuple-element.49.own_in, bf16[320,256]{1,0:T(8,128)(2,1)S(1)} %get-tuple-element.50.refs_0_, bf16[320,256]{1,0:T(8,128)(2,1)S(1)} %collective-permute-done.11.refs_1_, ...), custom_call_target="tpu_custom_call" | custom-call | tf_op jit(solution)/shard_map/pallas_call | solution.py:32
  73.8 2.3 %collective-permute-done.10.refs_2_ = bf16[40,320]{1,0:T(8,128)(2,1)S(1)} collective-permute-done((bf16[40,320]{1,0:T(8,128)(2,1)S(1)}, bf16[40,320]{1,0:T(8,128)(2,1)S(1)}, u32[]{:S(2)}, u32[]{:S(2)}) %collective-permute-start.10) | collective-permute-done | bytes 25632 | tf_op jit(solution)/shard_map/ppermute | solution.py:262
  76.1 0.8 shard_map.112
  76.9 0.8 %shard_map.115 = (f32[160,320]{1,0:T(8,128)S(1)}, f32[160,320]{1,0:T(8,128)S(1)}) custom-call(bf16[320,160]{1,0:T(8,128)(2,1)S(1)} %get-tuple-element.48.own_out, bf16[160,2048]{1,0:T(8,128)(2,1)S(1)} %get-tuple-element.51.active, f32[160,2048]{1,0:T(8,128)S(1)} %get-tuple-element.52.slope, bf16[320,256]{1,0:T(8,128)(2,1)S(1)} %get-tuple-element.50.refs_0_, ...), custom_call_target="tpu_custom_call" | custom-call | tf_op jit(solution)/shard_map/pallas_call | solution.py:32
  77.7 0.0 collective-permute-done.21.refs_4_
  77.7 0.0 collective-permute-done.22.refs_5_
  77.7 0.0 collective-permute-done.24.refs_7_
  77.7 0.0 collective-permute-done.23.refs_6_
  77.7 1.5 %shard_map.116 = (f32[160,320]{1,0:T(8,128)}, f32[160,320]{1,0:T(8,128)}) custom-call(bf16[320,160]{1,0:T(8,128)(2,1)S(1)} %get-tuple-element.48.own_out, bf16[160,2048]{1,0:T(8,128)(2,1)S(1)} %get-tuple-element.51.active, f32[160,2048]{1,0:T(8,128)S(1)} %get-tuple-element.52.slope, f32[160,320]{1,0:T(8,128)S(1)} %get-tuple-element.54.sum_in, ...), custom_call_target="tpu_custom_call" | custom-call | tf_op jit(solution)/shard_map/pallas_call | solution.py:32
  (11 shorter events, 0.1 us)
Async XLA Ops:
  0.6 9.5 %copy-start.1 = (bf16[1,1280,320]{1,2,0:T(8,128)(2,1)S(1)}, bf16[1,1280,320]{1,2,0:T(8,128)(2,1)}, u32[]{:S(2)}) copy-start(bf16[1,1280,320]{1,2,0:T(8,128)(2,1)} %param.12) | copy-start | bytes 2457604
  0.6 9.5 %copy-start.4 = (bf16[2,128,320]{1,2,0:T(8,128)(2,1)S(1)}, bf16[2,128,320]{1,2,0:T(8,128)(2,1)}, u32[]{:S(2)}) copy-start(bf16[2,128,320]{1,2,0:T(8,128)(2,1)} %param.13) | copy-start | bytes 491524
  0.7 12.9 %copy-start = (bf16[1,1280,320]{1,2,0:T(8,128)(2,1)S(1)}, bf16[1,1280,320]{1,2,0:T(8,128)(2,1)}, u32[]{:S(2)}) copy-start(bf16[1,1280,320]{1,2,0:T(8,128)(2,1)} %param.11) | copy-start | bytes 2457604
  0.7 12.9 %copy-start.2 = (bf16[1,320,320]{2,1,0:T(8,128)(2,1)S(1)}, bf16[1,320,320]{2,1,0:T(8,128)(2,1)}, u32[]{:S(2)}) copy-start(bf16[1,320,320]{2,1,0:T(8,128)(2,1)} %param.10) | copy-start | bytes 614404
  0.7 12.9 %copy-start.3 = (bf16[1,2,128,320]{2,3,1,0:T(8,128)(2,1)S(1)}, bf16[1,2,128,320]{2,3,1,0:T(8,128)(2,1)}, u32[]{:S(2)}) copy-start(bf16[1,2,128,320]{2,3,1,0:T(8,128)(2,1)} %param.7) | copy-start | bytes 491524
  4.2 9.3 %collective-permute-start = (bf16[320,256]{1,0:T(8,128)(2,1)S(1)}, bf16[320,256]{1,0:T(8,128)(2,1)S(1)}, u32[]{:S(2)}, u32[]{:S(2)}) collective-permute-start(bf16[320,256]{1,0:T(8,128)(2,1)S(1)} %get-tuple-element.31), channel_id=1, source_target_pairs={{0,24},{8,16},{1,25},{9,17},{2,26},{10,18},{3,27},{11,19},{4,28},{... | collective-permute-start | bytes 491528 | tf_op jit(solution)/shard_map/ppermute | solution.py:258
  15.1 2.3 %collective-permute-start.1 = (bf16[320,256]{1,0:T(8,128)(2,1)S(1)}, bf16[320,256]{1,0:T(8,128)(2,1)S(1)}, u32[]{:S(2)}, u32[]{:S(2)}) collective-permute-start(bf16[320,256]{1,0:T(8,128)(2,1)S(1)} %get-tuple-element.35.chain.chain_3), channel_id=1, source_target_pairs={{24,16},{25,17},{26,18},{27,19},{28,20},{29,21},{30,22},{31,23}} | collective-permute-start | bytes 491528 | tf_op jit(solution)/shard_map/ppermute | solution.py:258
  15.8 6.4 %collective-permute-start.3 = (bf16[320,320]{1,0:T(8,128)(2,1)S(1)}, bf16[320,320]{1,0:T(8,128)(2,1)S(1)}, u32[]{:S(2)}, u32[]{:S(2)}) collective-permute-start(bf16[320,320]{1,0:T(8,128)(2,1)S(1)} %bitcast.31), channel_id=1, source_target_pairs={{16,8},{17,9},{18,10},{19,11},{20,12},{21,13},{22,14},{23,15}} | collective-permute-start | bytes 614408 | tf_op jit(solution)/shard_map/ppermute | solution.py:258
  16.7 8.4 %collective-permute-start.4 = (bf16[320,256]{1,0:T(8,128)(2,1)S(1)}, bf16[320,256]{1,0:T(8,128)(2,1)S(1)}, u32[]{:S(2)}, u32[]{:S(2)}) collective-permute-start(bf16[320,256]{1,0:T(8,128)(2,1)S(1)} %shard_map.106), channel_id=1, source_target_pairs={{24,8},{25,9},{26,10},{27,11},{28,12},{29,13},{30,14},{31,15}} | collective-permute-start | bytes 491528 | tf_op jit(solution)/shard_map/ppermute | solution.py:258
  18.6 6.8 %collective-permute-start.2 = (bf16[320,256]{1,0:T(8,128)(2,1)S(1)}, bf16[320,256]{1,0:T(8,128)(2,1)S(1)}, u32[]{:S(2)}, u32[]{:S(2)}) collective-permute-start(bf16[320,256]{1,0:T(8,128)(2,1)S(1)} %shard_map.105.chain.chain_2), channel_id=1, source_target_pairs={{16,8},{17,9},{18,10},{19,11},{20,12},{21,13},{22,14},{23,15}} | collective-permute-start | bytes 491528 | tf_op jit(solution)/shard_map/ppermute | solution.py:258
  19.3 10.9 %collective-permute-start.6 = (bf16[320,256]{1,0:T(8,128)(2,1)S(1)}, bf16[320,256]{1,0:T(8,128)(2,1)S(1)}, u32[]{:S(2)}, u32[]{:S(2)}) collective-permute-start(bf16[320,256]{1,0:T(8,128)(2,1)S(1)} %shard_map.106), channel_id=1, source_target_pairs={{24,0},{25,1},{26,2},{27,3},{28,4},{29,5},{30,6},{31,7}} | collective-permute-start | bytes 491528 | tf_op jit(solution)/shard_map/ppermute | solution.py:258
  20.6 9.6 %collective-permute-start.11 = (bf16[320,256]{1,0:T(8,128)(2,1)S(1)}, bf16[320,256]{1,0:T(8,128)(2,1)S(1)}, u32[]{:S(2)}, u32[]{:S(2)}) collective-permute-start(bf16[320,256]{1,0:T(8,128)(2,1)S(1)} %get-tuple-element.50.refs_0_), channel_id=1, source_target_pairs={{0,2},{1,3},{2,0},{3,1},{4,6},{5,7},{6,4},{7,5},{8,10},{9,11},{10,... | collective-permute-start | bytes 491528 | tf_op jit(solution)/shard_map/ppermute | solution.py:262
  22.2 14.5 %collective-permute-start.12 = (bf16[320,256]{1,0:T(8,128)(2,1)S(1)}, bf16[320,256]{1,0:T(8,128)(2,1)S(1)}, u32[]{:S(2)}, u32[]{:S(2)}) collective-permute-start(bf16[320,256]{1,0:T(8,128)(2,1)S(1)} %get-tuple-element.50.refs_0_), channel_id=1, source_target_pairs={{0,4},{1,5},{2,6},{3,7},{4,0},{5,1},{6,2},{7,3},{8,12},{9,13},{10,... | collective-permute-start | bytes 491528 | tf_op jit(solution)/shard_map/ppermute | solution.py:262
  25.1 11.7 %collective-permute-start.13 = (bf16[320,256]{1,0:T(8,128)(2,1)S(1)}, bf16[320,256]{1,0:T(8,128)(2,1)S(1)}, u32[]{:S(2)}, u32[]{:S(2)}) collective-permute-start(bf16[320,256]{1,0:T(8,128)(2,1)S(1)} %get-tuple-element.50.refs_0_), channel_id=1, source_target_pairs={{0,6},{1,7},{2,4},{3,5},{4,2},{5,3},{6,0},{7,1},{8,14},{9,15},{10,... | collective-permute-start | bytes 491528 | tf_op jit(solution)/shard_map/ppermute | solution.py:262
  26.9 17.3 %collective-permute-start.5 = (bf16[320,256]{1,0:T(8,128)(2,1)S(1)}, bf16[320,256]{1,0:T(8,128)(2,1)S(1)}, u32[]{:S(2)}, u32[]{:S(2)}) collective-permute-start(bf16[320,256]{1,0:T(8,128)(2,1)S(1)} %get-tuple-element.38.chain_1), channel_id=1, source_target_pairs={{8,0},{9,1},{10,2},{11,3},{12,4},{13,5},{14,6},{15,7}} | collective-permute-start | bytes 491528 | tf_op jit(solution)/shard_map/ppermute | solution.py:258
  30.2 18.0 %collective-permute-start.14 = (bf16[320,256]{1,0:T(8,128)(2,1)S(1)}, bf16[320,256]{1,0:T(8,128)(2,1)S(1)}, u32[]{:S(2)}, u32[]{:S(2)}) collective-permute-start(bf16[320,256]{1,0:T(8,128)(2,1)S(1)} %get-tuple-element.50.refs_0_), channel_id=1, source_target_pairs={{0,1},{1,0},{2,3},{3,2},{4,5},{5,4},{6,7},{7,6},{8,9},{9,8},{10,11... | collective-permute-start | bytes 491528 | tf_op jit(solution)/shard_map/ppermute | solution.py:262
  30.2 20.0 %collective-permute-start.15 = (bf16[320,256]{1,0:T(8,128)(2,1)S(1)}, bf16[320,256]{1,0:T(8,128)(2,1)S(1)}, u32[]{:S(2)}, u32[]{:S(2)}) collective-permute-start(bf16[320,256]{1,0:T(8,128)(2,1)S(1)} %collective-permute-done.11.refs_1_), channel_id=1, source_target_pairs={{0,1},{1,0},{2,3},{3,2},{4,5},{5,4},{6,7},{7,6},{8,9},{9,8},{10,11... | collective-permute-start | bytes 491528 | tf_op jit(solution)/shard_map/ppermute | solution.py:262
  36.8 13.5 %collective-permute-start.16 = (bf16[320,256]{1,0:T(8,128)(2,1)S(1)}, bf16[320,256]{1,0:T(8,128)(2,1)S(1)}, u32[]{:S(2)}, u32[]{:S(2)}) collective-permute-start(bf16[320,256]{1,0:T(8,128)(2,1)S(1)} %collective-permute-done.12.refs_2_), channel_id=1, source_target_pairs={{0,1},{1,0},{2,3},{3,2},{4,5},{5,4},{6,7},{7,6},{8,9},{9,8},{10,11... | collective-permute-start | bytes 491528 | tf_op jit(solution)/shard_map/ppermute | solution.py:262
  36.8 14.0 %collective-permute-start.18 = (bf16[320,256]{1,0:T(8,128)(2,1)S(1)}, bf16[320,256]{1,0:T(8,128)(2,1)S(1)}, u32[]{:S(2)}, u32[]{:S(2)}) collective-permute-start(bf16[320,256]{1,0:T(8,128)(2,1)S(1)} %get-tuple-element.53), channel_id=1, source_target_pairs={{8,2},{9,3},{10,0},{11,1},{12,6},{13,7},{14,4},{15,5},{16,10},{17,... | collective-permute-start | bytes 491528 | tf_op jit(solution)/shard_map/ppermute | solution.py:271
  44.2 9.9 %collective-permute-start.20 = (bf16[320,256]{1,0:T(8,128)(2,1)S(1)}, bf16[320,256]{1,0:T(8,128)(2,1)S(1)}, u32[]{:S(2)}, u32[]{:S(2)}) collective-permute-start(bf16[320,256]{1,0:T(8,128)(2,1)S(1)} %get-tuple-element.53), channel_id=1, source_target_pairs={{8,6},{9,7},{10,4},{11,5},{12,2},{13,3},{14,0},{15,1},{16,14},{17,... | collective-permute-start | bytes 491528 | tf_op jit(solution)/shard_map/ppermute | solution.py:271
  48.2 13.4 %collective-permute-start.19 = (bf16[320,256]{1,0:T(8,128)(2,1)S(1)}, bf16[320,256]{1,0:T(8,128)(2,1)S(1)}, u32[]{:S(2)}, u32[]{:S(2)}) collective-permute-start(bf16[320,256]{1,0:T(8,128)(2,1)S(1)} %shard_map.109.grad_low.refs_4_), channel_id=1, source_target_pairs={{0,4},{1,5},{2,6},{3,7},{4,0},{5,1},{6,2},{7,3},{8,12},{9,13},{10,... | collective-permute-start | bytes 491528 | tf_op jit(solution)/shard_map/ppermute | solution.py:262
  50.2 3.9 %collective-permute-start.7 = (bf16[4,40,320]{2,1,0:T(8,128)(2,1)S(1)}, bf16[4,40,320]{2,1,0:T(8,128)(2,1)S(1)}, u32[]{:S(2)}, u32[]{:S(2)}) collective-permute-start(bf16[4,40,320]{2,1,0:T(8,128)(2,1)S(1)} %get-tuple-element.43), channel_id=1, source_target_pairs={{0,1},{1,0},{2,3},{3,2},{4,5},{5,4},{6,7},{7,6},{8,9},{9,8},{10,11... | collective-permute-start | bytes 307208 | tf_op jit(solution)/shard_map/ppermute | solution.py:262
  50.2 11.4 %collective-permute-start.17 = (bf16[320,256]{1,0:T(8,128)(2,1)S(1)}, bf16[320,256]{1,0:T(8,128)(2,1)S(1)}, u32[]{:S(2)}, u32[]{:S(2)}) collective-permute-start(bf16[320,256]{1,0:T(8,128)(2,1)S(1)} %collective-permute-done.13.refs_3_), channel_id=1, source_target_pairs={{0,1},{1,0},{2,3},{3,2},{4,5},{5,4},{6,7},{7,6},{8,9},{9,8},{10,11... | collective-permute-start | bytes 491528 | tf_op jit(solution)/shard_map/ppermute | solution.py:262
  50.8 27.0 %collective-permute-start.21 = (bf16[320,256]{1,0:T(8,128)(2,1)S(1)}, bf16[320,256]{1,0:T(8,128)(2,1)S(1)}, u32[]{:S(2)}, u32[]{:S(2)}) collective-permute-start(bf16[320,256]{1,0:T(8,128)(2,1)S(1)} %shard_map.109.grad_low.refs_4_), channel_id=1, source_target_pairs={{0,1},{1,0},{2,3},{3,2},{4,5},{5,4},{6,7},{7,6},{8,9},{9,8},{10,11... | collective-permute-start | bytes 491528 | tf_op jit(solution)/shard_map/ppermute | solution.py:262
  54.1 23.6 %collective-permute-start.22 = (bf16[320,256]{1,0:T(8,128)(2,1)S(1)}, bf16[320,256]{1,0:T(8,128)(2,1)S(1)}, u32[]{:S(2)}, u32[]{:S(2)}) collective-permute-start(bf16[320,256]{1,0:T(8,128)(2,1)S(1)} %collective-permute-done.18.refs_5_), channel_id=1, source_target_pairs={{0,1},{1,0},{2,3},{3,2},{4,5},{5,4},{6,7},{7,6},{8,9},{9,8},{10,11... | collective-permute-start | bytes 491528 | tf_op jit(solution)/shard_map/ppermute | solution.py:262
  54.1 23.6 %collective-permute-start.24 = (bf16[320,256]{1,0:T(8,128)(2,1)S(1)}, bf16[320,256]{1,0:T(8,128)(2,1)S(1)}, u32[]{:S(2)}, u32[]{:S(2)}) collective-permute-start(bf16[320,256]{1,0:T(8,128)(2,1)S(1)} %collective-permute-done.20.refs_7_), channel_id=1, source_target_pairs={{0,1},{1,0},{2,3},{3,2},{4,5},{5,4},{6,7},{7,6},{8,9},{9,8},{10,11... | collective-permute-start | bytes 491528 | tf_op jit(solution)/shard_map/ppermute | solution.py:262
  61.6 16.1 %collective-permute-start.23 = (bf16[320,256]{1,0:T(8,128)(2,1)S(1)}, bf16[320,256]{1,0:T(8,128)(2,1)S(1)}, u32[]{:S(2)}, u32[]{:S(2)}) collective-permute-start(bf16[320,256]{1,0:T(8,128)(2,1)S(1)} %collective-permute-done.19.refs_6_), channel_id=1, source_target_pairs={{0,1},{1,0},{2,3},{3,2},{4,5},{5,4},{6,7},{7,6},{8,9},{9,8},{10,11... | collective-permute-start | bytes 491528 | tf_op jit(solution)/shard_map/ppermute | solution.py:262
  61.7 4.0 %collective-permute-start.8 = (bf16[40,320]{1,0:T(8,128)(2,1)S(1)}, bf16[40,320]{1,0:T(8,128)(2,1)S(1)}, u32[]{:S(2)}, u32[]{:S(2)}) collective-permute-start(bf16[40,320]{1,0:T(8,128)(2,1)S(1)} %get-tuple-element.45), channel_id=1, source_target_pairs={{0,2},{1,3},{2,0},{3,1},{4,6},{5,7},{6,4},{7,5},{8,10},{9,11},{10,... | collective-permute-start | bytes 76808 | tf_op jit(solution)/shard_map/ppermute | solution.py:262
  65.6 4.8 %collective-permute-start.9 = (bf16[40,320]{1,0:T(8,128)(2,1)S(1)}, bf16[40,320]{1,0:T(8,128)(2,1)S(1)}, u32[]{:S(2)}, u32[]{:S(2)}) collective-permute-start(bf16[40,320]{1,0:T(8,128)(2,1)S(1)} %get-tuple-element.46), channel_id=1, source_target_pairs={{0,4},{1,5},{2,6},{3,7},{4,0},{5,1},{6,2},{7,3},{8,12},{9,13},{10,... | collective-permute-start | bytes 76808 | tf_op jit(solution)/shard_map/ppermute | solution.py:262
  70.4 5.7 %collective-permute-start.10 = (bf16[40,320]{1,0:T(8,128)(2,1)S(1)}, bf16[40,320]{1,0:T(8,128)(2,1)S(1)}, u32[]{:S(2)}, u32[]{:S(2)}) collective-permute-start(bf16[40,320]{1,0:T(8,128)(2,1)S(1)} %get-tuple-element.47), channel_id=1, source_target_pairs={{0,6},{1,7},{2,4},{3,5},{4,2},{5,3},{6,0},{7,1},{8,14},{9,15},{10,... | collective-permute-start | bytes 76808 | tf_op jit(solution)/shard_map/ppermute | solution.py:262

commit v4 on v3

--- a/solution.py
+++ b/solution.py
@@ -52,7 +52,10 @@
 
 
 def encode_body(*refs):
-    distant, (embed_out, value_out), local, sems = refs[:6], refs[6:8], refs[8:14], refs[14]
+    distant, (embed_out, value_out), kept, local, sems = (
+        refs[:6], refs[6:8], refs[8:12], refs[12:14], refs[14],
+    )
+    local = (*local, *kept)
     copies = [
         pltpu.make_async_copy(source, target, sems.at[index])
         for index, (source, target) in enumerate(zip(distant, local))
@@ -123,7 +126,7 @@
 
 def mirror_tick_body(
     received, w_mirror, united, slope, w_in, w_out, skip_far, back_2, chain_2, chain_3,
-    top_low, chain_out, low_out, next_out,
+    chain_out, low_out, next_out,
 ):
     back = dot(w_mirror[...], received[...], 1, 0).astype(LOW)
     grad_out = received[...].astype(F32) + back.astype(F32)
@@ -137,8 +140,7 @@
     ahead = jnp.where(
         section == 2, (chain_2[...].astype(F32) + back_2[...].astype(F32)).astype(LOW), ahead
     )
-    ahead = jnp.where(section == 3, chain_3[...], ahead)
-    next_out[...] = jnp.where(section == 0, top_low[...], ahead)
+    next_out[...] = jnp.where(section == 3, chain_3[...], ahead)
 
 
 def pick_body(received, skip_far, low_1, low_2, top_low, grad_low_out):
@@ -147,6 +149,12 @@
     own = jnp.where(section == 1, low_1[...], own)
     own = jnp.where(section == 2, low_2[...], own)
     grad_low_out[...] = jnp.where(section == 3, top_low[...], own)
+
+
+def merge_body(top_2, top_6, next_2, next_6, out_2, out_6):
+    last = lax.axis_index("section") == 3
+    out_2[...] = jnp.where(last, top_2[...], next_2[...])
+    out_6[...] = jnp.where(last, top_6[...], next_6[...])
 
 
 def last_body(
@@ -247,8 +255,9 @@
 
 def rest_grad_body(own_out, active, slope, sum_in, sum_out, *refs):
     half = (len(refs) - 2) // 2
+    first = active.shape[1] // refs[0].shape[1] - half
     part_in, part_out = slice_grad(
-        own_out, active, slope, refs[:half], refs[half : 2 * half], half
+        own_out, active, slope, refs[:half], refs[half : 2 * half], first
     )
     refs[-2][...] = sum_in[...] + part_in
     refs[-1][...] = sum_out[...] + part_out
@@ -258,16 +267,25 @@
     return lax.ppermute(value, "section", pairs)
 
 
+def in_turn(near, swapped):
+    return [*near[:3], *swapped[:3], near[3], swapped[3]]
+
+
 def exchange(value, count, mask):
     return lax.ppermute(value, "dp", [(i, i ^ mask) for i in range(count)])
 
 
 def from_next(value, count, mask):
     pairs = [
-        (((section + 1) % 4) * count + i, section * count + (i ^ mask))
-        for section in range(4)
+        ((section + 1) * count + i, section * count + (i ^ mask))
+        for section in range(3)
         for i in range(count)
     ]
+    return lax.ppermute(value, ("section", "dp"), pairs)
+
+
+def in_last(value, count, mask):
+    pairs = [(3 * count + i, 3 * count + (i ^ mask)) for i in range(count)]
     return lax.ppermute(value, ("section", "dp"), pairs)
 
 
@@ -289,9 +307,10 @@
     wide = ((hidden, rows), F32)
 
     distant = (timesteps, table, w_skip, inputs, w_in, w_out)
-    embed, value = call(
-        encode_body, [low, low], *distant,
-        scratch=[pltpu.VMEM(arg.shape, arg.dtype) for arg in distant]
+    embed, value, w_skip, inputs, w_in, w_out = call(
+        encode_body, [low, low] + [(arg.shape, arg.dtype) for arg in distant[2:]],
+        *distant,
+        scratch=[pltpu.VMEM(arg.shape, arg.dtype) for arg in distant[:2]]
         + [pltpu.SemaphoreType.DMA((len(distant),))],
         far=range(len(distant)),
     )
@@ -313,7 +332,6 @@
     chain_1, low_1, ahead = call(
         mirror_tick_body, [low, low, low],
         chain, w_mirror, united, slope, w_in, w_out, skip_next, back_2, chain_2, chain_3,
-        top_low,
     )
     chain = hop(chain_1, [(1, 0)])
     (grad_low,) = call(pick_body, [low], chain, skip_far, low_1, low_2, top_low)
@@ -326,19 +344,21 @@
 
     part = hidden // count
     own_in, own_out = call(cut_body, [((width, part), LOW)] * 2, w_in, w_out)
-    normed_all = [normed] + [exchange(normed, count, mask) for mask in (2, 4, 6)]
-    normed_all += [exchange(block, count, 1) for block in normed_all]
+    masks = (2, 6, 4)
+    normed_near = [normed] + [exchange(normed, count, m) for m in masks]
+    normed_all = in_turn(
+        normed_near,
+        [exchange(x, count, 1) for x in normed_near],
+    )
     active_all, slope_all = call(
         slice_forward_body,
         [((part, count * rows), LOW), ((part, count * rows), F32)], own_in, *normed_all,
     )
-    low_all = [
-        grad_low,
-        from_next(ahead, count, 2),
-        exchange(grad_low, count, 4),
-        from_next(ahead, count, 6),
-    ]
-    low_all += [exchange(block, count, 1) for block in low_all]
+    tops = [in_last(top_low, count, m) for m in masks[:2]]
+    aheads = [from_next(ahead, count, m) for m in masks[:2]]
+    low_2, low_6 = call(merge_body, [low, low], *tops, *aheads)
+    low_near = [grad_low, low_2, low_6, exchange(grad_low, count, 4)]
+    low_all = in_turn(low_near, [exchange(x, count, 1) for x in low_near])
     block = (count // 2, width // count, width)
     kept, keep, give = call(
         last_body, [((n_micro, width, span), LOW), (block, F32), (block, LOW)],
@@ -360,7 +380,7 @@
         ],
     )
     grads = ((part, width), F32)
-    half = count // 2
+    half = 6
     sums = call(
         half_grad_body, [grads] * 2,
         own_out, active_all, slope_all, *normed_all[:half], *low_all[:half],

time: 79.5 us -> 81.7 us (1.028)
  starting transfers between devices: 32.3 us -> 34.6 us
    ppermute x16, waiting for transfers between devices: 22.8 us -> 6.35 us  [exchange(): return lax.ppermute(value, 'dp', [(i, i ^ mask) for i in range(count)])]
    ppermute x7, waiting for transfers between devices: 5.04 us -> 19.7 us  [hop(): return lax.ppermute(value, 'section', pairs)]
    ppermute x16, starting transfers between devices: 9.99 us -> 19.5 us  [exchange(): return lax.ppermute(value, 'dp', [(i, i ^ mask) for i in range(count)])]
    ppermute x2, starting transfers between devices: 11.2 us -> 2.57 us  [from_next(): return lax.ppermute(value, ('section', 'dp'), pairs)]
    ppermute x2, waiting for transfers between devices: 3.28 us -> 4.86 us  [from_next(): return lax.ppermute(value, ('section', 'dp'), pairs)]
    ppermute x0 -> x2, starting transfers between devices: none -> 1.34 us  [in_last(): return lax.ppermute(value, ('section', 'dp'), pairs)]
    pallas_call x15 -> x16, Pallas kernels: 14.9 us -> 14.9 us  [call(): pl.pallas_call(body, out_shape=[jax.ShapeDtypeStruct(shape, kind) for sha...]
  transfers between devices with their start and end apart: 25 -> 27, of which waited for: 9 -> 8; matrix products, arithmetic and copies ran while one was open for 0% -> 0% of each run, Pallas kernels for 10% -> 11%
where the time goes in v4:
time: 81.7 us; the launch traced here: 81.4 us
  starting transfers between devices  34.6 us (42%)
  waiting for transfers between devices  31 us (38%)
  Pallas kernels  14.9 us (18%)
  between operations  0.96 us (1%)
    ppermute x7, waiting for transfers between devices, hop(): return lax.ppermute(value, 'section', pairs)  19.7 us
    ppermute x16, starting transfers between devices, exchange(): return lax.ppermute(value, 'dp', [(i, i ^ mask) for i in range(count)])  19.5 us
    pallas_call x16, Pallas kernels, call(): pl.pallas_call(body, out_shape=[jax.ShapeDtypeStruct(shape, kind) for sha...  14.9 us
    ppermute x7, starting transfers between devices, hop(): return lax.ppermute(value, 'section', pairs)  11.1 us
    ppermute x16, waiting for transfers between devices, exchange(): return lax.ppermute(value, 'dp', [(i, i ^ mask) for i in range(count)])  6.35 us
    ppermute x2, waiting for transfers between devices, from_next(): return lax.ppermute(value, ('section', 'dp'), pairs)  4.86 us
    ppermute x2, starting transfers between devices, from_next(): return lax.ppermute(value, ('section', 'dp'), pairs)  2.57 us
  transfers between devices with their start and end apart: 27, of which 8 were waited for; matrix products, arithmetic and copies ran while one was open for 0% of the time, Pallas kernels for 11%

profile of v4, /device:TPU:0, one launch (start us, length us, event | category | flops | bytes accessed | tf_op | source)
XLA Modules:
  0.0 81.4 jit_solution(2363146684147871456)
XLA Ops:
  0.6 3.4 %shard_map.102 = (bf16[320,256]{1,0:T(8,128)(2,1)S(1)}, bf16[320,256]{1,0:T(8,128)(2,1)S(1)}, bf16[320,320]{1,0:T(8,128)(2,1)S(1)}, bf16[2,320,128]{2,1,0:T(8,12...) custom-call(s32[2,128]{1,0:T(2,128)} %refs_0_.1, bf16[320,1000]{1,0:T(8,128)(2,1)} %bitcast.20, ...), custom_call_target="tpu_custom_call" | custom-call | tf_op jit(solution)/shard_map/pallas_call | solution.py:32
  4.1 5.8 %collective-permute-start = (bf16[320,256]{1,0:T(8,128)(2,1)S(1)}, bf16[320,256]{1,0:T(8,128)(2,1)S(1)}, u32[]{:S(2)}, u32[]{:S(2)}) collective-permute-start(bf16[320,256]{1,0:T(8,128)(2,1)S(1)} %get-tuple-element.37), channel_id=1, source_target_pairs={{0,24},{8,16},{1,25},{9,17},{2,26},{10,18},{3,27},{11,19},{4,28},{... | collective-permute-start | bytes 491528 | tf_op jit(solution)/shard_map/ppermute | solution.py:267
  10.0 0.5 shard_map.103
  10.5 2.9 %collective-permute-done.received = bf16[320,256]{1,0:T(8,128)(2,1)S(1)} collective-permute-done((bf16[320,256]{1,0:T(8,128)(2,1)S(1)}, bf16[320,256]{1,0:T(8,128)(2,1)S(1)}, u32[]{:S(2)}, u32[]{:S(2)}) %collective-permute-start) | collective-permute-done | bytes 163872 | tf_op jit(solution)/shard_map/ppermute | solution.py:267
  13.4 1.6 %shard_map.104 = (bf16[320,256]{1,0:T(8,128)(2,1)S(1)}, bf16[320,256]{1,0:T(8,128)(2,1)S(1)}, f32[320,256]{1,0:T(8,128)S(1)}, f32[1280,256]{1,0:T(8,128)S(1)}, bf16[320,256]{1,0:T(8,128)(2,1)S(1)}) custom-call(bf16[320,256]{1,0:T(8,128)(2,1)S(1)} %collective-permute-done.received, bf16[320,256]{1,0:T(8,128)(2,1)S(1)} %get-tuple-element.38.embed, ...), custom_call_target="tpu_custom_call" | custom-call | tf_op jit(solution)/shard_map/pallas_call | solution.py:32
  14.9 0.7 collective-permute-start.1
  15.6 0.7 collective-permute-start.3
  16.3 0.2 shard_map.106
  16.6 0.7 collective-permute-start.4
  17.2 0.0 collective-permute-done.1.received.low_2
  17.2 1.2 %shard_map.105.chain.chain_2 = bf16[320,256]{1,0:T(8,128)(2,1)S(1)} custom-call(bf16[320,256]{1,0:T(8,128)(2,1)S(1)} %collective-permute-done.1.received.low_2, f32[320,256]{1,0:T(8,128)S(1)} %get-tuple-element.46.united, f32[1280,256]{1,0:T(8,128)S(1)} %get-tuple-element.47.slope, bf16[320,1280]{1,0:T(8,128)(2,1)S(1)} %get-tuple-element.44.w_in, ...), custom_call_target="tpu_custom_call" | custom-call | tf_op jit(solution)/shard_map/pallas_call | solution.py:32
  18.4 0.7 collective-permute-start.2
  19.1 0.7 collective-permute-start.18
  19.8 0.7 collective-permute-start.19
  20.5 0.0 collective-permute-done.3.w_mirror
  20.5 1.3 %collective-permute-start.6 = (bf16[320,256]{1,0:T(8,128)(2,1)S(1)}, bf16[320,256]{1,0:T(8,128)(2,1)S(1)}, u32[]{:S(2)}, u32[]{:S(2)}) collective-permute-start(bf16[320,256]{1,0:T(8,128)(2,1)S(1)} %shard_map.106), channel_id=1, source_target_pairs={{24,0},{25,1},{26,2},{27,3},{28,4},{29,5},{30,6},{31,7}} | collective-permute-start | bytes 491528 | tf_op jit(solution)/shard_map/ppermute | solution.py:267
  21.8 0.0 collective-permute-done.4.skip_far
  21.8 1.6 %collective-permute-start.11 = (bf16[320,256]{1,0:T(8,128)(2,1)S(1)}, bf16[320,256]{1,0:T(8,128)(2,1)S(1)}, u32[]{:S(2)}, u32[]{:S(2)}) collective-permute-start(bf16[320,256]{1,0:T(8,128)(2,1)S(1)} %get-tuple-element.60.refs_0_), channel_id=1, source_target_pairs={{0,2},{1,3},{2,0},{3,1},{4,6},{5,7},{6,4},{7,5},{8,10},{9,11},{10,... | collective-permute-start | bytes 491528 | tf_op jit(solution)/shard_map/ppermute | solution.py:275
  23.4 0.0 collective-permute-done.2.received
  23.4 2.5 %collective-permute-start.12 = (bf16[320,256]{1,0:T(8,128)(2,1)S(1)}, bf16[320,256]{1,0:T(8,128)(2,1)S(1)}, u32[]{:S(2)}, u32[]{:S(2)}) collective-permute-start(bf16[320,256]{1,0:T(8,128)(2,1)S(1)} %get-tuple-element.60.refs_0_), channel_id=1, source_target_pairs={{0,6},{1,7},{2,4},{3,5},{4,2},{5,3},{6,0},{7,1},{8,14},{9,15},{10,... | collective-permute-start | bytes 491528 | tf_op jit(solution)/shard_map/ppermute | solution.py:275
  25.9 0.2 shard_map.107.back_2
  26.2 1.5 %shard_map.108 = (bf16[320,256]{1,0:T(8,128)(2,1)S(1)}, bf16[320,256]{1,0:T(8,128)(2,1)S(1)}, bf16[320,256]{1,0:T(8,128)(2,1)S(1)}) custom-call(bf16[320,256]{1,0:T(8,128)(2,1)S(1)} %collective-permute-done.2.received, bf16[320,320]{1,0:T(8,128)(2,1)S(1)} %collective-permute-done.3.w_mirror, f32[320,256]{1,0:T(8,128)S(1)} %get-tuple-element.46.united, ...), custom_call_target="tpu_custom_call" | custom-call | tf_op jit(solution)/shard_map/pallas_call | solution.py:32
  27.7 0.0 collective-permute-done.18.top_2
  27.7 0.1 collective-permute-start.13
  27.8 0.0 collective-permute-done.19.top_6
  27.8 1.3 %collective-permute-start.5 = (bf16[320,256]{1,0:T(8,128)(2,1)S(1)}, bf16[320,256]{1,0:T(8,128)(2,1)S(1)}, u32[]{:S(2)}, u32[]{:S(2)}) collective-permute-start(bf16[320,256]{1,0:T(8,128)(2,1)S(1)} %get-tuple-element.48.chain_1), channel_id=1, source_target_pairs={{8,0},{9,1},{10,2},{11,3},{12,4},{13,5},{14,6},{15,7}} | collective-permute-start | bytes 491528 | tf_op jit(solution)/shard_map/ppermute | solution.py:267
  29.1 8.8 %collective-permute-done.6.skip_far = bf16[320,256]{1,0:T(8,128)(2,1)S(1)} collective-permute-done((bf16[320,256]{1,0:T(8,128)(2,1)S(1)}, bf16[320,256]{1,0:T(8,128)(2,1)S(1)}, u32[]{:S(2)}, u32[]{:S(2)}) %collective-permute-start.6) | collective-permute-done | bytes 163872 | tf_op jit(solution)/shard_map/ppermute | solution.py:267
  37.9 0.1 collective-permute-start.16
  38.1 0.0 collective-permute-done.11.refs_1_
  38.1 1.3 %collective-permute-start.20 = (bf16[320,256]{1,0:T(8,128)(2,1)S(1)}, bf16[320,256]{1,0:T(8,128)(2,1)S(1)}, u32[]{:S(2)}, u32[]{:S(2)}) collective-permute-start(bf16[320,256]{1,0:T(8,128)(2,1)S(1)} %get-tuple-element.63), channel_id=1, source_target_pairs={{8,2},{9,3},{10,0},{11,1},{12,6},{13,7},{14,4},{15,5},{16,10},{17,... | collective-permute-start | bytes 491528 | tf_op jit(solution)/shard_map/ppermute | solution.py:284
  39.4 0.0 collective-permute-done.12.refs_2_
  39.4 1.3 %collective-permute-start.21 = (bf16[320,256]{1,0:T(8,128)(2,1)S(1)}, bf16[320,256]{1,0:T(8,128)(2,1)S(1)}, u32[]{:S(2)}, u32[]{:S(2)}) collective-permute-start(bf16[320,256]{1,0:T(8,128)(2,1)S(1)} %get-tuple-element.63), channel_id=1, source_target_pairs={{8,6},{9,7},{10,4},{11,5},{12,2},{13,3},{14,0},{15,1},{16,14},{17,... | collective-permute-start | bytes 491528 | tf_op jit(solution)/shard_map/ppermute | solution.py:284
  40.7 0.0 collective-permute-done.13.refs_3_
  40.7 0.1 collective-permute-start.14
  40.8 8.0 %collective-permute-done.5.received = bf16[320,256]{1,0:T(8,128)(2,1)S(1)} collective-permute-done((bf16[320,256]{1,0:T(8,128)(2,1)S(1)}, bf16[320,256]{1,0:T(8,128)(2,1)S(1)}, u32[]{:S(2)}, u32[]{:S(2)}) %collective-permute-start.5) | collective-permute-done | bytes 163872 | tf_op jit(solution)/shard_map/ppermute | solution.py:267
  48.8 0.0 collective-permute-start.15
  48.8 0.1 shard_map.109.grad_low.refs_6_
  48.8 0.0 collective-permute-done.16.refs_6_.refs_0_
  48.8 0.1 collective-permute-start.25
  48.9 2.0 %shard_map.110 = (bf16[2,320,128]{2,1,0:T(8,128)(2,1)}, f32[4,40,320]{2,1,0:T(8,128)S(1)}, bf16[4,40,320]{2,1,0:T(8,128)(2,1)S(1)}) custom-call(bf16[320,256]{1,0:T(8,128)(2,1)S(1)} %shard_map.109.grad_low.refs_6_, bf16[320,256]{1,0:T(8,128)(2,1)S(1)} %collective-permute-done.5.received, bf16[320,256]{1,0:T(8,128)(2,1)S(1)} %collective-permute-done.6.skip_far, ...), custom_call_target="tpu_custom_call" | custom-call | tf_op jit(solution)/shard_map/pallas_call | solution.py:32
  50.9 4.9 %collective-permute-done.20.next_2 = bf16[320,256]{1,0:T(8,128)(2,1)S(1)} collective-permute-done((bf16[320,256]{1,0:T(8,128)(2,1)S(1)}, bf16[320,256]{1,0:T(8,128)(2,1)S(1)}, u32[]{:S(2)}, u32[]{:S(2)}) %collective-permute-start.20) | collective-permute-done | bytes 163872 | tf_op jit(solution)/shard_map/ppermute | solution.py:284
  55.7 0.0 collective-permute-start.7
  55.7 0.0 collective-permute-done.21.next_6
  55.7 0.5 collective-permute-start.17
  56.3 0.0 collective-permute-done.14.refs_4_
  56.3 0.1 collective-permute-start.22
  56.4 0.5 collective-permute-start.23
  56.9 0.2 collective-permute-done.7.given
  57.1 0.1 collective-permute-start.24
  57.2 0.0 collective-permute-done.25.refs_2_
  57.2 0.4 collective-permute-start.26
  57.6 0.0 collective-permute-done.17.refs_7_.refs_1_
  57.6 5.0 %collective-permute-start.8 = (bf16[40,320]{1,0:T(8,128)(2,1)S(1)}, bf16[40,320]{1,0:T(8,128)(2,1)S(1)}, u32[]{:S(2)}, u32[]{:S(2)}) collective-permute-start(bf16[40,320]{1,0:T(8,128)(2,1)S(1)} %get-tuple-element.55), channel_id=1, source_target_pairs={{0,2},{1,3},{2,0},{3,1},{4,6},{5,7},{6,4},{7,5},{8,10},{9,11},{10,... | collective-permute-start | bytes 76808 | tf_op jit(solution)/shard_map/ppermute | solution.py:275
  62.6 1.9 %collective-permute-done.8.refs_0_ = bf16[40,320]{1,0:T(8,128)(2,1)S(1)} collective-permute-done((bf16[40,320]{1,0:T(8,128)(2,1)S(1)}, bf16[40,320]{1,0:T(8,128)(2,1)S(1)}, u32[]{:S(2)}, u32[]{:S(2)}) %collective-permute-start.8) | collective-permute-done | bytes 25632 | tf_op jit(solution)/shard_map/ppermute | solution.py:275
  64.5 6.1 %collective-permute-start.9 = (bf16[40,320]{1,0:T(8,128)(2,1)S(1)}, bf16[40,320]{1,0:T(8,128)(2,1)S(1)}, u32[]{:S(2)}, u32[]{:S(2)}) collective-permute-start(bf16[40,320]{1,0:T(8,128)(2,1)S(1)} %get-tuple-element.56), channel_id=1, source_target_pairs={{0,4},{1,5},{2,6},{3,7},{4,0},{5,1},{6,2},{7,3},{8,12},{9,13},{10,... | collective-permute-start | bytes 76808 | tf_op jit(solution)/shard_map/ppermute | solution.py:275
  70.6 1.9 %collective-permute-done.9.refs_1_ = bf16[40,320]{1,0:T(8,128)(2,1)S(1)} collective-permute-done((bf16[40,320]{1,0:T(8,128)(2,1)S(1)}, bf16[40,320]{1,0:T(8,128)(2,1)S(1)}, u32[]{:S(2)}, u32[]{:S(2)}) %collective-permute-start.9) | collective-permute-done | bytes 25632 | tf_op jit(solution)/shard_map/ppermute | solution.py:275
  72.5 2.4 %collective-permute-start.10 = (bf16[40,320]{1,0:T(8,128)(2,1)S(1)}, bf16[40,320]{1,0:T(8,128)(2,1)S(1)}, u32[]{:S(2)}, u32[]{:S(2)}) collective-permute-start(bf16[40,320]{1,0:T(8,128)(2,1)S(1)} %get-tuple-element.57), channel_id=1, source_target_pairs={{0,6},{1,7},{2,4},{3,5},{4,2},{5,3},{6,0},{7,1},{8,14},{9,15},{10,... | collective-permute-start | bytes 76808 | tf_op jit(solution)/shard_map/ppermute | solution.py:275
  74.9 0.1 shard_map.113
  74.9 0.8 %shard_map.114 = (bf16[160,2048]{1,0:T(8,128)(2,1)S(1)}, f32[160,2048]{1,0:T(8,128)S(1)}) custom-call(bf16[320,160]{1,0:T(8,128)(2,1)S(1)} %get-tuple-element.59.own_in, bf16[320,256]{1,0:T(8,128)(2,1)S(1)} %get-tuple-element.60.refs_0_, bf16[320,256]{1,0:T(8,128)(2,1)S(1)} %collective-permute-done.11.refs_1_, ...), custom_call_target="tpu_custom_call" | custom-call | tf_op jit(solution)/shard_map/pallas_call | solution.py:32
  75.8 2.4 %collective-permute-done.10.refs_2_ = bf16[40,320]{1,0:T(8,128)(2,1)S(1)} collective-permute-done((bf16[40,320]{1,0:T(8,128)(2,1)S(1)}, bf16[40,320]{1,0:T(8,128)(2,1)S(1)}, u32[]{:S(2)}, u32[]{:S(2)}) %collective-permute-start.10) | collective-permute-done | bytes 25632 | tf_op jit(solution)/shard_map/ppermute | solution.py:275
  78.2 0.8 shard_map.112
  78.9 0.0 collective-permute-done.24.refs_11_
  78.9 1.1 %shard_map.116 = (f32[160,320]{1,0:T(8,128)S(1)}, f32[160,320]{1,0:T(8,128)S(1)}) custom-call(bf16[320,160]{1,0:T(8,128)(2,1)S(1)} %get-tuple-element.58.own_out, bf16[160,2048]{1,0:T(8,128)(2,1)S(1)} %get-tuple-element.61.active, f32[160,2048]{1,0:T(8,128)S(1)} %get-tuple-element.62.slope, bf16[320,256]{1,0:T(8,128)(2,1)S(1)} %get-tuple-element.60.refs_0_, ...), custom_call_target="tpu_custom_call" | custom-call | tf_op jit(solution)/shard_map/pallas_call | solution.py:32
  80.1 1.3 %shard_map.117 = (f32[160,320]{1,0:T(8,128)}, f32[160,320]{1,0:T(8,128)}) custom-call(bf16[320,160]{1,0:T(8,128)(2,1)S(1)} %get-tuple-element.58.own_out, bf16[160,2048]{1,0:T(8,128)(2,1)S(1)} %get-tuple-element.61.active, f32[160,2048]{1,0:T(8,128)S(1)} %get-tuple-element.62.slope, f32[160,320]{1,0:T(8,128)S(1)} %get-tuple-element.66.sum_in, ...), custom_call_target="tpu_custom_call" | custom-call | tf_op jit(solution)/shard_map/pallas_call | solution.py:32
  (8 shorter events, 0.1 us)
Async XLA Ops:
  0.6 9.3 %copy-start = (bf16[2,128,320]{1,2,0:T(8,128)(2,1)S(1)}, bf16[2,128,320]{1,2,0:T(8,128)(2,1)}, u32[]{:S(2)}) copy-start(bf16[2,128,320]{1,2,0:T(8,128)(2,1)} %param.13) | copy-start | bytes 491524
  4.1 9.3 %collective-permute-start = (bf16[320,256]{1,0:T(8,128)(2,1)S(1)}, bf16[320,256]{1,0:T(8,128)(2,1)S(1)}, u32[]{:S(2)}, u32[]{:S(2)}) collective-permute-start(bf16[320,256]{1,0:T(8,128)(2,1)S(1)} %get-tuple-element.37), channel_id=1, source_target_pairs={{0,24},{8,16},{1,25},{9,17},{2,26},{10,18},{3,27},{11,19},{4,28},{... | collective-permute-start | bytes 491528 | tf_op jit(solution)/shard_map/ppermute | solution.py:267
  14.9 2.3 %collective-permute-start.1 = (bf16[320,256]{1,0:T(8,128)(2,1)S(1)}, bf16[320,256]{1,0:T(8,128)(2,1)S(1)}, u32[]{:S(2)}, u32[]{:S(2)}) collective-permute-start(bf16[320,256]{1,0:T(8,128)(2,1)S(1)} %get-tuple-element.45.chain.chain_3), channel_id=1, source_target_pairs={{24,16},{25,17},{26,18},{27,19},{28,20},{29,21},{30,22},{31,23}} | collective-permute-start | bytes 491528 | tf_op jit(solution)/shard_map/ppermute | solution.py:267
  15.6 4.9 %collective-permute-start.3 = (bf16[320,320]{1,0:T(8,128)(2,1)S(1)}, bf16[320,320]{1,0:T(8,128)(2,1)S(1)}, u32[]{:S(2)}, u32[]{:S(2)}) collective-permute-start(bf16[320,320]{1,0:T(8,128)(2,1)S(1)} %get-tuple-element.43.w_skip), channel_id=1, source_target_pairs={{16,8},{17,9},{18,10},{19,11},{20,12},{21,13},{22,14},{23,15}} | collective-permute-start | bytes 614408 | tf_op jit(solution)/shard_map/ppermute | solution.py:267
  16.6 5.2 %collective-permute-start.4 = (bf16[320,256]{1,0:T(8,128)(2,1)S(1)}, bf16[320,256]{1,0:T(8,128)(2,1)S(1)}, u32[]{:S(2)}, u32[]{:S(2)}) collective-permute-start(bf16[320,256]{1,0:T(8,128)(2,1)S(1)} %shard_map.106), channel_id=1, source_target_pairs={{24,8},{25,9},{26,10},{27,11},{28,12},{29,13},{30,14},{31,15}} | collective-permute-start | bytes 491528 | tf_op jit(solution)/shard_map/ppermute | solution.py:267
  18.4 5.0 %collective-permute-start.2 = (bf16[320,256]{1,0:T(8,128)(2,1)S(1)}, bf16[320,256]{1,0:T(8,128)(2,1)S(1)}, u32[]{:S(2)}, u32[]{:S(2)}) collective-permute-start(bf16[320,256]{1,0:T(8,128)(2,1)S(1)} %shard_map.105.chain.chain_2), channel_id=1, source_target_pairs={{16,8},{17,9},{18,10},{19,11},{20,12},{21,13},{22,14},{23,15}} | collective-permute-start | bytes 491528 | tf_op jit(solution)/shard_map/ppermute | solution.py:267
  19.1 8.6 %collective-permute-start.18 = (bf16[320,256]{1,0:T(8,128)(2,1)S(1)}, bf16[320,256]{1,0:T(8,128)(2,1)S(1)}, u32[]{:S(2)}, u32[]{:S(2)}) collective-permute-start(bf16[320,256]{1,0:T(8,128)(2,1)S(1)} %get-tuple-element.41.top_low), channel_id=1, source_target_pairs={{24,26},{25,27},{26,24},{27,25},{28,30},{29,31},{30,28},{31,29}} | collective-permute-start | bytes 491528 | tf_op jit(solution)/shard_map/ppermute | solution.py:289
  19.8 8.0 %collective-permute-start.19 = (bf16[320,256]{1,0:T(8,128)(2,1)S(1)}, bf16[320,256]{1,0:T(8,128)(2,1)S(1)}, u32[]{:S(2)}, u32[]{:S(2)}) collective-permute-start(bf16[320,256]{1,0:T(8,128)(2,1)S(1)} %get-tuple-element.41.top_low), channel_id=1, source_target_pairs={{24,30},{25,31},{26,28},{27,29},{28,26},{29,27},{30,24},{31,25}} | collective-permute-start | bytes 491528 | tf_op jit(solution)/shard_map/ppermute | solution.py:289
  20.5 17.4 %collective-permute-start.6 = (bf16[320,256]{1,0:T(8,128)(2,1)S(1)}, bf16[320,256]{1,0:T(8,128)(2,1)S(1)}, u32[]{:S(2)}, u32[]{:S(2)}) collective-permute-start(bf16[320,256]{1,0:T(8,128)(2,1)S(1)} %shard_map.106), channel_id=1, source_target_pairs={{24,0},{25,1},{26,2},{27,3},{28,4},{29,5},{30,6},{31,7}} | collective-permute-start | bytes 491528 | tf_op jit(solution)/shard_map/ppermute | solution.py:267
  21.8 16.3 %collective-permute-start.11 = (bf16[320,256]{1,0:T(8,128)(2,1)S(1)}, bf16[320,256]{1,0:T(8,128)(2,1)S(1)}, u32[]{:S(2)}, u32[]{:S(2)}) collective-permute-start(bf16[320,256]{1,0:T(8,128)(2,1)S(1)} %get-tuple-element.60.refs_0_), channel_id=1, source_target_pairs={{0,2},{1,3},{2,0},{3,1},{4,6},{5,7},{6,4},{7,5},{8,10},{9,11},{10,... | collective-permute-start | bytes 491528 | tf_op jit(solution)/shard_map/ppermute | solution.py:275
  23.4 15.9 %collective-permute-start.12 = (bf16[320,256]{1,0:T(8,128)(2,1)S(1)}, bf16[320,256]{1,0:T(8,128)(2,1)S(1)}, u32[]{:S(2)}, u32[]{:S(2)}) collective-permute-start(bf16[320,256]{1,0:T(8,128)(2,1)S(1)} %get-tuple-element.60.refs_0_), channel_id=1, source_target_pairs={{0,6},{1,7},{2,4},{3,5},{4,2},{5,3},{6,0},{7,1},{8,14},{9,15},{10,... | collective-permute-start | bytes 491528 | tf_op jit(solution)/shard_map/ppermute | solution.py:275
  27.7 13.0 %collective-permute-start.13 = (bf16[320,256]{1,0:T(8,128)(2,1)S(1)}, bf16[320,256]{1,0:T(8,128)(2,1)S(1)}, u32[]{:S(2)}, u32[]{:S(2)}) collective-permute-start(bf16[320,256]{1,0:T(8,128)(2,1)S(1)} %get-tuple-element.60.refs_0_), channel_id=1, source_target_pairs={{0,1},{1,0},{2,3},{3,2},{4,5},{5,4},{6,7},{7,6},{8,9},{9,8},{10,11... | collective-permute-start | bytes 491528 | tf_op jit(solution)/shard_map/ppermute | solution.py:275
  27.8 21.0 %collective-permute-start.5 = (bf16[320,256]{1,0:T(8,128)(2,1)S(1)}, bf16[320,256]{1,0:T(8,128)(2,1)S(1)}, u32[]{:S(2)}, u32[]{:S(2)}) collective-permute-start(bf16[320,256]{1,0:T(8,128)(2,1)S(1)} %get-tuple-element.48.chain_1), channel_id=1, source_target_pairs={{8,0},{9,1},{10,2},{11,3},{12,4},{13,5},{14,6},{15,7}} | collective-permute-start | bytes 491528 | tf_op jit(solution)/shard_map/ppermute | solution.py:267
  37.9 10.9 %collective-permute-start.16 = (bf16[320,256]{1,0:T(8,128)(2,1)S(1)}, bf16[320,256]{1,0:T(8,128)(2,1)S(1)}, u32[]{:S(2)}, u32[]{:S(2)}) collective-permute-start(bf16[320,256]{1,0:T(8,128)(2,1)S(1)} %get-tuple-element.60.refs_0_), channel_id=1, source_target_pairs={{0,4},{1,5},{2,6},{3,7},{4,0},{5,1},{6,2},{7,3},{8,12},{9,13},{10,... | collective-permute-start | bytes 491528 | tf_op jit(solution)/shard_map/ppermute | solution.py:275
  38.1 17.7 %collective-permute-start.20 = (bf16[320,256]{1,0:T(8,128)(2,1)S(1)}, bf16[320,256]{1,0:T(8,128)(2,1)S(1)}, u32[]{:S(2)}, u32[]{:S(2)}) collective-permute-start(bf16[320,256]{1,0:T(8,128)(2,1)S(1)} %get-tuple-element.63), channel_id=1, source_target_pairs={{8,2},{9,3},{10,0},{11,1},{12,6},{13,7},{14,4},{15,5},{16,10},{17,... | collective-permute-start | bytes 491528 | tf_op jit(solution)/shard_map/ppermute | solution.py:284
  39.4 16.4 %collective-permute-start.21 = (bf16[320,256]{1,0:T(8,128)(2,1)S(1)}, bf16[320,256]{1,0:T(8,128)(2,1)S(1)}, u32[]{:S(2)}, u32[]{:S(2)}) collective-permute-start(bf16[320,256]{1,0:T(8,128)(2,1)S(1)} %get-tuple-element.63), channel_id=1, source_target_pairs={{8,6},{9,7},{10,4},{11,5},{12,2},{13,3},{14,0},{15,1},{16,14},{17,... | collective-permute-start | bytes 491528 | tf_op jit(solution)/shard_map/ppermute | solution.py:284
  40.7 15.6 %collective-permute-start.14 = (bf16[320,256]{1,0:T(8,128)(2,1)S(1)}, bf16[320,256]{1,0:T(8,128)(2,1)S(1)}, u32[]{:S(2)}, u32[]{:S(2)}) collective-permute-start(bf16[320,256]{1,0:T(8,128)(2,1)S(1)} %collective-permute-done.11.refs_1_), channel_id=1, source_target_pairs={{0,1},{1,0},{2,3},{3,2},{4,5},{5,4},{6,7},{7,6},{8,9},{9,8},{10,11... | collective-permute-start | bytes 491528 | tf_op jit(solution)/shard_map/ppermute | solution.py:275
  48.8 7.6 %collective-permute-start.15 = (bf16[320,256]{1,0:T(8,128)(2,1)S(1)}, bf16[320,256]{1,0:T(8,128)(2,1)S(1)}, u32[]{:S(2)}, u32[]{:S(2)}) collective-permute-start(bf16[320,256]{1,0:T(8,128)(2,1)S(1)} %collective-permute-done.12.refs_2_), channel_id=1, source_target_pairs={{0,1},{1,0},{2,3},{3,2},{4,5},{5,4},{6,7},{7,6},{8,9},{9,8},{10,11... | collective-permute-start | bytes 491528 | tf_op jit(solution)/shard_map/ppermute | solution.py:275
  48.8 8.4 %collective-permute-start.25 = (bf16[320,256]{1,0:T(8,128)(2,1)S(1)}, bf16[320,256]{1,0:T(8,128)(2,1)S(1)}, u32[]{:S(2)}, u32[]{:S(2)}) collective-permute-start(bf16[320,256]{1,0:T(8,128)(2,1)S(1)} %shard_map.109.grad_low.refs_6_), channel_id=1, source_target_pairs={{0,4},{1,5},{2,6},{3,7},{4,0},{5,1},{6,2},{7,3},{8,12},{9,13},{10,... | collective-permute-start | bytes 491528 | tf_op jit(solution)/shard_map/ppermute | solution.py:275
  55.7 1.3 %collective-permute-start.7 = (bf16[4,40,320]{2,1,0:T(8,128)(2,1)S(1)}, bf16[4,40,320]{2,1,0:T(8,128)(2,1)S(1)}, u32[]{:S(2)}, u32[]{:S(2)}) collective-permute-start(bf16[4,40,320]{2,1,0:T(8,128)(2,1)S(1)} %get-tuple-element.53), channel_id=1, source_target_pairs={{0,1},{1,0},{2,3},{3,2},{4,5},{5,4},{6,7},{7,6},{8,9},{9,8},{10,11... | collective-permute-start | bytes 307208 | tf_op jit(solution)/shard_map/ppermute | solution.py:275
  55.7 1.9 %collective-permute-start.17 = (bf16[320,256]{1,0:T(8,128)(2,1)S(1)}, bf16[320,256]{1,0:T(8,128)(2,1)S(1)}, u32[]{:S(2)}, u32[]{:S(2)}) collective-permute-start(bf16[320,256]{1,0:T(8,128)(2,1)S(1)} %collective-permute-done.16.refs_6_.refs_0_), channel_id=1, source_target_pairs={{0,1},{1,0},{2,3},{3,2},{4,5},{5,4},{6,7},{7,6},{8,9},{9,8},{10,11... | collective-permute-start | bytes 491528 | tf_op jit(solution)/shard_map/ppermute | solution.py:275
  56.3 22.6 %collective-permute-start.22 = (bf16[320,256]{1,0:T(8,128)(2,1)S(1)}, bf16[320,256]{1,0:T(8,128)(2,1)S(1)}, u32[]{:S(2)}, u32[]{:S(2)}) collective-permute-start(bf16[320,256]{1,0:T(8,128)(2,1)S(1)} %shard_map.109.grad_low.refs_6_), channel_id=1, source_target_pairs={{0,1},{1,0},{2,3},{3,2},{4,5},{5,4},{6,7},{7,6},{8,9},{9,8},{10,11... | collective-permute-start | bytes 491528 | tf_op jit(solution)/shard_map/ppermute | solution.py:275
  56.4 22.6 %collective-permute-start.23 = (bf16[320,256]{1,0:T(8,128)(2,1)S(1)}, bf16[320,256]{1,0:T(8,128)(2,1)S(1)}, u32[]{:S(2)}, u32[]{:S(2)}) collective-permute-start(bf16[320,256]{1,0:T(8,128)(2,1)S(1)} %get-tuple-element.64.refs_7_), channel_id=1, source_target_pairs={{0,1},{1,0},{2,3},{3,2},{4,5},{5,4},{6,7},{7,6},{8,9},{9,8},{10,11... | collective-permute-start | bytes 491528 | tf_op jit(solution)/shard_map/ppermute | solution.py:275
  57.1 21.9 %collective-permute-start.24 = (bf16[320,256]{1,0:T(8,128)(2,1)S(1)}, bf16[320,256]{1,0:T(8,128)(2,1)S(1)}, u32[]{:S(2)}, u32[]{:S(2)}) collective-permute-start(bf16[320,256]{1,0:T(8,128)(2,1)S(1)} %get-tuple-element.65.refs_8_), channel_id=1, source_target_pairs={{0,1},{1,0},{2,3},{3,2},{4,5},{5,4},{6,7},{7,6},{8,9},{9,8},{10,11... | collective-permute-start | bytes 491528 | tf_op jit(solution)/shard_map/ppermute | solution.py:275
  57.2 22.9 %collective-permute-start.26 = (bf16[320,256]{1,0:T(8,128)(2,1)S(1)}, bf16[320,256]{1,0:T(8,128)(2,1)S(1)}, u32[]{:S(2)}, u32[]{:S(2)}) collective-permute-start(bf16[320,256]{1,0:T(8,128)(2,1)S(1)} %collective-permute-done.25.refs_2_), channel_id=1, source_target_pairs={{0,1},{1,0},{2,3},{3,2},{4,5},{5,4},{6,7},{7,6},{8,9},{9,8},{10,11... | collective-permute-start | bytes 491528 | tf_op jit(solution)/shard_map/ppermute | solution.py:275
  57.6 6.8 %collective-permute-start.8 = (bf16[40,320]{1,0:T(8,128)(2,1)S(1)}, bf16[40,320]{1,0:T(8,128)(2,1)S(1)}, u32[]{:S(2)}, u32[]{:S(2)}) collective-permute-start(bf16[40,320]{1,0:T(8,128)(2,1)S(1)} %get-tuple-element.55), channel_id=1, source_target_pairs={{0,2},{1,3},{2,0},{3,1},{4,6},{5,7},{6,4},{7,5},{8,10},{9,11},{10,... | collective-permute-start | bytes 76808 | tf_op jit(solution)/shard_map/ppermute | solution.py:275
  64.5 8.0 %collective-permute-start.9 = (bf16[40,320]{1,0:T(8,128)(2,1)S(1)}, bf16[40,320]{1,0:T(8,128)(2,1)S(1)}, u32[]{:S(2)}, u32[]{:S(2)}) collective-permute-start(bf16[40,320]{1,0:T(8,128)(2,1)S(1)} %get-tuple-element.56), channel_id=1, source_target_pairs={{0,4},{1,5},{2,6},{3,7},{4,0},{5,1},{6,2},{7,3},{8,12},{9,13},{10,... | collective-permute-start | bytes 76808 | tf_op jit(solution)/shard_map/ppermute | solution.py:275
  72.5 5.7 %collective-permute-start.10 = (bf16[40,320]{1,0:T(8,128)(2,1)S(1)}, bf16[40,320]{1,0:T(8,128)(2,1)S(1)}, u32[]{:S(2)}, u32[]{:S(2)}) collective-permute-start(bf16[40,320]{1,0:T(8,128)(2,1)S(1)} %get-tuple-element.57), channel_id=1, source_target_pairs={{0,6},{1,7},{2,4},{3,5},{4,2},{5,3},{6,0},{7,1},{8,14},{9,15},{10,... | collective-permute-start | bytes 76808 | tf_op jit(solution)/shard_map/ppermute | solution.py:275

commit v5 on v4

--- a/solution.py
+++ b/solution.py
@@ -151,10 +151,8 @@
     grad_low_out[...] = jnp.where(section == 3, top_low[...], own)
 
 
-def merge_body(top_2, top_6, next_2, next_6, out_2, out_6):
-    last = lax.axis_index("section") == 3
-    out_2[...] = jnp.where(last, top_2[...], next_2[...])
-    out_6[...] = jnp.where(last, top_6[...], next_6[...])
+def merge_body(top, following, out):
+    out[...] = jnp.where(lax.axis_index("section") == 3, top[...], following[...])
 
 
 def last_body(
@@ -344,8 +342,7 @@
 
     part = hidden // count
     own_in, own_out = call(cut_body, [((width, part), LOW)] * 2, w_in, w_out)
-    masks = (2, 6, 4)
-    normed_near = [normed] + [exchange(normed, count, m) for m in masks]
+    normed_near = [normed] + [exchange(normed, count, m) for m in (2, 6, 4)]
     normed_all = in_turn(
         normed_near,
         [exchange(x, count, 1) for x in normed_near],
@@ -354,10 +351,11 @@
         slice_forward_body,
         [((part, count * rows), LOW), ((part, count * rows), F32)], own_in, *normed_all,
     )
-    tops = [in_last(top_low, count, m) for m in masks[:2]]
-    aheads = [from_next(ahead, count, m) for m in masks[:2]]
-    low_2, low_6 = call(merge_body, [low, low], *tops, *aheads)
-    low_near = [grad_low, low_2, low_6, exchange(grad_low, count, 4)]
+    top_6 = in_last(top_low, count, 6)
+    next_6 = from_next(ahead, count, 6)
+    (low_6,) = call(merge_body, [low], top_6, next_6)
+    low_2, low_4 = (exchange(grad_low, count, m) for m in (2, 4))
+    low_near = [grad_low, low_2, low_6, low_4]
     low_all = in_turn(low_near, [exchange(x, count, 1) for x in low_near])
     block = (count // 2, width // count, width)
     kept, keep, give = call(

time: 81.7 us -> 83.2 us (1.018)
  the two profiles are of different devices: /device:TPU:0 before, /device:TPU:4 now
where the time goes in v5:
time: 83.2 us; the launch traced here: 82.9 us
  starting transfers between devices  34.6 us (42%)
  waiting for transfers between devices  32.4 us (39%)
  Pallas kernels  14.9 us (18%)
  between operations  0.92 us (1%)
    ppermute x17, waiting for transfers between devices, exchange(): return lax.ppermute(value, 'dp', [(i, i ^ mask) for i in range(count)])  21.9 us
    ppermute x17, starting transfers between devices, exchange(): return lax.ppermute(value, 'dp', [(i, i ^ mask) for i in range(count)])  16.9 us
    pallas_call x16, Pallas kernels, call(): pl.pallas_call(body, out_shape=[jax.ShapeDtypeStruct(shape, kind) for sha...  14.9 us
    ppermute x7, waiting for transfers between devices, hop(): return lax.ppermute(value, 'section', pairs)  10.6 us
    ppermute x1, starting transfers between devices, from_next(): return lax.ppermute(value, ('section', 'dp'), pairs)  9.83 us
    ppermute x7, starting transfers between devices, hop(): return lax.ppermute(value, 'section', pairs)  7.2 us
  transfers between devices with their start and end apart: 26, of which 10 were waited for; matrix products, arithmetic and copies ran while one was open for 0% of the time, Pallas kernels for 10%

profile of v5, /device:TPU:4, one launch (start us, length us, event | category | flops | bytes accessed | tf_op | source)
XLA Modules:
  0.0 82.9 jit_solution(18063910379965608130)
XLA Ops:
  0.6 3.4 %shard_map.102 = (bf16[320,256]{1,0:T(8,128)(2,1)S(1)}, bf16[320,256]{1,0:T(8,128)(2,1)S(1)}, bf16[320,320]{1,0:T(8,128)(2,1)S(1)}, bf16[2,320,128]{2,1,0:T(8,12...) custom-call(s32[2,128]{1,0:T(2,128)} %refs_0_.1, bf16[320,1000]{1,0:T(8,128)(2,1)} %bitcast.20, ...), custom_call_target="tpu_custom_call" | custom-call | tf_op jit(solution)/shard_map/pallas_call | solution.py:32
  4.1 1.3 %collective-permute-start = (bf16[320,256]{1,0:T(8,128)(2,1)S(1)}, bf16[320,256]{1,0:T(8,128)(2,1)S(1)}, u32[]{:S(2)}, u32[]{:S(2)}) collective-permute-start(bf16[320,256]{1,0:T(8,128)(2,1)S(1)} %get-tuple-element.35), channel_id=1, source_target_pairs={{0,24},{8,16},{1,25},{9,17},{2,26},{10,18},{3,27},{11,19},{4,28},{... | collective-permute-start | bytes 491528 | tf_op jit(solution)/shard_map/ppermute | solution.py:265
  5.4 0.5 shard_map.103
  6.0 6.9 %collective-permute-done.received = bf16[320,256]{1,0:T(8,128)(2,1)S(1)} collective-permute-done((bf16[320,256]{1,0:T(8,128)(2,1)S(1)}, bf16[320,256]{1,0:T(8,128)(2,1)S(1)}, u32[]{:S(2)}, u32[]{:S(2)}) %collective-permute-start) | collective-permute-done | bytes 163872 | tf_op jit(solution)/shard_map/ppermute | solution.py:265
  12.8 1.6 %shard_map.104 = (bf16[320,256]{1,0:T(8,128)(2,1)S(1)}, bf16[320,256]{1,0:T(8,128)(2,1)S(1)}, f32[320,256]{1,0:T(8,128)S(1)}, f32[1280,256]{1,0:T(8,128)S(1)}, bf16[320,256]{1,0:T(8,128)(2,1)S(1)}) custom-call(bf16[320,256]{1,0:T(8,128)(2,1)S(1)} %collective-permute-done.received, bf16[320,256]{1,0:T(8,128)(2,1)S(1)} %get-tuple-element.36.embed, ...), custom_call_target="tpu_custom_call" | custom-call | tf_op jit(solution)/shard_map/pallas_call | solution.py:32
  14.4 1.3 %collective-permute-start.1 = (bf16[320,256]{1,0:T(8,128)(2,1)S(1)}, bf16[320,256]{1,0:T(8,128)(2,1)S(1)}, u32[]{:S(2)}, u32[]{:S(2)}) collective-permute-start(bf16[320,256]{1,0:T(8,128)(2,1)S(1)} %get-tuple-element.43.chain.chain_3), channel_id=1, source_target_pairs={{24,16},{25,17},{26,18},{27,19},{28,20},{29,21},{30,22},{31,23}} | collective-permute-start | bytes 491528 | tf_op jit(solution)/shard_map/ppermute | solution.py:265
  15.7 1.3 %collective-permute-start.3 = (bf16[320,320]{1,0:T(8,128)(2,1)S(1)}, bf16[320,320]{1,0:T(8,128)(2,1)S(1)}, u32[]{:S(2)}, u32[]{:S(2)}) collective-permute-start(bf16[320,320]{1,0:T(8,128)(2,1)S(1)} %get-tuple-element.41.w_skip), channel_id=1, source_target_pairs={{16,8},{17,9},{18,10},{19,11},{20,12},{21,13},{22,14},{23,15}} | collective-permute-start | bytes 614408 | tf_op jit(solution)/shard_map/ppermute | solution.py:265
  17.0 0.2 shard_map.106
  17.3 0.7 collective-permute-start.4
  17.9 3.7 %collective-permute-done.1.received.low_2 = bf16[320,256]{1,0:T(8,128)(2,1)S(1)} collective-permute-done((bf16[320,256]{1,0:T(8,128)(2,1)S(1)}, bf16[320,256]{1,0:T(8,128)(2,1)S(1)}, u32[]{:S(2)}, u32[]{:S(2)}) %collective-permute-start.1) | collective-permute-done | bytes 163872 | tf_op jit(solution)/shard_map/ppermute | solution.py:265
  21.6 1.2 %shard_map.105.chain.chain_2 = bf16[320,256]{1,0:T(8,128)(2,1)S(1)} custom-call(bf16[320,256]{1,0:T(8,128)(2,1)S(1)} %collective-permute-done.1.received.low_2, f32[320,256]{1,0:T(8,128)S(1)} %get-tuple-element.44.united, f32[1280,256]{1,0:T(8,128)S(1)} %get-tuple-element.45.slope, bf16[320,1280]{1,0:T(8,128)(2,1)S(1)} %get-tuple-element.42.w_in, ...), custom_call_target="tpu_custom_call" | custom-call | tf_op jit(solution)/shard_map/pallas_call | solution.py:32
  22.8 1.3 %collective-permute-start.2 = (bf16[320,256]{1,0:T(8,128)(2,1)S(1)}, bf16[320,256]{1,0:T(8,128)(2,1)S(1)}, u32[]{:S(2)}, u32[]{:S(2)}) collective-permute-start(bf16[320,256]{1,0:T(8,128)(2,1)S(1)} %shard_map.105.chain.chain_2), channel_id=1, source_target_pairs={{16,8},{17,9},{18,10},{19,11},{20,12},{21,13},{22,14},{23,15}} | collective-permute-start | bytes 491528 | tf_op jit(solution)/shard_map/ppermute | solution.py:265
  24.1 0.7 collective-permute-start.19
  24.8 0.7 collective-permute-start.6
  25.5 0.0 collective-permute-done.3.w_mirror
  25.5 1.6 %collective-permute-start.11 = (bf16[320,256]{1,0:T(8,128)(2,1)S(1)}, bf16[320,256]{1,0:T(8,128)(2,1)S(1)}, u32[]{:S(2)}, u32[]{:S(2)}) collective-permute-start(bf16[320,256]{1,0:T(8,128)(2,1)S(1)} %get-tuple-element.58.refs_0_), channel_id=1, source_target_pairs={{0,2},{1,3},{2,0},{3,1},{4,6},{5,7},{6,4},{7,5},{8,10},{9,11},{10,... | collective-permute-start | bytes 491528 | tf_op jit(solution)/shard_map/ppermute | solution.py:273
  27.1 0.0 collective-permute-done.4.skip_far
  27.1 2.5 %collective-permute-start.12 = (bf16[320,256]{1,0:T(8,128)(2,1)S(1)}, bf16[320,256]{1,0:T(8,128)(2,1)S(1)}, u32[]{:S(2)}, u32[]{:S(2)}) collective-permute-start(bf16[320,256]{1,0:T(8,128)(2,1)S(1)} %get-tuple-element.58.refs_0_), channel_id=1, source_target_pairs={{0,6},{1,7},{2,4},{3,5},{4,2},{5,3},{6,0},{7,1},{8,14},{9,15},{10,... | collective-permute-start | bytes 491528 | tf_op jit(solution)/shard_map/ppermute | solution.py:273
  29.6 0.2 shard_map.107.back_2
  29.9 0.0 collective-permute-done.2.received
  29.9 1.5 %shard_map.108 = (bf16[320,256]{1,0:T(8,128)(2,1)S(1)}, bf16[320,256]{1,0:T(8,128)(2,1)S(1)}, bf16[320,256]{1,0:T(8,128)(2,1)S(1)}) custom-call(bf16[320,256]{1,0:T(8,128)(2,1)S(1)} %collective-permute-done.2.received, bf16[320,320]{1,0:T(8,128)(2,1)S(1)} %collective-permute-done.3.w_mirror, f32[320,256]{1,0:T(8,128)S(1)} %get-tuple-element.44.united, ...), custom_call_target="tpu_custom_call" | custom-call | tf_op jit(solution)/shard_map/pallas_call | solution.py:32
  31.4 0.7 collective-permute-start.5
  32.1 0.0 collective-permute-done.19.top
  32.1 0.1 collective-permute-start.13
  32.2 0.0 collective-permute-done.6.skip_far
  32.2 0.2 collective-permute-start.16
  32.4 0.3 collective-permute-done.11.refs_1_
  32.6 0.1 collective-permute-start.14
  32.7 2.4 %collective-permute-done.12.refs_2_ = bf16[320,256]{1,0:T(8,128)(2,1)S(1)} collective-permute-done((bf16[320,256]{1,0:T(8,128)(2,1)S(1)}, bf16[320,256]{1,0:T(8,128)(2,1)S(1)}, u32[]{:S(2)}, u32[]{:S(2)}) %collective-permute-start.12) | collective-permute-done | bytes 163872 | tf_op jit(solution)/shard_map/ppermute | solution.py:273
  35.1 9.8 %collective-permute-start.20 = (bf16[320,256]{1,0:T(8,128)(2,1)S(1)}, bf16[320,256]{1,0:T(8,128)(2,1)S(1)}, u32[]{:S(2)}, u32[]{:S(2)}) collective-permute-start(bf16[320,256]{1,0:T(8,128)(2,1)S(1)} %get-tuple-element.61), channel_id=1, source_target_pairs={{8,6},{9,7},{10,4},{11,5},{12,2},{13,3},{14,0},{15,1},{16,14},{17,... | collective-permute-start | bytes 491528 | tf_op jit(solution)/shard_map/ppermute | solution.py:282
  45.0 0.0 collective-permute-done.5.received
  45.0 0.1 collective-permute-start.15
  45.1 0.1 shard_map.109.grad_low.refs_6_
  45.1 0.0 collective-permute-done.13.refs_3_
  45.2 9.2 %collective-permute-start.18 = (bf16[320,256]{1,0:T(8,128)(2,1)S(1)}, bf16[320,256]{1,0:T(8,128)(2,1)S(1)}, u32[]{:S(2)}, u32[]{:S(2)}) collective-permute-start(bf16[320,256]{1,0:T(8,128)(2,1)S(1)} %shard_map.109.grad_low.refs_6_), channel_id=1, source_target_pairs={{0,2},{1,3},{2,0},{3,1},{4,6},{5,7},{6,4},{7,5},{8,10},{9,11},{10,... | collective-permute-start | bytes 491528 | tf_op jit(solution)/shard_map/ppermute | solution.py:273
  54.4 0.0 collective-permute-done.16.refs_6_.refs_0_
  54.4 0.0 collective-permute-start.24
  54.4 2.0 %shard_map.110 = (bf16[2,320,128]{2,1,0:T(8,128)(2,1)}, f32[4,40,320]{2,1,0:T(8,128)S(1)}, bf16[4,40,320]{2,1,0:T(8,128)(2,1)S(1)}) custom-call(bf16[320,256]{1,0:T(8,128)(2,1)S(1)} %shard_map.109.grad_low.refs_6_, bf16[320,256]{1,0:T(8,128)(2,1)S(1)} %collective-permute-done.5.received, bf16[320,256]{1,0:T(8,128)(2,1)S(1)} %collective-permute-done.6.skip_far, ...), custom_call_target="tpu_custom_call" | custom-call | tf_op jit(solution)/shard_map/pallas_call | solution.py:32
  56.3 0.0 collective-permute-done.14.refs_4_
  56.3 0.2 collective-permute-start.7
  56.5 0.0 collective-permute-done.20.following
  56.5 0.3 collective-permute-start.17
  56.9 0.0 collective-permute-done.15.refs_5_
  56.9 0.3 collective-permute-start.21
  57.1 0.5 collective-permute-done.7.given
  57.7 0.2 collective-permute-start.23
  57.9 3.5 %collective-permute-done.18.refs_7_ = bf16[320,256]{1,0:T(8,128)(2,1)S(1)} collective-permute-done((bf16[320,256]{1,0:T(8,128)(2,1)S(1)}, bf16[320,256]{1,0:T(8,128)(2,1)S(1)}, u32[]{:S(2)}, u32[]{:S(2)}) %collective-permute-start.18) | collective-permute-done | bytes 163872 | tf_op jit(solution)/shard_map/ppermute | solution.py:273
  61.3 0.0 collective-permute-start.22
  61.3 3.8 %collective-permute-done.24.refs_2_ = bf16[320,256]{1,0:T(8,128)(2,1)S(1)} collective-permute-done((bf16[320,256]{1,0:T(8,128)(2,1)S(1)}, bf16[320,256]{1,0:T(8,128)(2,1)S(1)}, u32[]{:S(2)}, u32[]{:S(2)}) %collective-permute-start.24) | collective-permute-done | bytes 163872 | tf_op jit(solution)/shard_map/ppermute | solution.py:273
  65.1 0.0 collective-permute-start.25
  65.2 0.1 collective-permute-start.8
  65.3 3.9 %collective-permute-done.8.refs_0_ = bf16[40,320]{1,0:T(8,128)(2,1)S(1)} collective-permute-done((bf16[40,320]{1,0:T(8,128)(2,1)S(1)}, bf16[40,320]{1,0:T(8,128)(2,1)S(1)}, u32[]{:S(2)}, u32[]{:S(2)}) %collective-permute-start.8) | collective-permute-done | bytes 25632 | tf_op jit(solution)/shard_map/ppermute | solution.py:273
  69.1 0.4 collective-permute-start.9
  69.5 4.4 %collective-permute-done.9.refs_1_ = bf16[40,320]{1,0:T(8,128)(2,1)S(1)} collective-permute-done((bf16[40,320]{1,0:T(8,128)(2,1)S(1)}, bf16[40,320]{1,0:T(8,128)(2,1)S(1)}, u32[]{:S(2)}, u32[]{:S(2)}) %collective-permute-start.9) | collective-permute-done | bytes 25632 | tf_op jit(solution)/shard_map/ppermute | solution.py:273
  73.9 1.7 %collective-permute-start.10 = (bf16[40,320]{1,0:T(8,128)(2,1)S(1)}, bf16[40,320]{1,0:T(8,128)(2,1)S(1)}, u32[]{:S(2)}, u32[]{:S(2)}) collective-permute-start(bf16[40,320]{1,0:T(8,128)(2,1)S(1)} %get-tuple-element.55), channel_id=1, source_target_pairs={{0,6},{1,7},{2,4},{3,5},{4,2},{5,3},{6,0},{7,1},{8,14},{9,15},{10,... | collective-permute-start | bytes 76808 | tf_op jit(solution)/shard_map/ppermute | solution.py:273
  75.6 0.1 shard_map.113
  75.7 0.8 %shard_map.114 = (bf16[160,2048]{1,0:T(8,128)(2,1)S(1)}, f32[160,2048]{1,0:T(8,128)S(1)}) custom-call(bf16[320,160]{1,0:T(8,128)(2,1)S(1)} %get-tuple-element.57.own_in, bf16[320,256]{1,0:T(8,128)(2,1)S(1)} %get-tuple-element.58.refs_0_, bf16[320,256]{1,0:T(8,128)(2,1)S(1)} %collective-permute-done.11.refs_1_, ...), custom_call_target="tpu_custom_call" | custom-call | tf_op jit(solution)/shard_map/pallas_call | solution.py:32
  76.5 3.1 %collective-permute-done.10.refs_2_ = bf16[40,320]{1,0:T(8,128)(2,1)S(1)} collective-permute-done((bf16[40,320]{1,0:T(8,128)(2,1)S(1)}, bf16[40,320]{1,0:T(8,128)(2,1)S(1)}, u32[]{:S(2)}, u32[]{:S(2)}) %collective-permute-start.10) | collective-permute-done | bytes 25632 | tf_op jit(solution)/shard_map/ppermute | solution.py:273
  79.6 0.8 shard_map.112
  80.4 0.0 collective-permute-done.23.refs_11_
  80.4 0.0 collective-permute-done.22.refs_10_
  80.4 1.1 %shard_map.116 = (f32[160,320]{1,0:T(8,128)S(1)}, f32[160,320]{1,0:T(8,128)S(1)}) custom-call(bf16[320,160]{1,0:T(8,128)(2,1)S(1)} %get-tuple-element.56.own_out, bf16[160,2048]{1,0:T(8,128)(2,1)S(1)} %get-tuple-element.59.active, f32[160,2048]{1,0:T(8,128)S(1)} %get-tuple-element.60.slope, bf16[320,256]{1,0:T(8,128)(2,1)S(1)} %get-tuple-element.58.refs_0_, ...), custom_call_target="tpu_custom_call" | custom-call | tf_op jit(solution)/shard_map/pallas_call | solution.py:32
  81.6 0.0 collective-permute-done.25.refs_3_
  81.6 1.3 %shard_map.117 = (f32[160,320]{1,0:T(8,128)}, f32[160,320]{1,0:T(8,128)}) custom-call(bf16[320,160]{1,0:T(8,128)(2,1)S(1)} %get-tuple-element.56.own_out, bf16[160,2048]{1,0:T(8,128)(2,1)S(1)} %get-tuple-element.59.active, f32[160,2048]{1,0:T(8,128)S(1)} %get-tuple-element.60.slope, f32[160,320]{1,0:T(8,128)S(1)} %get-tuple-element.62.sum_in, ...), custom_call_target="tpu_custom_call" | custom-call | tf_op jit(solution)/shard_map/pallas_call | solution.py:32
  (6 shorter events, 0.1 us)
Async XLA Ops:
  0.6 4.8 %copy-start = (bf16[2,128,320]{1,2,0:T(8,128)(2,1)S(1)}, bf16[2,128,320]{1,2,0:T(8,128)(2,1)}, u32[]{:S(2)}) copy-start(bf16[2,128,320]{1,2,0:T(8,128)(2,1)} %param.13) | copy-start | bytes 491524
  4.1 8.7 %collective-permute-start = (bf16[320,256]{1,0:T(8,128)(2,1)S(1)}, bf16[320,256]{1,0:T(8,128)(2,1)S(1)}, u32[]{:S(2)}, u32[]{:S(2)}) collective-permute-start(bf16[320,256]{1,0:T(8,128)(2,1)S(1)} %get-tuple-element.35), channel_id=1, source_target_pairs={{0,24},{8,16},{1,25},{9,17},{2,26},{10,18},{3,27},{11,19},{4,28},{... | collective-permute-start | bytes 491528 | tf_op jit(solution)/shard_map/ppermute | solution.py:265
  14.4 7.2 %collective-permute-start.1 = (bf16[320,256]{1,0:T(8,128)(2,1)S(1)}, bf16[320,256]{1,0:T(8,128)(2,1)S(1)}, u32[]{:S(2)}, u32[]{:S(2)}) collective-permute-start(bf16[320,256]{1,0:T(8,128)(2,1)S(1)} %get-tuple-element.43.chain.chain_3), channel_id=1, source_target_pairs={{24,16},{25,17},{26,18},{27,19},{28,20},{29,21},{30,22},{31,23}} | collective-permute-start | bytes 491528 | tf_op jit(solution)/shard_map/ppermute | solution.py:265
  15.7 9.8 %collective-permute-start.3 = (bf16[320,320]{1,0:T(8,128)(2,1)S(1)}, bf16[320,320]{1,0:T(8,128)(2,1)S(1)}, u32[]{:S(2)}, u32[]{:S(2)}) collective-permute-start(bf16[320,320]{1,0:T(8,128)(2,1)S(1)} %get-tuple-element.41.w_skip), channel_id=1, source_target_pairs={{16,8},{17,9},{18,10},{19,11},{20,12},{21,13},{22,14},{23,15}} | collective-permute-start | bytes 614408 | tf_op jit(solution)/shard_map/ppermute | solution.py:265
  17.3 9.9 %collective-permute-start.4 = (bf16[320,256]{1,0:T(8,128)(2,1)S(1)}, bf16[320,256]{1,0:T(8,128)(2,1)S(1)}, u32[]{:S(2)}, u32[]{:S(2)}) collective-permute-start(bf16[320,256]{1,0:T(8,128)(2,1)S(1)} %shard_map.106), channel_id=1, source_target_pairs={{24,8},{25,9},{26,10},{27,11},{28,12},{29,13},{30,14},{31,15}} | collective-permute-start | bytes 491528 | tf_op jit(solution)/shard_map/ppermute | solution.py:265
  22.8 7.0 %collective-permute-start.2 = (bf16[320,256]{1,0:T(8,128)(2,1)S(1)}, bf16[320,256]{1,0:T(8,128)(2,1)S(1)}, u32[]{:S(2)}, u32[]{:S(2)}) collective-permute-start(bf16[320,256]{1,0:T(8,128)(2,1)S(1)} %shard_map.105.chain.chain_2), channel_id=1, source_target_pairs={{16,8},{17,9},{18,10},{19,11},{20,12},{21,13},{22,14},{23,15}} | collective-permute-start | bytes 491528 | tf_op jit(solution)/shard_map/ppermute | solution.py:265
  24.1 7.9 %collective-permute-start.19 = (bf16[320,256]{1,0:T(8,128)(2,1)S(1)}, bf16[320,256]{1,0:T(8,128)(2,1)S(1)}, u32[]{:S(2)}, u32[]{:S(2)}) collective-permute-start(bf16[320,256]{1,0:T(8,128)(2,1)S(1)} %get-tuple-element.39.top_low), channel_id=1, source_target_pairs={{24,30},{25,31},{26,28},{27,29},{28,26},{29,27},{30,24},{31,25}} | collective-permute-start | bytes 491528 | tf_op jit(solution)/shard_map/ppermute | solution.py:287
  24.8 7.4 %collective-permute-start.6 = (bf16[320,256]{1,0:T(8,128)(2,1)S(1)}, bf16[320,256]{1,0:T(8,128)(2,1)S(1)}, u32[]{:S(2)}, u32[]{:S(2)}) collective-permute-start(bf16[320,256]{1,0:T(8,128)(2,1)S(1)} %shard_map.106), channel_id=1, source_target_pairs={{24,0},{25,1},{26,2},{27,3},{28,4},{29,5},{30,6},{31,7}} | collective-permute-start | bytes 491528 | tf_op jit(solution)/shard_map/ppermute | solution.py:265
  25.5 7.1 %collective-permute-start.11 = (bf16[320,256]{1,0:T(8,128)(2,1)S(1)}, bf16[320,256]{1,0:T(8,128)(2,1)S(1)}, u32[]{:S(2)}, u32[]{:S(2)}) collective-permute-start(bf16[320,256]{1,0:T(8,128)(2,1)S(1)} %get-tuple-element.58.refs_0_), channel_id=1, source_target_pairs={{0,2},{1,3},{2,0},{3,1},{4,6},{5,7},{6,4},{7,5},{8,10},{9,11},{10,... | collective-permute-start | bytes 491528 | tf_op jit(solution)/shard_map/ppermute | solution.py:273
  27.1 8.0 %collective-permute-start.12 = (bf16[320,256]{1,0:T(8,128)(2,1)S(1)}, bf16[320,256]{1,0:T(8,128)(2,1)S(1)}, u32[]{:S(2)}, u32[]{:S(2)}) collective-permute-start(bf16[320,256]{1,0:T(8,128)(2,1)S(1)} %get-tuple-element.58.refs_0_), channel_id=1, source_target_pairs={{0,6},{1,7},{2,4},{3,5},{4,2},{5,3},{6,0},{7,1},{8,14},{9,15},{10,... | collective-permute-start | bytes 491528 | tf_op jit(solution)/shard_map/ppermute | solution.py:273
  31.4 13.6 %collective-permute-start.5 = (bf16[320,256]{1,0:T(8,128)(2,1)S(1)}, bf16[320,256]{1,0:T(8,128)(2,1)S(1)}, u32[]{:S(2)}, u32[]{:S(2)}) collective-permute-start(bf16[320,256]{1,0:T(8,128)(2,1)S(1)} %get-tuple-element.46.chain_1), channel_id=1, source_target_pairs={{8,0},{9,1},{10,2},{11,3},{12,4},{13,5},{14,6},{15,7}} | collective-permute-start | bytes 491528 | tf_op jit(solution)/shard_map/ppermute | solution.py:265
  32.1 13.1 %collective-permute-start.13 = (bf16[320,256]{1,0:T(8,128)(2,1)S(1)}, bf16[320,256]{1,0:T(8,128)(2,1)S(1)}, u32[]{:S(2)}, u32[]{:S(2)}) collective-permute-start(bf16[320,256]{1,0:T(8,128)(2,1)S(1)} %get-tuple-element.58.refs_0_), channel_id=1, source_target_pairs={{0,1},{1,0},{2,3},{3,2},{4,5},{5,4},{6,7},{7,6},{8,9},{9,8},{10,11... | collective-permute-start | bytes 491528 | tf_op jit(solution)/shard_map/ppermute | solution.py:273
  32.2 22.2 %collective-permute-start.16 = (bf16[320,256]{1,0:T(8,128)(2,1)S(1)}, bf16[320,256]{1,0:T(8,128)(2,1)S(1)}, u32[]{:S(2)}, u32[]{:S(2)}) collective-permute-start(bf16[320,256]{1,0:T(8,128)(2,1)S(1)} %get-tuple-element.58.refs_0_), channel_id=1, source_target_pairs={{0,4},{1,5},{2,6},{3,7},{4,0},{5,1},{6,2},{7,3},{8,12},{9,13},{10,... | collective-permute-start | bytes 491528 | tf_op jit(solution)/shard_map/ppermute | solution.py:273
  32.6 23.7 %collective-permute-start.14 = (bf16[320,256]{1,0:T(8,128)(2,1)S(1)}, bf16[320,256]{1,0:T(8,128)(2,1)S(1)}, u32[]{:S(2)}, u32[]{:S(2)}) collective-permute-start(bf16[320,256]{1,0:T(8,128)(2,1)S(1)} %collective-permute-done.11.refs_1_), channel_id=1, source_target_pairs={{0,1},{1,0},{2,3},{3,2},{4,5},{5,4},{6,7},{7,6},{8,9},{9,8},{10,11... | collective-permute-start | bytes 491528 | tf_op jit(solution)/shard_map/ppermute | solution.py:273
  35.1 21.4 %collective-permute-start.20 = (bf16[320,256]{1,0:T(8,128)(2,1)S(1)}, bf16[320,256]{1,0:T(8,128)(2,1)S(1)}, u32[]{:S(2)}, u32[]{:S(2)}) collective-permute-start(bf16[320,256]{1,0:T(8,128)(2,1)S(1)} %get-tuple-element.61), channel_id=1, source_target_pairs={{8,6},{9,7},{10,4},{11,5},{12,2},{13,3},{14,0},{15,1},{16,14},{17,... | collective-permute-start | bytes 491528 | tf_op jit(solution)/shard_map/ppermute | solution.py:282
  45.0 11.9 %collective-permute-start.15 = (bf16[320,256]{1,0:T(8,128)(2,1)S(1)}, bf16[320,256]{1,0:T(8,128)(2,1)S(1)}, u32[]{:S(2)}, u32[]{:S(2)}) collective-permute-start(bf16[320,256]{1,0:T(8,128)(2,1)S(1)} %collective-permute-done.12.refs_2_), channel_id=1, source_target_pairs={{0,1},{1,0},{2,3},{3,2},{4,5},{5,4},{6,7},{7,6},{8,9},{9,8},{10,11... | collective-permute-start | bytes 491528 | tf_op jit(solution)/shard_map/ppermute | solution.py:273
  45.2 16.2 %collective-permute-start.18 = (bf16[320,256]{1,0:T(8,128)(2,1)S(1)}, bf16[320,256]{1,0:T(8,128)(2,1)S(1)}, u32[]{:S(2)}, u32[]{:S(2)}) collective-permute-start(bf16[320,256]{1,0:T(8,128)(2,1)S(1)} %shard_map.109.grad_low.refs_6_), channel_id=1, source_target_pairs={{0,2},{1,3},{2,0},{3,1},{4,6},{5,7},{6,4},{7,5},{8,10},{9,11},{10,... | collective-permute-start | bytes 491528 | tf_op jit(solution)/shard_map/ppermute | solution.py:273
  54.4 10.8 %collective-permute-start.24 = (bf16[320,256]{1,0:T(8,128)(2,1)S(1)}, bf16[320,256]{1,0:T(8,128)(2,1)S(1)}, u32[]{:S(2)}, u32[]{:S(2)}) collective-permute-start(bf16[320,256]{1,0:T(8,128)(2,1)S(1)} %shard_map.109.grad_low.refs_6_), channel_id=1, source_target_pairs={{0,4},{1,5},{2,6},{3,7},{4,0},{5,1},{6,2},{7,3},{8,12},{9,13},{10,... | collective-permute-start | bytes 491528 | tf_op jit(solution)/shard_map/ppermute | solution.py:273
  56.3 1.3 %collective-permute-start.7 = (bf16[4,40,320]{2,1,0:T(8,128)(2,1)S(1)}, bf16[4,40,320]{2,1,0:T(8,128)(2,1)S(1)}, u32[]{:S(2)}, u32[]{:S(2)}) collective-permute-start(bf16[4,40,320]{2,1,0:T(8,128)(2,1)S(1)} %get-tuple-element.51), channel_id=1, source_target_pairs={{0,1},{1,0},{2,3},{3,2},{4,5},{5,4},{6,7},{7,6},{8,9},{9,8},{10,11... | collective-permute-start | bytes 307208 | tf_op jit(solution)/shard_map/ppermute | solution.py:273
  56.5 8.6 %collective-permute-start.17 = (bf16[320,256]{1,0:T(8,128)(2,1)S(1)}, bf16[320,256]{1,0:T(8,128)(2,1)S(1)}, u32[]{:S(2)}, u32[]{:S(2)}) collective-permute-start(bf16[320,256]{1,0:T(8,128)(2,1)S(1)} %collective-permute-done.16.refs_6_.refs_0_), channel_id=1, source_target_pairs={{0,1},{1,0},{2,3},{3,2},{4,5},{5,4},{6,7},{7,6},{8,9},{9,8},{10,11... | collective-permute-start | bytes 491528 | tf_op jit(solution)/shard_map/ppermute | solution.py:273
  56.9 23.5 %collective-permute-start.21 = (bf16[320,256]{1,0:T(8,128)(2,1)S(1)}, bf16[320,256]{1,0:T(8,128)(2,1)S(1)}, u32[]{:S(2)}, u32[]{:S(2)}) collective-permute-start(bf16[320,256]{1,0:T(8,128)(2,1)S(1)} %shard_map.109.grad_low.refs_6_), channel_id=1, source_target_pairs={{0,1},{1,0},{2,3},{3,2},{4,5},{5,4},{6,7},{7,6},{8,9},{9,8},{10,11... | collective-permute-start | bytes 491528 | tf_op jit(solution)/shard_map/ppermute | solution.py:273
  57.7 22.8 %collective-permute-start.23 = (bf16[320,256]{1,0:T(8,128)(2,1)S(1)}, bf16[320,256]{1,0:T(8,128)(2,1)S(1)}, u32[]{:S(2)}, u32[]{:S(2)}) collective-permute-start(bf16[320,256]{1,0:T(8,128)(2,1)S(1)} %shard_map.115.refs_8_), channel_id=1, source_target_pairs={{0,1},{1,0},{2,3},{3,2},{4,5},{5,4},{6,7},{7,6},{8,9},{9,8},{10,11... | collective-permute-start | bytes 491528 | tf_op jit(solution)/shard_map/ppermute | solution.py:273
  61.3 19.1 %collective-permute-start.22 = (bf16[320,256]{1,0:T(8,128)(2,1)S(1)}, bf16[320,256]{1,0:T(8,128)(2,1)S(1)}, u32[]{:S(2)}, u32[]{:S(2)}) collective-permute-start(bf16[320,256]{1,0:T(8,128)(2,1)S(1)} %collective-permute-done.18.refs_7_), channel_id=1, source_target_pairs={{0,1},{1,0},{2,3},{3,2},{4,5},{5,4},{6,7},{7,6},{8,9},{9,8},{10,11... | collective-permute-start | bytes 491528 | tf_op jit(solution)/shard_map/ppermute | solution.py:273
  65.1 16.4 %collective-permute-start.25 = (bf16[320,256]{1,0:T(8,128)(2,1)S(1)}, bf16[320,256]{1,0:T(8,128)(2,1)S(1)}, u32[]{:S(2)}, u32[]{:S(2)}) collective-permute-start(bf16[320,256]{1,0:T(8,128)(2,1)S(1)} %collective-permute-done.24.refs_2_), channel_id=1, source_target_pairs={{0,1},{1,0},{2,3},{3,2},{4,5},{5,4},{6,7},{7,6},{8,9},{9,8},{10,11... | collective-permute-start | bytes 491528 | tf_op jit(solution)/shard_map/ppermute | solution.py:273
  65.2 4.0 %collective-permute-start.8 = (bf16[40,320]{1,0:T(8,128)(2,1)S(1)}, bf16[40,320]{1,0:T(8,128)(2,1)S(1)}, u32[]{:S(2)}, u32[]{:S(2)}) collective-permute-start(bf16[40,320]{1,0:T(8,128)(2,1)S(1)} %get-tuple-element.53), channel_id=1, source_target_pairs={{0,2},{1,3},{2,0},{3,1},{4,6},{5,7},{6,4},{7,5},{8,10},{9,11},{10,... | collective-permute-start | bytes 76808 | tf_op jit(solution)/shard_map/ppermute | solution.py:273
  69.1 4.8 %collective-permute-start.9 = (bf16[40,320]{1,0:T(8,128)(2,1)S(1)}, bf16[40,320]{1,0:T(8,128)(2,1)S(1)}, u32[]{:S(2)}, u32[]{:S(2)}) collective-permute-start(bf16[40,320]{1,0:T(8,128)(2,1)S(1)} %get-tuple-element.54), channel_id=1, source_target_pairs={{0,4},{1,5},{2,6},{3,7},{4,0},{5,1},{6,2},{7,3},{8,12},{9,13},{10,... | collective-permute-start | bytes 76808 | tf_op jit(solution)/shard_map/ppermute | solution.py:273
  73.9 5.7 %collective-permute-start.10 = (bf16[40,320]{1,0:T(8,128)(2,1)S(1)}, bf16[40,320]{1,0:T(8,128)(2,1)S(1)}, u32[]{:S(2)}, u32[]{:S(2)}) collective-permute-start(bf16[40,320]{1,0:T(8,128)(2,1)S(1)} %get-tuple-element.55), channel_id=1, source_target_pairs={{0,6},{1,7},{2,4},{3,5},{4,2},{5,3},{6,0},{7,1},{8,14},{9,15},{10,... | collective-permute-start | bytes 76808 | tf_op jit(solution)/shard_map/ppermute | solution.py:273

commit v6 on v5

--- a/solution.py
+++ b/solution.py
@@ -151,8 +151,8 @@
     grad_low_out[...] = jnp.where(section == 3, top_low[...], own)
 
 
-def merge_body(top, following, out):
-    out[...] = jnp.where(lax.axis_index("section") == 3, top[...], following[...])
+def merge_body(following, passed, out):
+    out[...] = jnp.where(lax.axis_index("section") == 0, following[...], passed[...])
 
 
 def last_body(
@@ -166,9 +166,7 @@
     kept = jnp.where(section == 1, chain_1[...], kept)
     kept = jnp.where(section == 2, chain_2[...], kept)
     kept = jnp.where(section == 3, chain_3[...], kept)
-    span = kept_out.shape[2]
-    for m in range(kept_out.shape[0]):
-        kept_out[m] = kept[:, m * span : (m + 1) * span]
+    kept_out[...] = kept
     partial = dot(source[...], kept, 1, 1)
     size = keep_out.shape[1]
     first_core = lax.axis_index("dp") % 2 == 0
@@ -180,19 +178,24 @@
         give_out[block] = jnp.where(first_core, odd, even).astype(LOW)
 
 
-def join_body(keep, given, own_out, *piece_outs):
+def join_body(keep, given, own_out, near_out, pair_out):
     chip = lax.axis_index("dp") // 2
-    own_out[...] = keep[chip] + given[chip].astype(F32)
-    for mask, piece_out in enumerate(piece_outs, 1):
-        far = chip ^ mask
-        piece_out[...] = (keep[far] + given[far].astype(F32)).astype(LOW)
-
-
-def flat_body(own, *refs):
-    pieces, out, lanes, square = refs[:-3], refs[-3], refs[-2], refs[-1]
-    total = own[...]
-    for piece in pieces:
-        total = total + piece[...].astype(F32)
+
+    def joined(mask):
+        return keep[chip ^ mask] + given[chip ^ mask].astype(F32)
+
+    own_out[...] = joined(0)
+    near_out[...] = joined(1)
+    pair_out[0] = joined(2).astype(LOW)
+    pair_out[1] = joined(3).astype(LOW)
+
+
+def meet_body(own, near, pair, own_out, near_out):
+    own_out[...] = own[...] + pair[0].astype(F32)
+    near_out[...] = (near[...] + pair[1].astype(F32)).astype(LOW)
+
+
+def flatten(total, out, lanes, square):
     lanes[0] = total[:, :128]
     lanes[1] = total[:, 128:256]
     lanes[2] = jnp.concatenate([total[:, 256:], total[:, 256:]], axis=1)
@@ -224,66 +227,70 @@
             own_out[...] = w_out[:, columns]
 
 
+def curve(preact):
+    sigma = sigmoid(preact)
+    return (preact * sigma).astype(LOW), sigma * (1.0 + preact * (1.0 - sigma))
+
+
 def slice_forward_body(own_in, *refs):
     blocks, active_out, slope_out = refs[:-2], refs[-2], refs[-1]
     rows = blocks[0].shape[1]
     for place, block in enumerate(blocks):
         columns = slice(place * rows, (place + 1) * rows)
-        preact = dot(own_in[...], block[...], 0, 0)
-        sigma = sigmoid(preact)
-        active_out[:, columns] = (preact * sigma).astype(LOW)
-        slope_out[:, columns] = sigma * (1.0 + preact * (1.0 - sigma))
-
-
-def slice_grad(own_out, active, slope, normed, low, first):
-    rows = low[0].shape[1]
-    columns = slice(first * rows, (first + len(low)) * rows)
-    lows = jnp.concatenate([block[...] for block in low], axis=1)
-    grad_pre = (dot(own_out[...], lows, 0, 0) * slope[:, columns]).astype(LOW)
-    normeds = jnp.concatenate([block[...] for block in normed], axis=1)
-    return dot(grad_pre, normeds, 1, 1), dot(active[:, columns], lows, 1, 1)
+        active_out[:, columns], slope_out[:, columns] = curve(dot(own_in[...], block[...], 0, 0))
+
+
+def side(refs):
+    return jnp.concatenate([block[...] for block in refs], axis=1)
+
+
+def slice_grad(own_out, active, slope, normed, low):
+    grad_pre = (dot(own_out[...], low, 0, 0) * slope).astype(LOW)
+    return dot(grad_pre, normed, 1, 1), dot(active, low, 1, 1)
 
 
 def half_grad_body(own_out, active, slope, *refs):
     half = (len(refs) - 2) // 2
     refs[-2][...], refs[-1][...] = slice_grad(
-        own_out, active, slope, refs[:half], refs[half : 2 * half], 0
-    )
-
-
-def rest_grad_body(own_out, active, slope, sum_in, sum_out, *refs):
-    half = (len(refs) - 2) // 2
-    first = active.shape[1] // refs[0].shape[1] - half
-    part_in, part_out = slice_grad(
-        own_out, active, slope, refs[:half], refs[half : 2 * half], first
-    )
-    refs[-2][...] = sum_in[...] + part_in
-    refs[-1][...] = sum_out[...] + part_out
+        own_out, active[...], slope[...], side(refs[:half]), side(refs[half : 2 * half])
+    )
+
+
+def rest_body(
+    own_in, own_out, sum_in, sum_out, normed_0, normed_1, low_0, low_1, own, near, kept,
+    in_out, out_out, skip_out, kept_out, lanes, square,
+):
+    span = kept_out.shape[2]
+    for m in range(kept_out.shape[0]):
+        kept_out[m] = kept[:, m * span : (m + 1) * span]
+    flatten(own[...] + near[...].astype(F32), skip_out, lanes, square)
+    normed = side([normed_0, normed_1])
+    active, slope = curve(dot(own_in[...], normed, 0, 0))
+    part_in, part_out = slice_grad(own_out, active, slope, normed, side([low_0, low_1]))
+    in_out[...] = sum_in[...] + part_in
+    out_out[...] = sum_out[...] + part_out
 
 
 def hop(value, pairs):
     return lax.ppermute(value, "section", pairs)
 
 
-def in_turn(near, swapped):
-    return [*near[:3], *swapped[:3], near[3], swapped[3]]
-
-
 def exchange(value, count, mask):
     return lax.ppermute(value, "dp", [(i, i ^ mask) for i in range(count)])
 
 
 def from_next(value, count, mask):
+    return lax.ppermute(
+        value, ("section", "dp"), [(count + i, i ^ mask) for i in range(count)]
+    )
+
+
+def forwarded(value, count, mask):
     pairs = [
-        ((section + 1) * count + i, section * count + (i ^ mask))
-        for section in range(3)
+        (section * count + i, section * count + (i ^ mask))
+        for section in range(1, 4)
         for i in range(count)
     ]
-    return lax.ppermute(value, ("section", "dp"), pairs)
-
-
-def in_last(value, count, mask):
-    pairs = [(3 * count + i, 3 * count + (i ^ mask)) for i in range(count)]
     return lax.ppermute(value, ("section", "dp"), pairs)
 
 
@@ -342,50 +349,47 @@
 
     part = hidden // count
     own_in, own_out = call(cut_body, [((width, part), LOW)] * 2, w_in, w_out)
-    normed_near = [normed] + [exchange(normed, count, m) for m in (2, 6, 4)]
-    normed_all = in_turn(
-        normed_near,
-        [exchange(x, count, 1) for x in normed_near],
-    )
-    active_all, slope_all = call(
+    norm_2, norm_4 = (exchange(normed, count, m) for m in (2, 4))
+    normed_near = [normed, norm_2, norm_4, exchange(norm_4, count, 2)]
+    normed_swap = [exchange(x, count, 1) for x in normed_near]
+    normed_most = normed_near[:3] + normed_swap[:3]
+    most = len(normed_most)
+    active_most, slope_most = call(
         slice_forward_body,
-        [((part, count * rows), LOW), ((part, count * rows), F32)], own_in, *normed_all,
-    )
-    top_6 = in_last(top_low, count, 6)
+        [((part, most * rows), LOW), ((part, most * rows), F32)], own_in, *normed_most,
+    )
     next_6 = from_next(ahead, count, 6)
-    (low_6,) = call(merge_body, [low], top_6, next_6)
     low_2, low_4 = (exchange(grad_low, count, m) for m in (2, 4))
-    low_near = [grad_low, low_2, low_6, low_4]
-    low_all = in_turn(low_near, [exchange(x, count, 1) for x in low_near])
+    passed_6 = forwarded(low_4, count, 2)
+    (low_6,) = call(merge_body, [low], next_6, passed_6)
+    low_near = [grad_low, low_2, low_4, low_6]
+    low_swap = [exchange(x, count, 1) for x in low_near]
     block = (count // 2, width // count, width)
     kept, keep, give = call(
-        last_body, [((n_micro, width, span), LOW), (block, F32), (block, LOW)],
+        last_body, [low, (block, F32), (block, LOW)],
         grad_low, chain, skip_far, united, slope, w_in, w_out, source, chain_1, chain_2,
         chain_3,
     )
     given = exchange(give, count, 1)
     piece = block[1:]
-    own, *pieces = call(
-        join_body, [(piece, F32)] + [(piece, LOW)] * (count // 2 - 1),
-        keep, given,
-    )
-    pieces = [exchange(value, count, 2 * i) for i, value in enumerate(pieces, 1)]
-    (grad_skip,) = call(
-        flat_body, [((1, piece[0] * piece[1]), F32)], own, *pieces,
+    own, near, pair = call(join_body, [(piece, F32), (piece, F32), ((2, *piece), LOW)], keep, given)
+    pair = exchange(pair, count, 4)
+    own, near = call(meet_body, [(piece, F32), (piece, LOW)], own, near, pair)
+    near = exchange(near, count, 2)
+    grads = ((part, width), F32)
+    sums = call(
+        half_grad_body, [grads] * 2,
+        own_out, active_most, slope_most, *normed_most, *low_near[:3], *low_swap[:3],
+    )
+    grad_in, grad_out_w, grad_skip, kept = call(
+        rest_body,
+        [grads, grads, ((1, piece[0] * piece[1]), F32), ((n_micro, width, span), LOW)],
+        own_in, own_out, *sums, normed_near[3], normed_swap[3], low_near[3], low_swap[3],
+        own, near, kept,
         scratch=[
             pltpu.VMEM((3, piece[0], 128), F32),
             pltpu.VMEM((piece[0] * piece[1] // 128, 128), F32),
         ],
-    )
-    grads = ((part, width), F32)
-    half = 6
-    sums = call(
-        half_grad_body, [grads] * 2,
-        own_out, active_all, slope_all, *normed_all[:half], *low_all[:half],
-    )
-    grad_in, grad_out_w = call(
-        rest_grad_body, [grads] * 2,
-        own_out, active_all, slope_all, *sums, *normed_all[half:], *low_all[half:],
     )
     kept = jnp.swapaxes(kept, 1, 2)
     return (kept[None], grad_skip, grad_in[None], grad_out_w[None])

time: 83.2 us -> 71.4 us (0.86)
  the two profiles are of different devices: /device:TPU:4 before, /device:TPU:2 now
where the time goes in v6:
time: 71.4 us; the launch traced here: 71.1 us
  starting transfers between devices  31.6 us (44%)
  waiting for transfers between devices  24.9 us (35%)
  Pallas kernels  13.7 us (19%)
  between operations  0.92 us (1%)
    pallas_call x16, Pallas kernels, call(): pl.pallas_call(body, out_shape=[jax.ShapeDtypeStruct(shape, kind) for sha...  13.7 us
    ppermute x7, waiting for transfers between devices, hop(): return lax.ppermute(value, 'section', pairs)  13.1 us
    ppermute x16, starting transfers between devices, exchange(): return lax.ppermute(value, 'dp', [(i, i ^ mask) for i in range(count)])  12.6 us
    ppermute x7, starting transfers between devices, hop(): return lax.ppermute(value, 'section', pairs)  9.92 us
    ppermute x16, waiting for transfers between devices, exchange(): return lax.ppermute(value, 'dp', [(i, i ^ mask) for i in range(count)])  8.33 us
    ppermute x1, starting transfers between devices, from_next(): lax.ppermute(value, ('section', 'dp'), [(count + i, i ^ mask) for i in ra...  5.17 us
    ppermute x1, starting transfers between devices, forwarded(): return lax.ppermute(value, ('section', 'dp'), pairs)  3.9 us
    ppermute x1, waiting for transfers between devices, forwarded(): return lax.ppermute(value, ('section', 'dp'), pairs)  3.51 us
  transfers between devices with their start and end apart: 25, of which 8 were waited for; matrix products, arithmetic and copies ran while one was open for 0% of the time, Pallas kernels for 10%

profile of v6, /device:TPU:2, one launch (start us, length us, event | category | flops | bytes accessed | tf_op | source)
XLA Modules:
  0.0 71.1 jit_solution(5121286590756720874)
XLA Ops:
  0.6 3.4 %shard_map.102 = (bf16[320,256]{1,0:T(8,128)(2,1)S(1)}, bf16[320,256]{1,0:T(8,128)(2,1)S(1)}, bf16[320,320]{1,0:T(8,128)(2,1)S(1)}, bf16[2,320,128]{2,1,0:T(8,12...) custom-call(s32[2,128]{1,0:T(2,128)} %refs_0_.1, bf16[320,1000]{1,0:T(8,128)(2,1)} %bitcast.20, ...), custom_call_target="tpu_custom_call" | custom-call | tf_op jit(solution)/shard_map/pallas_call | solution.py:32
  4.1 3.4 %collective-permute-start = (bf16[320,256]{1,0:T(8,128)(2,1)S(1)}, bf16[320,256]{1,0:T(8,128)(2,1)S(1)}, u32[]{:S(2)}, u32[]{:S(2)}) collective-permute-start(bf16[320,256]{1,0:T(8,128)(2,1)S(1)} %get-tuple-element.42), channel_id=1, source_target_pairs={{0,24},{8,16},{1,25},{9,17},{2,26},{10,18},{3,27},{11,19},{4,28},{... | collective-permute-start | bytes 491528 | tf_op jit(solution)/shard_map/ppermute | solution.py:275
  7.5 0.0 copy-done
  7.5 0.5 shard_map.104
  8.1 2.9 %collective-permute-done.received = bf16[320,256]{1,0:T(8,128)(2,1)S(1)} collective-permute-done((bf16[320,256]{1,0:T(8,128)(2,1)S(1)}, bf16[320,256]{1,0:T(8,128)(2,1)S(1)}, u32[]{:S(2)}, u32[]{:S(2)}) %collective-permute-start) | collective-permute-done | bytes 163872 | tf_op jit(solution)/shard_map/ppermute | solution.py:275
  10.9 1.6 %shard_map.105 = (bf16[320,256]{1,0:T(8,128)(2,1)S(1)}, bf16[320,256]{1,0:T(8,128)(2,1)S(1)}, f32[320,256]{1,0:T(8,128)S(1)}, f32[1280,256]{1,0:T(8,128)S(1)}, bf16[320,256]{1,0:T(8,128)(2,1)S(1)}) custom-call(bf16[320,256]{1,0:T(8,128)(2,1)S(1)} %collective-permute-done.received, bf16[320,256]{1,0:T(8,128)(2,1)S(1)} %get-tuple-element.43.embed, ...), custom_call_target="tpu_custom_call" | custom-call | tf_op jit(solution)/shard_map/pallas_call | solution.py:32
  12.5 0.7 collective-permute-start.6
  13.2 1.3 %collective-permute-start.8 = (bf16[320,320]{1,0:T(8,128)(2,1)S(1)}, bf16[320,320]{1,0:T(8,128)(2,1)S(1)}, u32[]{:S(2)}, u32[]{:S(2)}) collective-permute-start(bf16[320,320]{1,0:T(8,128)(2,1)S(1)} %get-tuple-element.47.w_skip), channel_id=1, source_target_pairs={{16,8},{17,9},{18,10},{19,11},{20,12},{21,13},{22,14},{23,15}} | collective-permute-start | bytes 614408 | tf_op jit(solution)/shard_map/ppermute | solution.py:275
  14.5 0.2 shard_map.108
  14.7 1.3 %collective-permute-start.9 = (bf16[320,256]{1,0:T(8,128)(2,1)S(1)}, bf16[320,256]{1,0:T(8,128)(2,1)S(1)}, u32[]{:S(2)}, u32[]{:S(2)}) collective-permute-start(bf16[320,256]{1,0:T(8,128)(2,1)S(1)} %shard_map.108), channel_id=1, source_target_pairs={{24,8},{25,9},{26,10},{27,11},{28,12},{29,13},{30,14},{31,15}} | collective-permute-start | bytes 491528 | tf_op jit(solution)/shard_map/ppermute | solution.py:275
  16.0 0.0 collective-permute-done.6.received.low_2
  16.1 1.2 %shard_map.107.chain.chain_2 = bf16[320,256]{1,0:T(8,128)(2,1)S(1)} custom-call(bf16[320,256]{1,0:T(8,128)(2,1)S(1)} %collective-permute-done.6.received.low_2, f32[320,256]{1,0:T(8,128)S(1)} %get-tuple-element.52.united, f32[1280,256]{1,0:T(8,128)S(1)} %get-tuple-element.53.slope, bf16[320,1280]{1,0:T(8,128)(2,1)S(1)} %get-tuple-element.38.w_in, ...), custom_call_target="tpu_custom_call" | custom-call | tf_op jit(solution)/shard_map/pallas_call | solution.py:32
  17.3 1.3 %collective-permute-start.7 = (bf16[320,256]{1,0:T(8,128)(2,1)S(1)}, bf16[320,256]{1,0:T(8,128)(2,1)S(1)}, u32[]{:S(2)}, u32[]{:S(2)}) collective-permute-start(bf16[320,256]{1,0:T(8,128)(2,1)S(1)} %shard_map.107.chain.chain_2), channel_id=1, source_target_pairs={{16,8},{17,9},{18,10},{19,11},{20,12},{21,13},{22,14},{23,15}} | collective-permute-start | bytes 491528 | tf_op jit(solution)/shard_map/ppermute | solution.py:275
  18.6 0.7 collective-permute-start.11
  19.2 2.7 %collective-permute-start.2 = (bf16[320,256]{1,0:T(8,128)(2,1)S(1)}, bf16[320,256]{1,0:T(8,128)(2,1)S(1)}, u32[]{:S(2)}, u32[]{:S(2)}) collective-permute-start(bf16[320,256]{1,0:T(8,128)(2,1)S(1)} %get-tuple-element.48.refs_0_), channel_id=1, source_target_pairs={{0,4},{1,5},{2,6},{3,7},{4,0},{5,1},{6,2},{7,3},{8,12},{9,13},{10,... | collective-permute-start | bytes 491528 | tf_op jit(solution)/shard_map/ppermute | solution.py:279
  21.9 0.2 shard_map.109.back_2
  22.1 1.5 %collective-permute-done.8.w_mirror = bf16[320,320]{1,0:T(8,128)(2,1)S(1)} collective-permute-done((bf16[320,320]{1,0:T(8,128)(2,1)S(1)}, bf16[320,320]{1,0:T(8,128)(2,1)S(1)}, u32[]{:S(2)}, u32[]{:S(2)}) %collective-permute-start.8) | collective-permute-done | bytes 204832 | tf_op jit(solution)/shard_map/ppermute | solution.py:275
  23.7 6.9 %collective-permute-done.9.skip_far = bf16[320,256]{1,0:T(8,128)(2,1)S(1)} collective-permute-done((bf16[320,256]{1,0:T(8,128)(2,1)S(1)}, bf16[320,256]{1,0:T(8,128)(2,1)S(1)}, u32[]{:S(2)}, u32[]{:S(2)}) %collective-permute-start.9) | collective-permute-done | bytes 163872 | tf_op jit(solution)/shard_map/ppermute | solution.py:275
  30.6 0.0 collective-permute-done.7.received
  30.6 1.5 %shard_map.110 = (bf16[320,256]{1,0:T(8,128)(2,1)S(1)}, bf16[320,256]{1,0:T(8,128)(2,1)S(1)}, bf16[320,256]{1,0:T(8,128)(2,1)S(1)}) custom-call(bf16[320,256]{1,0:T(8,128)(2,1)S(1)} %collective-permute-done.7.received, bf16[320,320]{1,0:T(8,128)(2,1)S(1)} %collective-permute-done.8.w_mirror, f32[320,256]{1,0:T(8,128)S(1)} %get-tuple-element.52.united, ...), custom_call_target="tpu_custom_call" | custom-call | tf_op jit(solution)/shard_map/pallas_call | solution.py:32
  32.1 1.3 %collective-permute-start.10 = (bf16[320,256]{1,0:T(8,128)(2,1)S(1)}, bf16[320,256]{1,0:T(8,128)(2,1)S(1)}, u32[]{:S(2)}, u32[]{:S(2)}) collective-permute-start(bf16[320,256]{1,0:T(8,128)(2,1)S(1)} %get-tuple-element.54.chain_1), channel_id=1, source_target_pairs={{8,0},{9,1},{10,2},{11,3},{12,4},{13,5},{14,6},{15,7}} | collective-permute-start | bytes 491528 | tf_op jit(solution)/shard_map/ppermute | solution.py:275
  33.4 1.6 %collective-permute-start.1 = (bf16[320,256]{1,0:T(8,128)(2,1)S(1)}, bf16[320,256]{1,0:T(8,128)(2,1)S(1)}, u32[]{:S(2)}, u32[]{:S(2)}) collective-permute-start(bf16[320,256]{1,0:T(8,128)(2,1)S(1)} %get-tuple-element.48.refs_0_), channel_id=1, source_target_pairs={{0,2},{1,3},{2,0},{3,1},{4,6},{5,7},{6,4},{7,5},{8,10},{9,11},{10,... | collective-permute-start | bytes 491528 | tf_op jit(solution)/shard_map/ppermute | solution.py:279
  35.1 0.0 collective-permute-start.3
  35.1 0.0 collective-permute-done.2.refs_2_
  35.1 0.5 collective-permute-start.5
  35.6 0.0 collective-permute-done.11.skip_far
  35.6 1.7 %collective-permute-done.10.received = bf16[320,256]{1,0:T(8,128)(2,1)S(1)} collective-permute-done((bf16[320,256]{1,0:T(8,128)(2,1)S(1)}, bf16[320,256]{1,0:T(8,128)(2,1)S(1)}, u32[]{:S(2)}, u32[]{:S(2)}) %collective-permute-start.10) | collective-permute-done | bytes 163872 | tf_op jit(solution)/shard_map/ppermute | solution.py:275
  37.3 0.1 shard_map.111.refs_6_.grad_low
  37.4 2.7 %collective-permute-start.13 = (bf16[320,256]{1,0:T(8,128)(2,1)S(1)}, bf16[320,256]{1,0:T(8,128)(2,1)S(1)}, u32[]{:S(2)}, u32[]{:S(2)}) collective-permute-start(bf16[320,256]{1,0:T(8,128)(2,1)S(1)} %shard_map.111.refs_6_.grad_low), channel_id=1, source_target_pairs={{0,4},{1,5},{2,6},{3,7},{4,0},{5,1},{6,2},{7,3},{8,12},{9,13},{10,... | collective-permute-start | bytes 491528 | tf_op jit(solution)/shard_map/ppermute | solution.py:279
  40.0 1.6 %shard_map.114 = (bf16[320,256]{1,0:T(8,128)(2,1)S(1)}, f32[4,40,320]{2,1,0:T(8,128)S(1)}, bf16[4,40,320]{2,1,0:T(8,128)(2,1)S(1)}) custom-call(bf16[320,256]{1,0:T(8,128)(2,1)S(1)} %shard_map.111.refs_6_.grad_low, bf16[320,256]{1,0:T(8,128)(2,1)S(1)} %collective-permute-done.10.received, bf16[320,256]{1,0:T(8,128)(2,1)S(1)} %collective-permute-done.11.skip_far, ...), custom_call_target="tpu_custom_call" | custom-call | tf_op jit(solution)/shard_map/pallas_call | solution.py:32
  41.6 0.1 collective-permute-start.22
  41.7 0.0 collective-permute-done.1.refs_1_
  41.7 0.5 collective-permute-start.4
  42.2 0.0 collective-permute-done.3.refs_3_
  42.2 5.2 %collective-permute-start.19 = (bf16[320,256]{1,0:T(8,128)(2,1)S(1)}, bf16[320,256]{1,0:T(8,128)(2,1)S(1)}, u32[]{:S(2)}, u32[]{:S(2)}) collective-permute-start(bf16[320,256]{1,0:T(8,128)(2,1)S(1)} %get-tuple-element.58), channel_id=1, source_target_pairs={{8,6},{9,7},{10,4},{11,5},{12,2},{13,3},{14,0},{15,1}} | collective-permute-start | bytes 491528 | tf_op jit(solution)/shard_map/ppermute | solution.py:283
  47.3 0.0 collective-permute-done.5.refs_5_
  47.4 0.1 collective-permute-start.12
  47.4 0.0 collective-permute-done.13.refs_8_
  47.4 3.9 %collective-permute-start.20 = (bf16[320,256]{1,0:T(8,128)(2,1)S(1)}, bf16[320,256]{1,0:T(8,128)(2,1)S(1)}, u32[]{:S(2)}, u32[]{:S(2)}) collective-permute-start(bf16[320,256]{1,0:T(8,128)(2,1)S(1)} %collective-permute-done.13.refs_8_), channel_id=1, source_target_pairs={{8,10},{9,11},{10,8},{11,9},{12,14},{13,15},{14,12},{15,13},{16,18... | collective-permute-start | bytes 491528 | tf_op jit(solution)/shard_map/ppermute | solution.py:294
  51.4 0.0 collective-permute-done.22.given
  51.4 0.1 collective-permute-start.17
  51.5 0.0 collective-permute-done.4.refs_4_
  51.5 3.1 %collective-permute-start.23 = (bf16[2,40,320]{2,1,0:T(8,128)(2,1)S(1)}, bf16[2,40,320]{2,1,0:T(8,128)(2,1)S(1)}, u32[]{:S(2)}, u32[]{:S(2)}) collective-permute-start(bf16[2,40,320]{2,1,0:T(8,128)(2,1)S(1)} %get-tuple-element.64), channel_id=1, source_target_pairs={{0,4},{1,5},{2,6},{3,7},{4,0},{5,1},{6,2},{7,3},{8,12},{9,13},{10,... | collective-permute-start | bytes 153608 | tf_op jit(solution)/shard_map/ppermute | solution.py:279
  54.6 0.0 collective-permute-done.19.following
  54.6 0.0 collective-permute-start.14
  54.6 4.3 %collective-permute-done.12.refs_7_ = bf16[320,256]{1,0:T(8,128)(2,1)S(1)} collective-permute-done((bf16[320,256]{1,0:T(8,128)(2,1)S(1)}, bf16[320,256]{1,0:T(8,128)(2,1)S(1)}, u32[]{:S(2)}, u32[]{:S(2)}) %collective-permute-start.12) | collective-permute-done | bytes 163872 | tf_op jit(solution)/shard_map/ppermute | solution.py:279
  58.9 0.0 collective-permute-start.15
  58.9 3.5 %collective-permute-done.20.passed = bf16[320,256]{1,0:T(8,128)(2,1)S(1)} collective-permute-done((bf16[320,256]{1,0:T(8,128)(2,1)S(1)}, bf16[320,256]{1,0:T(8,128)(2,1)S(1)}, u32[]{:S(2)}, u32[]{:S(2)}) %collective-permute-start.20) | collective-permute-done | bytes 163872 | tf_op jit(solution)/shard_map/ppermute | solution.py:294
  62.4 0.0 collective-permute-start.16
  62.4 2.8 %collective-permute-done.17.normed_0 = bf16[320,256]{1,0:T(8,128)(2,1)S(1)} collective-permute-done((bf16[320,256]{1,0:T(8,128)(2,1)S(1)}, bf16[320,256]{1,0:T(8,128)(2,1)S(1)}, u32[]{:S(2)}, u32[]{:S(2)}) %collective-permute-start.17) | collective-permute-done | bytes 163872 | tf_op jit(solution)/shard_map/ppermute | solution.py:279
  65.2 0.0 collective-permute-start.18
  65.2 0.0 collective-permute-done.23.pair
  65.2 0.5 collective-permute-start.21
  65.7 0.0 collective-permute-done.14.refs_9_
  65.7 0.8 %collective-permute-start.24 = (bf16[40,320]{1,0:T(8,128)(2,1)S(1)}, bf16[40,320]{1,0:T(8,128)(2,1)S(1)}, u32[]{:S(2)}, u32[]{:S(2)}) collective-permute-start(bf16[40,320]{1,0:T(8,128)(2,1)S(1)} %get-tuple-element.66), channel_id=1, source_target_pairs={{0,2},{1,3},{2,0},{3,1},{4,6},{5,7},{6,4},{7,5},{8,10},{9,11},{10,... | collective-permute-start | bytes 76808 | tf_op jit(solution)/shard_map/ppermute | solution.py:279
  66.5 0.1 shard_map.103
  66.6 0.7 shard_map.106
  67.3 0.0 collective-permute-done.15.refs_10_
  67.3 0.0 collective-permute-done.16.refs_11_
  67.3 1.1 %shard_map.112 = (f32[160,320]{1,0:T(8,128)S(1)}, f32[160,320]{1,0:T(8,128)S(1)}) custom-call(bf16[320,160]{1,0:T(8,128)(2,1)S(1)} %get-tuple-element.41.own_out, bf16[160,1536]{1,0:T(8,128)(2,1)S(1)} %get-tuple-element.49.active, f32[160,1536]{1,0:T(8,128)S(1)} %get-tuple-element.50.slope, bf16[320,256]{1,0:T(8,128)(2,1)S(1)} %get-tuple-element.48.refs_0_, ...), custom_call_target="tpu_custom_call" | custom-call | tf_op jit(solution)/shard_map/pallas_call | solution.py:32
  68.4 0.0 collective-permute-done.18.normed_1
  68.4 1.2 %collective-permute-done.24.near = bf16[40,320]{1,0:T(8,128)(2,1)S(1)} collective-permute-done((bf16[40,320]{1,0:T(8,128)(2,1)S(1)}, bf16[40,320]{1,0:T(8,128)(2,1)S(1)}, u32[]{:S(2)}, u32[]{:S(2)}) %collective-permute-start.24) | collective-permute-done | bytes 25632 | tf_op jit(solution)/shard_map/ppermute | solution.py:279
  69.7 0.0 collective-permute-done.21.low_1
  69.7 1.4 %shard_map.117 = (f32[160,320]{1,0:T(8,128)}, f32[160,320]{1,0:T(8,128)}, f32[1,12800]{1,0:T(1,128)}, bf16[2,320,128]{2,1,0:T(8,128)(2,1)}) custom-call(bf16[320,160]{1,0:T(8,128)(2,1)S(1)} %get-tuple-element.40.own_in, bf16[320,160]{1,0:T(8,128)(2,1)S(1)} %get-tuple-element.41.own_out, f32[160,320]{1,0:T(8,128)S(1)} %get-tuple-element.56.sum_in, ...), custom_call_target="tpu_custom_call" | custom-call | tf_op jit(solution)/shard_map/pallas_call | solution.py:32
  (4 shorter events, 0.1 us)
Async XLA Ops:
  0.6 6.9 %copy-start = (bf16[2,128,320]{1,2,0:T(8,128)(2,1)S(1)}, bf16[2,128,320]{1,2,0:T(8,128)(2,1)}, u32[]{:S(2)}) copy-start(bf16[2,128,320]{1,2,0:T(8,128)(2,1)} %param.13) | copy-start | bytes 491524
  4.1 6.8 %collective-permute-start = (bf16[320,256]{1,0:T(8,128)(2,1)S(1)}, bf16[320,256]{1,0:T(8,128)(2,1)S(1)}, u32[]{:S(2)}, u32[]{:S(2)}) collective-permute-start(bf16[320,256]{1,0:T(8,128)(2,1)S(1)} %get-tuple-element.42), channel_id=1, source_target_pairs={{0,24},{8,16},{1,25},{9,17},{2,26},{10,18},{3,27},{11,19},{4,28},{... | collective-permute-start | bytes 491528 | tf_op jit(solution)/shard_map/ppermute | solution.py:275
  12.5 3.5 %collective-permute-start.6 = (bf16[320,256]{1,0:T(8,128)(2,1)S(1)}, bf16[320,256]{1,0:T(8,128)(2,1)S(1)}, u32[]{:S(2)}, u32[]{:S(2)}) collective-permute-start(bf16[320,256]{1,0:T(8,128)(2,1)S(1)} %get-tuple-element.51.chain.chain_3), channel_id=1, source_target_pairs={{24,16},{25,17},{26,18},{27,19},{28,20},{29,21},{30,22},{31,23}} | collective-permute-start | bytes 491528 | tf_op jit(solution)/shard_map/ppermute | solution.py:275
  13.2 10.5 %collective-permute-start.8 = (bf16[320,320]{1,0:T(8,128)(2,1)S(1)}, bf16[320,320]{1,0:T(8,128)(2,1)S(1)}, u32[]{:S(2)}, u32[]{:S(2)}) collective-permute-start(bf16[320,320]{1,0:T(8,128)(2,1)S(1)} %get-tuple-element.47.w_skip), channel_id=1, source_target_pairs={{16,8},{17,9},{18,10},{19,11},{20,12},{21,13},{22,14},{23,15}} | collective-permute-start | bytes 614408 | tf_op jit(solution)/shard_map/ppermute | solution.py:275
  14.7 15.8 %collective-permute-start.9 = (bf16[320,256]{1,0:T(8,128)(2,1)S(1)}, bf16[320,256]{1,0:T(8,128)(2,1)S(1)}, u32[]{:S(2)}, u32[]{:S(2)}) collective-permute-start(bf16[320,256]{1,0:T(8,128)(2,1)S(1)} %shard_map.108), channel_id=1, source_target_pairs={{24,8},{25,9},{26,10},{27,11},{28,12},{29,13},{30,14},{31,15}} | collective-permute-start | bytes 491528 | tf_op jit(solution)/shard_map/ppermute | solution.py:275
  17.3 13.3 %collective-permute-start.7 = (bf16[320,256]{1,0:T(8,128)(2,1)S(1)}, bf16[320,256]{1,0:T(8,128)(2,1)S(1)}, u32[]{:S(2)}, u32[]{:S(2)}) collective-permute-start(bf16[320,256]{1,0:T(8,128)(2,1)S(1)} %shard_map.107.chain.chain_2), channel_id=1, source_target_pairs={{16,8},{17,9},{18,10},{19,11},{20,12},{21,13},{22,14},{23,15}} | collective-permute-start | bytes 491528 | tf_op jit(solution)/shard_map/ppermute | solution.py:275
  18.6 17.0 %collective-permute-start.11 = (bf16[320,256]{1,0:T(8,128)(2,1)S(1)}, bf16[320,256]{1,0:T(8,128)(2,1)S(1)}, u32[]{:S(2)}, u32[]{:S(2)}) collective-permute-start(bf16[320,256]{1,0:T(8,128)(2,1)S(1)} %shard_map.108), channel_id=1, source_target_pairs={{24,0},{25,1},{26,2},{27,3},{28,4},{29,5},{30,6},{31,7}} | collective-permute-start | bytes 491528 | tf_op jit(solution)/shard_map/ppermute | solution.py:275
  19.2 15.8 %collective-permute-start.2 = (bf16[320,256]{1,0:T(8,128)(2,1)S(1)}, bf16[320,256]{1,0:T(8,128)(2,1)S(1)}, u32[]{:S(2)}, u32[]{:S(2)}) collective-permute-start(bf16[320,256]{1,0:T(8,128)(2,1)S(1)} %get-tuple-element.48.refs_0_), channel_id=1, source_target_pairs={{0,4},{1,5},{2,6},{3,7},{4,0},{5,1},{6,2},{7,3},{8,12},{9,13},{10,... | collective-permute-start | bytes 491528 | tf_op jit(solution)/shard_map/ppermute | solution.py:279
  32.1 5.2 %collective-permute-start.10 = (bf16[320,256]{1,0:T(8,128)(2,1)S(1)}, bf16[320,256]{1,0:T(8,128)(2,1)S(1)}, u32[]{:S(2)}, u32[]{:S(2)}) collective-permute-start(bf16[320,256]{1,0:T(8,128)(2,1)S(1)} %get-tuple-element.54.chain_1), channel_id=1, source_target_pairs={{8,0},{9,1},{10,2},{11,3},{12,4},{13,5},{14,6},{15,7}} | collective-permute-start | bytes 491528 | tf_op jit(solution)/shard_map/ppermute | solution.py:275
  33.4 8.2 %collective-permute-start.1 = (bf16[320,256]{1,0:T(8,128)(2,1)S(1)}, bf16[320,256]{1,0:T(8,128)(2,1)S(1)}, u32[]{:S(2)}, u32[]{:S(2)}) collective-permute-start(bf16[320,256]{1,0:T(8,128)(2,1)S(1)} %get-tuple-element.48.refs_0_), channel_id=1, source_target_pairs={{0,2},{1,3},{2,0},{3,1},{4,6},{5,7},{6,4},{7,5},{8,10},{9,11},{10,... | collective-permute-start | bytes 491528 | tf_op jit(solution)/shard_map/ppermute | solution.py:279
  35.1 7.1 %collective-permute-start.3 = (bf16[320,256]{1,0:T(8,128)(2,1)S(1)}, bf16[320,256]{1,0:T(8,128)(2,1)S(1)}, u32[]{:S(2)}, u32[]{:S(2)}) collective-permute-start(bf16[320,256]{1,0:T(8,128)(2,1)S(1)} %get-tuple-element.48.refs_0_), channel_id=1, source_target_pairs={{0,1},{1,0},{2,3},{3,2},{4,5},{5,4},{6,7},{7,6},{8,9},{9,8},{10,11... | collective-permute-start | bytes 491528 | tf_op jit(solution)/shard_map/ppermute | solution.py:279
  35.1 12.3 %collective-permute-start.5 = (bf16[320,256]{1,0:T(8,128)(2,1)S(1)}, bf16[320,256]{1,0:T(8,128)(2,1)S(1)}, u32[]{:S(2)}, u32[]{:S(2)}) collective-permute-start(bf16[320,256]{1,0:T(8,128)(2,1)S(1)} %collective-permute-done.2.refs_2_), channel_id=1, source_target_pairs={{0,1},{1,0},{2,3},{3,2},{4,5},{5,4},{6,7},{7,6},{8,9},{9,8},{10,11... | collective-permute-start | bytes 491528 | tf_op jit(solution)/shard_map/ppermute | solution.py:279
  37.4 10.1 %collective-permute-start.13 = (bf16[320,256]{1,0:T(8,128)(2,1)S(1)}, bf16[320,256]{1,0:T(8,128)(2,1)S(1)}, u32[]{:S(2)}, u32[]{:S(2)}) collective-permute-start(bf16[320,256]{1,0:T(8,128)(2,1)S(1)} %shard_map.111.refs_6_.grad_low), channel_id=1, source_target_pairs={{0,4},{1,5},{2,6},{3,7},{4,0},{5,1},{6,2},{7,3},{8,12},{9,13},{10,... | collective-permute-start | bytes 491528 | tf_op jit(solution)/shard_map/ppermute | solution.py:279
  41.6 9.8 %collective-permute-start.22 = (bf16[4,40,320]{2,1,0:T(8,128)(2,1)S(1)}, bf16[4,40,320]{2,1,0:T(8,128)(2,1)S(1)}, u32[]{:S(2)}, u32[]{:S(2)}) collective-permute-start(bf16[4,40,320]{2,1,0:T(8,128)(2,1)S(1)} %get-tuple-element.61), channel_id=1, source_target_pairs={{0,1},{1,0},{2,3},{3,2},{4,5},{5,4},{6,7},{7,6},{8,9},{9,8},{10,11... | collective-permute-start | bytes 307208 | tf_op jit(solution)/shard_map/ppermute | solution.py:279
  41.7 9.8 %collective-permute-start.4 = (bf16[320,256]{1,0:T(8,128)(2,1)S(1)}, bf16[320,256]{1,0:T(8,128)(2,1)S(1)}, u32[]{:S(2)}, u32[]{:S(2)}) collective-permute-start(bf16[320,256]{1,0:T(8,128)(2,1)S(1)} %collective-permute-done.1.refs_1_), channel_id=1, source_target_pairs={{0,1},{1,0},{2,3},{3,2},{4,5},{5,4},{6,7},{7,6},{8,9},{9,8},{10,11... | collective-permute-start | bytes 491528 | tf_op jit(solution)/shard_map/ppermute | solution.py:279
  42.2 12.4 %collective-permute-start.19 = (bf16[320,256]{1,0:T(8,128)(2,1)S(1)}, bf16[320,256]{1,0:T(8,128)(2,1)S(1)}, u32[]{:S(2)}, u32[]{:S(2)}) collective-permute-start(bf16[320,256]{1,0:T(8,128)(2,1)S(1)} %get-tuple-element.58), channel_id=1, source_target_pairs={{8,6},{9,7},{10,4},{11,5},{12,2},{13,3},{14,0},{15,1}} | collective-permute-start | bytes 491528 | tf_op jit(solution)/shard_map/ppermute | solution.py:283
  47.4 11.5 %collective-permute-start.12 = (bf16[320,256]{1,0:T(8,128)(2,1)S(1)}, bf16[320,256]{1,0:T(8,128)(2,1)S(1)}, u32[]{:S(2)}, u32[]{:S(2)}) collective-permute-start(bf16[320,256]{1,0:T(8,128)(2,1)S(1)} %shard_map.111.refs_6_.grad_low), channel_id=1, source_target_pairs={{0,2},{1,3},{2,0},{3,1},{4,6},{5,7},{6,4},{7,5},{8,10},{9,11},{10,... | collective-permute-start | bytes 491528 | tf_op jit(solution)/shard_map/ppermute | solution.py:279
  47.4 14.9 %collective-permute-start.20 = (bf16[320,256]{1,0:T(8,128)(2,1)S(1)}, bf16[320,256]{1,0:T(8,128)(2,1)S(1)}, u32[]{:S(2)}, u32[]{:S(2)}) collective-permute-start(bf16[320,256]{1,0:T(8,128)(2,1)S(1)} %collective-permute-done.13.refs_8_), channel_id=1, source_target_pairs={{8,10},{9,11},{10,8},{11,9},{12,14},{13,15},{14,12},{15,13},{16,18... | collective-permute-start | bytes 491528 | tf_op jit(solution)/shard_map/ppermute | solution.py:294
  51.4 13.8 %collective-permute-start.17 = (bf16[320,256]{1,0:T(8,128)(2,1)S(1)}, bf16[320,256]{1,0:T(8,128)(2,1)S(1)}, u32[]{:S(2)}, u32[]{:S(2)}) collective-permute-start(bf16[320,256]{1,0:T(8,128)(2,1)S(1)} %collective-permute-done.2.refs_2_), channel_id=1, source_target_pairs={{0,2},{1,3},{2,0},{3,1},{4,6},{5,7},{6,4},{7,5},{8,10},{9,11},{10,... | collective-permute-start | bytes 491528 | tf_op jit(solution)/shard_map/ppermute | solution.py:279
  51.5 13.7 %collective-permute-start.23 = (bf16[2,40,320]{2,1,0:T(8,128)(2,1)S(1)}, bf16[2,40,320]{2,1,0:T(8,128)(2,1)S(1)}, u32[]{:S(2)}, u32[]{:S(2)}) collective-permute-start(bf16[2,40,320]{2,1,0:T(8,128)(2,1)S(1)} %get-tuple-element.64), channel_id=1, source_target_pairs={{0,4},{1,5},{2,6},{3,7},{4,0},{5,1},{6,2},{7,3},{8,12},{9,13},{10,... | collective-permute-start | bytes 153608 | tf_op jit(solution)/shard_map/ppermute | solution.py:279
  54.6 11.1 %collective-permute-start.14 = (bf16[320,256]{1,0:T(8,128)(2,1)S(1)}, bf16[320,256]{1,0:T(8,128)(2,1)S(1)}, u32[]{:S(2)}, u32[]{:S(2)}) collective-permute-start(bf16[320,256]{1,0:T(8,128)(2,1)S(1)} %shard_map.111.refs_6_.grad_low), channel_id=1, source_target_pairs={{0,1},{1,0},{2,3},{3,2},{4,5},{5,4},{6,7},{7,6},{8,9},{9,8},{10,11... | collective-permute-start | bytes 491528 | tf_op jit(solution)/shard_map/ppermute | solution.py:279
  58.9 8.4 %collective-permute-start.15 = (bf16[320,256]{1,0:T(8,128)(2,1)S(1)}, bf16[320,256]{1,0:T(8,128)(2,1)S(1)}, u32[]{:S(2)}, u32[]{:S(2)}) collective-permute-start(bf16[320,256]{1,0:T(8,128)(2,1)S(1)} %collective-permute-done.12.refs_7_), channel_id=1, source_target_pairs={{0,1},{1,0},{2,3},{3,2},{4,5},{5,4},{6,7},{7,6},{8,9},{9,8},{10,11... | collective-permute-start | bytes 491528 | tf_op jit(solution)/shard_map/ppermute | solution.py:279
  62.4 4.9 %collective-permute-start.16 = (bf16[320,256]{1,0:T(8,128)(2,1)S(1)}, bf16[320,256]{1,0:T(8,128)(2,1)S(1)}, u32[]{:S(2)}, u32[]{:S(2)}) collective-permute-start(bf16[320,256]{1,0:T(8,128)(2,1)S(1)} %collective-permute-done.13.refs_8_), channel_id=1, source_target_pairs={{0,1},{1,0},{2,3},{3,2},{4,5},{5,4},{6,7},{7,6},{8,9},{9,8},{10,11... | collective-permute-start | bytes 491528 | tf_op jit(solution)/shard_map/ppermute | solution.py:279
  65.2 3.2 %collective-permute-start.18 = (bf16[320,256]{1,0:T(8,128)(2,1)S(1)}, bf16[320,256]{1,0:T(8,128)(2,1)S(1)}, u32[]{:S(2)}, u32[]{:S(2)}) collective-permute-start(bf16[320,256]{1,0:T(8,128)(2,1)S(1)} %collective-permute-done.17.normed_0), channel_id=1, source_target_pairs={{0,1},{1,0},{2,3},{3,2},{4,5},{5,4},{6,7},{7,6},{8,9},{9,8},{10,11... | collective-permute-start | bytes 491528 | tf_op jit(solution)/shard_map/ppermute | solution.py:279
  65.2 4.5 %collective-permute-start.21 = (bf16[320,256]{1,0:T(8,128)(2,1)S(1)}, bf16[320,256]{1,0:T(8,128)(2,1)S(1)}, u32[]{:S(2)}, u32[]{:S(2)}) collective-permute-start(bf16[320,256]{1,0:T(8,128)(2,1)S(1)} %shard_map.113.low_0), channel_id=1, source_target_pairs={{0,1},{1,0},{2,3},{3,2},{4,5},{5,4},{6,7},{7,6},{8,9},{9,8},{10,11... | collective-permute-start | bytes 491528 | tf_op jit(solution)/shard_map/ppermute | solution.py:279
  65.7 4.0 %collective-permute-start.24 = (bf16[40,320]{1,0:T(8,128)(2,1)S(1)}, bf16[40,320]{1,0:T(8,128)(2,1)S(1)}, u32[]{:S(2)}, u32[]{:S(2)}) collective-permute-start(bf16[40,320]{1,0:T(8,128)(2,1)S(1)} %get-tuple-element.66), channel_id=1, source_target_pairs={{0,2},{1,3},{2,0},{3,1},{4,6},{5,7},{6,4},{7,5},{8,10},{9,11},{10,... | collective-permute-start | bytes 76808 | tf_op jit(solution)/shard_map/ppermute | solution.py:279

commit v7 on v5

--- a/solution.py
+++ b/solution.py
@@ -1,3 +1,6 @@
+from functools import partial
+
+
 import jax
 import jax.numpy as jnp
 from jax import lax
@@ -63,30 +66,46 @@
     for copy in copies:
         copy.start()
     times, table, w_skip, inputs, w_in, w_out = local
-    copies[0].wait()
-    levels = lax.broadcasted_iota(jnp.int32, (table.shape[1], times.shape[1]), 0)
-    hot = [
-        jnp.where(levels == times[m : m + 1, :], 1.0, 0.0).astype(LOW)
-        for m in range(times.shape[0])
-    ]
-    copies[1].wait()
-    embed = dot(table[...], jnp.concatenate(hot, axis=1), 1, 0).astype(LOW)
-    embed_out[...] = embed
-    copies[2].wait()
-    copies[3].wait()
-    united = side_by_side(inputs).astype(F32) + dot(w_skip[...], embed, 0, 0)
-    normed = (united * norm_of(united)).astype(LOW)
-    copies[4].wait()
-    preact = dot(w_in[...], normed, 0, 0)
-    active = (preact * sigmoid(preact)).astype(LOW)
-    copies[5].wait()
-    value_out[...] = (united + dot(w_out[...], active, 1, 0)).astype(LOW)
+    encoder = lax.axis_index("section") < 2
+
+    @pl.when(encoder)
+    def _():
+        copies[0].wait()
+        levels = lax.broadcasted_iota(jnp.int32, (table.shape[1], times.shape[1]), 0)
+        hot = [
+            jnp.where(levels == times[m : m + 1, :], 1.0, 0.0).astype(LOW)
+            for m in range(times.shape[0])
+        ]
+        copies[1].wait()
+        embed = dot(table[...], jnp.concatenate(hot, axis=1), 1, 0).astype(LOW)
+        embed_out[...] = embed
+        copies[2].wait()
+        copies[3].wait()
+        united = side_by_side(inputs).astype(F32) + dot(w_skip[...], embed, 0, 0)
+        normed = (united * norm_of(united)).astype(LOW)
+        copies[4].wait()
+        preact = dot(w_in[...], normed, 0, 0)
+        active = (preact * sigmoid(preact)).astype(LOW)
+        copies[5].wait()
+        value_out[...] = (united + dot(w_out[...], active, 1, 0)).astype(LOW)
+
+    @pl.when(jnp.logical_not(encoder))
+    def _():
+        for copy in copies:
+            copy.wait()
+
+
+def active_in(section):
+    return pl.when(lax.axis_index("section") == section)
 
 
 def early_body(upstream, w_out, low_out, grad_act_out):
     low = side_by_side(upstream)
     low_out[...] = low
-    grad_act_out[...] = dot(w_out[...], low, 0, 0)
+
+    @active_in(3)
+    def _():
+        grad_act_out[...] = dot(w_out[...], low, 0, 0)
 
 
 def back_through(grad_out, grad_act, united, slope, w_in):
@@ -111,36 +130,50 @@
     sigma = sigmoid(preact)
     slope = sigma * (1.0 + preact * (1.0 - sigma))
     slope_out[...] = slope
-    chain_out[...] = back_through(top_low[...].astype(F32), grad_act[...], united, slope, w_in)
-
-
-def back_body(chain, w_skip, back_out):
-    back_out[...] = dot(w_skip[...], chain[...], 1, 0).astype(LOW)
+
+    @active_in(3)
+    def _():
+        chain_out[...] = back_through(
+            top_low[...].astype(F32), grad_act[...], united, slope, w_in
+        )
+
+
+def back_body(owner, chain, w_skip, back_out):
+    @active_in(owner)
+    def _():
+        back_out[...] = dot(w_skip[...], chain[...], 1, 0).astype(LOW)
 
 
 def tick_body(received, united, slope, w_in, w_out, chain_out):
-    low = received[...]
-    grad_act = dot(w_out[...], low, 0, 0)
-    chain_out[...] = back_through(low.astype(F32), grad_act, united[...], slope[...], w_in)
+    @active_in(2)
+    def _():
+        low = received[...]
+        grad_act = dot(w_out[...], low, 0, 0)
+        chain_out[...] = back_through(low.astype(F32), grad_act, united[...], slope[...], w_in)
 
 
 def mirror_tick_body(
     received, w_mirror, united, slope, w_in, w_out, skip_far, back_2, chain_2, chain_3,
     chain_out, low_out, next_out,
 ):
-    back = dot(w_mirror[...], received[...], 1, 0).astype(LOW)
-    grad_out = received[...].astype(F32) + back.astype(F32)
-    low = grad_out.astype(LOW)
-    low_out[...] = low
-    grad_act = dot(w_out[...], low, 0, 0)
-    chain = back_through(grad_out, grad_act, united[...], slope[...], w_in)
-    chain_out[...] = chain
-    section = lax.axis_index("section")
-    ahead = (chain.astype(F32) + skip_far[...].astype(F32)).astype(LOW)
-    ahead = jnp.where(
-        section == 2, (chain_2[...].astype(F32) + back_2[...].astype(F32)).astype(LOW), ahead
-    )
-    next_out[...] = jnp.where(section == 3, chain_3[...], ahead)
+    @active_in(1)
+    def _():
+        back = dot(w_mirror[...], received[...], 1, 0).astype(LOW)
+        grad_out = received[...].astype(F32) + back.astype(F32)
+        low = grad_out.astype(LOW)
+        low_out[...] = low
+        grad_act = dot(w_out[...], low, 0, 0)
+        chain = back_through(grad_out, grad_act, united[...], slope[...], w_in)
+        chain_out[...] = chain
+        next_out[...] = (chain.astype(F32) + skip_far[...].astype(F32)).astype(LOW)
+
+    @active_in(2)
+    def _():
+        next_out[...] = (chain_2[...].astype(F32) + back_2[...].astype(F32)).astype(LOW)
+
+    @active_in(3)
+    def _():
+        next_out[...] = chain_3[...]
 
 
 def pick_body(received, skip_far, low_1, low_2, top_low, grad_low_out):
@@ -159,23 +192,25 @@
     grad_low, received, skip_far, united, slope, w_in, w_out, source, chain_1, chain_2,
     chain_3, kept_out, keep_out, give_out,
 ):
-    grad_out = received[...].astype(F32) + skip_far[...].astype(F32)
-    grad_act = dot(w_out[...], grad_low[...], 0, 0)
-    section = lax.axis_index("section")
-    kept = back_through(grad_out, grad_act, united[...], slope[...], w_in)
-    kept = jnp.where(section == 1, chain_1[...], kept)
-    kept = jnp.where(section == 2, chain_2[...], kept)
-    kept = jnp.where(section == 3, chain_3[...], kept)
-    span = kept_out.shape[2]
-    for m in range(kept_out.shape[0]):
-        kept_out[m] = kept[:, m * span : (m + 1) * span]
-    partial = dot(source[...], kept, 1, 1)
+    @active_in(0)
+    def _():
+        grad_out = received[...].astype(F32) + skip_far[...].astype(F32)
+        grad_act = dot(w_out[...], grad_low[...], 0, 0)
+        kept_out[...] = back_through(grad_out, grad_act, united[...], slope[...], w_in)
+
+    for owner, chain in enumerate((chain_1, chain_2, chain_3), 1):
+
+        @active_in(owner)
+        def _():
+            kept_out[...] = chain[...]
+
+    product = dot(source[...], kept_out[...], 1, 1)
     size = keep_out.shape[1]
     first_core = lax.axis_index("dp") % 2 == 0
     for block in range(keep_out.shape[0]):
         start = 2 * block * size
-        even = partial[start : start + size, :]
-        odd = partial[start + size : start + 2 * size, :]
+        even = product[start : start + size, :]
+        odd = product[start + size : start + 2 * size, :]
         keep_out[block] = jnp.where(first_core, even, odd)
         give_out[block] = jnp.where(first_core, odd, even).astype(LOW)
 
@@ -188,11 +223,7 @@
         piece_out[...] = (keep[far] + given[far].astype(F32)).astype(LOW)
 
 
-def flat_body(own, *refs):
-    pieces, out, lanes, square = refs[:-3], refs[-3], refs[-2], refs[-1]
-    total = own[...]
-    for piece in pieces:
-        total = total + piece[...].astype(F32)
+def flatten(total, out, lanes, square):
     lanes[0] = total[:, :128]
     lanes[1] = total[:, 128:256]
     lanes[2] = jnp.concatenate([total[:, 256:], total[:, 256:]], axis=1)
@@ -251,14 +282,23 @@
     )
 
 
-def rest_grad_body(own_out, active, slope, sum_in, sum_out, *refs):
-    half = (len(refs) - 2) // 2
-    first = active.shape[1] // refs[0].shape[1] - half
+def rest_grad_body(
+    own_out, active, slope, sum_in, sum_out, normed_0, normed_1, low_0, low_1, own, piece_1,
+    piece_2, piece_3, kept, in_out, out_out, skip_out, kept_out, lanes, square,
+):
+    span = kept_out.shape[2]
+    for m in range(kept_out.shape[0]):
+        kept_out[m] = kept[:, m * span : (m + 1) * span]
+    total = own[...]
+    for piece in (piece_1, piece_2, piece_3):
+        total = total + piece[...].astype(F32)
+    flatten(total, skip_out, lanes, square)
+    first = active.shape[1] // normed_0.shape[1] - 2
     part_in, part_out = slice_grad(
-        own_out, active, slope, refs[:half], refs[half : 2 * half], first
-    )
-    refs[-2][...] = sum_in[...] + part_in
-    refs[-1][...] = sum_out[...] + part_out
+        own_out, active, slope, (normed_0, normed_1), (low_0, low_1), first
+    )
+    in_out[...] = sum_in[...] + part_in
+    out_out[...] = sum_out[...] + part_out
 
 
 def hop(value, pairs):
@@ -320,13 +360,13 @@
     )
     chain = hop(chain_3, [(3, 2)])
     w_mirror = hop(w_skip, [(2, 1)])
-    (back,) = call(back_body, [low], chain_3, w_skip)
+    (back,) = call(partial(back_body, 3), [low], chain_3, w_skip)
     skip_far = hop(back, [(3, 0)])
     skip_next = hop(back, [(3, 1)])
     low_2 = chain
     (chain_2,) = call(tick_body, [low], chain, united, slope, w_in, w_out)
     chain = hop(chain_2, [(2, 1)])
-    (back_2,) = call(back_body, [low], chain_2, w_skip)
+    (back_2,) = call(partial(back_body, 2), [low], chain_2, w_skip)
     chain_1, low_1, ahead = call(
         mirror_tick_body, [low, low, low],
         chain, w_mirror, united, slope, w_in, w_out, skip_next, back_2, chain_2, chain_3,
@@ -359,7 +399,7 @@
     low_all = in_turn(low_near, [exchange(x, count, 1) for x in low_near])
     block = (count // 2, width // count, width)
     kept, keep, give = call(
-        last_body, [((n_micro, width, span), LOW), (block, F32), (block, LOW)],
+        last_body, [low, (block, F32), (block, LOW)],
         grad_low, chain, skip_far, united, slope, w_in, w_out, source, chain_1, chain_2,
         chain_3,
     )
@@ -370,22 +410,21 @@
         keep, given,
     )
     pieces = [exchange(value, count, 2 * i) for i, value in enumerate(pieces, 1)]
-    (grad_skip,) = call(
-        flat_body, [((1, piece[0] * piece[1]), F32)], own, *pieces,
-        scratch=[
-            pltpu.VMEM((3, piece[0], 128), F32),
-            pltpu.VMEM((piece[0] * piece[1] // 128, 128), F32),
-        ],
-    )
     grads = ((part, width), F32)
     half = 6
     sums = call(
         half_grad_body, [grads] * 2,
         own_out, active_all, slope_all, *normed_all[:half], *low_all[:half],
     )
-    grad_in, grad_out_w = call(
-        rest_grad_body, [grads] * 2,
-        own_out, active_all, slope_all, *sums, *normed_all[half:], *low_all[half:],
+    grad_in, grad_out_w, grad_skip, kept = call(
+        rest_grad_body,
+        [grads, grads, ((1, piece[0] * piece[1]), F32), ((n_micro, width, span), LOW)],
+        own_out, active_all, slope_all, *sums, *normed_all[half:], *low_all[half:], own, *pieces,
+        kept,
+        scratch=[
+            pltpu.VMEM((3, piece[0], 128), F32),
+            pltpu.VMEM((piece[0] * piece[1] // 128, 128), F32),
+        ],
     )
     kept = jnp.swapaxes(kept, 1, 2)
     return (kept[None], grad_skip, grad_in[None], grad_out_w[None])

time: 83.2 us -> 72.7 us (0.87)
  Pallas kernels: 14.9 us -> 8.16 us
  waiting for transfers between devices: 32.4 us -> 28.1 us
    pallas_call x16 -> x15, Pallas kernels: 14.9 us -> 8.16 us  [call(): pl.pallas_call(body, out_shape=[jax.ShapeDtypeStruct(shape, kind) for sha...]
    ppermute x17, waiting for transfers between devices: 21.9 us -> 16.8 us  [exchange(): return lax.ppermute(value, 'dp', [(i, i ^ mask) for i in range(count)])]
    ppermute x17, starting transfers between devices: 16.9 us -> 18.5 us  [exchange(): return lax.ppermute(value, 'dp', [(i, i ^ mask) for i in range(count)])]
    ppermute x1, starting transfers between devices: 9.83 us -> 8.85 us  [from_next(): return lax.ppermute(value, ('section', 'dp'), pairs)]
  transfers between devices with their start and end apart: 26 -> 26, of which waited for: 10 -> 8; matrix products, arithmetic and copies ran while one was open for 0% -> 0% of each run, Pallas kernels for 10% -> 5%
where the time goes in v7:
time: 72.7 us; the launch traced here: 72.4 us
  starting transfers between devices  35.2 us (48%)
  waiting for transfers between devices  28.1 us (39%)
  Pallas kernels  8.16 us (11%)
  between operations  0.94 us (1%)
    ppermute x17, starting transfers between devices, exchange(): return lax.ppermute(value, 'dp', [(i, i ^ mask) for i in range(count)])  18.5 us
    ppermute x17, waiting for transfers between devices, exchange(): return lax.ppermute(value, 'dp', [(i, i ^ mask) for i in range(count)])  16.8 us
    ppermute x7, waiting for transfers between devices, hop(): return lax.ppermute(value, 'section', pairs)  11.3 us
    ppermute x1, starting transfers between devices, from_next(): return lax.ppermute(value, ('section', 'dp'), pairs)  8.85 us
    pallas_call x15, Pallas kernels, call(): pl.pallas_call(body, out_shape=[jax.ShapeDtypeStruct(shape, kind) for sha...  8.16 us
    ppermute x7, starting transfers between devices, hop(): return lax.ppermute(value, 'section', pairs)  7.2 us
  transfers between devices with their start and end apart: 26, of which 8 were waited for; matrix products, arithmetic and copies ran while one was open for 0% of the time, Pallas kernels for 5%

profile of v7, /device:TPU:4, one launch (start us, length us, event | category | flops | bytes accessed | tf_op | source)
XLA Modules:
  0.0 72.4 jit_solution(2675910139776689458)
XLA Ops:
  0.6 0.0 copy-start
  0.6 1.8 %shard_map.102 = (bf16[320,256]{1,0:T(8,128)(2,1)S(1)}, bf16[320,256]{1,0:T(8,128)(2,1)S(1)}, bf16[320,320]{1,0:T(8,128)(2,1)S(1)}, bf16[2,320,128]{2,1,0:T(8,12...) custom-call(s32[2,128]{1,0:T(2,128)} %refs_0_.1, bf16[320,1000]{1,0:T(8,128)(2,1)} %bitcast.20, ...), custom_call_target="tpu_custom_call" | custom-call | tf_op jit(solution)/shard_map/pallas_call | solution.py:35
  2.5 1.3 %collective-permute-start = (bf16[320,256]{1,0:T(8,128)(2,1)S(1)}, bf16[320,256]{1,0:T(8,128)(2,1)S(1)}, u32[]{:S(2)}, u32[]{:S(2)}) collective-permute-start(bf16[320,256]{1,0:T(8,128)(2,1)S(1)} %get-tuple-element.41), channel_id=1, source_target_pairs={{0,24},{8,16},{1,25},{9,17},{2,26},{10,18},{3,27},{11,19},{4,28},{... | collective-permute-start | bytes 491528 | tf_op jit(solution)/shard_map/ppermute | solution.py:305
  3.8 0.0 copy-done
  3.8 7.4 %collective-permute-done.received = bf16[320,256]{1,0:T(8,128)(2,1)S(1)} collective-permute-done((bf16[320,256]{1,0:T(8,128)(2,1)S(1)}, bf16[320,256]{1,0:T(8,128)(2,1)S(1)}, u32[]{:S(2)}, u32[]{:S(2)}) %collective-permute-start) | collective-permute-done | bytes 163872 | tf_op jit(solution)/shard_map/ppermute | solution.py:305
  11.2 1.1 %shard_map.105 = (bf16[320,256]{1,0:T(8,128)(2,1)S(1)}, bf16[320,256]{1,0:T(8,128)(2,1)S(1)}, f32[320,256]{1,0:T(8,128)S(1)}, f32[1280,256]{1,0:T(8,128)S(1)}, bf16[320,256]{1,0:T(8,128)(2,1)S(1)}) custom-call(bf16[320,256]{1,0:T(8,128)(2,1)S(1)} %collective-permute-done.received, bf16[320,256]{1,0:T(8,128)(2,1)S(1)} %get-tuple-element.42.embed, ...), custom_call_target="tpu_custom_call" | custom-call | tf_op jit(solution)/shard_map/pallas_call | solution.py:35
  12.3 1.3 %collective-permute-start.8 = (bf16[320,256]{1,0:T(8,128)(2,1)S(1)}, bf16[320,256]{1,0:T(8,128)(2,1)S(1)}, u32[]{:S(2)}, u32[]{:S(2)}) collective-permute-start(bf16[320,256]{1,0:T(8,128)(2,1)S(1)} %get-tuple-element.50.chain.chain_3), channel_id=1, source_target_pairs={{24,16},{25,17},{26,18},{27,19},{28,20},{29,21},{30,22},{31,23}} | collective-permute-start | bytes 491528 | tf_op jit(solution)/shard_map/ppermute | solution.py:305
  13.6 1.3 %collective-permute-start.10 = (bf16[320,320]{1,0:T(8,128)(2,1)S(1)}, bf16[320,320]{1,0:T(8,128)(2,1)S(1)}, u32[]{:S(2)}, u32[]{:S(2)}) collective-permute-start(bf16[320,320]{1,0:T(8,128)(2,1)S(1)} %get-tuple-element.46.w_skip), channel_id=1, source_target_pairs={{16,8},{17,9},{18,10},{19,11},{20,12},{21,13},{22,14},{23,15}} | collective-permute-start | bytes 614408 | tf_op jit(solution)/shard_map/ppermute | solution.py:305
  14.9 0.7 collective-permute-start.11
  15.6 3.9 %collective-permute-done.8.received.low_2 = bf16[320,256]{1,0:T(8,128)(2,1)S(1)} collective-permute-done((bf16[320,256]{1,0:T(8,128)(2,1)S(1)}, bf16[320,256]{1,0:T(8,128)(2,1)S(1)}, u32[]{:S(2)}, u32[]{:S(2)}) %collective-permute-start.8) | collective-permute-done | bytes 163872 | tf_op jit(solution)/shard_map/ppermute | solution.py:305
  19.5 1.2 %shard_map.107.chain.chain_2 = bf16[320,256]{1,0:T(8,128)(2,1)S(1)} custom-call(bf16[320,256]{1,0:T(8,128)(2,1)S(1)} %collective-permute-done.8.received.low_2, f32[320,256]{1,0:T(8,128)S(1)} %get-tuple-element.51.united, f32[1280,256]{1,0:T(8,128)S(1)} %get-tuple-element.52.slope, bf16[320,1280]{1,0:T(8,128)(2,1)S(1)} %get-tuple-element.37.w_in, ...), custom_call_target="tpu_custom_call" | custom-call | tf_op jit(solution)/shard_map/pallas_call | solution.py:35
  20.7 1.3 %collective-permute-start.9 = (bf16[320,256]{1,0:T(8,128)(2,1)S(1)}, bf16[320,256]{1,0:T(8,128)(2,1)S(1)}, u32[]{:S(2)}, u32[]{:S(2)}) collective-permute-start(bf16[320,256]{1,0:T(8,128)(2,1)S(1)} %shard_map.107.chain.chain_2), channel_id=1, source_target_pairs={{16,8},{17,9},{18,10},{19,11},{20,12},{21,13},{22,14},{23,15}} | collective-permute-start | bytes 491528 | tf_op jit(solution)/shard_map/ppermute | solution.py:305
  22.0 0.7 collective-permute-start.15
  22.7 0.7 collective-permute-start.13
  23.4 0.0 collective-permute-done.10.w_mirror
  23.4 1.6 %collective-permute-start.1 = (bf16[320,256]{1,0:T(8,128)(2,1)S(1)}, bf16[320,256]{1,0:T(8,128)(2,1)S(1)}, u32[]{:S(2)}, u32[]{:S(2)}) collective-permute-start(bf16[320,256]{1,0:T(8,128)(2,1)S(1)} %get-tuple-element.47.refs_0_), channel_id=1, source_target_pairs={{0,2},{1,3},{2,0},{3,1},{4,6},{5,7},{6,4},{7,5},{8,10},{9,11},{10,... | collective-permute-start | bytes 491528 | tf_op jit(solution)/shard_map/ppermute | solution.py:313
  25.0 0.2 shard_map.109.back_2
  25.2 0.0 collective-permute-done.11.skip_far
  25.3 2.5 %collective-permute-start.2 = (bf16[320,256]{1,0:T(8,128)(2,1)S(1)}, bf16[320,256]{1,0:T(8,128)(2,1)S(1)}, u32[]{:S(2)}, u32[]{:S(2)}) collective-permute-start(bf16[320,256]{1,0:T(8,128)(2,1)S(1)} %get-tuple-element.47.refs_0_), channel_id=1, source_target_pairs={{0,6},{1,7},{2,4},{3,5},{4,2},{5,3},{6,0},{7,1},{8,14},{9,15},{10,... | collective-permute-start | bytes 491528 | tf_op jit(solution)/shard_map/ppermute | solution.py:313
  27.8 0.0 collective-permute-done.9.received
  27.9 0.7 collective-permute-start.12
  28.5 0.0 collective-permute-done.15.top
  28.5 0.2 collective-permute-start.6
  28.8 0.0 collective-permute-done.13.skip_far
  28.8 0.0 collective-permute-start.3
  28.8 1.8 %collective-permute-done.1.refs_1_ = bf16[320,256]{1,0:T(8,128)(2,1)S(1)} collective-permute-done((bf16[320,256]{1,0:T(8,128)(2,1)S(1)}, bf16[320,256]{1,0:T(8,128)(2,1)S(1)}, u32[]{:S(2)}, u32[]{:S(2)}) %collective-permute-start.1) | collective-permute-done | bytes 163872 | tf_op jit(solution)/shard_map/ppermute | solution.py:313
  30.6 0.0 collective-permute-start.4
  30.6 4.1 %collective-permute-done.2.refs_2_ = bf16[320,256]{1,0:T(8,128)(2,1)S(1)} collective-permute-done((bf16[320,256]{1,0:T(8,128)(2,1)S(1)}, bf16[320,256]{1,0:T(8,128)(2,1)S(1)}, u32[]{:S(2)}, u32[]{:S(2)}) %collective-permute-start.2) | collective-permute-done | bytes 163872 | tf_op jit(solution)/shard_map/ppermute | solution.py:313
  34.7 8.9 %collective-permute-start.16 = (bf16[320,256]{1,0:T(8,128)(2,1)S(1)}, bf16[320,256]{1,0:T(8,128)(2,1)S(1)}, u32[]{:S(2)}, u32[]{:S(2)}) collective-permute-start(bf16[320,256]{1,0:T(8,128)(2,1)S(1)} %get-tuple-element.55), channel_id=1, source_target_pairs={{8,6},{9,7},{10,4},{11,5},{12,2},{13,3},{14,0},{15,1},{16,14},{17,... | collective-permute-start | bytes 491528 | tf_op jit(solution)/shard_map/ppermute | solution.py:322
  43.6 0.0 collective-permute-done.12.received
  43.6 0.1 collective-permute-start.5
  43.7 0.1 shard_map.111.refs_6_.grad_low
  43.7 0.0 collective-permute-done.6.refs_6_.normed_0
  43.7 8.5 %collective-permute-start.14 = (bf16[320,256]{1,0:T(8,128)(2,1)S(1)}, bf16[320,256]{1,0:T(8,128)(2,1)S(1)}, u32[]{:S(2)}, u32[]{:S(2)}) collective-permute-start(bf16[320,256]{1,0:T(8,128)(2,1)S(1)} %shard_map.111.refs_6_.grad_low), channel_id=1, source_target_pairs={{0,2},{1,3},{2,0},{3,1},{4,6},{5,7},{6,4},{7,5},{8,10},{9,11},{10,... | collective-permute-start | bytes 491528 | tf_op jit(solution)/shard_map/ppermute | solution.py:313
  52.2 0.0 collective-permute-done.3.refs_3_
  52.2 0.0 collective-permute-start.20
  52.2 0.3 shard_map.114
  52.5 0.0 collective-permute-done.4.refs_4_
  52.5 0.3 collective-permute-start.22
  52.8 0.0 collective-permute-done.16.following
  52.8 0.3 collective-permute-start.7
  53.1 0.0 collective-permute-done.5.refs_5_
  53.2 0.3 collective-permute-start.19
  53.4 0.5 collective-permute-done.22.given
  53.9 0.2 collective-permute-start.17
  54.1 5.2 %collective-permute-done.14.refs_7_ = bf16[320,256]{1,0:T(8,128)(2,1)S(1)} collective-permute-done((bf16[320,256]{1,0:T(8,128)(2,1)S(1)}, bf16[320,256]{1,0:T(8,128)(2,1)S(1)}, u32[]{:S(2)}, u32[]{:S(2)}) %collective-permute-start.14) | collective-permute-done | bytes 163872 | tf_op jit(solution)/shard_map/ppermute | solution.py:313
  59.3 0.0 collective-permute-start.18
  59.3 3.7 %collective-permute-done.20.low_0 = bf16[320,256]{1,0:T(8,128)(2,1)S(1)} collective-permute-done((bf16[320,256]{1,0:T(8,128)(2,1)S(1)}, bf16[320,256]{1,0:T(8,128)(2,1)S(1)}, u32[]{:S(2)}, u32[]{:S(2)}) %collective-permute-start.20) | collective-permute-done | bytes 163872 | tf_op jit(solution)/shard_map/ppermute | solution.py:313
  63.0 0.0 collective-permute-start.21
  63.0 0.0 collective-permute-done.7.refs_7_.normed_1
  63.0 0.1 collective-permute-start.23
  63.1 0.0 collective-permute-done.19.refs_11_
  63.1 2.2 %collective-permute-start.24 = (bf16[40,320]{1,0:T(8,128)(2,1)S(1)}, bf16[40,320]{1,0:T(8,128)(2,1)S(1)}, u32[]{:S(2)}, u32[]{:S(2)}) collective-permute-start(bf16[40,320]{1,0:T(8,128)(2,1)S(1)} %get-tuple-element.63), channel_id=1, source_target_pairs={{0,4},{1,5},{2,6},{3,7},{4,0},{5,1},{6,2},{7,3},{8,12},{9,13},{10,... | collective-permute-start | bytes 76808 | tf_op jit(solution)/shard_map/ppermute | solution.py:313
  65.4 0.0 collective-permute-done.17.refs_9_
  65.4 2.1 %collective-permute-start.25 = (bf16[40,320]{1,0:T(8,128)(2,1)S(1)}, bf16[40,320]{1,0:T(8,128)(2,1)S(1)}, u32[]{:S(2)}, u32[]{:S(2)}) collective-permute-start(bf16[40,320]{1,0:T(8,128)(2,1)S(1)} %get-tuple-element.64), channel_id=1, source_target_pairs={{0,6},{1,7},{2,4},{3,5},{4,2},{5,3},{6,0},{7,1},{8,14},{9,15},{10,... | collective-permute-start | bytes 76808 | tf_op jit(solution)/shard_map/ppermute | solution.py:313
  67.5 0.1 shard_map.103
  67.6 0.8 %shard_map.106 = (bf16[160,2048]{1,0:T(8,128)(2,1)S(1)}, f32[160,2048]{1,0:T(8,128)S(1)}) custom-call(bf16[320,160]{1,0:T(8,128)(2,1)S(1)} %get-tuple-element.40.own_in, bf16[320,256]{1,0:T(8,128)(2,1)S(1)} %get-tuple-element.47.refs_0_, bf16[320,256]{1,0:T(8,128)(2,1)S(1)} %collective-permute-done.1.refs_1_, ...), custom_call_target="tpu_custom_call" | custom-call | tf_op jit(solution)/shard_map/pallas_call | solution.py:35
  68.4 0.0 collective-permute-done.18.refs_10_
  68.4 1.1 %shard_map.113 = (f32[160,320]{1,0:T(8,128)S(1)}, f32[160,320]{1,0:T(8,128)S(1)}) custom-call(bf16[320,160]{1,0:T(8,128)(2,1)S(1)} %get-tuple-element.39.own_out, bf16[160,2048]{1,0:T(8,128)(2,1)S(1)} %get-tuple-element.48.active, f32[160,2048]{1,0:T(8,128)S(1)} %get-tuple-element.49.slope, bf16[320,256]{1,0:T(8,128)(2,1)S(1)} %get-tuple-element.47.refs_0_, ...), custom_call_target="tpu_custom_call" | custom-call | tf_op jit(solution)/shard_map/pallas_call | solution.py:35
  69.6 0.0 collective-permute-done.23.piece_1
  69.6 0.0 collective-permute-done.24.piece_2
  69.6 1.5 %collective-permute-done.25.piece_3 = bf16[40,320]{1,0:T(8,128)(2,1)S(1)} collective-permute-done((bf16[40,320]{1,0:T(8,128)(2,1)S(1)}, bf16[40,320]{1,0:T(8,128)(2,1)S(1)}, u32[]{:S(2)}, u32[]{:S(2)}) %collective-permute-start.25) | collective-permute-done | bytes 25632 | tf_op jit(solution)/shard_map/ppermute | solution.py:313
  71.1 0.0 collective-permute-done.21.low_1
  71.1 1.3 %shard_map.116 = (f32[160,320]{1,0:T(8,128)}, f32[160,320]{1,0:T(8,128)}, f32[1,12800]{1,0:T(1,128)}, bf16[2,320,128]{2,1,0:T(8,128)(2,1)}) custom-call(bf16[320,160]{1,0:T(8,128)(2,1)S(1)} %get-tuple-element.39.own_out, bf16[160,2048]{1,0:T(8,128)(2,1)S(1)} %get-tuple-element.48.active, f32[160,2048]{1,0:T(8,128)S(1)} %get-tuple-element.49.slope, ...), custom_call_target="tpu_custom_call" | custom-call | tf_op jit(solution)/shard_map/pallas_call | solution.py:35
  (5 shorter events, 0.1 us)
Async XLA Ops:
  0.6 3.1 %copy-start = (bf16[2,128,320]{1,2,0:T(8,128)(2,1)S(1)}, bf16[2,128,320]{1,2,0:T(8,128)(2,1)}, u32[]{:S(2)}) copy-start(bf16[2,128,320]{1,2,0:T(8,128)(2,1)} %param.13) | copy-start | bytes 491524
  2.5 8.7 %collective-permute-start = (bf16[320,256]{1,0:T(8,128)(2,1)S(1)}, bf16[320,256]{1,0:T(8,128)(2,1)S(1)}, u32[]{:S(2)}, u32[]{:S(2)}) collective-permute-start(bf16[320,256]{1,0:T(8,128)(2,1)S(1)} %get-tuple-element.41), channel_id=1, source_target_pairs={{0,24},{8,16},{1,25},{9,17},{2,26},{10,18},{3,27},{11,19},{4,28},{... | collective-permute-start | bytes 491528 | tf_op jit(solution)/shard_map/ppermute | solution.py:305
  12.3 7.2 %collective-permute-start.8 = (bf16[320,256]{1,0:T(8,128)(2,1)S(1)}, bf16[320,256]{1,0:T(8,128)(2,1)S(1)}, u32[]{:S(2)}, u32[]{:S(2)}) collective-permute-start(bf16[320,256]{1,0:T(8,128)(2,1)S(1)} %get-tuple-element.50.chain.chain_3), channel_id=1, source_target_pairs={{24,16},{25,17},{26,18},{27,19},{28,20},{29,21},{30,22},{31,23}} | collective-permute-start | bytes 491528 | tf_op jit(solution)/shard_map/ppermute | solution.py:305
  13.6 9.8 %collective-permute-start.10 = (bf16[320,320]{1,0:T(8,128)(2,1)S(1)}, bf16[320,320]{1,0:T(8,128)(2,1)S(1)}, u32[]{:S(2)}, u32[]{:S(2)}) collective-permute-start(bf16[320,320]{1,0:T(8,128)(2,1)S(1)} %get-tuple-element.46.w_skip), channel_id=1, source_target_pairs={{16,8},{17,9},{18,10},{19,11},{20,12},{21,13},{22,14},{23,15}} | collective-permute-start | bytes 614408 | tf_op jit(solution)/shard_map/ppermute | solution.py:305
  14.9 10.3 %collective-permute-start.11 = (bf16[320,256]{1,0:T(8,128)(2,1)S(1)}, bf16[320,256]{1,0:T(8,128)(2,1)S(1)}, u32[]{:S(2)}, u32[]{:S(2)}) collective-permute-start(bf16[320,256]{1,0:T(8,128)(2,1)S(1)} %shard_map.108), channel_id=1, source_target_pairs={{24,8},{25,9},{26,10},{27,11},{28,12},{29,13},{30,14},{31,15}} | collective-permute-start | bytes 491528 | tf_op jit(solution)/shard_map/ppermute | solution.py:305
  20.7 7.1 %collective-permute-start.9 = (bf16[320,256]{1,0:T(8,128)(2,1)S(1)}, bf16[320,256]{1,0:T(8,128)(2,1)S(1)}, u32[]{:S(2)}, u32[]{:S(2)}) collective-permute-start(bf16[320,256]{1,0:T(8,128)(2,1)S(1)} %shard_map.107.chain.chain_2), channel_id=1, source_target_pairs={{16,8},{17,9},{18,10},{19,11},{20,12},{21,13},{22,14},{23,15}} | collective-permute-start | bytes 491528 | tf_op jit(solution)/shard_map/ppermute | solution.py:305
  22.0 6.5 %collective-permute-start.15 = (bf16[320,256]{1,0:T(8,128)(2,1)S(1)}, bf16[320,256]{1,0:T(8,128)(2,1)S(1)}, u32[]{:S(2)}, u32[]{:S(2)}) collective-permute-start(bf16[320,256]{1,0:T(8,128)(2,1)S(1)} %get-tuple-element.44.top_low), channel_id=1, source_target_pairs={{24,30},{25,31},{26,28},{27,29},{28,26},{29,27},{30,24},{31,25}} | collective-permute-start | bytes 491528 | tf_op jit(solution)/shard_map/ppermute | solution.py:327
  22.7 6.1 %collective-permute-start.13 = (bf16[320,256]{1,0:T(8,128)(2,1)S(1)}, bf16[320,256]{1,0:T(8,128)(2,1)S(1)}, u32[]{:S(2)}, u32[]{:S(2)}) collective-permute-start(bf16[320,256]{1,0:T(8,128)(2,1)S(1)} %shard_map.108), channel_id=1, source_target_pairs={{24,0},{25,1},{26,2},{27,3},{28,4},{29,5},{30,6},{31,7}} | collective-permute-start | bytes 491528 | tf_op jit(solution)/shard_map/ppermute | solution.py:305
  23.4 7.2 %collective-permute-start.1 = (bf16[320,256]{1,0:T(8,128)(2,1)S(1)}, bf16[320,256]{1,0:T(8,128)(2,1)S(1)}, u32[]{:S(2)}, u32[]{:S(2)}) collective-permute-start(bf16[320,256]{1,0:T(8,128)(2,1)S(1)} %get-tuple-element.47.refs_0_), channel_id=1, source_target_pairs={{0,2},{1,3},{2,0},{3,1},{4,6},{5,7},{6,4},{7,5},{8,10},{9,11},{10,... | collective-permute-start | bytes 491528 | tf_op jit(solution)/shard_map/ppermute | solution.py:313
  25.3 9.4 %collective-permute-start.2 = (bf16[320,256]{1,0:T(8,128)(2,1)S(1)}, bf16[320,256]{1,0:T(8,128)(2,1)S(1)}, u32[]{:S(2)}, u32[]{:S(2)}) collective-permute-start(bf16[320,256]{1,0:T(8,128)(2,1)S(1)} %get-tuple-element.47.refs_0_), channel_id=1, source_target_pairs={{0,6},{1,7},{2,4},{3,5},{4,2},{5,3},{6,0},{7,1},{8,14},{9,15},{10,... | collective-permute-start | bytes 491528 | tf_op jit(solution)/shard_map/ppermute | solution.py:313
  27.9 15.7 %collective-permute-start.12 = (bf16[320,256]{1,0:T(8,128)(2,1)S(1)}, bf16[320,256]{1,0:T(8,128)(2,1)S(1)}, u32[]{:S(2)}, u32[]{:S(2)}) collective-permute-start(bf16[320,256]{1,0:T(8,128)(2,1)S(1)} %get-tuple-element.53.chain_1), channel_id=1, source_target_pairs={{8,0},{9,1},{10,2},{11,3},{12,4},{13,5},{14,6},{15,7}} | collective-permute-start | bytes 491528 | tf_op jit(solution)/shard_map/ppermute | solution.py:305
  28.5 15.2 %collective-permute-start.6 = (bf16[320,256]{1,0:T(8,128)(2,1)S(1)}, bf16[320,256]{1,0:T(8,128)(2,1)S(1)}, u32[]{:S(2)}, u32[]{:S(2)}) collective-permute-start(bf16[320,256]{1,0:T(8,128)(2,1)S(1)} %get-tuple-element.47.refs_0_), channel_id=1, source_target_pairs={{0,4},{1,5},{2,6},{3,7},{4,0},{5,1},{6,2},{7,3},{8,12},{9,13},{10,... | collective-permute-start | bytes 491528 | tf_op jit(solution)/shard_map/ppermute | solution.py:313
  28.8 23.5 %collective-permute-start.3 = (bf16[320,256]{1,0:T(8,128)(2,1)S(1)}, bf16[320,256]{1,0:T(8,128)(2,1)S(1)}, u32[]{:S(2)}, u32[]{:S(2)}) collective-permute-start(bf16[320,256]{1,0:T(8,128)(2,1)S(1)} %get-tuple-element.47.refs_0_), channel_id=1, source_target_pairs={{0,1},{1,0},{2,3},{3,2},{4,5},{5,4},{6,7},{7,6},{8,9},{9,8},{10,11... | collective-permute-start | bytes 491528 | tf_op jit(solution)/shard_map/ppermute | solution.py:313
  30.6 21.9 %collective-permute-start.4 = (bf16[320,256]{1,0:T(8,128)(2,1)S(1)}, bf16[320,256]{1,0:T(8,128)(2,1)S(1)}, u32[]{:S(2)}, u32[]{:S(2)}) collective-permute-start(bf16[320,256]{1,0:T(8,128)(2,1)S(1)} %collective-permute-done.1.refs_1_), channel_id=1, source_target_pairs={{0,1},{1,0},{2,3},{3,2},{4,5},{5,4},{6,7},{7,6},{8,9},{9,8},{10,11... | collective-permute-start | bytes 491528 | tf_op jit(solution)/shard_map/ppermute | solution.py:313
  34.7 18.1 %collective-permute-start.16 = (bf16[320,256]{1,0:T(8,128)(2,1)S(1)}, bf16[320,256]{1,0:T(8,128)(2,1)S(1)}, u32[]{:S(2)}, u32[]{:S(2)}) collective-permute-start(bf16[320,256]{1,0:T(8,128)(2,1)S(1)} %get-tuple-element.55), channel_id=1, source_target_pairs={{8,6},{9,7},{10,4},{11,5},{12,2},{13,3},{14,0},{15,1},{16,14},{17,... | collective-permute-start | bytes 491528 | tf_op jit(solution)/shard_map/ppermute | solution.py:322
  43.6 9.6 %collective-permute-start.5 = (bf16[320,256]{1,0:T(8,128)(2,1)S(1)}, bf16[320,256]{1,0:T(8,128)(2,1)S(1)}, u32[]{:S(2)}, u32[]{:S(2)}) collective-permute-start(bf16[320,256]{1,0:T(8,128)(2,1)S(1)} %collective-permute-done.2.refs_2_), channel_id=1, source_target_pairs={{0,1},{1,0},{2,3},{3,2},{4,5},{5,4},{6,7},{7,6},{8,9},{9,8},{10,11... | collective-permute-start | bytes 491528 | tf_op jit(solution)/shard_map/ppermute | solution.py:313
  43.7 15.6 %collective-permute-start.14 = (bf16[320,256]{1,0:T(8,128)(2,1)S(1)}, bf16[320,256]{1,0:T(8,128)(2,1)S(1)}, u32[]{:S(2)}, u32[]{:S(2)}) collective-permute-start(bf16[320,256]{1,0:T(8,128)(2,1)S(1)} %shard_map.111.refs_6_.grad_low), channel_id=1, source_target_pairs={{0,2},{1,3},{2,0},{3,1},{4,6},{5,7},{6,4},{7,5},{8,10},{9,11},{10,... | collective-permute-start | bytes 491528 | tf_op jit(solution)/shard_map/ppermute | solution.py:313
  52.2 10.8 %collective-permute-start.20 = (bf16[320,256]{1,0:T(8,128)(2,1)S(1)}, bf16[320,256]{1,0:T(8,128)(2,1)S(1)}, u32[]{:S(2)}, u32[]{:S(2)}) collective-permute-start(bf16[320,256]{1,0:T(8,128)(2,1)S(1)} %shard_map.111.refs_6_.grad_low), channel_id=1, source_target_pairs={{0,4},{1,5},{2,6},{3,7},{4,0},{5,1},{6,2},{7,3},{8,12},{9,13},{10,... | collective-permute-start | bytes 491528 | tf_op jit(solution)/shard_map/ppermute | solution.py:313
  52.5 1.4 %collective-permute-start.22 = (bf16[4,40,320]{2,1,0:T(8,128)(2,1)S(1)}, bf16[4,40,320]{2,1,0:T(8,128)(2,1)S(1)}, u32[]{:S(2)}, u32[]{:S(2)}) collective-permute-start(bf16[4,40,320]{2,1,0:T(8,128)(2,1)S(1)} %get-tuple-element.60), channel_id=1, source_target_pairs={{0,1},{1,0},{2,3},{3,2},{4,5},{5,4},{6,7},{7,6},{8,9},{9,8},{10,11... | collective-permute-start | bytes 307208 | tf_op jit(solution)/shard_map/ppermute | solution.py:313
  52.8 10.2 %collective-permute-start.7 = (bf16[320,256]{1,0:T(8,128)(2,1)S(1)}, bf16[320,256]{1,0:T(8,128)(2,1)S(1)}, u32[]{:S(2)}, u32[]{:S(2)}) collective-permute-start(bf16[320,256]{1,0:T(8,128)(2,1)S(1)} %collective-permute-done.6.refs_6_.normed_0), channel_id=1, source_target_pairs={{0,1},{1,0},{2,3},{3,2},{4,5},{5,4},{6,7},{7,6},{8,9},{9,8},{10,11... | collective-permute-start | bytes 491528 | tf_op jit(solution)/shard_map/ppermute | solution.py:313
  53.2 10.0 %collective-permute-start.19 = (bf16[320,256]{1,0:T(8,128)(2,1)S(1)}, bf16[320,256]{1,0:T(8,128)(2,1)S(1)}, u32[]{:S(2)}, u32[]{:S(2)}) collective-permute-start(bf16[320,256]{1,0:T(8,128)(2,1)S(1)} %shard_map.112.refs_8_), channel_id=1, source_target_pairs={{0,1},{1,0},{2,3},{3,2},{4,5},{5,4},{6,7},{7,6},{8,9},{9,8},{10,11... | collective-permute-start | bytes 491528 | tf_op jit(solution)/shard_map/ppermute | solution.py:313
  53.9 11.4 %collective-permute-start.17 = (bf16[320,256]{1,0:T(8,128)(2,1)S(1)}, bf16[320,256]{1,0:T(8,128)(2,1)S(1)}, u32[]{:S(2)}, u32[]{:S(2)}) collective-permute-start(bf16[320,256]{1,0:T(8,128)(2,1)S(1)} %shard_map.111.refs_6_.grad_low), channel_id=1, source_target_pairs={{0,1},{1,0},{2,3},{3,2},{4,5},{5,4},{6,7},{7,6},{8,9},{9,8},{10,11... | collective-permute-start | bytes 491528 | tf_op jit(solution)/shard_map/ppermute | solution.py:313
  59.3 9.1 %collective-permute-start.18 = (bf16[320,256]{1,0:T(8,128)(2,1)S(1)}, bf16[320,256]{1,0:T(8,128)(2,1)S(1)}, u32[]{:S(2)}, u32[]{:S(2)}) collective-permute-start(bf16[320,256]{1,0:T(8,128)(2,1)S(1)} %collective-permute-done.14.refs_7_), channel_id=1, source_target_pairs={{0,1},{1,0},{2,3},{3,2},{4,5},{5,4},{6,7},{7,6},{8,9},{9,8},{10,11... | collective-permute-start | bytes 491528 | tf_op jit(solution)/shard_map/ppermute | solution.py:313
  63.0 8.1 %collective-permute-start.21 = (bf16[320,256]{1,0:T(8,128)(2,1)S(1)}, bf16[320,256]{1,0:T(8,128)(2,1)S(1)}, u32[]{:S(2)}, u32[]{:S(2)}) collective-permute-start(bf16[320,256]{1,0:T(8,128)(2,1)S(1)} %collective-permute-done.20.low_0), channel_id=1, source_target_pairs={{0,1},{1,0},{2,3},{3,2},{4,5},{5,4},{6,7},{7,6},{8,9},{9,8},{10,11... | collective-permute-start | bytes 491528 | tf_op jit(solution)/shard_map/ppermute | solution.py:313
  63.0 6.5 %collective-permute-start.23 = (bf16[40,320]{1,0:T(8,128)(2,1)S(1)}, bf16[40,320]{1,0:T(8,128)(2,1)S(1)}, u32[]{:S(2)}, u32[]{:S(2)}) collective-permute-start(bf16[40,320]{1,0:T(8,128)(2,1)S(1)} %get-tuple-element.62), channel_id=1, source_target_pairs={{0,2},{1,3},{2,0},{3,1},{4,6},{5,7},{6,4},{7,5},{8,10},{9,11},{10,... | collective-permute-start | bytes 76808 | tf_op jit(solution)/shard_map/ppermute | solution.py:313
  63.1 6.5 %collective-permute-start.24 = (bf16[40,320]{1,0:T(8,128)(2,1)S(1)}, bf16[40,320]{1,0:T(8,128)(2,1)S(1)}, u32[]{:S(2)}, u32[]{:S(2)}) collective-permute-start(bf16[40,320]{1,0:T(8,128)(2,1)S(1)} %get-tuple-element.63), channel_id=1, source_target_pairs={{0,4},{1,5},{2,6},{3,7},{4,0},{5,1},{6,2},{7,3},{8,12},{9,13},{10,... | collective-permute-start | bytes 76808 | tf_op jit(solution)/shard_map/ppermute | solution.py:313
  65.4 5.7 %collective-permute-start.25 = (bf16[40,320]{1,0:T(8,128)(2,1)S(1)}, bf16[40,320]{1,0:T(8,128)(2,1)S(1)}, u32[]{:S(2)}, u32[]{:S(2)}) collective-permute-start(bf16[40,320]{1,0:T(8,128)(2,1)S(1)} %get-tuple-element.64), channel_id=1, source_target_pairs={{0,6},{1,7},{2,4},{3,5},{4,2},{5,3},{6,0},{7,1},{8,14},{9,15},{10,... | collective-permute-start | bytes 76808 | tf_op jit(solution)/shard_map/ppermute | solution.py:313

commit v8 on v7

--- a/solution.py
+++ b/solution.py
@@ -184,8 +184,13 @@
     grad_low_out[...] = jnp.where(section == 3, top_low[...], own)
 
 
-def merge_body(top, following, out):
-    out[...] = jnp.where(lax.axis_index("section") == 3, top[...], following[...])
+def merge_body(late, middle, top, out):
+    section = lax.axis_index("section")
+    out[...] = jnp.where(section == 0, late[...], jnp.where(section == 3, top[...], middle[...]))
+
+
+def own_body(low_1, low_2, out):
+    out[...] = jnp.where(lax.axis_index("section") == 1, low_1[...], low_2[...])
 
 
 def last_body(
@@ -322,8 +327,12 @@
     return lax.ppermute(value, ("section", "dp"), pairs)
 
 
-def in_last(value, count, mask):
-    pairs = [(3 * count + i, 3 * count + (i ^ mask)) for i in range(count)]
+def within(value, sections, count, mask):
+    pairs = [
+        (section * count + i, section * count + (i ^ mask))
+        for section in sections
+        for i in range(count)
+    ]
     return lax.ppermute(value, ("section", "dp"), pairs)
 
 
@@ -391,10 +400,16 @@
         slice_forward_body,
         [((part, count * rows), LOW), ((part, count * rows), F32)], own_in, *normed_all,
     )
-    top_6 = in_last(top_low, count, 6)
+    tops = {mask: within(top_low, [3], count, mask) for mask in (2, 4, 6)}
+    (own_low,) = call(own_body, [low], low_1, low_2)
     next_6 = from_next(ahead, count, 6)
-    (low_6,) = call(merge_body, [low], top_6, next_6)
-    low_2, low_4 = (exchange(grad_low, count, m) for m in (2, 4))
+    middle = {mask: within(own_low, [1, 2], count, mask) for mask in (2, 4)}
+    late = {mask: within(grad_low, [0], count, mask) for mask in (2, 4)}
+    late[6] = middle[6] = next_6
+    low_2, low_4, low_6 = (
+        call(merge_body, [low], late[mask], middle[mask], tops[mask])[0]
+        for mask in (2, 4, 6)
+    )
     low_near = [grad_low, low_2, low_6, low_4]
     low_all = in_turn(low_near, [exchange(x, count, 1) for x in low_near])
     block = (count // 2, width // count, width)

time: 72.7 us -> 75.9 us (1.044)
  the two profiles are of different devices: /device:TPU:4 before, /device:TPU:0 now
where the time goes in v8:
time: 75.9 us; the launch traced here: 75.6 us
  starting transfers between devices  36 us (47%)
  waiting for transfers between devices  28.9 us (38%)
  Pallas kernels  9.62 us (13%)
  between operations  1.03 us (1%)
    ppermute x7, waiting for transfers between devices, hop(): return lax.ppermute(value, 'section', pairs)  23.7 us
    ppermute x15, starting transfers between devices, exchange(): return lax.ppermute(value, 'dp', [(i, i ^ mask) for i in range(count)])  13 us
    ppermute x7, starting transfers between devices, within(): return lax.ppermute(value, ('section', 'dp'), pairs)  12.2 us
    pallas_call x18, Pallas kernels, call(): pl.pallas_call(body, out_shape=[jax.ShapeDtypeStruct(shape, kind) for sha...  9.62 us
    ppermute x7, starting transfers between devices, hop(): return lax.ppermute(value, 'section', pairs)  9.47 us
    ppermute x7, waiting for transfers between devices, within(): return lax.ppermute(value, ('section', 'dp'), pairs)  2.23 us
    ppermute x1, waiting for transfers between devices, from_next(): return lax.ppermute(value, ('section', 'dp'), pairs)  1.63 us
  transfers between devices with their start and end apart: 30, of which 7 were waited for; matrix products, arithmetic and copies ran while one was open for 0% of the time, Pallas kernels for 5%

profile of v8, /device:TPU:0, one launch (start us, length us, event | category | flops | bytes accessed | tf_op | source)
XLA Modules:
  0.0 75.6 jit_solution(11210064044179045993)
XLA Ops:
  0.6 3.4 %shard_map.102 = (bf16[320,256]{1,0:T(8,128)(2,1)S(1)}, bf16[320,256]{1,0:T(8,128)(2,1)S(1)}, bf16[320,320]{1,0:T(8,128)(2,1)S(1)}, bf16[2,320,128]{2,1,0:T(8,12...) custom-call(s32[2,128]{1,0:T(2,128)} %refs_0_.1, bf16[320,1000]{1,0:T(8,128)(2,1)} %bitcast.20, ...), custom_call_target="tpu_custom_call" | custom-call | tf_op jit(solution)/shard_map/pallas_call | solution.py:35
  4.1 4.2 %collective-permute-start = (bf16[320,256]{1,0:T(8,128)(2,1)S(1)}, bf16[320,256]{1,0:T(8,128)(2,1)S(1)}, u32[]{:S(2)}, u32[]{:S(2)}) collective-permute-start(bf16[320,256]{1,0:T(8,128)(2,1)S(1)} %get-tuple-element.41), channel_id=1, source_target_pairs={{0,24},{8,16},{1,25},{9,17},{2,26},{10,18},{3,27},{11,19},{4,28},{... | collective-permute-start | bytes 491528 | tf_op jit(solution)/shard_map/ppermute | solution.py:310
  8.4 3.4 %collective-permute-done.received = bf16[320,256]{1,0:T(8,128)(2,1)S(1)} collective-permute-done((bf16[320,256]{1,0:T(8,128)(2,1)S(1)}, bf16[320,256]{1,0:T(8,128)(2,1)S(1)}, u32[]{:S(2)}, u32[]{:S(2)}) %collective-permute-start) | collective-permute-done | bytes 163872 | tf_op jit(solution)/shard_map/ppermute | solution.py:310
  11.7 1.1 %shard_map.105 = (bf16[320,256]{1,0:T(8,128)(2,1)S(1)}, bf16[320,256]{1,0:T(8,128)(2,1)S(1)}, f32[320,256]{1,0:T(8,128)S(1)}, f32[1280,256]{1,0:T(8,128)S(1)}, bf16[320,256]{1,0:T(8,128)(2,1)S(1)}) custom-call(bf16[320,256]{1,0:T(8,128)(2,1)S(1)} %collective-permute-done.received, bf16[320,256]{1,0:T(8,128)(2,1)S(1)} %get-tuple-element.42.embed, ...), custom_call_target="tpu_custom_call" | custom-call | tf_op jit(solution)/shard_map/pallas_call | solution.py:35
  12.8 0.7 collective-permute-start.8
  13.5 0.7 collective-permute-start.10
  14.2 0.7 collective-permute-start.24
  14.9 0.7 collective-permute-start.18
  15.5 0.7 collective-permute-start.16
  16.2 0.0 collective-permute-done.8.received.low_2
  16.3 0.7 collective-permute-start.11
  17.0 0.0 collective-permute-done.24.top
  17.0 0.7 collective-permute-start.9
  17.6 0.0 collective-permute-done.18.top
  17.7 1.3 %collective-permute-start.13 = (bf16[320,256]{1,0:T(8,128)(2,1)S(1)}, bf16[320,256]{1,0:T(8,128)(2,1)S(1)}, u32[]{:S(2)}, u32[]{:S(2)}) collective-permute-start(bf16[320,256]{1,0:T(8,128)(2,1)S(1)} %shard_map.108), channel_id=1, source_target_pairs={{24,0},{25,1},{26,2},{27,3},{28,4},{29,5},{30,6},{31,7}} | collective-permute-start | bytes 491528 | tf_op jit(solution)/shard_map/ppermute | solution.py:310
  19.0 0.0 collective-permute-done.16.top
  19.0 1.6 %collective-permute-start.1 = (bf16[320,256]{1,0:T(8,128)(2,1)S(1)}, bf16[320,256]{1,0:T(8,128)(2,1)S(1)}, u32[]{:S(2)}, u32[]{:S(2)}) collective-permute-start(bf16[320,256]{1,0:T(8,128)(2,1)S(1)} %get-tuple-element.47.refs_0_), channel_id=1, source_target_pairs={{0,2},{1,3},{2,0},{3,1},{4,6},{5,7},{6,4},{7,5},{8,10},{9,11},{10,... | collective-permute-start | bytes 491528 | tf_op jit(solution)/shard_map/ppermute | solution.py:318
  20.6 0.0 collective-permute-done.10.w_mirror
  20.6 2.5 %collective-permute-start.2 = (bf16[320,256]{1,0:T(8,128)(2,1)S(1)}, bf16[320,256]{1,0:T(8,128)(2,1)S(1)}, u32[]{:S(2)}, u32[]{:S(2)}) collective-permute-start(bf16[320,256]{1,0:T(8,128)(2,1)S(1)} %get-tuple-element.47.refs_0_), channel_id=1, source_target_pairs={{0,6},{1,7},{2,4},{3,5},{4,2},{5,3},{6,0},{7,1},{8,14},{9,15},{10,... | collective-permute-start | bytes 491528 | tf_op jit(solution)/shard_map/ppermute | solution.py:318
  23.1 0.0 collective-permute-done.11.skip_far
  23.1 0.2 collective-permute-start.6
  23.3 0.0 collective-permute-done.9.received
  23.3 0.0 collective-permute-start.3
  23.3 17.0 %collective-permute-done.13.skip_far = bf16[320,256]{1,0:T(8,128)(2,1)S(1)} collective-permute-done((bf16[320,256]{1,0:T(8,128)(2,1)S(1)}, bf16[320,256]{1,0:T(8,128)(2,1)S(1)}, u32[]{:S(2)}, u32[]{:S(2)}) %collective-permute-start.13) | collective-permute-done | bytes 163872 | tf_op jit(solution)/shard_map/ppermute | solution.py:310
  40.3 1.3 %collective-permute-start.12 = (bf16[320,256]{1,0:T(8,128)(2,1)S(1)}, bf16[320,256]{1,0:T(8,128)(2,1)S(1)}, u32[]{:S(2)}, u32[]{:S(2)}) collective-permute-start(bf16[320,256]{1,0:T(8,128)(2,1)S(1)} %get-tuple-element.53.chain_1), channel_id=1, source_target_pairs={{8,0},{9,1},{10,2},{11,3},{12,4},{13,5},{14,6},{15,7}} | collective-permute-start | bytes 491528 | tf_op jit(solution)/shard_map/ppermute | solution.py:310
  41.6 0.0 collective-permute-done.1.refs_1_
  41.6 0.1 collective-permute-start.4
  41.7 0.0 collective-permute-done.2.refs_2_
  41.7 0.5 collective-permute-start.5
  42.2 0.0 collective-permute-done.6.refs_6_.normed_0
  42.2 0.7 collective-permute-start.23
  42.9 0.0 collective-permute-done.3.refs_3_
  42.9 1.3 %collective-permute-start.17 = (bf16[320,256]{1,0:T(8,128)(2,1)S(1)}, bf16[320,256]{1,0:T(8,128)(2,1)S(1)}, u32[]{:S(2)}, u32[]{:S(2)}) collective-permute-start(bf16[320,256]{1,0:T(8,128)(2,1)S(1)} %get-tuple-element.55), channel_id=1, source_target_pairs={{8,6},{9,7},{10,4},{11,5},{12,2},{13,3},{14,0},{15,1},{16,14},{17,... | collective-permute-start | bytes 491528 | tf_op jit(solution)/shard_map/ppermute | solution.py:327
  44.2 3.3 %collective-permute-done.12.received = bf16[320,256]{1,0:T(8,128)(2,1)S(1)} collective-permute-done((bf16[320,256]{1,0:T(8,128)(2,1)S(1)}, bf16[320,256]{1,0:T(8,128)(2,1)S(1)}, u32[]{:S(2)}, u32[]{:S(2)}) %collective-permute-start.12) | collective-permute-done | bytes 163872 | tf_op jit(solution)/shard_map/ppermute | solution.py:310
  47.5 0.7 collective-permute-start.15
  48.2 0.1 shard_map.111.refs_6_.grad_low
  48.3 0.0 collective-permute-done.4.refs_4_
  48.3 5.0 %collective-permute-start.14 = (bf16[320,256]{1,0:T(8,128)(2,1)S(1)}, bf16[320,256]{1,0:T(8,128)(2,1)S(1)}, u32[]{:S(2)}, u32[]{:S(2)}) collective-permute-start(bf16[320,256]{1,0:T(8,128)(2,1)S(1)} %shard_map.111.refs_6_.grad_low), channel_id=1, source_target_pairs={{0,2},{1,3},{2,0},{3,1},{4,6},{5,7},{6,4},{7,5}} | collective-permute-start | bytes 491528 | tf_op jit(solution)/shard_map/ppermute | solution.py:336
  53.3 0.0 collective-permute-done.5.refs_5_
  53.3 3.8 %collective-permute-start.22 = (bf16[320,256]{1,0:T(8,128)(2,1)S(1)}, bf16[320,256]{1,0:T(8,128)(2,1)S(1)}, u32[]{:S(2)}, u32[]{:S(2)}) collective-permute-start(bf16[320,256]{1,0:T(8,128)(2,1)S(1)} %shard_map.111.refs_6_.grad_low), channel_id=1, source_target_pairs={{0,4},{1,5},{2,6},{3,7},{4,0},{5,1},{6,2},{7,3}} | collective-permute-start | bytes 491528 | tf_op jit(solution)/shard_map/ppermute | solution.py:336
  57.1 1.5 %shard_map.117 = (bf16[320,256]{1,0:T(8,128)(2,1)S(1)}, f32[4,40,320]{2,1,0:T(8,128)S(1)}, bf16[4,40,320]{2,1,0:T(8,128)(2,1)S(1)}) custom-call(bf16[320,256]{1,0:T(8,128)(2,1)S(1)} %shard_map.111.refs_6_.grad_low, bf16[320,256]{1,0:T(8,128)(2,1)S(1)} %collective-permute-done.12.received, bf16[320,256]{1,0:T(8,128)(2,1)S(1)} %collective-permute-done.13.skip_far, ...), custom_call_target="tpu_custom_call" | custom-call | tf_op jit(solution)/shard_map/pallas_call | solution.py:35
  58.6 0.0 collective-permute-done.23.middle
  58.6 0.1 collective-permute-start.26
  58.7 1.6 %collective-permute-done.17.late.middle = bf16[320,256]{1,0:T(8,128)(2,1)S(1)} collective-permute-done((bf16[320,256]{1,0:T(8,128)(2,1)S(1)}, bf16[320,256]{1,0:T(8,128)(2,1)S(1)}, u32[]{:S(2)}, u32[]{:S(2)}) %collective-permute-start.17) | collective-permute-done | bytes 163872 | tf_op jit(solution)/shard_map/ppermute | solution.py:327
  60.3 0.0 collective-permute-start.7
  60.4 0.0 collective-permute-done.15.middle
  60.4 0.6 collective-permute-start.21
  60.9 0.0 collective-permute-done.14.late
  60.9 0.1 collective-permute-start.19
  61.1 2.2 %collective-permute-done.22.late = bf16[320,256]{1,0:T(8,128)(2,1)S(1)} collective-permute-done((bf16[320,256]{1,0:T(8,128)(2,1)S(1)}, bf16[320,256]{1,0:T(8,128)(2,1)S(1)}, u32[]{:S(2)}, u32[]{:S(2)}) %collective-permute-start.22) | collective-permute-done | bytes 163872 | tf_op jit(solution)/shard_map/ppermute | solution.py:336
  63.3 0.0 collective-permute-start.20
  63.3 0.0 collective-permute-done.26.given
  63.3 0.6 collective-permute-start.25
  63.9 0.0 collective-permute-done.7.refs_7_.normed_1
  63.9 4.4 %collective-permute-start.27 = (bf16[40,320]{1,0:T(8,128)(2,1)S(1)}, bf16[40,320]{1,0:T(8,128)(2,1)S(1)}, u32[]{:S(2)}, u32[]{:S(2)}) collective-permute-start(bf16[40,320]{1,0:T(8,128)(2,1)S(1)} %get-tuple-element.62), channel_id=1, source_target_pairs={{0,2},{1,3},{2,0},{3,1},{4,6},{5,7},{6,4},{7,5},{8,10},{9,11},{10,... | collective-permute-start | bytes 76808 | tf_op jit(solution)/shard_map/ppermute | solution.py:318
  68.4 0.0 collective-permute-done.21.refs_11_
  68.4 0.0 collective-permute-start.28
  68.4 2.5 %collective-permute-start.29 = (bf16[40,320]{1,0:T(8,128)(2,1)S(1)}, bf16[40,320]{1,0:T(8,128)(2,1)S(1)}, u32[]{:S(2)}, u32[]{:S(2)}) collective-permute-start(bf16[40,320]{1,0:T(8,128)(2,1)S(1)} %get-tuple-element.64), channel_id=1, source_target_pairs={{0,6},{1,7},{2,4},{3,5},{4,2},{5,3},{6,0},{7,1},{8,14},{9,15},{10,... | collective-permute-start | bytes 76808 | tf_op jit(solution)/shard_map/ppermute | solution.py:318
  70.8 0.1 shard_map.103
  70.9 0.8 %shard_map.106 = (bf16[160,2048]{1,0:T(8,128)(2,1)S(1)}, f32[160,2048]{1,0:T(8,128)S(1)}) custom-call(bf16[320,160]{1,0:T(8,128)(2,1)S(1)} %get-tuple-element.40.own_in, bf16[320,256]{1,0:T(8,128)(2,1)S(1)} %get-tuple-element.47.refs_0_, bf16[320,256]{1,0:T(8,128)(2,1)S(1)} %collective-permute-done.1.refs_1_, ...), custom_call_target="tpu_custom_call" | custom-call | tf_op jit(solution)/shard_map/pallas_call | solution.py:35
  71.7 1.1 %shard_map.115 = (f32[160,320]{1,0:T(8,128)S(1)}, f32[160,320]{1,0:T(8,128)S(1)}) custom-call(bf16[320,160]{1,0:T(8,128)(2,1)S(1)} %get-tuple-element.39.own_out, bf16[160,2048]{1,0:T(8,128)(2,1)S(1)} %get-tuple-element.48.active, f32[160,2048]{1,0:T(8,128)S(1)} %get-tuple-element.49.slope, bf16[320,256]{1,0:T(8,128)(2,1)S(1)} %get-tuple-element.47.refs_0_, ...), custom_call_target="tpu_custom_call" | custom-call | tf_op jit(solution)/shard_map/pallas_call | solution.py:35
  72.9 0.9 %collective-permute-done.28.piece_2 = bf16[40,320]{1,0:T(8,128)(2,1)S(1)} collective-permute-done((bf16[40,320]{1,0:T(8,128)(2,1)S(1)}, bf16[40,320]{1,0:T(8,128)(2,1)S(1)}, u32[]{:S(2)}, u32[]{:S(2)}) %collective-permute-start.28) | collective-permute-done | bytes 25632 | tf_op jit(solution)/shard_map/ppermute | solution.py:318
  73.8 0.4 collective-permute-done.29.piece_3
  74.2 1.3 %shard_map.119 = (f32[160,320]{1,0:T(8,128)}, f32[160,320]{1,0:T(8,128)}, f32[1,12800]{1,0:T(1,128)}, bf16[2,320,128]{2,1,0:T(8,128)(2,1)}) custom-call(bf16[320,160]{1,0:T(8,128)(2,1)S(1)} %get-tuple-element.39.own_out, bf16[160,2048]{1,0:T(8,128)(2,1)S(1)} %get-tuple-element.48.active, f32[160,2048]{1,0:T(8,128)S(1)} %get-tuple-element.49.slope, ...), custom_call_target="tpu_custom_call" | custom-call | tf_op jit(solution)/shard_map/pallas_call | solution.py:35
  (16 shorter events, 0.2 us)
Async XLA Ops:
  0.6 7.7 %copy-start = (bf16[2,128,320]{1,2,0:T(8,128)(2,1)S(1)}, bf16[2,128,320]{1,2,0:T(8,128)(2,1)}, u32[]{:S(2)}) copy-start(bf16[2,128,320]{1,2,0:T(8,128)(2,1)} %param.13) | copy-start | bytes 491524
  4.1 7.6 %collective-permute-start = (bf16[320,256]{1,0:T(8,128)(2,1)S(1)}, bf16[320,256]{1,0:T(8,128)(2,1)S(1)}, u32[]{:S(2)}, u32[]{:S(2)}) collective-permute-start(bf16[320,256]{1,0:T(8,128)(2,1)S(1)} %get-tuple-element.41), channel_id=1, source_target_pairs={{0,24},{8,16},{1,25},{9,17},{2,26},{10,18},{3,27},{11,19},{4,28},{... | collective-permute-start | bytes 491528 | tf_op jit(solution)/shard_map/ppermute | solution.py:310
  12.8 3.4 %collective-permute-start.8 = (bf16[320,256]{1,0:T(8,128)(2,1)S(1)}, bf16[320,256]{1,0:T(8,128)(2,1)S(1)}, u32[]{:S(2)}, u32[]{:S(2)}) collective-permute-start(bf16[320,256]{1,0:T(8,128)(2,1)S(1)} %get-tuple-element.50.chain.chain_3), channel_id=1, source_target_pairs={{24,16},{25,17},{26,18},{27,19},{28,20},{29,21},{30,22},{31,23}} | collective-permute-start | bytes 491528 | tf_op jit(solution)/shard_map/ppermute | solution.py:310
  13.5 7.1 %collective-permute-start.10 = (bf16[320,320]{1,0:T(8,128)(2,1)S(1)}, bf16[320,320]{1,0:T(8,128)(2,1)S(1)}, u32[]{:S(2)}, u32[]{:S(2)}) collective-permute-start(bf16[320,320]{1,0:T(8,128)(2,1)S(1)} %get-tuple-element.46.w_skip), channel_id=1, source_target_pairs={{16,8},{17,9},{18,10},{19,11},{20,12},{21,13},{22,14},{23,15}} | collective-permute-start | bytes 614408 | tf_op jit(solution)/shard_map/ppermute | solution.py:310
  14.2 2.8 %collective-permute-start.24 = (bf16[320,256]{1,0:T(8,128)(2,1)S(1)}, bf16[320,256]{1,0:T(8,128)(2,1)S(1)}, u32[]{:S(2)}, u32[]{:S(2)}) collective-permute-start(bf16[320,256]{1,0:T(8,128)(2,1)S(1)} %get-tuple-element.44.top_low), channel_id=1, source_target_pairs={{24,28},{25,29},{26,30},{27,31},{28,24},{29,25},{30,26},{31,27}} | collective-permute-start | bytes 491528 | tf_op jit(solution)/shard_map/ppermute | solution.py:336
  14.9 2.8 %collective-permute-start.18 = (bf16[320,256]{1,0:T(8,128)(2,1)S(1)}, bf16[320,256]{1,0:T(8,128)(2,1)S(1)}, u32[]{:S(2)}, u32[]{:S(2)}) collective-permute-start(bf16[320,256]{1,0:T(8,128)(2,1)S(1)} %get-tuple-element.44.top_low), channel_id=1, source_target_pairs={{24,30},{25,31},{26,28},{27,29},{28,26},{29,27},{30,24},{31,25}} | collective-permute-start | bytes 491528 | tf_op jit(solution)/shard_map/ppermute | solution.py:336
  15.5 3.4 %collective-permute-start.16 = (bf16[320,256]{1,0:T(8,128)(2,1)S(1)}, bf16[320,256]{1,0:T(8,128)(2,1)S(1)}, u32[]{:S(2)}, u32[]{:S(2)}) collective-permute-start(bf16[320,256]{1,0:T(8,128)(2,1)S(1)} %get-tuple-element.44.top_low), channel_id=1, source_target_pairs={{24,26},{25,27},{26,24},{27,25},{28,30},{29,31},{30,28},{31,29}} | collective-permute-start | bytes 491528 | tf_op jit(solution)/shard_map/ppermute | solution.py:336
  16.3 6.8 %collective-permute-start.11 = (bf16[320,256]{1,0:T(8,128)(2,1)S(1)}, bf16[320,256]{1,0:T(8,128)(2,1)S(1)}, u32[]{:S(2)}, u32[]{:S(2)}) collective-permute-start(bf16[320,256]{1,0:T(8,128)(2,1)S(1)} %shard_map.108), channel_id=1, source_target_pairs={{24,8},{25,9},{26,10},{27,11},{28,12},{29,13},{30,14},{31,15}} | collective-permute-start | bytes 491528 | tf_op jit(solution)/shard_map/ppermute | solution.py:310
  17.0 6.3 %collective-permute-start.9 = (bf16[320,256]{1,0:T(8,128)(2,1)S(1)}, bf16[320,256]{1,0:T(8,128)(2,1)S(1)}, u32[]{:S(2)}, u32[]{:S(2)}) collective-permute-start(bf16[320,256]{1,0:T(8,128)(2,1)S(1)} %shard_map.107.chain.chain_2), channel_id=1, source_target_pairs={{16,8},{17,9},{18,10},{19,11},{20,12},{21,13},{22,14},{23,15}} | collective-permute-start | bytes 491528 | tf_op jit(solution)/shard_map/ppermute | solution.py:310
  17.7 22.7 %collective-permute-start.13 = (bf16[320,256]{1,0:T(8,128)(2,1)S(1)}, bf16[320,256]{1,0:T(8,128)(2,1)S(1)}, u32[]{:S(2)}, u32[]{:S(2)}) collective-permute-start(bf16[320,256]{1,0:T(8,128)(2,1)S(1)} %shard_map.108), channel_id=1, source_target_pairs={{24,0},{25,1},{26,2},{27,3},{28,4},{29,5},{30,6},{31,7}} | collective-permute-start | bytes 491528 | tf_op jit(solution)/shard_map/ppermute | solution.py:310
  19.0 22.6 %collective-permute-start.1 = (bf16[320,256]{1,0:T(8,128)(2,1)S(1)}, bf16[320,256]{1,0:T(8,128)(2,1)S(1)}, u32[]{:S(2)}, u32[]{:S(2)}) collective-permute-start(bf16[320,256]{1,0:T(8,128)(2,1)S(1)} %get-tuple-element.47.refs_0_), channel_id=1, source_target_pairs={{0,2},{1,3},{2,0},{3,1},{4,6},{5,7},{6,4},{7,5},{8,10},{9,11},{10,... | collective-permute-start | bytes 491528 | tf_op jit(solution)/shard_map/ppermute | solution.py:318
  20.6 21.1 %collective-permute-start.2 = (bf16[320,256]{1,0:T(8,128)(2,1)S(1)}, bf16[320,256]{1,0:T(8,128)(2,1)S(1)}, u32[]{:S(2)}, u32[]{:S(2)}) collective-permute-start(bf16[320,256]{1,0:T(8,128)(2,1)S(1)} %get-tuple-element.47.refs_0_), channel_id=1, source_target_pairs={{0,6},{1,7},{2,4},{3,5},{4,2},{5,3},{6,0},{7,1},{8,14},{9,15},{10,... | collective-permute-start | bytes 491528 | tf_op jit(solution)/shard_map/ppermute | solution.py:318
  23.1 19.1 %collective-permute-start.6 = (bf16[320,256]{1,0:T(8,128)(2,1)S(1)}, bf16[320,256]{1,0:T(8,128)(2,1)S(1)}, u32[]{:S(2)}, u32[]{:S(2)}) collective-permute-start(bf16[320,256]{1,0:T(8,128)(2,1)S(1)} %get-tuple-element.47.refs_0_), channel_id=1, source_target_pairs={{0,4},{1,5},{2,6},{3,7},{4,0},{5,1},{6,2},{7,3},{8,12},{9,13},{10,... | collective-permute-start | bytes 491528 | tf_op jit(solution)/shard_map/ppermute | solution.py:318
  23.3 19.6 %collective-permute-start.3 = (bf16[320,256]{1,0:T(8,128)(2,1)S(1)}, bf16[320,256]{1,0:T(8,128)(2,1)S(1)}, u32[]{:S(2)}, u32[]{:S(2)}) collective-permute-start(bf16[320,256]{1,0:T(8,128)(2,1)S(1)} %get-tuple-element.47.refs_0_), channel_id=1, source_target_pairs={{0,1},{1,0},{2,3},{3,2},{4,5},{5,4},{6,7},{7,6},{8,9},{9,8},{10,11... | collective-permute-start | bytes 491528 | tf_op jit(solution)/shard_map/ppermute | solution.py:318
  40.3 7.2 %collective-permute-start.12 = (bf16[320,256]{1,0:T(8,128)(2,1)S(1)}, bf16[320,256]{1,0:T(8,128)(2,1)S(1)}, u32[]{:S(2)}, u32[]{:S(2)}) collective-permute-start(bf16[320,256]{1,0:T(8,128)(2,1)S(1)} %get-tuple-element.53.chain_1), channel_id=1, source_target_pairs={{8,0},{9,1},{10,2},{11,3},{12,4},{13,5},{14,6},{15,7}} | collective-permute-start | bytes 491528 | tf_op jit(solution)/shard_map/ppermute | solution.py:310
  41.6 6.6 %collective-permute-start.4 = (bf16[320,256]{1,0:T(8,128)(2,1)S(1)}, bf16[320,256]{1,0:T(8,128)(2,1)S(1)}, u32[]{:S(2)}, u32[]{:S(2)}) collective-permute-start(bf16[320,256]{1,0:T(8,128)(2,1)S(1)} %collective-permute-done.1.refs_1_), channel_id=1, source_target_pairs={{0,1},{1,0},{2,3},{3,2},{4,5},{5,4},{6,7},{7,6},{8,9},{9,8},{10,11... | collective-permute-start | bytes 491528 | tf_op jit(solution)/shard_map/ppermute | solution.py:318
  41.7 11.6 %collective-permute-start.5 = (bf16[320,256]{1,0:T(8,128)(2,1)S(1)}, bf16[320,256]{1,0:T(8,128)(2,1)S(1)}, u32[]{:S(2)}, u32[]{:S(2)}) collective-permute-start(bf16[320,256]{1,0:T(8,128)(2,1)S(1)} %collective-permute-done.2.refs_2_), channel_id=1, source_target_pairs={{0,1},{1,0},{2,3},{3,2},{4,5},{5,4},{6,7},{7,6},{8,9},{9,8},{10,11... | collective-permute-start | bytes 491528 | tf_op jit(solution)/shard_map/ppermute | solution.py:318
  42.2 16.4 %collective-permute-start.23 = (bf16[320,256]{1,0:T(8,128)(2,1)S(1)}, bf16[320,256]{1,0:T(8,128)(2,1)S(1)}, u32[]{:S(2)}, u32[]{:S(2)}) collective-permute-start(bf16[320,256]{1,0:T(8,128)(2,1)S(1)} %shard_map.112), channel_id=1, source_target_pairs={{8,12},{9,13},{10,14},{11,15},{12,8},{13,9},{14,10},{15,11},{16,20... | collective-permute-start | bytes 491528 | tf_op jit(solution)/shard_map/ppermute | solution.py:336
  42.9 17.4 %collective-permute-start.17 = (bf16[320,256]{1,0:T(8,128)(2,1)S(1)}, bf16[320,256]{1,0:T(8,128)(2,1)S(1)}, u32[]{:S(2)}, u32[]{:S(2)}) collective-permute-start(bf16[320,256]{1,0:T(8,128)(2,1)S(1)} %get-tuple-element.55), channel_id=1, source_target_pairs={{8,6},{9,7},{10,4},{11,5},{12,2},{13,3},{14,0},{15,1},{16,14},{17,... | collective-permute-start | bytes 491528 | tf_op jit(solution)/shard_map/ppermute | solution.py:327
  47.5 12.8 %collective-permute-start.15 = (bf16[320,256]{1,0:T(8,128)(2,1)S(1)}, bf16[320,256]{1,0:T(8,128)(2,1)S(1)}, u32[]{:S(2)}, u32[]{:S(2)}) collective-permute-start(bf16[320,256]{1,0:T(8,128)(2,1)S(1)} %shard_map.112), channel_id=1, source_target_pairs={{8,10},{9,11},{10,8},{11,9},{12,14},{13,15},{14,12},{15,13},{16,18... | collective-permute-start | bytes 491528 | tf_op jit(solution)/shard_map/ppermute | solution.py:336
  48.3 12.7 %collective-permute-start.14 = (bf16[320,256]{1,0:T(8,128)(2,1)S(1)}, bf16[320,256]{1,0:T(8,128)(2,1)S(1)}, u32[]{:S(2)}, u32[]{:S(2)}) collective-permute-start(bf16[320,256]{1,0:T(8,128)(2,1)S(1)} %shard_map.111.refs_6_.grad_low), channel_id=1, source_target_pairs={{0,2},{1,3},{2,0},{3,1},{4,6},{5,7},{6,4},{7,5}} | collective-permute-start | bytes 491528 | tf_op jit(solution)/shard_map/ppermute | solution.py:336
  53.3 10.0 %collective-permute-start.22 = (bf16[320,256]{1,0:T(8,128)(2,1)S(1)}, bf16[320,256]{1,0:T(8,128)(2,1)S(1)}, u32[]{:S(2)}, u32[]{:S(2)}) collective-permute-start(bf16[320,256]{1,0:T(8,128)(2,1)S(1)} %shard_map.111.refs_6_.grad_low), channel_id=1, source_target_pairs={{0,4},{1,5},{2,6},{3,7},{4,0},{5,1},{6,2},{7,3}} | collective-permute-start | bytes 491528 | tf_op jit(solution)/shard_map/ppermute | solution.py:336
  58.6 4.7 %collective-permute-start.26 = (bf16[4,40,320]{2,1,0:T(8,128)(2,1)S(1)}, bf16[4,40,320]{2,1,0:T(8,128)(2,1)S(1)}, u32[]{:S(2)}, u32[]{:S(2)}) collective-permute-start(bf16[4,40,320]{2,1,0:T(8,128)(2,1)S(1)} %get-tuple-element.60), channel_id=1, source_target_pairs={{0,1},{1,0},{2,3},{3,2},{4,5},{5,4},{6,7},{7,6},{8,9},{9,8},{10,11... | collective-permute-start | bytes 307208 | tf_op jit(solution)/shard_map/ppermute | solution.py:318
  60.3 3.6 %collective-permute-start.7 = (bf16[320,256]{1,0:T(8,128)(2,1)S(1)}, bf16[320,256]{1,0:T(8,128)(2,1)S(1)}, u32[]{:S(2)}, u32[]{:S(2)}) collective-permute-start(bf16[320,256]{1,0:T(8,128)(2,1)S(1)} %collective-permute-done.6.refs_6_.normed_0), channel_id=1, source_target_pairs={{0,1},{1,0},{2,3},{3,2},{4,5},{5,4},{6,7},{7,6},{8,9},{9,8},{10,11... | collective-permute-start | bytes 491528 | tf_op jit(solution)/shard_map/ppermute | solution.py:318
  60.4 8.0 %collective-permute-start.21 = (bf16[320,256]{1,0:T(8,128)(2,1)S(1)}, bf16[320,256]{1,0:T(8,128)(2,1)S(1)}, u32[]{:S(2)}, u32[]{:S(2)}) collective-permute-start(bf16[320,256]{1,0:T(8,128)(2,1)S(1)} %shard_map.114.refs_8_), channel_id=1, source_target_pairs={{0,1},{1,0},{2,3},{3,2},{4,5},{5,4},{6,7},{7,6},{8,9},{9,8},{10,11... | collective-permute-start | bytes 491528 | tf_op jit(solution)/shard_map/ppermute | solution.py:318
  60.9 7.4 %collective-permute-start.19 = (bf16[320,256]{1,0:T(8,128)(2,1)S(1)}, bf16[320,256]{1,0:T(8,128)(2,1)S(1)}, u32[]{:S(2)}, u32[]{:S(2)}) collective-permute-start(bf16[320,256]{1,0:T(8,128)(2,1)S(1)} %shard_map.111.refs_6_.grad_low), channel_id=1, source_target_pairs={{0,1},{1,0},{2,3},{3,2},{4,5},{5,4},{6,7},{7,6},{8,9},{9,8},{10,11... | collective-permute-start | bytes 491528 | tf_op jit(solution)/shard_map/ppermute | solution.py:318
  63.3 8.5 %collective-permute-start.20 = (bf16[320,256]{1,0:T(8,128)(2,1)S(1)}, bf16[320,256]{1,0:T(8,128)(2,1)S(1)}, u32[]{:S(2)}, u32[]{:S(2)}) collective-permute-start(bf16[320,256]{1,0:T(8,128)(2,1)S(1)} %shard_map.113.refs_7_), channel_id=1, source_target_pairs={{0,1},{1,0},{2,3},{3,2},{4,5},{5,4},{6,7},{7,6},{8,9},{9,8},{10,11... | collective-permute-start | bytes 491528 | tf_op jit(solution)/shard_map/ppermute | solution.py:318
  63.3 10.9 %collective-permute-start.25 = (bf16[320,256]{1,0:T(8,128)(2,1)S(1)}, bf16[320,256]{1,0:T(8,128)(2,1)S(1)}, u32[]{:S(2)}, u32[]{:S(2)}) collective-permute-start(bf16[320,256]{1,0:T(8,128)(2,1)S(1)} %shard_map.116.low_0), channel_id=1, source_target_pairs={{0,1},{1,0},{2,3},{3,2},{4,5},{5,4},{6,7},{7,6},{8,9},{9,8},{10,11... | collective-permute-start | bytes 491528 | tf_op jit(solution)/shard_map/ppermute | solution.py:318
  63.9 9.0 %collective-permute-start.27 = (bf16[40,320]{1,0:T(8,128)(2,1)S(1)}, bf16[40,320]{1,0:T(8,128)(2,1)S(1)}, u32[]{:S(2)}, u32[]{:S(2)}) collective-permute-start(bf16[40,320]{1,0:T(8,128)(2,1)S(1)} %get-tuple-element.62), channel_id=1, source_target_pairs={{0,2},{1,3},{2,0},{3,1},{4,6},{5,7},{6,4},{7,5},{8,10},{9,11},{10,... | collective-permute-start | bytes 76808 | tf_op jit(solution)/shard_map/ppermute | solution.py:318
  68.4 5.4 %collective-permute-start.28 = (bf16[40,320]{1,0:T(8,128)(2,1)S(1)}, bf16[40,320]{1,0:T(8,128)(2,1)S(1)}, u32[]{:S(2)}, u32[]{:S(2)}) collective-permute-start(bf16[40,320]{1,0:T(8,128)(2,1)S(1)} %get-tuple-element.63), channel_id=1, source_target_pairs={{0,4},{1,5},{2,6},{3,7},{4,0},{5,1},{6,2},{7,3},{8,12},{9,13},{10,... | collective-permute-start | bytes 76808 | tf_op jit(solution)/shard_map/ppermute | solution.py:318
  68.4 5.9 %collective-permute-start.29 = (bf16[40,320]{1,0:T(8,128)(2,1)S(1)}, bf16[40,320]{1,0:T(8,128)(2,1)S(1)}, u32[]{:S(2)}, u32[]{:S(2)}) collective-permute-start(bf16[40,320]{1,0:T(8,128)(2,1)S(1)} %get-tuple-element.64), channel_id=1, source_target_pairs={{0,6},{1,7},{2,4},{3,5},{4,2},{5,3},{6,0},{7,1},{8,14},{9,15},{10,... | collective-permute-start | bytes 76808 | tf_op jit(solution)/shard_map/ppermute | solution.py:318

commit v9 on v8

--- a/solution.py
+++ b/solution.py
@@ -402,10 +402,9 @@
     )
     tops = {mask: within(top_low, [3], count, mask) for mask in (2, 4, 6)}
     (own_low,) = call(own_body, [low], low_1, low_2)
-    next_6 = from_next(ahead, count, 6)
-    middle = {mask: within(own_low, [1, 2], count, mask) for mask in (2, 4)}
-    late = {mask: within(grad_low, [0], count, mask) for mask in (2, 4)}
-    late[6] = middle[6] = next_6
+    middle = {mask: from_next(ahead, count, mask) for mask in (2, 6)}
+    middle[4] = within(own_low, [1, 2], count, 4)
+    late = {**middle, 4: within(grad_low, [0], count, 4)}
     low_2, low_4, low_6 = (
         call(merge_body, [low], late[mask], middle[mask], tops[mask])[0]
         for mask in (2, 4, 6)

time: 75.9 us -> 76 us (level)
  the two profiles are of different devices: /device:TPU:0 before, /device:TPU:4 now
where the time goes in v9:
time: 76 us; the launch traced here: 75.7 us
  waiting for transfers between devices  34.2 us (45%)
  starting transfers between devices  32.1 us (42%)
  Pallas kernels  8.31 us (11%)
  between operations  1.02 us (1%)
    ppermute x15, waiting for transfers between devices, exchange(): return lax.ppermute(value, 'dp', [(i, i ^ mask) for i in range(count)])  14.3 us
    ppermute x2, starting transfers between devices, from_next(): return lax.ppermute(value, ('section', 'dp'), pairs)  10.2 us
    ppermute x7, waiting for transfers between devices, hop(): return lax.ppermute(value, 'section', pairs)  9.93 us
    ppermute x15, starting transfers between devices, exchange(): return lax.ppermute(value, 'dp', [(i, i ^ mask) for i in range(count)])  9.92 us
    pallas_call x18, Pallas kernels, call(): pl.pallas_call(body, out_shape=[jax.ShapeDtypeStruct(shape, kind) for sha...  8.31 us
    ppermute x2, waiting for transfers between devices, from_next(): return lax.ppermute(value, ('section', 'dp'), pairs)  7.99 us
    ppermute x7, starting transfers between devices, hop(): return lax.ppermute(value, 'section', pairs)  7.19 us
    ppermute x5, starting transfers between devices, within(): return lax.ppermute(value, ('section', 'dp'), pairs)  4.77 us
  transfers between devices with their start and end apart: 29, of which 9 were waited for; matrix products, arithmetic and copies ran while one was open for 0% of the time, Pallas kernels for 5%

profile of v9, /device:TPU:4, one launch (start us, length us, event | category | flops | bytes accessed | tf_op | source)
XLA Modules:
  0.0 75.7 jit_solution(16040008143180341861)
XLA Ops:
  0.6 1.8 %shard_map.102 = (bf16[320,256]{1,0:T(8,128)(2,1)S(1)}, bf16[320,256]{1,0:T(8,128)(2,1)S(1)}, bf16[320,320]{1,0:T(8,128)(2,1)S(1)}, bf16[2,320,128]{2,1,0:T(8,12...) custom-call(s32[2,128]{1,0:T(2,128)} %refs_0_.1, bf16[320,1000]{1,0:T(8,128)(2,1)} %bitcast.20, ...), custom_call_target="tpu_custom_call" | custom-call | tf_op jit(solution)/shard_map/pallas_call | solution.py:35
  2.5 1.3 %collective-permute-start = (bf16[320,256]{1,0:T(8,128)(2,1)S(1)}, bf16[320,256]{1,0:T(8,128)(2,1)S(1)}, u32[]{:S(2)}, u32[]{:S(2)}) collective-permute-start(bf16[320,256]{1,0:T(8,128)(2,1)S(1)} %get-tuple-element.41), channel_id=1, source_target_pairs={{0,24},{8,16},{1,25},{9,17},{2,26},{10,18},{3,27},{11,19},{4,28},{... | collective-permute-start | bytes 491528 | tf_op jit(solution)/shard_map/ppermute | solution.py:310
  3.8 7.4 %collective-permute-done.received = bf16[320,256]{1,0:T(8,128)(2,1)S(1)} collective-permute-done((bf16[320,256]{1,0:T(8,128)(2,1)S(1)}, bf16[320,256]{1,0:T(8,128)(2,1)S(1)}, u32[]{:S(2)}, u32[]{:S(2)}) %collective-permute-start) | collective-permute-done | bytes 163872 | tf_op jit(solution)/shard_map/ppermute | solution.py:310
  11.2 1.1 %shard_map.105 = (bf16[320,256]{1,0:T(8,128)(2,1)S(1)}, bf16[320,256]{1,0:T(8,128)(2,1)S(1)}, f32[320,256]{1,0:T(8,128)S(1)}, f32[1280,256]{1,0:T(8,128)S(1)}, bf16[320,256]{1,0:T(8,128)(2,1)S(1)}) custom-call(bf16[320,256]{1,0:T(8,128)(2,1)S(1)} %collective-permute-done.received, bf16[320,256]{1,0:T(8,128)(2,1)S(1)} %get-tuple-element.42.embed, ...), custom_call_target="tpu_custom_call" | custom-call | tf_op jit(solution)/shard_map/pallas_call | solution.py:35
  12.3 1.3 %collective-permute-start.8 = (bf16[320,256]{1,0:T(8,128)(2,1)S(1)}, bf16[320,256]{1,0:T(8,128)(2,1)S(1)}, u32[]{:S(2)}, u32[]{:S(2)}) collective-permute-start(bf16[320,256]{1,0:T(8,128)(2,1)S(1)} %get-tuple-element.50.chain.chain_3), channel_id=1, source_target_pairs={{24,16},{25,17},{26,18},{27,19},{28,20},{29,21},{30,22},{31,23}} | collective-permute-start | bytes 491528 | tf_op jit(solution)/shard_map/ppermute | solution.py:310
  13.6 0.7 collective-permute-start.23
  14.3 0.7 collective-permute-start.17
  14.9 0.7 collective-permute-start.15
  15.6 1.3 %collective-permute-start.10 = (bf16[320,320]{1,0:T(8,128)(2,1)S(1)}, bf16[320,320]{1,0:T(8,128)(2,1)S(1)}, u32[]{:S(2)}, u32[]{:S(2)}) collective-permute-start(bf16[320,320]{1,0:T(8,128)(2,1)S(1)} %get-tuple-element.46.w_skip), channel_id=1, source_target_pairs={{16,8},{17,9},{18,10},{19,11},{20,12},{21,13},{22,14},{23,15}} | collective-permute-start | bytes 614408 | tf_op jit(solution)/shard_map/ppermute | solution.py:310
  17.0 2.5 %collective-permute-done.8.received.low_2 = bf16[320,256]{1,0:T(8,128)(2,1)S(1)} collective-permute-done((bf16[320,256]{1,0:T(8,128)(2,1)S(1)}, bf16[320,256]{1,0:T(8,128)(2,1)S(1)}, u32[]{:S(2)}, u32[]{:S(2)}) %collective-permute-start.8) | collective-permute-done | bytes 163872 | tf_op jit(solution)/shard_map/ppermute | solution.py:310
  19.5 0.7 collective-permute-start.11
  20.2 1.2 %shard_map.107.chain.chain_2 = bf16[320,256]{1,0:T(8,128)(2,1)S(1)} custom-call(bf16[320,256]{1,0:T(8,128)(2,1)S(1)} %collective-permute-done.8.received.low_2, f32[320,256]{1,0:T(8,128)S(1)} %get-tuple-element.51.united, f32[1280,256]{1,0:T(8,128)S(1)} %get-tuple-element.52.slope, bf16[320,1280]{1,0:T(8,128)(2,1)S(1)} %get-tuple-element.37.w_in, ...), custom_call_target="tpu_custom_call" | custom-call | tf_op jit(solution)/shard_map/pallas_call | solution.py:35
  21.4 0.0 collective-permute-done.23.top
  21.4 1.3 %collective-permute-start.9 = (bf16[320,256]{1,0:T(8,128)(2,1)S(1)}, bf16[320,256]{1,0:T(8,128)(2,1)S(1)}, u32[]{:S(2)}, u32[]{:S(2)}) collective-permute-start(bf16[320,256]{1,0:T(8,128)(2,1)S(1)} %shard_map.107.chain.chain_2), channel_id=1, source_target_pairs={{16,8},{17,9},{18,10},{19,11},{20,12},{21,13},{22,14},{23,15}} | collective-permute-start | bytes 491528 | tf_op jit(solution)/shard_map/ppermute | solution.py:310
  22.7 0.0 collective-permute-done.17.top
  22.7 0.7 collective-permute-start.13
  23.4 0.0 collective-permute-done.15.top
  23.4 1.6 %collective-permute-start.1 = (bf16[320,256]{1,0:T(8,128)(2,1)S(1)}, bf16[320,256]{1,0:T(8,128)(2,1)S(1)}, u32[]{:S(2)}, u32[]{:S(2)}) collective-permute-start(bf16[320,256]{1,0:T(8,128)(2,1)S(1)} %get-tuple-element.47.refs_0_), channel_id=1, source_target_pairs={{0,2},{1,3},{2,0},{3,1},{4,6},{5,7},{6,4},{7,5},{8,10},{9,11},{10,... | collective-permute-start | bytes 491528 | tf_op jit(solution)/shard_map/ppermute | solution.py:318
  25.0 0.0 collective-permute-done.10.w_mirror
  25.0 2.5 %collective-permute-start.2 = (bf16[320,256]{1,0:T(8,128)(2,1)S(1)}, bf16[320,256]{1,0:T(8,128)(2,1)S(1)}, u32[]{:S(2)}, u32[]{:S(2)}) collective-permute-start(bf16[320,256]{1,0:T(8,128)(2,1)S(1)} %get-tuple-element.47.refs_0_), channel_id=1, source_target_pairs={{0,6},{1,7},{2,4},{3,5},{4,2},{5,3},{6,0},{7,1},{8,14},{9,15},{10,... | collective-permute-start | bytes 491528 | tf_op jit(solution)/shard_map/ppermute | solution.py:318
  27.5 0.0 collective-permute-done.11.skip_far
  27.5 0.2 collective-permute-start.6
  27.7 0.2 shard_map.109.back_2
  27.9 0.0 collective-permute-done.9.received
  27.9 0.1 collective-permute-start.3
  28.0 0.1 shard_map.110
  28.1 0.0 collective-permute-done.13.skip_far
  28.1 0.7 collective-permute-start.12
  28.8 2.2 %collective-permute-done.1.refs_1_ = bf16[320,256]{1,0:T(8,128)(2,1)S(1)} collective-permute-done((bf16[320,256]{1,0:T(8,128)(2,1)S(1)}, bf16[320,256]{1,0:T(8,128)(2,1)S(1)}, u32[]{:S(2)}, u32[]{:S(2)}) %collective-permute-start.1) | collective-permute-done | bytes 163872 | tf_op jit(solution)/shard_map/ppermute | solution.py:318
  31.0 0.0 collective-permute-start.4
  31.0 3.8 %collective-permute-done.2.refs_2_ = bf16[320,256]{1,0:T(8,128)(2,1)S(1)} collective-permute-done((bf16[320,256]{1,0:T(8,128)(2,1)S(1)}, bf16[320,256]{1,0:T(8,128)(2,1)S(1)}, u32[]{:S(2)}, u32[]{:S(2)}) %collective-permute-start.2) | collective-permute-done | bytes 163872 | tf_op jit(solution)/shard_map/ppermute | solution.py:318
  34.7 0.0 collective-permute-start.5
  34.7 5.3 %collective-permute-done.6.refs_6_.normed_0 = bf16[320,256]{1,0:T(8,128)(2,1)S(1)} collective-permute-done((bf16[320,256]{1,0:T(8,128)(2,1)S(1)}, bf16[320,256]{1,0:T(8,128)(2,1)S(1)}, u32[]{:S(2)}, u32[]{:S(2)}) %collective-permute-start.6) | collective-permute-done | bytes 163872 | tf_op jit(solution)/shard_map/ppermute | solution.py:318
  40.1 7.0 %collective-permute-start.16 = (bf16[320,256]{1,0:T(8,128)(2,1)S(1)}, bf16[320,256]{1,0:T(8,128)(2,1)S(1)}, u32[]{:S(2)}, u32[]{:S(2)}) collective-permute-start(bf16[320,256]{1,0:T(8,128)(2,1)S(1)} %get-tuple-element.55), channel_id=1, source_target_pairs={{8,6},{9,7},{10,4},{11,5},{12,2},{13,3},{14,0},{15,1},{16,14},{17,... | collective-permute-start | bytes 491528 | tf_op jit(solution)/shard_map/ppermute | solution.py:327
  47.1 0.0 collective-permute-done.3.refs_3_
  47.1 3.2 %collective-permute-start.14 = (bf16[320,256]{1,0:T(8,128)(2,1)S(1)}, bf16[320,256]{1,0:T(8,128)(2,1)S(1)}, u32[]{:S(2)}, u32[]{:S(2)}) collective-permute-start(bf16[320,256]{1,0:T(8,128)(2,1)S(1)} %get-tuple-element.55), channel_id=1, source_target_pairs={{8,2},{9,3},{10,0},{11,1},{12,6},{13,7},{14,4},{15,5},{16,10},{17,... | collective-permute-start | bytes 491528 | tf_op jit(solution)/shard_map/ppermute | solution.py:327
  50.3 0.0 collective-permute-done.12.received
  50.3 2.1 %collective-permute-start.22 = (bf16[320,256]{1,0:T(8,128)(2,1)S(1)}, bf16[320,256]{1,0:T(8,128)(2,1)S(1)}, u32[]{:S(2)}, u32[]{:S(2)}) collective-permute-start(bf16[320,256]{1,0:T(8,128)(2,1)S(1)} %shard_map.115), channel_id=1, source_target_pairs={{8,12},{9,13},{10,14},{11,15},{12,8},{13,9},{14,10},{15,11},{16,20... | collective-permute-start | bytes 491528 | tf_op jit(solution)/shard_map/ppermute | solution.py:336
  52.4 0.1 shard_map.111.refs_6_.grad_low
  52.5 0.0 collective-permute-done.4.refs_4_
  52.5 0.7 collective-permute-start.21
  53.2 0.3 shard_map.117
  53.5 0.0 collective-permute-done.5.refs_5_
  53.5 0.1 collective-permute-start.25
  53.6 7.8 %collective-permute-done.16.late.middle = bf16[320,256]{1,0:T(8,128)(2,1)S(1)} collective-permute-done((bf16[320,256]{1,0:T(8,128)(2,1)S(1)}, bf16[320,256]{1,0:T(8,128)(2,1)S(1)}, u32[]{:S(2)}, u32[]{:S(2)}) %collective-permute-start.16) | collective-permute-done | bytes 163872 | tf_op jit(solution)/shard_map/ppermute | solution.py:327
  61.4 0.0 collective-permute-start.7
  61.4 0.2 collective-permute-done.14.late.middle
  61.6 0.4 collective-permute-start.20
  62.0 2.1 %collective-permute-done.22.middle = bf16[320,256]{1,0:T(8,128)(2,1)S(1)} collective-permute-done((bf16[320,256]{1,0:T(8,128)(2,1)S(1)}, bf16[320,256]{1,0:T(8,128)(2,1)S(1)}, u32[]{:S(2)}, u32[]{:S(2)}) %collective-permute-start.22) | collective-permute-done | bytes 163872 | tf_op jit(solution)/shard_map/ppermute | solution.py:336
  64.1 0.0 collective-permute-start.19
  64.1 0.0 collective-permute-done.21.late
  64.1 0.5 collective-permute-start.18
  64.7 0.1 collective-permute-start.24
  64.8 0.4 collective-permute-start.26
  65.2 0.0 collective-permute-done.20.refs_11_
  65.2 3.4 %collective-permute-start.27 = (bf16[40,320]{1,0:T(8,128)(2,1)S(1)}, bf16[40,320]{1,0:T(8,128)(2,1)S(1)}, u32[]{:S(2)}, u32[]{:S(2)}) collective-permute-start(bf16[40,320]{1,0:T(8,128)(2,1)S(1)} %get-tuple-element.63), channel_id=1, source_target_pairs={{0,4},{1,5},{2,6},{3,7},{4,0},{5,1},{6,2},{7,3},{8,12},{9,13},{10,... | collective-permute-start | bytes 76808 | tf_op jit(solution)/shard_map/ppermute | solution.py:318
  68.6 0.0 collective-permute-done.19.refs_10_
  68.6 0.7 collective-permute-start.28
  69.3 0.1 shard_map.103
  69.3 0.8 %shard_map.106 = (bf16[160,2048]{1,0:T(8,128)(2,1)S(1)}, f32[160,2048]{1,0:T(8,128)S(1)}) custom-call(bf16[320,160]{1,0:T(8,128)(2,1)S(1)} %get-tuple-element.40.own_in, bf16[320,256]{1,0:T(8,128)(2,1)S(1)} %get-tuple-element.47.refs_0_, bf16[320,256]{1,0:T(8,128)(2,1)S(1)} %collective-permute-done.1.refs_1_, ...), custom_call_target="tpu_custom_call" | custom-call | tf_op jit(solution)/shard_map/pallas_call | solution.py:35
  70.2 1.1 %shard_map.114 = (f32[160,320]{1,0:T(8,128)S(1)}, f32[160,320]{1,0:T(8,128)S(1)}) custom-call(bf16[320,160]{1,0:T(8,128)(2,1)S(1)} %get-tuple-element.39.own_out, bf16[160,2048]{1,0:T(8,128)(2,1)S(1)} %get-tuple-element.48.active, f32[160,2048]{1,0:T(8,128)S(1)} %get-tuple-element.49.slope, bf16[320,256]{1,0:T(8,128)(2,1)S(1)} %get-tuple-element.47.refs_0_, ...), custom_call_target="tpu_custom_call" | custom-call | tf_op jit(solution)/shard_map/pallas_call | solution.py:35
  71.3 0.0 collective-permute-done.26.piece_1
  71.4 3.0 %collective-permute-done.28.piece_3 = bf16[40,320]{1,0:T(8,128)(2,1)S(1)} collective-permute-done((bf16[40,320]{1,0:T(8,128)(2,1)S(1)}, bf16[40,320]{1,0:T(8,128)(2,1)S(1)}, u32[]{:S(2)}, u32[]{:S(2)}) %collective-permute-start.28) | collective-permute-done | bytes 25632 | tf_op jit(solution)/shard_map/ppermute | solution.py:318
  74.3 1.3 %shard_map.119 = (f32[160,320]{1,0:T(8,128)}, f32[160,320]{1,0:T(8,128)}, f32[1,12800]{1,0:T(1,128)}, bf16[2,320,128]{2,1,0:T(8,128)(2,1)}) custom-call(bf16[320,160]{1,0:T(8,128)(2,1)S(1)} %get-tuple-element.39.own_out, bf16[160,2048]{1,0:T(8,128)(2,1)S(1)} %get-tuple-element.48.active, f32[160,2048]{1,0:T(8,128)S(1)} %get-tuple-element.49.slope, ...), custom_call_target="tpu_custom_call" | custom-call | tf_op jit(solution)/shard_map/pallas_call | solution.py:35
  (14 shorter events, 0.2 us)
Async XLA Ops:
  0.6 3.1 %copy-start = (bf16[2,128,320]{1,2,0:T(8,128)(2,1)S(1)}, bf16[2,128,320]{1,2,0:T(8,128)(2,1)}, u32[]{:S(2)}) copy-start(bf16[2,128,320]{1,2,0:T(8,128)(2,1)} %param.13) | copy-start | bytes 491524
  2.5 8.7 %collective-permute-start = (bf16[320,256]{1,0:T(8,128)(2,1)S(1)}, bf16[320,256]{1,0:T(8,128)(2,1)S(1)}, u32[]{:S(2)}, u32[]{:S(2)}) collective-permute-start(bf16[320,256]{1,0:T(8,128)(2,1)S(1)} %get-tuple-element.41), channel_id=1, source_target_pairs={{0,24},{8,16},{1,25},{9,17},{2,26},{10,18},{3,27},{11,19},{4,28},{... | collective-permute-start | bytes 491528 | tf_op jit(solution)/shard_map/ppermute | solution.py:310
  12.3 7.2 %collective-permute-start.8 = (bf16[320,256]{1,0:T(8,128)(2,1)S(1)}, bf16[320,256]{1,0:T(8,128)(2,1)S(1)}, u32[]{:S(2)}, u32[]{:S(2)}) collective-permute-start(bf16[320,256]{1,0:T(8,128)(2,1)S(1)} %get-tuple-element.50.chain.chain_3), channel_id=1, source_target_pairs={{24,16},{25,17},{26,18},{27,19},{28,20},{29,21},{30,22},{31,23}} | collective-permute-start | bytes 491528 | tf_op jit(solution)/shard_map/ppermute | solution.py:310
  13.6 7.8 %collective-permute-start.23 = (bf16[320,256]{1,0:T(8,128)(2,1)S(1)}, bf16[320,256]{1,0:T(8,128)(2,1)S(1)}, u32[]{:S(2)}, u32[]{:S(2)}) collective-permute-start(bf16[320,256]{1,0:T(8,128)(2,1)S(1)} %get-tuple-element.44.top_low), channel_id=1, source_target_pairs={{24,28},{25,29},{26,30},{27,31},{28,24},{29,25},{30,26},{31,27}} | collective-permute-start | bytes 491528 | tf_op jit(solution)/shard_map/ppermute | solution.py:336
  14.3 8.4 %collective-permute-start.17 = (bf16[320,256]{1,0:T(8,128)(2,1)S(1)}, bf16[320,256]{1,0:T(8,128)(2,1)S(1)}, u32[]{:S(2)}, u32[]{:S(2)}) collective-permute-start(bf16[320,256]{1,0:T(8,128)(2,1)S(1)} %get-tuple-element.44.top_low), channel_id=1, source_target_pairs={{24,30},{25,31},{26,28},{27,29},{28,26},{29,27},{30,24},{31,25}} | collective-permute-start | bytes 491528 | tf_op jit(solution)/shard_map/ppermute | solution.py:336
  14.9 8.4 %collective-permute-start.15 = (bf16[320,256]{1,0:T(8,128)(2,1)S(1)}, bf16[320,256]{1,0:T(8,128)(2,1)S(1)}, u32[]{:S(2)}, u32[]{:S(2)}) collective-permute-start(bf16[320,256]{1,0:T(8,128)(2,1)S(1)} %get-tuple-element.44.top_low), channel_id=1, source_target_pairs={{24,26},{25,27},{26,24},{27,25},{28,30},{29,31},{30,28},{31,29}} | collective-permute-start | bytes 491528 | tf_op jit(solution)/shard_map/ppermute | solution.py:336
  15.6 9.4 %collective-permute-start.10 = (bf16[320,320]{1,0:T(8,128)(2,1)S(1)}, bf16[320,320]{1,0:T(8,128)(2,1)S(1)}, u32[]{:S(2)}, u32[]{:S(2)}) collective-permute-start(bf16[320,320]{1,0:T(8,128)(2,1)S(1)} %get-tuple-element.46.w_skip), channel_id=1, source_target_pairs={{16,8},{17,9},{18,10},{19,11},{20,12},{21,13},{22,14},{23,15}} | collective-permute-start | bytes 614408 | tf_op jit(solution)/shard_map/ppermute | solution.py:310
  19.5 8.0 %collective-permute-start.11 = (bf16[320,256]{1,0:T(8,128)(2,1)S(1)}, bf16[320,256]{1,0:T(8,128)(2,1)S(1)}, u32[]{:S(2)}, u32[]{:S(2)}) collective-permute-start(bf16[320,256]{1,0:T(8,128)(2,1)S(1)} %shard_map.108), channel_id=1, source_target_pairs={{24,8},{25,9},{26,10},{27,11},{28,12},{29,13},{30,14},{31,15}} | collective-permute-start | bytes 491528 | tf_op jit(solution)/shard_map/ppermute | solution.py:310
  21.4 6.6 %collective-permute-start.9 = (bf16[320,256]{1,0:T(8,128)(2,1)S(1)}, bf16[320,256]{1,0:T(8,128)(2,1)S(1)}, u32[]{:S(2)}, u32[]{:S(2)}) collective-permute-start(bf16[320,256]{1,0:T(8,128)(2,1)S(1)} %shard_map.107.chain.chain_2), channel_id=1, source_target_pairs={{16,8},{17,9},{18,10},{19,11},{20,12},{21,13},{22,14},{23,15}} | collective-permute-start | bytes 491528 | tf_op jit(solution)/shard_map/ppermute | solution.py:310
  22.7 5.4 %collective-permute-start.13 = (bf16[320,256]{1,0:T(8,128)(2,1)S(1)}, bf16[320,256]{1,0:T(8,128)(2,1)S(1)}, u32[]{:S(2)}, u32[]{:S(2)}) collective-permute-start(bf16[320,256]{1,0:T(8,128)(2,1)S(1)} %shard_map.108), channel_id=1, source_target_pairs={{24,0},{25,1},{26,2},{27,3},{28,4},{29,5},{30,6},{31,7}} | collective-permute-start | bytes 491528 | tf_op jit(solution)/shard_map/ppermute | solution.py:310
  23.4 7.6 %collective-permute-start.1 = (bf16[320,256]{1,0:T(8,128)(2,1)S(1)}, bf16[320,256]{1,0:T(8,128)(2,1)S(1)}, u32[]{:S(2)}, u32[]{:S(2)}) collective-permute-start(bf16[320,256]{1,0:T(8,128)(2,1)S(1)} %get-tuple-element.47.refs_0_), channel_id=1, source_target_pairs={{0,2},{1,3},{2,0},{3,1},{4,6},{5,7},{6,4},{7,5},{8,10},{9,11},{10,... | collective-permute-start | bytes 491528 | tf_op jit(solution)/shard_map/ppermute | solution.py:318
  25.0 9.7 %collective-permute-start.2 = (bf16[320,256]{1,0:T(8,128)(2,1)S(1)}, bf16[320,256]{1,0:T(8,128)(2,1)S(1)}, u32[]{:S(2)}, u32[]{:S(2)}) collective-permute-start(bf16[320,256]{1,0:T(8,128)(2,1)S(1)} %get-tuple-element.47.refs_0_), channel_id=1, source_target_pairs={{0,6},{1,7},{2,4},{3,5},{4,2},{5,3},{6,0},{7,1},{8,14},{9,15},{10,... | collective-permute-start | bytes 491528 | tf_op jit(solution)/shard_map/ppermute | solution.py:318
  27.5 12.6 %collective-permute-start.6 = (bf16[320,256]{1,0:T(8,128)(2,1)S(1)}, bf16[320,256]{1,0:T(8,128)(2,1)S(1)}, u32[]{:S(2)}, u32[]{:S(2)}) collective-permute-start(bf16[320,256]{1,0:T(8,128)(2,1)S(1)} %get-tuple-element.47.refs_0_), channel_id=1, source_target_pairs={{0,4},{1,5},{2,6},{3,7},{4,0},{5,1},{6,2},{7,3},{8,12},{9,13},{10,... | collective-permute-start | bytes 491528 | tf_op jit(solution)/shard_map/ppermute | solution.py:318
  27.9 19.1 %collective-permute-start.3 = (bf16[320,256]{1,0:T(8,128)(2,1)S(1)}, bf16[320,256]{1,0:T(8,128)(2,1)S(1)}, u32[]{:S(2)}, u32[]{:S(2)}) collective-permute-start(bf16[320,256]{1,0:T(8,128)(2,1)S(1)} %get-tuple-element.47.refs_0_), channel_id=1, source_target_pairs={{0,1},{1,0},{2,3},{3,2},{4,5},{5,4},{6,7},{7,6},{8,9},{9,8},{10,11... | collective-permute-start | bytes 491528 | tf_op jit(solution)/shard_map/ppermute | solution.py:318
  28.1 22.2 %collective-permute-start.12 = (bf16[320,256]{1,0:T(8,128)(2,1)S(1)}, bf16[320,256]{1,0:T(8,128)(2,1)S(1)}, u32[]{:S(2)}, u32[]{:S(2)}) collective-permute-start(bf16[320,256]{1,0:T(8,128)(2,1)S(1)} %get-tuple-element.53.chain_1), channel_id=1, source_target_pairs={{8,0},{9,1},{10,2},{11,3},{12,4},{13,5},{14,6},{15,7}} | collective-permute-start | bytes 491528 | tf_op jit(solution)/shard_map/ppermute | solution.py:310
  31.0 21.5 %collective-permute-start.4 = (bf16[320,256]{1,0:T(8,128)(2,1)S(1)}, bf16[320,256]{1,0:T(8,128)(2,1)S(1)}, u32[]{:S(2)}, u32[]{:S(2)}) collective-permute-start(bf16[320,256]{1,0:T(8,128)(2,1)S(1)} %collective-permute-done.1.refs_1_), channel_id=1, source_target_pairs={{0,1},{1,0},{2,3},{3,2},{4,5},{5,4},{6,7},{7,6},{8,9},{9,8},{10,11... | collective-permute-start | bytes 491528 | tf_op jit(solution)/shard_map/ppermute | solution.py:318
  34.7 18.8 %collective-permute-start.5 = (bf16[320,256]{1,0:T(8,128)(2,1)S(1)}, bf16[320,256]{1,0:T(8,128)(2,1)S(1)}, u32[]{:S(2)}, u32[]{:S(2)}) collective-permute-start(bf16[320,256]{1,0:T(8,128)(2,1)S(1)} %collective-permute-done.2.refs_2_), channel_id=1, source_target_pairs={{0,1},{1,0},{2,3},{3,2},{4,5},{5,4},{6,7},{7,6},{8,9},{9,8},{10,11... | collective-permute-start | bytes 491528 | tf_op jit(solution)/shard_map/ppermute | solution.py:318
  40.1 21.3 %collective-permute-start.16 = (bf16[320,256]{1,0:T(8,128)(2,1)S(1)}, bf16[320,256]{1,0:T(8,128)(2,1)S(1)}, u32[]{:S(2)}, u32[]{:S(2)}) collective-permute-start(bf16[320,256]{1,0:T(8,128)(2,1)S(1)} %get-tuple-element.55), channel_id=1, source_target_pairs={{8,6},{9,7},{10,4},{11,5},{12,2},{13,3},{14,0},{15,1},{16,14},{17,... | collective-permute-start | bytes 491528 | tf_op jit(solution)/shard_map/ppermute | solution.py:327
  47.1 14.5 %collective-permute-start.14 = (bf16[320,256]{1,0:T(8,128)(2,1)S(1)}, bf16[320,256]{1,0:T(8,128)(2,1)S(1)}, u32[]{:S(2)}, u32[]{:S(2)}) collective-permute-start(bf16[320,256]{1,0:T(8,128)(2,1)S(1)} %get-tuple-element.55), channel_id=1, source_target_pairs={{8,2},{9,3},{10,0},{11,1},{12,6},{13,7},{14,4},{15,5},{16,10},{17,... | collective-permute-start | bytes 491528 | tf_op jit(solution)/shard_map/ppermute | solution.py:327
  50.3 13.8 %collective-permute-start.22 = (bf16[320,256]{1,0:T(8,128)(2,1)S(1)}, bf16[320,256]{1,0:T(8,128)(2,1)S(1)}, u32[]{:S(2)}, u32[]{:S(2)}) collective-permute-start(bf16[320,256]{1,0:T(8,128)(2,1)S(1)} %shard_map.115), channel_id=1, source_target_pairs={{8,12},{9,13},{10,14},{11,15},{12,8},{13,9},{14,10},{15,11},{16,20... | collective-permute-start | bytes 491528 | tf_op jit(solution)/shard_map/ppermute | solution.py:336
  52.5 11.6 %collective-permute-start.21 = (bf16[320,256]{1,0:T(8,128)(2,1)S(1)}, bf16[320,256]{1,0:T(8,128)(2,1)S(1)}, u32[]{:S(2)}, u32[]{:S(2)}) collective-permute-start(bf16[320,256]{1,0:T(8,128)(2,1)S(1)} %shard_map.111.refs_6_.grad_low), channel_id=1, source_target_pairs={{0,4},{1,5},{2,6},{3,7},{4,0},{5,1},{6,2},{7,3}} | collective-permute-start | bytes 491528 | tf_op jit(solution)/shard_map/ppermute | solution.py:336
  53.5 11.2 %collective-permute-start.25 = (bf16[4,40,320]{2,1,0:T(8,128)(2,1)S(1)}, bf16[4,40,320]{2,1,0:T(8,128)(2,1)S(1)}, u32[]{:S(2)}, u32[]{:S(2)}) collective-permute-start(bf16[4,40,320]{2,1,0:T(8,128)(2,1)S(1)} %get-tuple-element.60), channel_id=1, source_target_pairs={{0,1},{1,0},{2,3},{3,2},{4,5},{5,4},{6,7},{7,6},{8,9},{9,8},{10,11... | collective-permute-start | bytes 307208 | tf_op jit(solution)/shard_map/ppermute | solution.py:318
  61.4 3.4 %collective-permute-start.7 = (bf16[320,256]{1,0:T(8,128)(2,1)S(1)}, bf16[320,256]{1,0:T(8,128)(2,1)S(1)}, u32[]{:S(2)}, u32[]{:S(2)}) collective-permute-start(bf16[320,256]{1,0:T(8,128)(2,1)S(1)} %collective-permute-done.6.refs_6_.normed_0), channel_id=1, source_target_pairs={{0,1},{1,0},{2,3},{3,2},{4,5},{5,4},{6,7},{7,6},{8,9},{9,8},{10,11... | collective-permute-start | bytes 491528 | tf_op jit(solution)/shard_map/ppermute | solution.py:318
  61.6 3.6 %collective-permute-start.20 = (bf16[320,256]{1,0:T(8,128)(2,1)S(1)}, bf16[320,256]{1,0:T(8,128)(2,1)S(1)}, u32[]{:S(2)}, u32[]{:S(2)}) collective-permute-start(bf16[320,256]{1,0:T(8,128)(2,1)S(1)} %shard_map.113.refs_8_), channel_id=1, source_target_pairs={{0,1},{1,0},{2,3},{3,2},{4,5},{5,4},{6,7},{7,6},{8,9},{9,8},{10,11... | collective-permute-start | bytes 491528 | tf_op jit(solution)/shard_map/ppermute | solution.py:318
  64.1 4.5 %collective-permute-start.19 = (bf16[320,256]{1,0:T(8,128)(2,1)S(1)}, bf16[320,256]{1,0:T(8,128)(2,1)S(1)}, u32[]{:S(2)}, u32[]{:S(2)}) collective-permute-start(bf16[320,256]{1,0:T(8,128)(2,1)S(1)} %shard_map.112.refs_7_), channel_id=1, source_target_pairs={{0,1},{1,0},{2,3},{3,2},{4,5},{5,4},{6,7},{7,6},{8,9},{9,8},{10,11... | collective-permute-start | bytes 491528 | tf_op jit(solution)/shard_map/ppermute | solution.py:318
  64.1 6.0 %collective-permute-start.18 = (bf16[320,256]{1,0:T(8,128)(2,1)S(1)}, bf16[320,256]{1,0:T(8,128)(2,1)S(1)}, u32[]{:S(2)}, u32[]{:S(2)}) collective-permute-start(bf16[320,256]{1,0:T(8,128)(2,1)S(1)} %shard_map.111.refs_6_.grad_low), channel_id=1, source_target_pairs={{0,1},{1,0},{2,3},{3,2},{4,5},{5,4},{6,7},{7,6},{8,9},{9,8},{10,11... | collective-permute-start | bytes 491528 | tf_op jit(solution)/shard_map/ppermute | solution.py:318
  64.7 9.6 %collective-permute-start.24 = (bf16[320,256]{1,0:T(8,128)(2,1)S(1)}, bf16[320,256]{1,0:T(8,128)(2,1)S(1)}, u32[]{:S(2)}, u32[]{:S(2)}) collective-permute-start(bf16[320,256]{1,0:T(8,128)(2,1)S(1)} %shard_map.116.low_0), channel_id=1, source_target_pairs={{0,1},{1,0},{2,3},{3,2},{4,5},{5,4},{6,7},{7,6},{8,9},{9,8},{10,11... | collective-permute-start | bytes 491528 | tf_op jit(solution)/shard_map/ppermute | solution.py:318
  64.8 6.5 %collective-permute-start.26 = (bf16[40,320]{1,0:T(8,128)(2,1)S(1)}, bf16[40,320]{1,0:T(8,128)(2,1)S(1)}, u32[]{:S(2)}, u32[]{:S(2)}) collective-permute-start(bf16[40,320]{1,0:T(8,128)(2,1)S(1)} %get-tuple-element.62), channel_id=1, source_target_pairs={{0,2},{1,3},{2,0},{3,1},{4,6},{5,7},{6,4},{7,5},{8,10},{9,11},{10,... | collective-permute-start | bytes 76808 | tf_op jit(solution)/shard_map/ppermute | solution.py:318
  65.2 6.1 %collective-permute-start.27 = (bf16[40,320]{1,0:T(8,128)(2,1)S(1)}, bf16[40,320]{1,0:T(8,128)(2,1)S(1)}, u32[]{:S(2)}, u32[]{:S(2)}) collective-permute-start(bf16[40,320]{1,0:T(8,128)(2,1)S(1)} %get-tuple-element.63), channel_id=1, source_target_pairs={{0,4},{1,5},{2,6},{3,7},{4,0},{5,1},{6,2},{7,3},{8,12},{9,13},{10,... | collective-permute-start | bytes 76808 | tf_op jit(solution)/shard_map/ppermute | solution.py:318
  68.6 5.7 %collective-permute-start.28 = (bf16[40,320]{1,0:T(8,128)(2,1)S(1)}, bf16[40,320]{1,0:T(8,128)(2,1)S(1)}, u32[]{:S(2)}, u32[]{:S(2)}) collective-permute-start(bf16[40,320]{1,0:T(8,128)(2,1)S(1)} %get-tuple-element.64), channel_id=1, source_target_pairs={{0,6},{1,7},{2,4},{3,5},{4,2},{5,3},{6,0},{7,1},{8,14},{9,15},{10,... | collective-permute-start | bytes 76808 | tf_op jit(solution)/shard_map/ppermute | solution.py:318

commit v10 on v9

--- a/solution.py
+++ b/solution.py
@@ -1,6 +1,3 @@
-from functools import partial
-
-
 import jax
 import jax.numpy as jnp
 from jax import lax
@@ -138,10 +135,21 @@
         )
 
 
-def back_body(owner, chain, w_skip, back_out):
-    @active_in(owner)
+def back_body(chain, w_skip, back_out):
+    @active_in(3)
     def _():
         back_out[...] = dot(w_skip[...], chain[...], 1, 0).astype(LOW)
+
+
+def prior_body(chain_2, chain_3, w_skip, prior_out):
+    @active_in(2)
+    def _():
+        back = dot(w_skip[...], chain_2[...], 1, 0).astype(LOW)
+        prior_out[...] = (chain_2[...].astype(F32) + back.astype(F32)).astype(LOW)
+
+    @active_in(3)
+    def _():
+        prior_out[...] = chain_3[...]
 
 
 def tick_body(received, united, slope, w_in, w_out, chain_out):
@@ -153,8 +161,7 @@
 
 
 def mirror_tick_body(
-    received, w_mirror, united, slope, w_in, w_out, skip_far, back_2, chain_2, chain_3,
-    chain_out, low_out, next_out,
+    received, w_mirror, united, slope, w_in, w_out, skip_far, chain_out, low_out, next_out,
 ):
     @active_in(1)
     def _():
@@ -166,14 +173,6 @@
         chain = back_through(grad_out, grad_act, united[...], slope[...], w_in)
         chain_out[...] = chain
         next_out[...] = (chain.astype(F32) + skip_far[...].astype(F32)).astype(LOW)
-
-    @active_in(2)
-    def _():
-        next_out[...] = (chain_2[...].astype(F32) + back_2[...].astype(F32)).astype(LOW)
-
-    @active_in(3)
-    def _():
-        next_out[...] = chain_3[...]
 
 
 def pick_body(received, skip_far, low_1, low_2, top_low, grad_low_out):
@@ -318,10 +317,10 @@
     return lax.ppermute(value, "dp", [(i, i ^ mask) for i in range(count)])
 
 
-def from_next(value, count, mask):
+def from_next(value, sections, count, mask):
     pairs = [
         ((section + 1) * count + i, section * count + (i ^ mask))
-        for section in range(3)
+        for section in sections
         for i in range(count)
     ]
     return lax.ppermute(value, ("section", "dp"), pairs)
@@ -369,16 +368,16 @@
     )
     chain = hop(chain_3, [(3, 2)])
     w_mirror = hop(w_skip, [(2, 1)])
-    (back,) = call(partial(back_body, 3), [low], chain_3, w_skip)
+    (back,) = call(back_body, [low], chain_3, w_skip)
     skip_far = hop(back, [(3, 0)])
     skip_next = hop(back, [(3, 1)])
     low_2 = chain
     (chain_2,) = call(tick_body, [low], chain, united, slope, w_in, w_out)
     chain = hop(chain_2, [(2, 1)])
-    (back_2,) = call(partial(back_body, 2), [low], chain_2, w_skip)
+    (prior,) = call(prior_body, [low], chain_2, chain_3, w_skip)
     chain_1, low_1, ahead = call(
         mirror_tick_body, [low, low, low],
-        chain, w_mirror, united, slope, w_in, w_out, skip_next, back_2, chain_2, chain_3,
+        chain, w_mirror, united, slope, w_in, w_out, skip_next,
     )
     chain = hop(chain_1, [(1, 0)])
     (grad_low,) = call(pick_body, [low], chain, skip_far, low_1, low_2, top_low)
@@ -400,11 +399,13 @@
         slice_forward_body,
         [((part, count * rows), LOW), ((part, count * rows), F32)], own_in, *normed_all,
     )
-    tops = {mask: within(top_low, [3], count, mask) for mask in (2, 4, 6)}
+    tops = {mask: within(top_low, [3], count, mask) for mask in (2, 4)}
+    tops[6] = within(tops[4], [3], count, 2)
     (own_low,) = call(own_body, [low], low_1, low_2)
-    middle = {mask: from_next(ahead, count, mask) for mask in (2, 6)}
+    middle = {m: from_next(prior, [1, 2], count, m) for m in (2, 6)}
     middle[4] = within(own_low, [1, 2], count, 4)
-    late = {**middle, 4: within(grad_low, [0], count, 4)}
+    late = {m: from_next(ahead, [0], count, m) for m in (2, 6)}
+    late[4] = within(grad_low, [0], count, 4)
     low_2, low_4, low_6 = (
         call(merge_body, [low], late[mask], middle[mask], tops[mask])[0]
         for mask in (2, 4, 6)

time: 76 us -> 71.9 us (0.946)
  the two profiles are of different devices: /device:TPU:4 before, /device:TPU:0 now
where the time goes in v10:
time: 71.9 us; the launch traced here: 71.2 us
  starting transfers between devices  36.5 us (51%)
  waiting for transfers between devices  24.1 us (34%)
  Pallas kernels  9.62 us (13%)
  between operations  1.04 us (1%)
    ppermute x15, starting transfers between devices, exchange(): return lax.ppermute(value, 'dp', [(i, i ^ mask) for i in range(count)])  14 us
    pallas_call x18, Pallas kernels, call(): pl.pallas_call(body, out_shape=[jax.ShapeDtypeStruct(shape, kind) for sha...  9.62 us
    ppermute x7, starting transfers between devices, hop(): return lax.ppermute(value, 'section', pairs)  9.47 us
    ppermute x5, starting transfers between devices, within(): return lax.ppermute(value, ('section', 'dp'), pairs)  9.05 us
    ppermute x4, waiting for transfers between devices, from_next(): return lax.ppermute(value, ('section', 'dp'), pairs)  8.58 us
    ppermute x15, waiting for transfers between devices, exchange(): return lax.ppermute(value, 'dp', [(i, i ^ mask) for i in range(count)])  8.25 us
    ppermute x7, waiting for transfers between devices, hop(): return lax.ppermute(value, 'section', pairs)  7.22 us
    ppermute x4, starting transfers between devices, from_next(): return lax.ppermute(value, ('section', 'dp'), pairs)  3.92 us
  transfers between devices with their start and end apart: 31, of which 5 were waited for; matrix products, arithmetic and copies ran while one was open for 0% of the time, Pallas kernels for 7%

profile of v10, /device:TPU:0, one launch (start us, length us, event | category | flops | bytes accessed | tf_op | source)
XLA Modules:
  0.0 71.2 jit_solution(17135613935642242768)
XLA Ops:
  0.6 3.4 %shard_map.102 = (bf16[320,256]{1,0:T(8,128)(2,1)S(1)}, bf16[320,256]{1,0:T(8,128)(2,1)S(1)}, bf16[320,320]{1,0:T(8,128)(2,1)S(1)}, bf16[2,320,128]{2,1,0:T(8,12...) custom-call(s32[2,128]{1,0:T(2,128)} %refs_0_.1, bf16[320,1000]{1,0:T(8,128)(2,1)} %bitcast.20, ...), custom_call_target="tpu_custom_call" | custom-call | tf_op jit(solution)/shard_map/pallas_call | solution.py:32
  4.1 4.2 %collective-permute-start = (bf16[320,256]{1,0:T(8,128)(2,1)S(1)}, bf16[320,256]{1,0:T(8,128)(2,1)S(1)}, u32[]{:S(2)}, u32[]{:S(2)}) collective-permute-start(bf16[320,256]{1,0:T(8,128)(2,1)S(1)} %get-tuple-element.41), channel_id=1, source_target_pairs={{0,24},{8,16},{1,25},{9,17},{2,26},{10,18},{3,27},{11,19},{4,28},{... | collective-permute-start | bytes 491528 | tf_op jit(solution)/shard_map/ppermute | solution.py:309
  8.4 0.7 collective-permute-start.19
  9.0 0.7 collective-permute-start.16
  9.7 0.7 collective-permute-start.10
  10.4 1.3 %collective-permute-done.received = bf16[320,256]{1,0:T(8,128)(2,1)S(1)} collective-permute-done((bf16[320,256]{1,0:T(8,128)(2,1)S(1)}, bf16[320,256]{1,0:T(8,128)(2,1)S(1)}, u32[]{:S(2)}, u32[]{:S(2)}) %collective-permute-start) | collective-permute-done | bytes 163872 | tf_op jit(solution)/shard_map/ppermute | solution.py:309
  11.7 1.1 %shard_map.105 = (bf16[320,256]{1,0:T(8,128)(2,1)S(1)}, bf16[320,256]{1,0:T(8,128)(2,1)S(1)}, f32[320,256]{1,0:T(8,128)S(1)}, f32[1280,256]{1,0:T(8,128)S(1)}, bf16[320,256]{1,0:T(8,128)(2,1)S(1)}) custom-call(bf16[320,256]{1,0:T(8,128)(2,1)S(1)} %collective-permute-done.received, bf16[320,256]{1,0:T(8,128)(2,1)S(1)} %get-tuple-element.42.embed, ...), custom_call_target="tpu_custom_call" | custom-call | tf_op jit(solution)/shard_map/pallas_call | solution.py:32
  12.8 0.7 collective-permute-start.8
  13.5 0.7 collective-permute-start.11
  14.2 0.0 collective-permute-done.19.top
  14.2 1.3 %collective-permute-start.13 = (bf16[320,256]{1,0:T(8,128)(2,1)S(1)}, bf16[320,256]{1,0:T(8,128)(2,1)S(1)}, u32[]{:S(2)}, u32[]{:S(2)}) collective-permute-start(bf16[320,256]{1,0:T(8,128)(2,1)S(1)} %shard_map.108), channel_id=1, source_target_pairs={{24,0},{25,1},{26,2},{27,3},{28,4},{29,5},{30,6},{31,7}} | collective-permute-start | bytes 491528 | tf_op jit(solution)/shard_map/ppermute | solution.py:309
  15.5 0.0 collective-permute-done.16.top
  15.5 0.7 collective-permute-start.20
  16.2 0.0 collective-permute-done.8.received.low_2
  16.2 1.6 %collective-permute-start.1 = (bf16[320,256]{1,0:T(8,128)(2,1)S(1)}, bf16[320,256]{1,0:T(8,128)(2,1)S(1)}, u32[]{:S(2)}, u32[]{:S(2)}) collective-permute-start(bf16[320,256]{1,0:T(8,128)(2,1)S(1)} %get-tuple-element.47.refs_0_), channel_id=1, source_target_pairs={{0,2},{1,3},{2,0},{3,1},{4,6},{5,7},{6,4},{7,5},{8,10},{9,11},{10,... | collective-permute-start | bytes 491528 | tf_op jit(solution)/shard_map/ppermute | solution.py:317
  17.9 0.0 collective-permute-done.10.w_mirror
  17.9 0.7 collective-permute-start.9
  18.5 0.0 collective-permute-done.11.skip_far
  18.5 2.5 %collective-permute-start.2 = (bf16[320,256]{1,0:T(8,128)(2,1)S(1)}, bf16[320,256]{1,0:T(8,128)(2,1)S(1)}, u32[]{:S(2)}, u32[]{:S(2)}) collective-permute-start(bf16[320,256]{1,0:T(8,128)(2,1)S(1)} %get-tuple-element.47.refs_0_), channel_id=1, source_target_pairs={{0,6},{1,7},{2,4},{3,5},{4,2},{5,3},{6,0},{7,1},{8,14},{9,15},{10,... | collective-permute-start | bytes 491528 | tf_op jit(solution)/shard_map/ppermute | solution.py:317
  21.1 5.9 %collective-permute-done.13.skip_far = bf16[320,256]{1,0:T(8,128)(2,1)S(1)} collective-permute-done((bf16[320,256]{1,0:T(8,128)(2,1)S(1)}, bf16[320,256]{1,0:T(8,128)(2,1)S(1)}, u32[]{:S(2)}, u32[]{:S(2)}) %collective-permute-start.13) | collective-permute-done | bytes 163872 | tf_op jit(solution)/shard_map/ppermute | solution.py:309
  26.9 1.1 %collective-permute-start.6 = (bf16[320,256]{1,0:T(8,128)(2,1)S(1)}, bf16[320,256]{1,0:T(8,128)(2,1)S(1)}, u32[]{:S(2)}, u32[]{:S(2)}) collective-permute-start(bf16[320,256]{1,0:T(8,128)(2,1)S(1)} %get-tuple-element.47.refs_0_), channel_id=1, source_target_pairs={{0,4},{1,5},{2,6},{3,7},{4,0},{5,1},{6,2},{7,3},{8,12},{9,13},{10,... | collective-permute-start | bytes 491528 | tf_op jit(solution)/shard_map/ppermute | solution.py:317
  28.0 0.0 collective-permute-done.20.top
  28.0 0.0 collective-permute-start.3
  28.0 0.0 collective-permute-done.1.refs_1_
  28.0 0.7 collective-permute-start.18
  28.7 0.0 collective-permute-done.9.received
  28.7 0.7 collective-permute-start.15
  29.4 0.0 collective-permute-done.2.refs_2_
  29.4 1.3 %collective-permute-start.12 = (bf16[320,256]{1,0:T(8,128)(2,1)S(1)}, bf16[320,256]{1,0:T(8,128)(2,1)S(1)}, u32[]{:S(2)}, u32[]{:S(2)}) collective-permute-start(bf16[320,256]{1,0:T(8,128)(2,1)S(1)} %get-tuple-element.53.chain_1), channel_id=1, source_target_pairs={{8,0},{9,1},{10,2},{11,3},{12,4},{13,5},{14,6},{15,7}} | collective-permute-start | bytes 491528 | tf_op jit(solution)/shard_map/ppermute | solution.py:309
  30.7 6.0 %collective-permute-done.6.refs_6_.normed_0 = bf16[320,256]{1,0:T(8,128)(2,1)S(1)} collective-permute-done((bf16[320,256]{1,0:T(8,128)(2,1)S(1)}, bf16[320,256]{1,0:T(8,128)(2,1)S(1)}, u32[]{:S(2)}, u32[]{:S(2)}) %collective-permute-start.6) | collective-permute-done | bytes 163872 | tf_op jit(solution)/shard_map/ppermute | solution.py:317
  36.8 0.0 collective-permute-start.4
  36.8 0.0 collective-permute-done.3.refs_3_
  36.8 0.5 collective-permute-start.5
  37.3 0.0 collective-permute-done.18.middle
  37.3 1.3 %collective-permute-start.17 = (bf16[320,256]{1,0:T(8,128)(2,1)S(1)}, bf16[320,256]{1,0:T(8,128)(2,1)S(1)}, u32[]{:S(2)}, u32[]{:S(2)}) collective-permute-start(bf16[320,256]{1,0:T(8,128)(2,1)S(1)} %get-tuple-element.55), channel_id=1, source_target_pairs={{8,6},{9,7},{10,4},{11,5},{12,2},{13,3},{14,0},{15,1}} | collective-permute-start | bytes 491528 | tf_op jit(solution)/shard_map/ppermute | solution.py:326
  38.6 0.0 collective-permute-done.15.middle
  38.6 1.3 %collective-permute-start.14 = (bf16[320,256]{1,0:T(8,128)(2,1)S(1)}, bf16[320,256]{1,0:T(8,128)(2,1)S(1)}, u32[]{:S(2)}, u32[]{:S(2)}) collective-permute-start(bf16[320,256]{1,0:T(8,128)(2,1)S(1)} %get-tuple-element.55), channel_id=1, source_target_pairs={{8,2},{9,3},{10,0},{11,1},{12,6},{13,7},{14,4},{15,5}} | collective-permute-start | bytes 491528 | tf_op jit(solution)/shard_map/ppermute | solution.py:326
  39.9 0.0 collective-permute-done.12.received
  40.0 0.7 collective-permute-start.25
  40.6 0.1 shard_map.110.refs_6_.grad_low
  40.7 0.0 collective-permute-done.4.refs_4_
  40.7 6.4 %collective-permute-start.24 = (bf16[320,256]{1,0:T(8,128)(2,1)S(1)}, bf16[320,256]{1,0:T(8,128)(2,1)S(1)}, u32[]{:S(2)}, u32[]{:S(2)}) collective-permute-start(bf16[320,256]{1,0:T(8,128)(2,1)S(1)} %shard_map.110.refs_6_.grad_low), channel_id=1, source_target_pairs={{0,4},{1,5},{2,6},{3,7},{4,0},{5,1},{6,2},{7,3}} | collective-permute-start | bytes 491528 | tf_op jit(solution)/shard_map/ppermute | solution.py:335
  47.1 1.5 %shard_map.117 = (bf16[320,256]{1,0:T(8,128)(2,1)S(1)}, f32[4,40,320]{2,1,0:T(8,128)S(1)}, bf16[4,40,320]{2,1,0:T(8,128)(2,1)S(1)}) custom-call(bf16[320,256]{1,0:T(8,128)(2,1)S(1)} %shard_map.110.refs_6_.grad_low, bf16[320,256]{1,0:T(8,128)(2,1)S(1)} %collective-permute-done.12.received, bf16[320,256]{1,0:T(8,128)(2,1)S(1)} %collective-permute-done.13.skip_far, ...), custom_call_target="tpu_custom_call" | custom-call | tf_op jit(solution)/shard_map/pallas_call | solution.py:32
  48.6 0.0 collective-permute-done.5.refs_5_
  48.6 0.1 collective-permute-start.27
  48.7 0.0 collective-permute-done.17.late
  48.7 0.5 collective-permute-start.7
  49.2 8.6 %collective-permute-done.14.late = bf16[320,256]{1,0:T(8,128)(2,1)S(1)} collective-permute-done((bf16[320,256]{1,0:T(8,128)(2,1)S(1)}, bf16[320,256]{1,0:T(8,128)(2,1)S(1)}, u32[]{:S(2)}, u32[]{:S(2)}) %collective-permute-start.14) | collective-permute-done | bytes 163872 | tf_op jit(solution)/shard_map/ppermute | solution.py:326
  57.8 0.0 collective-permute-start.23
  57.8 0.0 collective-permute-done.25.middle
  57.8 0.6 collective-permute-start.22
  58.4 0.1 collective-permute-start.21
  58.5 0.5 collective-permute-start.26
  59.0 0.0 collective-permute-done.7.refs_7_.normed_1
  59.0 1.8 %collective-permute-start.28 = (bf16[40,320]{1,0:T(8,128)(2,1)S(1)}, bf16[40,320]{1,0:T(8,128)(2,1)S(1)}, u32[]{:S(2)}, u32[]{:S(2)}) collective-permute-start(bf16[40,320]{1,0:T(8,128)(2,1)S(1)} %get-tuple-element.62), channel_id=1, source_target_pairs={{0,2},{1,3},{2,0},{3,1},{4,6},{5,7},{6,4},{7,5},{8,10},{9,11},{10,... | collective-permute-start | bytes 76808 | tf_op jit(solution)/shard_map/ppermute | solution.py:317
  60.9 3.3 %collective-permute-start.29 = (bf16[40,320]{1,0:T(8,128)(2,1)S(1)}, bf16[40,320]{1,0:T(8,128)(2,1)S(1)}, u32[]{:S(2)}, u32[]{:S(2)}) collective-permute-start(bf16[40,320]{1,0:T(8,128)(2,1)S(1)} %get-tuple-element.63), channel_id=1, source_target_pairs={{0,4},{1,5},{2,6},{3,7},{4,0},{5,1},{6,2},{7,3},{8,12},{9,13},{10,... | collective-permute-start | bytes 76808 | tf_op jit(solution)/shard_map/ppermute | solution.py:317
  64.2 1.4 %collective-permute-start.30 = (bf16[40,320]{1,0:T(8,128)(2,1)S(1)}, bf16[40,320]{1,0:T(8,128)(2,1)S(1)}, u32[]{:S(2)}, u32[]{:S(2)}) collective-permute-start(bf16[40,320]{1,0:T(8,128)(2,1)S(1)} %get-tuple-element.64), channel_id=1, source_target_pairs={{0,6},{1,7},{2,4},{3,5},{4,2},{5,3},{6,0},{7,1},{8,14},{9,15},{10,... | collective-permute-start | bytes 76808 | tf_op jit(solution)/shard_map/ppermute | solution.py:317
  65.6 0.1 shard_map.103
  65.6 0.8 %shard_map.106 = (bf16[160,2048]{1,0:T(8,128)(2,1)S(1)}, f32[160,2048]{1,0:T(8,128)S(1)}) custom-call(bf16[320,160]{1,0:T(8,128)(2,1)S(1)} %get-tuple-element.40.own_in, bf16[320,256]{1,0:T(8,128)(2,1)S(1)} %get-tuple-element.47.refs_0_, bf16[320,256]{1,0:T(8,128)(2,1)S(1)} %collective-permute-done.1.refs_1_, ...), custom_call_target="tpu_custom_call" | custom-call | tf_op jit(solution)/shard_map/pallas_call | solution.py:32
  66.5 1.1 %shard_map.114 = (f32[160,320]{1,0:T(8,128)S(1)}, f32[160,320]{1,0:T(8,128)S(1)}) custom-call(bf16[320,160]{1,0:T(8,128)(2,1)S(1)} %get-tuple-element.39.own_out, bf16[160,2048]{1,0:T(8,128)(2,1)S(1)} %get-tuple-element.48.active, f32[160,2048]{1,0:T(8,128)S(1)} %get-tuple-element.49.slope, bf16[320,256]{1,0:T(8,128)(2,1)S(1)} %get-tuple-element.47.refs_0_, ...), custom_call_target="tpu_custom_call" | custom-call | tf_op jit(solution)/shard_map/pallas_call | solution.py:32
  67.7 0.0 collective-permute-done.29.piece_2
  67.7 2.2 %collective-permute-done.30.piece_3 = bf16[40,320]{1,0:T(8,128)(2,1)S(1)} collective-permute-done((bf16[40,320]{1,0:T(8,128)(2,1)S(1)}, bf16[40,320]{1,0:T(8,128)(2,1)S(1)}, u32[]{:S(2)}, u32[]{:S(2)}) %collective-permute-start.30) | collective-permute-done | bytes 25632 | tf_op jit(solution)/shard_map/ppermute | solution.py:317
  69.8 0.0 collective-permute-done.26.low_1
  69.8 1.3 %shard_map.119 = (f32[160,320]{1,0:T(8,128)}, f32[160,320]{1,0:T(8,128)}, f32[1,12800]{1,0:T(1,128)}, bf16[2,320,128]{2,1,0:T(8,128)(2,1)}) custom-call(bf16[320,160]{1,0:T(8,128)(2,1)S(1)} %get-tuple-element.39.own_out, bf16[160,2048]{1,0:T(8,128)(2,1)S(1)} %get-tuple-element.48.active, f32[160,2048]{1,0:T(8,128)S(1)} %get-tuple-element.49.slope, ...), custom_call_target="tpu_custom_call" | custom-call | tf_op jit(solution)/shard_map/pallas_call | solution.py:32
  (18 shorter events, 0.2 us)
Async XLA Ops:
  0.6 7.7 %copy-start = (bf16[2,128,320]{1,2,0:T(8,128)(2,1)S(1)}, bf16[2,128,320]{1,2,0:T(8,128)(2,1)}, u32[]{:S(2)}) copy-start(bf16[2,128,320]{1,2,0:T(8,128)(2,1)} %param.13) | copy-start | bytes 491524
  4.1 7.6 %collective-permute-start = (bf16[320,256]{1,0:T(8,128)(2,1)S(1)}, bf16[320,256]{1,0:T(8,128)(2,1)S(1)}, u32[]{:S(2)}, u32[]{:S(2)}) collective-permute-start(bf16[320,256]{1,0:T(8,128)(2,1)S(1)} %get-tuple-element.41), channel_id=1, source_target_pairs={{0,24},{8,16},{1,25},{9,17},{2,26},{10,18},{3,27},{11,19},{4,28},{... | collective-permute-start | bytes 491528 | tf_op jit(solution)/shard_map/ppermute | solution.py:309
  8.4 5.8 %collective-permute-start.19 = (bf16[320,256]{1,0:T(8,128)(2,1)S(1)}, bf16[320,256]{1,0:T(8,128)(2,1)S(1)}, u32[]{:S(2)}, u32[]{:S(2)}) collective-permute-start(bf16[320,256]{1,0:T(8,128)(2,1)S(1)} %get-tuple-element.44.top_low), channel_id=1, source_target_pairs={{24,28},{25,29},{26,30},{27,31},{28,24},{29,25},{30,26},{31,27}} | collective-permute-start | bytes 491528 | tf_op jit(solution)/shard_map/ppermute | solution.py:335
  9.0 6.5 %collective-permute-start.16 = (bf16[320,256]{1,0:T(8,128)(2,1)S(1)}, bf16[320,256]{1,0:T(8,128)(2,1)S(1)}, u32[]{:S(2)}, u32[]{:S(2)}) collective-permute-start(bf16[320,256]{1,0:T(8,128)(2,1)S(1)} %get-tuple-element.44.top_low), channel_id=1, source_target_pairs={{24,26},{25,27},{26,24},{27,25},{28,30},{29,31},{30,28},{31,29}} | collective-permute-start | bytes 491528 | tf_op jit(solution)/shard_map/ppermute | solution.py:335
  9.7 8.1 %collective-permute-start.10 = (bf16[320,320]{1,0:T(8,128)(2,1)S(1)}, bf16[320,320]{1,0:T(8,128)(2,1)S(1)}, u32[]{:S(2)}, u32[]{:S(2)}) collective-permute-start(bf16[320,320]{1,0:T(8,128)(2,1)S(1)} %get-tuple-element.46.w_skip), channel_id=1, source_target_pairs={{16,8},{17,9},{18,10},{19,11},{20,12},{21,13},{22,14},{23,15}} | collective-permute-start | bytes 614408 | tf_op jit(solution)/shard_map/ppermute | solution.py:309
  12.8 3.4 %collective-permute-start.8 = (bf16[320,256]{1,0:T(8,128)(2,1)S(1)}, bf16[320,256]{1,0:T(8,128)(2,1)S(1)}, u32[]{:S(2)}, u32[]{:S(2)}) collective-permute-start(bf16[320,256]{1,0:T(8,128)(2,1)S(1)} %get-tuple-element.50.chain.chain_3), channel_id=1, source_target_pairs={{24,16},{25,17},{26,18},{27,19},{28,20},{29,21},{30,22},{31,23}} | collective-permute-start | bytes 491528 | tf_op jit(solution)/shard_map/ppermute | solution.py:309
  13.5 5.0 %collective-permute-start.11 = (bf16[320,256]{1,0:T(8,128)(2,1)S(1)}, bf16[320,256]{1,0:T(8,128)(2,1)S(1)}, u32[]{:S(2)}, u32[]{:S(2)}) collective-permute-start(bf16[320,256]{1,0:T(8,128)(2,1)S(1)} %shard_map.108), channel_id=1, source_target_pairs={{24,8},{25,9},{26,10},{27,11},{28,12},{29,13},{30,14},{31,15}} | collective-permute-start | bytes 491528 | tf_op jit(solution)/shard_map/ppermute | solution.py:309
  14.2 12.7 %collective-permute-start.13 = (bf16[320,256]{1,0:T(8,128)(2,1)S(1)}, bf16[320,256]{1,0:T(8,128)(2,1)S(1)}, u32[]{:S(2)}, u32[]{:S(2)}) collective-permute-start(bf16[320,256]{1,0:T(8,128)(2,1)S(1)} %shard_map.108), channel_id=1, source_target_pairs={{24,0},{25,1},{26,2},{27,3},{28,4},{29,5},{30,6},{31,7}} | collective-permute-start | bytes 491528 | tf_op jit(solution)/shard_map/ppermute | solution.py:309
  15.5 12.5 %collective-permute-start.20 = (bf16[320,256]{1,0:T(8,128)(2,1)S(1)}, bf16[320,256]{1,0:T(8,128)(2,1)S(1)}, u32[]{:S(2)}, u32[]{:S(2)}) collective-permute-start(bf16[320,256]{1,0:T(8,128)(2,1)S(1)} %collective-permute-done.19.top), channel_id=1, source_target_pairs={{24,26},{25,27},{26,24},{27,25},{28,30},{29,31},{30,28},{31,29}} | collective-permute-start | bytes 491528 | tf_op jit(solution)/shard_map/ppermute | solution.py:335
  16.2 11.8 %collective-permute-start.1 = (bf16[320,256]{1,0:T(8,128)(2,1)S(1)}, bf16[320,256]{1,0:T(8,128)(2,1)S(1)}, u32[]{:S(2)}, u32[]{:S(2)}) collective-permute-start(bf16[320,256]{1,0:T(8,128)(2,1)S(1)} %get-tuple-element.47.refs_0_), channel_id=1, source_target_pairs={{0,2},{1,3},{2,0},{3,1},{4,6},{5,7},{6,4},{7,5},{8,10},{9,11},{10,... | collective-permute-start | bytes 491528 | tf_op jit(solution)/shard_map/ppermute | solution.py:317
  17.9 10.9 %collective-permute-start.9 = (bf16[320,256]{1,0:T(8,128)(2,1)S(1)}, bf16[320,256]{1,0:T(8,128)(2,1)S(1)}, u32[]{:S(2)}, u32[]{:S(2)}) collective-permute-start(bf16[320,256]{1,0:T(8,128)(2,1)S(1)} %shard_map.107.chain_2), channel_id=1, source_target_pairs={{16,8},{17,9},{18,10},{19,11},{20,12},{21,13},{22,14},{23,15}} | collective-permute-start | bytes 491528 | tf_op jit(solution)/shard_map/ppermute | solution.py:309
  18.5 10.9 %collective-permute-start.2 = (bf16[320,256]{1,0:T(8,128)(2,1)S(1)}, bf16[320,256]{1,0:T(8,128)(2,1)S(1)}, u32[]{:S(2)}, u32[]{:S(2)}) collective-permute-start(bf16[320,256]{1,0:T(8,128)(2,1)S(1)} %get-tuple-element.47.refs_0_), channel_id=1, source_target_pairs={{0,6},{1,7},{2,4},{3,5},{4,2},{5,3},{6,0},{7,1},{8,14},{9,15},{10,... | collective-permute-start | bytes 491528 | tf_op jit(solution)/shard_map/ppermute | solution.py:317
  26.9 9.8 %collective-permute-start.6 = (bf16[320,256]{1,0:T(8,128)(2,1)S(1)}, bf16[320,256]{1,0:T(8,128)(2,1)S(1)}, u32[]{:S(2)}, u32[]{:S(2)}) collective-permute-start(bf16[320,256]{1,0:T(8,128)(2,1)S(1)} %get-tuple-element.47.refs_0_), channel_id=1, source_target_pairs={{0,4},{1,5},{2,6},{3,7},{4,0},{5,1},{6,2},{7,3},{8,12},{9,13},{10,... | collective-permute-start | bytes 491528 | tf_op jit(solution)/shard_map/ppermute | solution.py:317
  28.0 8.8 %collective-permute-start.3 = (bf16[320,256]{1,0:T(8,128)(2,1)S(1)}, bf16[320,256]{1,0:T(8,128)(2,1)S(1)}, u32[]{:S(2)}, u32[]{:S(2)}) collective-permute-start(bf16[320,256]{1,0:T(8,128)(2,1)S(1)} %get-tuple-element.47.refs_0_), channel_id=1, source_target_pairs={{0,1},{1,0},{2,3},{3,2},{4,5},{5,4},{6,7},{7,6},{8,9},{9,8},{10,11... | collective-permute-start | bytes 491528 | tf_op jit(solution)/shard_map/ppermute | solution.py:317
  28.0 9.3 %collective-permute-start.18 = (bf16[320,256]{1,0:T(8,128)(2,1)S(1)}, bf16[320,256]{1,0:T(8,128)(2,1)S(1)}, u32[]{:S(2)}, u32[]{:S(2)}) collective-permute-start(bf16[320,256]{1,0:T(8,128)(2,1)S(1)} %shard_map.111), channel_id=1, source_target_pairs={{16,14},{17,15},{18,12},{19,13},{20,10},{21,11},{22,8},{23,9},{24,... | collective-permute-start | bytes 491528 | tf_op jit(solution)/shard_map/ppermute | solution.py:326
  28.7 9.9 %collective-permute-start.15 = (bf16[320,256]{1,0:T(8,128)(2,1)S(1)}, bf16[320,256]{1,0:T(8,128)(2,1)S(1)}, u32[]{:S(2)}, u32[]{:S(2)}) collective-permute-start(bf16[320,256]{1,0:T(8,128)(2,1)S(1)} %shard_map.111), channel_id=1, source_target_pairs={{16,10},{17,11},{18,8},{19,9},{20,14},{21,15},{22,12},{23,13},{24,... | collective-permute-start | bytes 491528 | tf_op jit(solution)/shard_map/ppermute | solution.py:326
  29.4 10.5 %collective-permute-start.12 = (bf16[320,256]{1,0:T(8,128)(2,1)S(1)}, bf16[320,256]{1,0:T(8,128)(2,1)S(1)}, u32[]{:S(2)}, u32[]{:S(2)}) collective-permute-start(bf16[320,256]{1,0:T(8,128)(2,1)S(1)} %get-tuple-element.53.chain_1), channel_id=1, source_target_pairs={{8,0},{9,1},{10,2},{11,3},{12,4},{13,5},{14,6},{15,7}} | collective-permute-start | bytes 491528 | tf_op jit(solution)/shard_map/ppermute | solution.py:309
  36.8 3.9 %collective-permute-start.4 = (bf16[320,256]{1,0:T(8,128)(2,1)S(1)}, bf16[320,256]{1,0:T(8,128)(2,1)S(1)}, u32[]{:S(2)}, u32[]{:S(2)}) collective-permute-start(bf16[320,256]{1,0:T(8,128)(2,1)S(1)} %collective-permute-done.1.refs_1_), channel_id=1, source_target_pairs={{0,1},{1,0},{2,3},{3,2},{4,5},{5,4},{6,7},{7,6},{8,9},{9,8},{10,11... | collective-permute-start | bytes 491528 | tf_op jit(solution)/shard_map/ppermute | solution.py:317
  36.8 11.8 %collective-permute-start.5 = (bf16[320,256]{1,0:T(8,128)(2,1)S(1)}, bf16[320,256]{1,0:T(8,128)(2,1)S(1)}, u32[]{:S(2)}, u32[]{:S(2)}) collective-permute-start(bf16[320,256]{1,0:T(8,128)(2,1)S(1)} %collective-permute-done.2.refs_2_), channel_id=1, source_target_pairs={{0,1},{1,0},{2,3},{3,2},{4,5},{5,4},{6,7},{7,6},{8,9},{9,8},{10,11... | collective-permute-start | bytes 491528 | tf_op jit(solution)/shard_map/ppermute | solution.py:317
  37.3 11.3 %collective-permute-start.17 = (bf16[320,256]{1,0:T(8,128)(2,1)S(1)}, bf16[320,256]{1,0:T(8,128)(2,1)S(1)}, u32[]{:S(2)}, u32[]{:S(2)}) collective-permute-start(bf16[320,256]{1,0:T(8,128)(2,1)S(1)} %get-tuple-element.55), channel_id=1, source_target_pairs={{8,6},{9,7},{10,4},{11,5},{12,2},{13,3},{14,0},{15,1}} | collective-permute-start | bytes 491528 | tf_op jit(solution)/shard_map/ppermute | solution.py:326
  38.6 19.2 %collective-permute-start.14 = (bf16[320,256]{1,0:T(8,128)(2,1)S(1)}, bf16[320,256]{1,0:T(8,128)(2,1)S(1)}, u32[]{:S(2)}, u32[]{:S(2)}) collective-permute-start(bf16[320,256]{1,0:T(8,128)(2,1)S(1)} %get-tuple-element.55), channel_id=1, source_target_pairs={{8,2},{9,3},{10,0},{11,1},{12,6},{13,7},{14,4},{15,5}} | collective-permute-start | bytes 491528 | tf_op jit(solution)/shard_map/ppermute | solution.py:326
  40.0 17.8 %collective-permute-start.25 = (bf16[320,256]{1,0:T(8,128)(2,1)S(1)}, bf16[320,256]{1,0:T(8,128)(2,1)S(1)}, u32[]{:S(2)}, u32[]{:S(2)}) collective-permute-start(bf16[320,256]{1,0:T(8,128)(2,1)S(1)} %shard_map.115), channel_id=1, source_target_pairs={{8,12},{9,13},{10,14},{11,15},{12,8},{13,9},{14,10},{15,11},{16,20... | collective-permute-start | bytes 491528 | tf_op jit(solution)/shard_map/ppermute | solution.py:335
  40.7 17.7 %collective-permute-start.24 = (bf16[320,256]{1,0:T(8,128)(2,1)S(1)}, bf16[320,256]{1,0:T(8,128)(2,1)S(1)}, u32[]{:S(2)}, u32[]{:S(2)}) collective-permute-start(bf16[320,256]{1,0:T(8,128)(2,1)S(1)} %shard_map.110.refs_6_.grad_low), channel_id=1, source_target_pairs={{0,4},{1,5},{2,6},{3,7},{4,0},{5,1},{6,2},{7,3}} | collective-permute-start | bytes 491528 | tf_op jit(solution)/shard_map/ppermute | solution.py:335
  48.6 9.9 %collective-permute-start.27 = (bf16[4,40,320]{2,1,0:T(8,128)(2,1)S(1)}, bf16[4,40,320]{2,1,0:T(8,128)(2,1)S(1)}, u32[]{:S(2)}, u32[]{:S(2)}) collective-permute-start(bf16[4,40,320]{2,1,0:T(8,128)(2,1)S(1)} %get-tuple-element.60), channel_id=1, source_target_pairs={{0,1},{1,0},{2,3},{3,2},{4,5},{5,4},{6,7},{7,6},{8,9},{9,8},{10,11... | collective-permute-start | bytes 307208 | tf_op jit(solution)/shard_map/ppermute | solution.py:317
  48.7 10.4 %collective-permute-start.7 = (bf16[320,256]{1,0:T(8,128)(2,1)S(1)}, bf16[320,256]{1,0:T(8,128)(2,1)S(1)}, u32[]{:S(2)}, u32[]{:S(2)}) collective-permute-start(bf16[320,256]{1,0:T(8,128)(2,1)S(1)} %collective-permute-done.6.refs_6_.normed_0), channel_id=1, source_target_pairs={{0,1},{1,0},{2,3},{3,2},{4,5},{5,4},{6,7},{7,6},{8,9},{9,8},{10,11... | collective-permute-start | bytes 491528 | tf_op jit(solution)/shard_map/ppermute | solution.py:317
  57.8 3.1 %collective-permute-start.23 = (bf16[320,256]{1,0:T(8,128)(2,1)S(1)}, bf16[320,256]{1,0:T(8,128)(2,1)S(1)}, u32[]{:S(2)}, u32[]{:S(2)}) collective-permute-start(bf16[320,256]{1,0:T(8,128)(2,1)S(1)} %shard_map.113.refs_8_), channel_id=1, source_target_pairs={{0,1},{1,0},{2,3},{3,2},{4,5},{5,4},{6,7},{7,6},{8,9},{9,8},{10,11... | collective-permute-start | bytes 491528 | tf_op jit(solution)/shard_map/ppermute | solution.py:317
  57.8 6.3 %collective-permute-start.22 = (bf16[320,256]{1,0:T(8,128)(2,1)S(1)}, bf16[320,256]{1,0:T(8,128)(2,1)S(1)}, u32[]{:S(2)}, u32[]{:S(2)}) collective-permute-start(bf16[320,256]{1,0:T(8,128)(2,1)S(1)} %shard_map.112.refs_7_), channel_id=1, source_target_pairs={{0,1},{1,0},{2,3},{3,2},{4,5},{5,4},{6,7},{7,6},{8,9},{9,8},{10,11... | collective-permute-start | bytes 491528 | tf_op jit(solution)/shard_map/ppermute | solution.py:317
  58.4 8.1 %collective-permute-start.21 = (bf16[320,256]{1,0:T(8,128)(2,1)S(1)}, bf16[320,256]{1,0:T(8,128)(2,1)S(1)}, u32[]{:S(2)}, u32[]{:S(2)}) collective-permute-start(bf16[320,256]{1,0:T(8,128)(2,1)S(1)} %shard_map.110.refs_6_.grad_low), channel_id=1, source_target_pairs={{0,1},{1,0},{2,3},{3,2},{4,5},{5,4},{6,7},{7,6},{8,9},{9,8},{10,11... | collective-permute-start | bytes 491528 | tf_op jit(solution)/shard_map/ppermute | solution.py:317
  58.5 11.3 %collective-permute-start.26 = (bf16[320,256]{1,0:T(8,128)(2,1)S(1)}, bf16[320,256]{1,0:T(8,128)(2,1)S(1)}, u32[]{:S(2)}, u32[]{:S(2)}) collective-permute-start(bf16[320,256]{1,0:T(8,128)(2,1)S(1)} %shard_map.116.low_0), channel_id=1, source_target_pairs={{0,1},{1,0},{2,3},{3,2},{4,5},{5,4},{6,7},{7,6},{8,9},{9,8},{10,11... | collective-permute-start | bytes 491528 | tf_op jit(solution)/shard_map/ppermute | solution.py:317
  59.0 8.6 %collective-permute-start.28 = (bf16[40,320]{1,0:T(8,128)(2,1)S(1)}, bf16[40,320]{1,0:T(8,128)(2,1)S(1)}, u32[]{:S(2)}, u32[]{:S(2)}) collective-permute-start(bf16[40,320]{1,0:T(8,128)(2,1)S(1)} %get-tuple-element.62), channel_id=1, source_target_pairs={{0,2},{1,3},{2,0},{3,1},{4,6},{5,7},{6,4},{7,5},{8,10},{9,11},{10,... | collective-permute-start | bytes 76808 | tf_op jit(solution)/shard_map/ppermute | solution.py:317
  60.9 6.8 %collective-permute-start.29 = (bf16[40,320]{1,0:T(8,128)(2,1)S(1)}, bf16[40,320]{1,0:T(8,128)(2,1)S(1)}, u32[]{:S(2)}, u32[]{:S(2)}) collective-permute-start(bf16[40,320]{1,0:T(8,128)(2,1)S(1)} %get-tuple-element.63), channel_id=1, source_target_pairs={{0,4},{1,5},{2,6},{3,7},{4,0},{5,1},{6,2},{7,3},{8,12},{9,13},{10,... | collective-permute-start | bytes 76808 | tf_op jit(solution)/shard_map/ppermute | solution.py:317
  64.2 5.7 %collective-permute-start.30 = (bf16[40,320]{1,0:T(8,128)(2,1)S(1)}, bf16[40,320]{1,0:T(8,128)(2,1)S(1)}, u32[]{:S(2)}, u32[]{:S(2)}) collective-permute-start(bf16[40,320]{1,0:T(8,128)(2,1)S(1)} %get-tuple-element.64), channel_id=1, source_target_pairs={{0,6},{1,7},{2,4},{3,5},{4,2},{5,3},{6,0},{7,1},{8,14},{9,15},{10,... | collective-permute-start | bytes 76808 | tf_op jit(solution)/shard_map/ppermute | solution.py:317

commit v11 on v10

--- a/solution.py
+++ b/solution.py
@@ -60,10 +60,16 @@
         pltpu.make_async_copy(source, target, sems.at[index])
         for index, (source, target) in enumerate(zip(distant, local))
     ]
-    for copy in copies:
-        copy.start()
     times, table, w_skip, inputs, w_in, w_out = local
     encoder = lax.axis_index("section") < 2
+
+    @pl.when(encoder)
+    def _():
+        for copy in copies[:2]:
+            copy.start()
+
+    for copy in copies[2:]:
+        copy.start()
 
     @pl.when(encoder)
     def _():
@@ -88,7 +94,7 @@
 
     @pl.when(jnp.logical_not(encoder))
     def _():
-        for copy in copies:
+        for copy in copies[2:]:
             copy.wait()
 
 
@@ -404,8 +410,8 @@
     (own_low,) = call(own_body, [low], low_1, low_2)
     middle = {m: from_next(prior, [1, 2], count, m) for m in (2, 6)}
     middle[4] = within(own_low, [1, 2], count, 4)
-    late = {m: from_next(ahead, [0], count, m) for m in (2, 6)}
-    late[4] = within(grad_low, [0], count, 4)
+    late = {m: within(grad_low, [0], count, m) for m in (2, 4)}
+    late[6] = from_next(ahead, [0], count, 6)
     low_2, low_4, low_6 = (
         call(merge_body, [low], late[mask], middle[mask], tops[mask])[0]
         for mask in (2, 4, 6)

time: 71.9 us -> 73.3 us (1.019)
    ppermute x4 -> x3, waiting for transfers between devices: 8.58 us -> 0.98 us  [from_next(): return lax.ppermute(value, ('section', 'dp'), pairs)]
    ppermute x7, waiting for transfers between devices: 7.22 us -> 14.4 us  [hop(): return lax.ppermute(value, 'section', pairs)]
    ppermute x5 -> x6, waiting for transfers between devices: 0.01 us -> 4.75 us  [within(): return lax.ppermute(value, ('section', 'dp'), pairs)]
    ppermute x15, waiting for transfers between devices: 8.25 us -> 4.11 us  [exchange(): return lax.ppermute(value, 'dp', [(i, i ^ mask) for i in range(count)])]
    ppermute x15, starting transfers between devices: 14 us -> 15.7 us  [exchange(): return lax.ppermute(value, 'dp', [(i, i ^ mask) for i in range(count)])]
    ppermute x4 -> x3, starting transfers between devices: 3.92 us -> 2.62 us  [from_next(): return lax.ppermute(value, ('section', 'dp'), pairs)]
    ppermute x5 -> x6, starting transfers between devices: 9.05 us -> 9.36 us  [within(): return lax.ppermute(value, ('section', 'dp'), pairs)]
  transfers between devices with their start and end apart: 31 -> 31, of which waited for: 5 -> 8; matrix products, arithmetic and copies ran while one was open for 0% -> 0% of each run, Pallas kernels for 7% -> 7%
where the time goes in v11:
time: 73.3 us; the launch traced here: 72 us
  starting transfers between devices  37 us (50%)
  waiting for transfers between devices  24.3 us (33%)
  Pallas kernels  9.64 us (13%)
  between operations  1.03 us (1%)
    ppermute x15, starting transfers between devices, exchange(): return lax.ppermute(value, 'dp', [(i, i ^ mask) for i in range(count)])  15.7 us
    ppermute x7, waiting for transfers between devices, hop(): return lax.ppermute(value, 'section', pairs)  14.4 us
    pallas_call x18, Pallas kernels, call(): pl.pallas_call(body, out_shape=[jax.ShapeDtypeStruct(shape, kind) for sha...  9.64 us
    ppermute x6, starting transfers between devices, within(): return lax.ppermute(value, ('section', 'dp'), pairs)  9.36 us
    ppermute x7, starting transfers between devices, hop(): return lax.ppermute(value, 'section', pairs)  9.35 us
    ppermute x6, waiting for transfers between devices, within(): return lax.ppermute(value, ('section', 'dp'), pairs)  4.75 us
    ppermute x15, waiting for transfers between devices, exchange(): return lax.ppermute(value, 'dp', [(i, i ^ mask) for i in range(count)])  4.11 us
    ppermute x3, starting transfers between devices, from_next(): return lax.ppermute(value, ('section', 'dp'), pairs)  2.62 us
  transfers between devices with their start and end apart: 31, of which 8 were waited for; matrix products, arithmetic and copies ran while one was open for 0% of the time, Pallas kernels for 7%

profile of v11, /device:TPU:0, one launch (start us, length us, event | category | flops | bytes accessed | tf_op | source)
XLA Modules:
  0.0 72.0 jit_solution(13790516864920579201)
XLA Ops:
  0.6 3.5 %shard_map.102 = (bf16[320,256]{1,0:T(8,128)(2,1)S(1)}, bf16[320,256]{1,0:T(8,128)(2,1)S(1)}, bf16[320,320]{1,0:T(8,128)(2,1)S(1)}, bf16[2,320,128]{2,1,0:T(8,12...) custom-call(s32[2,128]{1,0:T(2,128)} %refs_0_.1, bf16[320,1000]{1,0:T(8,128)(2,1)} %bitcast.20, ...), custom_call_target="tpu_custom_call" | custom-call | tf_op jit(solution)/shard_map/pallas_call | solution.py:32
  4.1 4.1 %collective-permute-start = (bf16[320,256]{1,0:T(8,128)(2,1)S(1)}, bf16[320,256]{1,0:T(8,128)(2,1)S(1)}, u32[]{:S(2)}, u32[]{:S(2)}) collective-permute-start(bf16[320,256]{1,0:T(8,128)(2,1)S(1)} %get-tuple-element.41), channel_id=1, source_target_pairs={{0,24},{8,16},{1,25},{9,17},{2,26},{10,18},{3,27},{11,19},{4,28},{... | collective-permute-start | bytes 491528 | tf_op jit(solution)/shard_map/ppermute | solution.py:315
  8.2 0.7 collective-permute-start.19
  8.9 2.7 %collective-permute-done.received = bf16[320,256]{1,0:T(8,128)(2,1)S(1)} collective-permute-done((bf16[320,256]{1,0:T(8,128)(2,1)S(1)}, bf16[320,256]{1,0:T(8,128)(2,1)S(1)}, u32[]{:S(2)}, u32[]{:S(2)}) %collective-permute-start) | collective-permute-done | bytes 163872 | tf_op jit(solution)/shard_map/ppermute | solution.py:315
  11.6 1.1 %shard_map.105 = (bf16[320,256]{1,0:T(8,128)(2,1)S(1)}, bf16[320,256]{1,0:T(8,128)(2,1)S(1)}, f32[320,256]{1,0:T(8,128)S(1)}, f32[1280,256]{1,0:T(8,128)S(1)}, bf16[320,256]{1,0:T(8,128)(2,1)S(1)}) custom-call(bf16[320,256]{1,0:T(8,128)(2,1)S(1)} %collective-permute-done.received, bf16[320,256]{1,0:T(8,128)(2,1)S(1)} %get-tuple-element.42.embed, ...), custom_call_target="tpu_custom_call" | custom-call | tf_op jit(solution)/shard_map/pallas_call | solution.py:32
  12.7 0.7 collective-permute-start.8
  13.4 0.7 collective-permute-start.10
  14.1 0.7 collective-permute-start.16
  14.8 0.7 collective-permute-start.11
  15.4 0.0 collective-permute-done.19.top
  15.5 1.3 %collective-permute-start.13 = (bf16[320,256]{1,0:T(8,128)(2,1)S(1)}, bf16[320,256]{1,0:T(8,128)(2,1)S(1)}, u32[]{:S(2)}, u32[]{:S(2)}) collective-permute-start(bf16[320,256]{1,0:T(8,128)(2,1)S(1)} %shard_map.108), channel_id=1, source_target_pairs={{24,0},{25,1},{26,2},{27,3},{28,4},{29,5},{30,6},{31,7}} | collective-permute-start | bytes 491528 | tf_op jit(solution)/shard_map/ppermute | solution.py:315
  16.8 0.0 collective-permute-done.8.received.low_2
  16.8 0.7 collective-permute-start.20
  17.5 0.0 collective-permute-done.16.top
  17.5 0.7 collective-permute-start.9
  18.2 0.0 collective-permute-done.10.w_mirror
  18.2 1.6 %collective-permute-start.1 = (bf16[320,256]{1,0:T(8,128)(2,1)S(1)}, bf16[320,256]{1,0:T(8,128)(2,1)S(1)}, u32[]{:S(2)}, u32[]{:S(2)}) collective-permute-start(bf16[320,256]{1,0:T(8,128)(2,1)S(1)} %get-tuple-element.47.refs_0_), channel_id=1, source_target_pairs={{0,2},{1,3},{2,0},{3,1},{4,6},{5,7},{6,4},{7,5},{8,10},{9,11},{10,... | collective-permute-start | bytes 491528 | tf_op jit(solution)/shard_map/ppermute | solution.py:323
  19.8 0.0 collective-permute-done.11.skip_far
  19.8 2.5 %collective-permute-start.2 = (bf16[320,256]{1,0:T(8,128)(2,1)S(1)}, bf16[320,256]{1,0:T(8,128)(2,1)S(1)}, u32[]{:S(2)}, u32[]{:S(2)}) collective-permute-start(bf16[320,256]{1,0:T(8,128)(2,1)S(1)} %get-tuple-element.47.refs_0_), channel_id=1, source_target_pairs={{0,6},{1,7},{2,4},{3,5},{4,2},{5,3},{6,0},{7,1},{8,14},{9,15},{10,... | collective-permute-start | bytes 491528 | tf_op jit(solution)/shard_map/ppermute | solution.py:323
  22.3 6.6 %collective-permute-done.13.skip_far = bf16[320,256]{1,0:T(8,128)(2,1)S(1)} collective-permute-done((bf16[320,256]{1,0:T(8,128)(2,1)S(1)}, bf16[320,256]{1,0:T(8,128)(2,1)S(1)}, u32[]{:S(2)}, u32[]{:S(2)}) %collective-permute-start.13) | collective-permute-done | bytes 163872 | tf_op jit(solution)/shard_map/ppermute | solution.py:315
  28.9 2.6 %collective-permute-start.6 = (bf16[320,256]{1,0:T(8,128)(2,1)S(1)}, bf16[320,256]{1,0:T(8,128)(2,1)S(1)}, u32[]{:S(2)}, u32[]{:S(2)}) collective-permute-start(bf16[320,256]{1,0:T(8,128)(2,1)S(1)} %get-tuple-element.47.refs_0_), channel_id=1, source_target_pairs={{0,4},{1,5},{2,6},{3,7},{4,0},{5,1},{6,2},{7,3},{8,12},{9,13},{10,... | collective-permute-start | bytes 491528 | tf_op jit(solution)/shard_map/ppermute | solution.py:323
  31.5 0.0 collective-permute-done.20.top
  31.5 0.0 collective-permute-start.3
  31.5 0.7 collective-permute-start.18
  32.2 0.0 collective-permute-done.1.refs_1_
  32.2 1.3 %collective-permute-start.12 = (bf16[320,256]{1,0:T(8,128)(2,1)S(1)}, bf16[320,256]{1,0:T(8,128)(2,1)S(1)}, u32[]{:S(2)}, u32[]{:S(2)}) collective-permute-start(bf16[320,256]{1,0:T(8,128)(2,1)S(1)} %get-tuple-element.53.chain_1), channel_id=1, source_target_pairs={{8,0},{9,1},{10,2},{11,3},{12,4},{13,5},{14,6},{15,7}} | collective-permute-start | bytes 491528 | tf_op jit(solution)/shard_map/ppermute | solution.py:315
  33.5 0.7 collective-permute-start.15
  34.2 2.8 %collective-permute-done.6.refs_6_.normed_0 = bf16[320,256]{1,0:T(8,128)(2,1)S(1)} collective-permute-done((bf16[320,256]{1,0:T(8,128)(2,1)S(1)}, bf16[320,256]{1,0:T(8,128)(2,1)S(1)}, u32[]{:S(2)}, u32[]{:S(2)}) %collective-permute-start.6) | collective-permute-done | bytes 163872 | tf_op jit(solution)/shard_map/ppermute | solution.py:323
  36.9 0.0 collective-permute-start.4
  36.9 0.5 collective-permute-start.5
  37.4 1.3 %collective-permute-start.17 = (bf16[320,256]{1,0:T(8,128)(2,1)S(1)}, bf16[320,256]{1,0:T(8,128)(2,1)S(1)}, u32[]{:S(2)}, u32[]{:S(2)}) collective-permute-start(bf16[320,256]{1,0:T(8,128)(2,1)S(1)} %get-tuple-element.55), channel_id=1, source_target_pairs={{8,6},{9,7},{10,4},{11,5},{12,2},{13,3},{14,0},{15,1}} | collective-permute-start | bytes 491528 | tf_op jit(solution)/shard_map/ppermute | solution.py:332
  38.8 5.1 %collective-permute-done.12.received = bf16[320,256]{1,0:T(8,128)(2,1)S(1)} collective-permute-done((bf16[320,256]{1,0:T(8,128)(2,1)S(1)}, bf16[320,256]{1,0:T(8,128)(2,1)S(1)}, u32[]{:S(2)}, u32[]{:S(2)}) %collective-permute-start.12) | collective-permute-done | bytes 163872 | tf_op jit(solution)/shard_map/ppermute | solution.py:315
  43.9 0.7 collective-permute-start.25
  44.6 0.1 shard_map.110.refs_6_.grad_low
  44.7 0.0 collective-permute-done.15.middle
  44.7 2.6 %collective-permute-start.14 = (bf16[320,256]{1,0:T(8,128)(2,1)S(1)}, bf16[320,256]{1,0:T(8,128)(2,1)S(1)}, u32[]{:S(2)}, u32[]{:S(2)}) collective-permute-start(bf16[320,256]{1,0:T(8,128)(2,1)S(1)} %shard_map.110.refs_6_.grad_low), channel_id=1, source_target_pairs={{0,2},{1,3},{2,0},{3,1},{4,6},{5,7},{6,4},{7,5}} | collective-permute-start | bytes 491528 | tf_op jit(solution)/shard_map/ppermute | solution.py:341
  47.3 0.0 collective-permute-done.4.refs_4_
  47.3 4.1 %collective-permute-start.24 = (bf16[320,256]{1,0:T(8,128)(2,1)S(1)}, bf16[320,256]{1,0:T(8,128)(2,1)S(1)}, u32[]{:S(2)}, u32[]{:S(2)}) collective-permute-start(bf16[320,256]{1,0:T(8,128)(2,1)S(1)} %shard_map.110.refs_6_.grad_low), channel_id=1, source_target_pairs={{0,4},{1,5},{2,6},{3,7},{4,0},{5,1},{6,2},{7,3}} | collective-permute-start | bytes 491528 | tf_op jit(solution)/shard_map/ppermute | solution.py:341
  51.4 1.5 %shard_map.117 = (bf16[320,256]{1,0:T(8,128)(2,1)S(1)}, f32[4,40,320]{2,1,0:T(8,128)S(1)}, bf16[4,40,320]{2,1,0:T(8,128)(2,1)S(1)}) custom-call(bf16[320,256]{1,0:T(8,128)(2,1)S(1)} %shard_map.110.refs_6_.grad_low, bf16[320,256]{1,0:T(8,128)(2,1)S(1)} %collective-permute-done.12.received, bf16[320,256]{1,0:T(8,128)(2,1)S(1)} %collective-permute-done.13.skip_far, ...), custom_call_target="tpu_custom_call" | custom-call | tf_op jit(solution)/shard_map/pallas_call | solution.py:32
  52.9 0.1 collective-permute-start.27
  52.9 1.0 %collective-permute-done.17.late = bf16[320,256]{1,0:T(8,128)(2,1)S(1)} collective-permute-done((bf16[320,256]{1,0:T(8,128)(2,1)S(1)}, bf16[320,256]{1,0:T(8,128)(2,1)S(1)}, u32[]{:S(2)}, u32[]{:S(2)}) %collective-permute-start.17) | collective-permute-done | bytes 163872 | tf_op jit(solution)/shard_map/ppermute | solution.py:332
  53.9 0.0 collective-permute-start.7
  54.0 0.0 collective-permute-done.25.middle
  54.0 0.6 collective-permute-start.23
  54.5 0.1 collective-permute-start.21
  54.7 4.7 %collective-permute-done.24.late = bf16[320,256]{1,0:T(8,128)(2,1)S(1)} collective-permute-done((bf16[320,256]{1,0:T(8,128)(2,1)S(1)}, bf16[320,256]{1,0:T(8,128)(2,1)S(1)}, u32[]{:S(2)}, u32[]{:S(2)}) %collective-permute-start.24) | collective-permute-done | bytes 163872 | tf_op jit(solution)/shard_map/ppermute | solution.py:341
  59.4 0.0 collective-permute-start.22
  59.4 0.0 collective-permute-done.27.given
  59.4 0.6 collective-permute-start.26
  60.0 0.0 collective-permute-done.7.refs_7_.normed_1
  60.1 4.7 %collective-permute-start.28 = (bf16[40,320]{1,0:T(8,128)(2,1)S(1)}, bf16[40,320]{1,0:T(8,128)(2,1)S(1)}, u32[]{:S(2)}, u32[]{:S(2)}) collective-permute-start(bf16[40,320]{1,0:T(8,128)(2,1)S(1)} %get-tuple-element.62), channel_id=1, source_target_pairs={{0,2},{1,3},{2,0},{3,1},{4,6},{5,7},{6,4},{7,5},{8,10},{9,11},{10,... | collective-permute-start | bytes 76808 | tf_op jit(solution)/shard_map/ppermute | solution.py:323
  64.8 0.0 collective-permute-done.23.refs_11_
  64.8 0.0 collective-permute-start.29
  64.8 0.0 collective-permute-done.21.refs_9_
  64.8 2.5 %collective-permute-start.30 = (bf16[40,320]{1,0:T(8,128)(2,1)S(1)}, bf16[40,320]{1,0:T(8,128)(2,1)S(1)}, u32[]{:S(2)}, u32[]{:S(2)}) collective-permute-start(bf16[40,320]{1,0:T(8,128)(2,1)S(1)} %get-tuple-element.64), channel_id=1, source_target_pairs={{0,6},{1,7},{2,4},{3,5},{4,2},{5,3},{6,0},{7,1},{8,14},{9,15},{10,... | collective-permute-start | bytes 76808 | tf_op jit(solution)/shard_map/ppermute | solution.py:323
  67.3 0.1 shard_map.103
  67.3 0.8 %shard_map.106 = (bf16[160,2048]{1,0:T(8,128)(2,1)S(1)}, f32[160,2048]{1,0:T(8,128)S(1)}) custom-call(bf16[320,160]{1,0:T(8,128)(2,1)S(1)} %get-tuple-element.40.own_in, bf16[320,256]{1,0:T(8,128)(2,1)S(1)} %get-tuple-element.47.refs_0_, bf16[320,256]{1,0:T(8,128)(2,1)S(1)} %collective-permute-done.1.refs_1_, ...), custom_call_target="tpu_custom_call" | custom-call | tf_op jit(solution)/shard_map/pallas_call | solution.py:32
  68.2 0.0 collective-permute-done.22.refs_10_
  68.2 1.1 %shard_map.114 = (f32[160,320]{1,0:T(8,128)S(1)}, f32[160,320]{1,0:T(8,128)S(1)}) custom-call(bf16[320,160]{1,0:T(8,128)(2,1)S(1)} %get-tuple-element.39.own_out, bf16[160,2048]{1,0:T(8,128)(2,1)S(1)} %get-tuple-element.48.active, f32[160,2048]{1,0:T(8,128)S(1)} %get-tuple-element.49.slope, bf16[320,256]{1,0:T(8,128)(2,1)S(1)} %get-tuple-element.47.refs_0_, ...), custom_call_target="tpu_custom_call" | custom-call | tf_op jit(solution)/shard_map/pallas_call | solution.py:32
  69.3 0.0 collective-permute-done.28.piece_1
  69.3 0.9 %collective-permute-done.29.piece_2 = bf16[40,320]{1,0:T(8,128)(2,1)S(1)} collective-permute-done((bf16[40,320]{1,0:T(8,128)(2,1)S(1)}, bf16[40,320]{1,0:T(8,128)(2,1)S(1)}, u32[]{:S(2)}, u32[]{:S(2)}) %collective-permute-start.29) | collective-permute-done | bytes 25632 | tf_op jit(solution)/shard_map/ppermute | solution.py:323
  70.2 0.4 collective-permute-done.30.piece_3
  70.7 0.0 collective-permute-done.26.low_1
  70.7 1.3 %shard_map.119 = (f32[160,320]{1,0:T(8,128)}, f32[160,320]{1,0:T(8,128)}, f32[1,12800]{1,0:T(1,128)}, bf16[2,320,128]{2,1,0:T(8,128)(2,1)}) custom-call(bf16[320,160]{1,0:T(8,128)(2,1)S(1)} %get-tuple-element.39.own_out, bf16[160,2048]{1,0:T(8,128)(2,1)S(1)} %get-tuple-element.48.active, f32[160,2048]{1,0:T(8,128)S(1)} %get-tuple-element.49.slope, ...), custom_call_target="tpu_custom_call" | custom-call | tf_op jit(solution)/shard_map/pallas_call | solution.py:32
  (18 shorter events, 0.2 us)
Async XLA Ops:
  0.6 7.6 %copy-start = (bf16[2,128,320]{1,2,0:T(8,128)(2,1)S(1)}, bf16[2,128,320]{1,2,0:T(8,128)(2,1)}, u32[]{:S(2)}) copy-start(bf16[2,128,320]{1,2,0:T(8,128)(2,1)} %param.13) | copy-start | bytes 491524
  4.1 7.5 %collective-permute-start = (bf16[320,256]{1,0:T(8,128)(2,1)S(1)}, bf16[320,256]{1,0:T(8,128)(2,1)S(1)}, u32[]{:S(2)}, u32[]{:S(2)}) collective-permute-start(bf16[320,256]{1,0:T(8,128)(2,1)S(1)} %get-tuple-element.41), channel_id=1, source_target_pairs={{0,24},{8,16},{1,25},{9,17},{2,26},{10,18},{3,27},{11,19},{4,28},{... | collective-permute-start | bytes 491528 | tf_op jit(solution)/shard_map/ppermute | solution.py:315
  8.2 7.2 %collective-permute-start.19 = (bf16[320,256]{1,0:T(8,128)(2,1)S(1)}, bf16[320,256]{1,0:T(8,128)(2,1)S(1)}, u32[]{:S(2)}, u32[]{:S(2)}) collective-permute-start(bf16[320,256]{1,0:T(8,128)(2,1)S(1)} %get-tuple-element.44.top_low), channel_id=1, source_target_pairs={{24,28},{25,29},{26,30},{27,31},{28,24},{29,25},{30,26},{31,27}} | collective-permute-start | bytes 491528 | tf_op jit(solution)/shard_map/ppermute | solution.py:341
  12.7 4.1 %collective-permute-start.8 = (bf16[320,256]{1,0:T(8,128)(2,1)S(1)}, bf16[320,256]{1,0:T(8,128)(2,1)S(1)}, u32[]{:S(2)}, u32[]{:S(2)}) collective-permute-start(bf16[320,256]{1,0:T(8,128)(2,1)S(1)} %get-tuple-element.50.chain.chain_3), channel_id=1, source_target_pairs={{24,16},{25,17},{26,18},{27,19},{28,20},{29,21},{30,22},{31,23}} | collective-permute-start | bytes 491528 | tf_op jit(solution)/shard_map/ppermute | solution.py:315
  13.4 4.8 %collective-permute-start.10 = (bf16[320,320]{1,0:T(8,128)(2,1)S(1)}, bf16[320,320]{1,0:T(8,128)(2,1)S(1)}, u32[]{:S(2)}, u32[]{:S(2)}) collective-permute-start(bf16[320,320]{1,0:T(8,128)(2,1)S(1)} %get-tuple-element.46.w_skip), channel_id=1, source_target_pairs={{16,8},{17,9},{18,10},{19,11},{20,12},{21,13},{22,14},{23,15}} | collective-permute-start | bytes 614408 | tf_op jit(solution)/shard_map/ppermute | solution.py:315
  14.1 3.4 %collective-permute-start.16 = (bf16[320,256]{1,0:T(8,128)(2,1)S(1)}, bf16[320,256]{1,0:T(8,128)(2,1)S(1)}, u32[]{:S(2)}, u32[]{:S(2)}) collective-permute-start(bf16[320,256]{1,0:T(8,128)(2,1)S(1)} %get-tuple-element.44.top_low), channel_id=1, source_target_pairs={{24,26},{25,27},{26,24},{27,25},{28,30},{29,31},{30,28},{31,29}} | collective-permute-start | bytes 491528 | tf_op jit(solution)/shard_map/ppermute | solution.py:341
  14.8 5.0 %collective-permute-start.11 = (bf16[320,256]{1,0:T(8,128)(2,1)S(1)}, bf16[320,256]{1,0:T(8,128)(2,1)S(1)}, u32[]{:S(2)}, u32[]{:S(2)}) collective-permute-start(bf16[320,256]{1,0:T(8,128)(2,1)S(1)} %shard_map.108), channel_id=1, source_target_pairs={{24,8},{25,9},{26,10},{27,11},{28,12},{29,13},{30,14},{31,15}} | collective-permute-start | bytes 491528 | tf_op jit(solution)/shard_map/ppermute | solution.py:315
  15.5 13.4 %collective-permute-start.13 = (bf16[320,256]{1,0:T(8,128)(2,1)S(1)}, bf16[320,256]{1,0:T(8,128)(2,1)S(1)}, u32[]{:S(2)}, u32[]{:S(2)}) collective-permute-start(bf16[320,256]{1,0:T(8,128)(2,1)S(1)} %shard_map.108), channel_id=1, source_target_pairs={{24,0},{25,1},{26,2},{27,3},{28,4},{29,5},{30,6},{31,7}} | collective-permute-start | bytes 491528 | tf_op jit(solution)/shard_map/ppermute | solution.py:315
  16.8 14.7 %collective-permute-start.20 = (bf16[320,256]{1,0:T(8,128)(2,1)S(1)}, bf16[320,256]{1,0:T(8,128)(2,1)S(1)}, u32[]{:S(2)}, u32[]{:S(2)}) collective-permute-start(bf16[320,256]{1,0:T(8,128)(2,1)S(1)} %collective-permute-done.19.top), channel_id=1, source_target_pairs={{24,26},{25,27},{26,24},{27,25},{28,30},{29,31},{30,28},{31,29}} | collective-permute-start | bytes 491528 | tf_op jit(solution)/shard_map/ppermute | solution.py:341
  17.5 14.0 %collective-permute-start.9 = (bf16[320,256]{1,0:T(8,128)(2,1)S(1)}, bf16[320,256]{1,0:T(8,128)(2,1)S(1)}, u32[]{:S(2)}, u32[]{:S(2)}) collective-permute-start(bf16[320,256]{1,0:T(8,128)(2,1)S(1)} %shard_map.107.chain_2), channel_id=1, source_target_pairs={{16,8},{17,9},{18,10},{19,11},{20,12},{21,13},{22,14},{23,15}} | collective-permute-start | bytes 491528 | tf_op jit(solution)/shard_map/ppermute | solution.py:315
  18.2 14.0 %collective-permute-start.1 = (bf16[320,256]{1,0:T(8,128)(2,1)S(1)}, bf16[320,256]{1,0:T(8,128)(2,1)S(1)}, u32[]{:S(2)}, u32[]{:S(2)}) collective-permute-start(bf16[320,256]{1,0:T(8,128)(2,1)S(1)} %get-tuple-element.47.refs_0_), channel_id=1, source_target_pairs={{0,2},{1,3},{2,0},{3,1},{4,6},{5,7},{6,4},{7,5},{8,10},{9,11},{10,... | collective-permute-start | bytes 491528 | tf_op jit(solution)/shard_map/ppermute | solution.py:323
  19.8 13.7 %collective-permute-start.2 = (bf16[320,256]{1,0:T(8,128)(2,1)S(1)}, bf16[320,256]{1,0:T(8,128)(2,1)S(1)}, u32[]{:S(2)}, u32[]{:S(2)}) collective-permute-start(bf16[320,256]{1,0:T(8,128)(2,1)S(1)} %get-tuple-element.47.refs_0_), channel_id=1, source_target_pairs={{0,6},{1,7},{2,4},{3,5},{4,2},{5,3},{6,0},{7,1},{8,14},{9,15},{10,... | collective-permute-start | bytes 491528 | tf_op jit(solution)/shard_map/ppermute | solution.py:323
  28.9 8.1 %collective-permute-start.6 = (bf16[320,256]{1,0:T(8,128)(2,1)S(1)}, bf16[320,256]{1,0:T(8,128)(2,1)S(1)}, u32[]{:S(2)}, u32[]{:S(2)}) collective-permute-start(bf16[320,256]{1,0:T(8,128)(2,1)S(1)} %get-tuple-element.47.refs_0_), channel_id=1, source_target_pairs={{0,4},{1,5},{2,6},{3,7},{4,0},{5,1},{6,2},{7,3},{8,12},{9,13},{10,... | collective-permute-start | bytes 491528 | tf_op jit(solution)/shard_map/ppermute | solution.py:323
  31.5 5.5 %collective-permute-start.3 = (bf16[320,256]{1,0:T(8,128)(2,1)S(1)}, bf16[320,256]{1,0:T(8,128)(2,1)S(1)}, u32[]{:S(2)}, u32[]{:S(2)}) collective-permute-start(bf16[320,256]{1,0:T(8,128)(2,1)S(1)} %get-tuple-element.47.refs_0_), channel_id=1, source_target_pairs={{0,1},{1,0},{2,3},{3,2},{4,5},{5,4},{6,7},{7,6},{8,9},{9,8},{10,11... | collective-permute-start | bytes 491528 | tf_op jit(solution)/shard_map/ppermute | solution.py:323
  31.5 6.0 %collective-permute-start.18 = (bf16[320,256]{1,0:T(8,128)(2,1)S(1)}, bf16[320,256]{1,0:T(8,128)(2,1)S(1)}, u32[]{:S(2)}, u32[]{:S(2)}) collective-permute-start(bf16[320,256]{1,0:T(8,128)(2,1)S(1)} %shard_map.111), channel_id=1, source_target_pairs={{16,14},{17,15},{18,12},{19,13},{20,10},{21,11},{22,8},{23,9},{24,... | collective-permute-start | bytes 491528 | tf_op jit(solution)/shard_map/ppermute | solution.py:332
  32.2 11.7 %collective-permute-start.12 = (bf16[320,256]{1,0:T(8,128)(2,1)S(1)}, bf16[320,256]{1,0:T(8,128)(2,1)S(1)}, u32[]{:S(2)}, u32[]{:S(2)}) collective-permute-start(bf16[320,256]{1,0:T(8,128)(2,1)S(1)} %get-tuple-element.53.chain_1), channel_id=1, source_target_pairs={{8,0},{9,1},{10,2},{11,3},{12,4},{13,5},{14,6},{15,7}} | collective-permute-start | bytes 491528 | tf_op jit(solution)/shard_map/ppermute | solution.py:315
  33.5 11.2 %collective-permute-start.15 = (bf16[320,256]{1,0:T(8,128)(2,1)S(1)}, bf16[320,256]{1,0:T(8,128)(2,1)S(1)}, u32[]{:S(2)}, u32[]{:S(2)}) collective-permute-start(bf16[320,256]{1,0:T(8,128)(2,1)S(1)} %shard_map.111), channel_id=1, source_target_pairs={{16,10},{17,11},{18,8},{19,9},{20,14},{21,15},{22,12},{23,13},{24,... | collective-permute-start | bytes 491528 | tf_op jit(solution)/shard_map/ppermute | solution.py:332
  36.9 10.4 %collective-permute-start.4 = (bf16[320,256]{1,0:T(8,128)(2,1)S(1)}, bf16[320,256]{1,0:T(8,128)(2,1)S(1)}, u32[]{:S(2)}, u32[]{:S(2)}) collective-permute-start(bf16[320,256]{1,0:T(8,128)(2,1)S(1)} %collective-permute-done.1.refs_1_), channel_id=1, source_target_pairs={{0,1},{1,0},{2,3},{3,2},{4,5},{5,4},{6,7},{7,6},{8,9},{9,8},{10,11... | collective-permute-start | bytes 491528 | tf_op jit(solution)/shard_map/ppermute | solution.py:323
  36.9 15.9 %collective-permute-start.5 = (bf16[320,256]{1,0:T(8,128)(2,1)S(1)}, bf16[320,256]{1,0:T(8,128)(2,1)S(1)}, u32[]{:S(2)}, u32[]{:S(2)}) collective-permute-start(bf16[320,256]{1,0:T(8,128)(2,1)S(1)} %collective-permute-done.2.refs_2_), channel_id=1, source_target_pairs={{0,1},{1,0},{2,3},{3,2},{4,5},{5,4},{6,7},{7,6},{8,9},{9,8},{10,11... | collective-permute-start | bytes 491528 | tf_op jit(solution)/shard_map/ppermute | solution.py:323
  37.4 16.5 %collective-permute-start.17 = (bf16[320,256]{1,0:T(8,128)(2,1)S(1)}, bf16[320,256]{1,0:T(8,128)(2,1)S(1)}, u32[]{:S(2)}, u32[]{:S(2)}) collective-permute-start(bf16[320,256]{1,0:T(8,128)(2,1)S(1)} %get-tuple-element.55), channel_id=1, source_target_pairs={{8,6},{9,7},{10,4},{11,5},{12,2},{13,3},{14,0},{15,1}} | collective-permute-start | bytes 491528 | tf_op jit(solution)/shard_map/ppermute | solution.py:332
  43.9 10.0 %collective-permute-start.25 = (bf16[320,256]{1,0:T(8,128)(2,1)S(1)}, bf16[320,256]{1,0:T(8,128)(2,1)S(1)}, u32[]{:S(2)}, u32[]{:S(2)}) collective-permute-start(bf16[320,256]{1,0:T(8,128)(2,1)S(1)} %shard_map.115), channel_id=1, source_target_pairs={{8,12},{9,13},{10,14},{11,15},{12,8},{13,9},{14,10},{15,11},{16,20... | collective-permute-start | bytes 491528 | tf_op jit(solution)/shard_map/ppermute | solution.py:341
  44.7 9.9 %collective-permute-start.14 = (bf16[320,256]{1,0:T(8,128)(2,1)S(1)}, bf16[320,256]{1,0:T(8,128)(2,1)S(1)}, u32[]{:S(2)}, u32[]{:S(2)}) collective-permute-start(bf16[320,256]{1,0:T(8,128)(2,1)S(1)} %shard_map.110.refs_6_.grad_low), channel_id=1, source_target_pairs={{0,2},{1,3},{2,0},{3,1},{4,6},{5,7},{6,4},{7,5}} | collective-permute-start | bytes 491528 | tf_op jit(solution)/shard_map/ppermute | solution.py:341
  47.3 12.1 %collective-permute-start.24 = (bf16[320,256]{1,0:T(8,128)(2,1)S(1)}, bf16[320,256]{1,0:T(8,128)(2,1)S(1)}, u32[]{:S(2)}, u32[]{:S(2)}) collective-permute-start(bf16[320,256]{1,0:T(8,128)(2,1)S(1)} %shard_map.110.refs_6_.grad_low), channel_id=1, source_target_pairs={{0,4},{1,5},{2,6},{3,7},{4,0},{5,1},{6,2},{7,3}} | collective-permute-start | bytes 491528 | tf_op jit(solution)/shard_map/ppermute | solution.py:341
  52.9 6.6 %collective-permute-start.27 = (bf16[4,40,320]{2,1,0:T(8,128)(2,1)S(1)}, bf16[4,40,320]{2,1,0:T(8,128)(2,1)S(1)}, u32[]{:S(2)}, u32[]{:S(2)}) collective-permute-start(bf16[4,40,320]{2,1,0:T(8,128)(2,1)S(1)} %get-tuple-element.60), channel_id=1, source_target_pairs={{0,1},{1,0},{2,3},{3,2},{4,5},{5,4},{6,7},{7,6},{8,9},{9,8},{10,11... | collective-permute-start | bytes 307208 | tf_op jit(solution)/shard_map/ppermute | solution.py:323
  53.9 6.1 %collective-permute-start.7 = (bf16[320,256]{1,0:T(8,128)(2,1)S(1)}, bf16[320,256]{1,0:T(8,128)(2,1)S(1)}, u32[]{:S(2)}, u32[]{:S(2)}) collective-permute-start(bf16[320,256]{1,0:T(8,128)(2,1)S(1)} %collective-permute-done.6.refs_6_.normed_0), channel_id=1, source_target_pairs={{0,1},{1,0},{2,3},{3,2},{4,5},{5,4},{6,7},{7,6},{8,9},{9,8},{10,11... | collective-permute-start | bytes 491528 | tf_op jit(solution)/shard_map/ppermute | solution.py:323
  54.0 10.8 %collective-permute-start.23 = (bf16[320,256]{1,0:T(8,128)(2,1)S(1)}, bf16[320,256]{1,0:T(8,128)(2,1)S(1)}, u32[]{:S(2)}, u32[]{:S(2)}) collective-permute-start(bf16[320,256]{1,0:T(8,128)(2,1)S(1)} %shard_map.113.refs_8_), channel_id=1, source_target_pairs={{0,1},{1,0},{2,3},{3,2},{4,5},{5,4},{6,7},{7,6},{8,9},{9,8},{10,11... | collective-permute-start | bytes 491528 | tf_op jit(solution)/shard_map/ppermute | solution.py:323
  54.5 10.3 %collective-permute-start.21 = (bf16[320,256]{1,0:T(8,128)(2,1)S(1)}, bf16[320,256]{1,0:T(8,128)(2,1)S(1)}, u32[]{:S(2)}, u32[]{:S(2)}) collective-permute-start(bf16[320,256]{1,0:T(8,128)(2,1)S(1)} %shard_map.110.refs_6_.grad_low), channel_id=1, source_target_pairs={{0,1},{1,0},{2,3},{3,2},{4,5},{5,4},{6,7},{7,6},{8,9},{9,8},{10,11... | collective-permute-start | bytes 491528 | tf_op jit(solution)/shard_map/ppermute | solution.py:323
  59.4 8.8 %collective-permute-start.22 = (bf16[320,256]{1,0:T(8,128)(2,1)S(1)}, bf16[320,256]{1,0:T(8,128)(2,1)S(1)}, u32[]{:S(2)}, u32[]{:S(2)}) collective-permute-start(bf16[320,256]{1,0:T(8,128)(2,1)S(1)} %shard_map.112.refs_7_), channel_id=1, source_target_pairs={{0,1},{1,0},{2,3},{3,2},{4,5},{5,4},{6,7},{7,6},{8,9},{9,8},{10,11... | collective-permute-start | bytes 491528 | tf_op jit(solution)/shard_map/ppermute | solution.py:323
  59.4 11.2 %collective-permute-start.26 = (bf16[320,256]{1,0:T(8,128)(2,1)S(1)}, bf16[320,256]{1,0:T(8,128)(2,1)S(1)}, u32[]{:S(2)}, u32[]{:S(2)}) collective-permute-start(bf16[320,256]{1,0:T(8,128)(2,1)S(1)} %shard_map.116.low_0), channel_id=1, source_target_pairs={{0,1},{1,0},{2,3},{3,2},{4,5},{5,4},{6,7},{7,6},{8,9},{9,8},{10,11... | collective-permute-start | bytes 491528 | tf_op jit(solution)/shard_map/ppermute | solution.py:323
  60.1 9.3 %collective-permute-start.28 = (bf16[40,320]{1,0:T(8,128)(2,1)S(1)}, bf16[40,320]{1,0:T(8,128)(2,1)S(1)}, u32[]{:S(2)}, u32[]{:S(2)}) collective-permute-start(bf16[40,320]{1,0:T(8,128)(2,1)S(1)} %get-tuple-element.62), channel_id=1, source_target_pairs={{0,2},{1,3},{2,0},{3,1},{4,6},{5,7},{6,4},{7,5},{8,10},{9,11},{10,... | collective-permute-start | bytes 76808 | tf_op jit(solution)/shard_map/ppermute | solution.py:323
  64.8 5.4 %collective-permute-start.29 = (bf16[40,320]{1,0:T(8,128)(2,1)S(1)}, bf16[40,320]{1,0:T(8,128)(2,1)S(1)}, u32[]{:S(2)}, u32[]{:S(2)}) collective-permute-start(bf16[40,320]{1,0:T(8,128)(2,1)S(1)} %get-tuple-element.63), channel_id=1, source_target_pairs={{0,4},{1,5},{2,6},{3,7},{4,0},{5,1},{6,2},{7,3},{8,12},{9,13},{10,... | collective-permute-start | bytes 76808 | tf_op jit(solution)/shard_map/ppermute | solution.py:323
  64.8 5.9 %collective-permute-start.30 = (bf16[40,320]{1,0:T(8,128)(2,1)S(1)}, bf16[40,320]{1,0:T(8,128)(2,1)S(1)}, u32[]{:S(2)}, u32[]{:S(2)}) collective-permute-start(bf16[40,320]{1,0:T(8,128)(2,1)S(1)} %get-tuple-element.64), channel_id=1, source_target_pairs={{0,6},{1,7},{2,4},{3,5},{4,2},{5,3},{6,0},{7,1},{8,14},{9,15},{10,... | collective-permute-start | bytes 76808 | tf_op jit(solution)/shard_map/ppermute | solution.py:323

commit v12 on v11

--- a/solution.py
+++ b/solution.py
@@ -396,7 +396,7 @@
 
     part = hidden // count
     own_in, own_out = call(cut_body, [((width, part), LOW)] * 2, w_in, w_out)
-    normed_near = [normed] + [exchange(normed, count, m) for m in (2, 6, 4)]
+    normed_near = [normed] + [exchange(normed, count, m) for m in (2, 4, 6)]
     normed_all = in_turn(
         normed_near,
         [exchange(x, count, 1) for x in normed_near],
@@ -410,13 +410,13 @@
     (own_low,) = call(own_body, [low], low_1, low_2)
     middle = {m: from_next(prior, [1, 2], count, m) for m in (2, 6)}
     middle[4] = within(own_low, [1, 2], count, 4)
-    late = {m: within(grad_low, [0], count, m) for m in (2, 4)}
-    late[6] = from_next(ahead, [0], count, 6)
+    late = {m: from_next(ahead, [0], count, m) for m in (2, 6)}
+    late[4] = within(grad_low, [0], count, 4)
     low_2, low_4, low_6 = (
         call(merge_body, [low], late[mask], middle[mask], tops[mask])[0]
         for mask in (2, 4, 6)
     )
-    low_near = [grad_low, low_2, low_6, low_4]
+    low_near = [grad_low, low_2, low_4, low_6]
     low_all = in_turn(low_near, [exchange(x, count, 1) for x in low_near])
     block = (count // 2, width // count, width)
     kept, keep, give = call(

time: 73.3 us -> 77.9 us (1.063); the launches traced: 72 us -> 77.6 us
  waiting for transfers between devices: 24.3 us -> 29.9 us
    ppermute x3 -> x4, waiting for transfers between devices: 0.98 us -> 11.2 us  [from_next(): return lax.ppermute(value, ('section', 'dp'), pairs)]
    ppermute x6 -> x5, waiting for transfers between devices: 4.75 us -> 0.01 us  [within(): return lax.ppermute(value, ('section', 'dp'), pairs)]
    ppermute x6 -> x5, starting transfers between devices: 9.36 us -> 6.27 us  [within(): return lax.ppermute(value, ('section', 'dp'), pairs)]
    ppermute x15, starting transfers between devices: 15.7 us -> 17.5 us  [exchange(): return lax.ppermute(value, 'dp', [(i, i ^ mask) for i in range(count)])]
    ppermute x3 -> x4, starting transfers between devices: 2.62 us -> 3.92 us  [from_next(): return lax.ppermute(value, ('section', 'dp'), pairs)]
    ppermute x7, waiting for transfers between devices: 14.4 us -> 15.4 us  [hop(): return lax.ppermute(value, 'section', pairs)]
    ppermute x15, waiting for transfers between devices: 4.11 us -> 3.3 us  [exchange(): return lax.ppermute(value, 'dp', [(i, i ^ mask) for i in range(count)])]
  transfers between devices with their start and end apart: 31 -> 31, of which waited for: 8 -> 8; matrix products, arithmetic and copies ran while one was open for 0% -> 0% of each run, Pallas kernels for 7% -> 6%
where the time goes in v12:
time: 77.9 us; the launch traced here: 77.6 us
  starting transfers between devices  37 us (47%)
  waiting for transfers between devices  29.9 us (38%)
  Pallas kernels  9.64 us (12%)
  between operations  1.03 us (1%)
    ppermute x15, starting transfers between devices, exchange(): return lax.ppermute(value, 'dp', [(i, i ^ mask) for i in range(count)])  17.5 us
    ppermute x7, waiting for transfers between devices, hop(): return lax.ppermute(value, 'section', pairs)  15.4 us
    ppermute x4, waiting for transfers between devices, from_next(): return lax.ppermute(value, ('section', 'dp'), pairs)  11.2 us
    pallas_call x18, Pallas kernels, call(): pl.pallas_call(body, out_shape=[jax.ShapeDtypeStruct(shape, kind) for sha...  9.64 us
    ppermute x7, starting transfers between devices, hop(): return lax.ppermute(value, 'section', pairs)  9.35 us
    ppermute x5, starting transfers between devices, within(): return lax.ppermute(value, ('section', 'dp'), pairs)  6.27 us
    ppermute x4, starting transfers between devices, from_next(): return lax.ppermute(value, ('section', 'dp'), pairs)  3.92 us
    ppermute x15, waiting for transfers between devices, exchange(): return lax.ppermute(value, 'dp', [(i, i ^ mask) for i in range(count)])  3.3 us
  transfers between devices with their start and end apart: 31, of which 8 were waited for; matrix products, arithmetic and copies ran while one was open for 0% of the time, Pallas kernels for 6%

profile of v12, /device:TPU:0, one launch (start us, length us, event | category | flops | bytes accessed | tf_op | source)
XLA Modules:
  0.0 77.6 jit_solution(1602936645447575345)
XLA Ops:
  0.6 3.5 %shard_map.102 = (bf16[320,256]{1,0:T(8,128)(2,1)S(1)}, bf16[320,256]{1,0:T(8,128)(2,1)S(1)}, bf16[320,320]{1,0:T(8,128)(2,1)S(1)}, bf16[2,320,128]{2,1,0:T(8,12...) custom-call(s32[2,128]{1,0:T(2,128)} %refs_0_.1, bf16[320,1000]{1,0:T(8,128)(2,1)} %bitcast.20, ...), custom_call_target="tpu_custom_call" | custom-call | tf_op jit(solution)/shard_map/pallas_call | solution.py:32
  4.1 4.1 %collective-permute-start = (bf16[320,256]{1,0:T(8,128)(2,1)S(1)}, bf16[320,256]{1,0:T(8,128)(2,1)S(1)}, u32[]{:S(2)}, u32[]{:S(2)}) collective-permute-start(bf16[320,256]{1,0:T(8,128)(2,1)S(1)} %get-tuple-element.41), channel_id=1, source_target_pairs={{0,24},{8,16},{1,25},{9,17},{2,26},{10,18},{3,27},{11,19},{4,28},{... | collective-permute-start | bytes 491528 | tf_op jit(solution)/shard_map/ppermute | solution.py:315
  8.2 0.7 collective-permute-start.19
  8.9 2.7 %collective-permute-done.received = bf16[320,256]{1,0:T(8,128)(2,1)S(1)} collective-permute-done((bf16[320,256]{1,0:T(8,128)(2,1)S(1)}, bf16[320,256]{1,0:T(8,128)(2,1)S(1)}, u32[]{:S(2)}, u32[]{:S(2)}) %collective-permute-start) | collective-permute-done | bytes 163872 | tf_op jit(solution)/shard_map/ppermute | solution.py:315
  11.6 1.1 %shard_map.105 = (bf16[320,256]{1,0:T(8,128)(2,1)S(1)}, bf16[320,256]{1,0:T(8,128)(2,1)S(1)}, f32[320,256]{1,0:T(8,128)S(1)}, f32[1280,256]{1,0:T(8,128)S(1)}, bf16[320,256]{1,0:T(8,128)(2,1)S(1)}) custom-call(bf16[320,256]{1,0:T(8,128)(2,1)S(1)} %collective-permute-done.received, bf16[320,256]{1,0:T(8,128)(2,1)S(1)} %get-tuple-element.42.embed, ...), custom_call_target="tpu_custom_call" | custom-call | tf_op jit(solution)/shard_map/pallas_call | solution.py:32
  12.7 0.7 collective-permute-start.8
  13.4 0.7 collective-permute-start.10
  14.1 0.7 collective-permute-start.16
  14.8 0.7 collective-permute-start.11
  15.4 0.0 collective-permute-done.19.top
  15.5 1.3 %collective-permute-start.13 = (bf16[320,256]{1,0:T(8,128)(2,1)S(1)}, bf16[320,256]{1,0:T(8,128)(2,1)S(1)}, u32[]{:S(2)}, u32[]{:S(2)}) collective-permute-start(bf16[320,256]{1,0:T(8,128)(2,1)S(1)} %shard_map.108), channel_id=1, source_target_pairs={{24,0},{25,1},{26,2},{27,3},{28,4},{29,5},{30,6},{31,7}} | collective-permute-start | bytes 491528 | tf_op jit(solution)/shard_map/ppermute | solution.py:315
  16.8 0.0 collective-permute-done.8.received.low_2
  16.8 0.7 collective-permute-start.25
  17.5 0.0 collective-permute-done.16.top
  17.5 0.7 collective-permute-start.9
  18.2 0.0 collective-permute-done.10.w_mirror
  18.2 1.6 %collective-permute-start.1 = (bf16[320,256]{1,0:T(8,128)(2,1)S(1)}, bf16[320,256]{1,0:T(8,128)(2,1)S(1)}, u32[]{:S(2)}, u32[]{:S(2)}) collective-permute-start(bf16[320,256]{1,0:T(8,128)(2,1)S(1)} %get-tuple-element.47.refs_0_), channel_id=1, source_target_pairs={{0,2},{1,3},{2,0},{3,1},{4,6},{5,7},{6,4},{7,5},{8,10},{9,11},{10,... | collective-permute-start | bytes 491528 | tf_op jit(solution)/shard_map/ppermute | solution.py:323
  19.8 0.0 collective-permute-done.11.skip_far
  19.8 2.6 %collective-permute-start.2 = (bf16[320,256]{1,0:T(8,128)(2,1)S(1)}, bf16[320,256]{1,0:T(8,128)(2,1)S(1)}, u32[]{:S(2)}, u32[]{:S(2)}) collective-permute-start(bf16[320,256]{1,0:T(8,128)(2,1)S(1)} %get-tuple-element.47.refs_0_), channel_id=1, source_target_pairs={{0,4},{1,5},{2,6},{3,7},{4,0},{5,1},{6,2},{7,3},{8,12},{9,13},{10,... | collective-permute-start | bytes 491528 | tf_op jit(solution)/shard_map/ppermute | solution.py:323
  22.4 6.5 %collective-permute-done.13.skip_far = bf16[320,256]{1,0:T(8,128)(2,1)S(1)} collective-permute-done((bf16[320,256]{1,0:T(8,128)(2,1)S(1)}, bf16[320,256]{1,0:T(8,128)(2,1)S(1)}, u32[]{:S(2)}, u32[]{:S(2)}) %collective-permute-start.13) | collective-permute-done | bytes 163872 | tf_op jit(solution)/shard_map/ppermute | solution.py:315
  28.9 2.5 %collective-permute-start.6 = (bf16[320,256]{1,0:T(8,128)(2,1)S(1)}, bf16[320,256]{1,0:T(8,128)(2,1)S(1)}, u32[]{:S(2)}, u32[]{:S(2)}) collective-permute-start(bf16[320,256]{1,0:T(8,128)(2,1)S(1)} %get-tuple-element.47.refs_0_), channel_id=1, source_target_pairs={{0,6},{1,7},{2,4},{3,5},{4,2},{5,3},{6,0},{7,1},{8,14},{9,15},{10,... | collective-permute-start | bytes 491528 | tf_op jit(solution)/shard_map/ppermute | solution.py:323
  31.3 0.0 collective-permute-done.25.top
  31.3 0.0 collective-permute-start.3
  31.3 0.0 collective-permute-done.9.received
  31.3 0.7 collective-permute-start.24
  32.1 0.0 collective-permute-done.1.refs_1_
  32.1 1.3 %collective-permute-start.12 = (bf16[320,256]{1,0:T(8,128)(2,1)S(1)}, bf16[320,256]{1,0:T(8,128)(2,1)S(1)}, u32[]{:S(2)}, u32[]{:S(2)}) collective-permute-start(bf16[320,256]{1,0:T(8,128)(2,1)S(1)} %get-tuple-element.53.chain_1), channel_id=1, source_target_pairs={{8,0},{9,1},{10,2},{11,3},{12,4},{13,5},{14,6},{15,7}} | collective-permute-start | bytes 491528 | tf_op jit(solution)/shard_map/ppermute | solution.py:315
  33.4 0.0 collective-permute-done.2.refs_2_
  33.4 0.7 collective-permute-start.15
  34.1 2.0 %collective-permute-done.6.refs_6_.normed_0 = bf16[320,256]{1,0:T(8,128)(2,1)S(1)} collective-permute-done((bf16[320,256]{1,0:T(8,128)(2,1)S(1)}, bf16[320,256]{1,0:T(8,128)(2,1)S(1)}, u32[]{:S(2)}, u32[]{:S(2)}) %collective-permute-start.6) | collective-permute-done | bytes 163872 | tf_op jit(solution)/shard_map/ppermute | solution.py:323
  36.1 0.0 collective-permute-start.4
  36.1 0.0 collective-permute-done.3.refs_3_
  36.1 0.5 collective-permute-start.5
  36.6 0.0 collective-permute-done.24.middle
  36.6 1.3 %collective-permute-start.14 = (bf16[320,256]{1,0:T(8,128)(2,1)S(1)}, bf16[320,256]{1,0:T(8,128)(2,1)S(1)}, u32[]{:S(2)}, u32[]{:S(2)}) collective-permute-start(bf16[320,256]{1,0:T(8,128)(2,1)S(1)} %get-tuple-element.55), channel_id=1, source_target_pairs={{8,2},{9,3},{10,0},{11,1},{12,6},{13,7},{14,4},{15,5}} | collective-permute-start | bytes 491528 | tf_op jit(solution)/shard_map/ppermute | solution.py:332
  37.9 6.3 %collective-permute-done.12.received = bf16[320,256]{1,0:T(8,128)(2,1)S(1)} collective-permute-done((bf16[320,256]{1,0:T(8,128)(2,1)S(1)}, bf16[320,256]{1,0:T(8,128)(2,1)S(1)}, u32[]{:S(2)}, u32[]{:S(2)}) %collective-permute-start.12) | collective-permute-done | bytes 163872 | tf_op jit(solution)/shard_map/ppermute | solution.py:315
  44.2 0.7 collective-permute-start.18
  44.8 0.1 shard_map.110.refs_6_.grad_low
  44.9 0.0 collective-permute-done.15.middle
  44.9 3.6 %collective-permute-start.17 = (bf16[320,256]{1,0:T(8,128)(2,1)S(1)}, bf16[320,256]{1,0:T(8,128)(2,1)S(1)}, u32[]{:S(2)}, u32[]{:S(2)}) collective-permute-start(bf16[320,256]{1,0:T(8,128)(2,1)S(1)} %shard_map.110.refs_6_.grad_low), channel_id=1, source_target_pairs={{0,4},{1,5},{2,6},{3,7},{4,0},{5,1},{6,2},{7,3}} | collective-permute-start | bytes 491528 | tf_op jit(solution)/shard_map/ppermute | solution.py:341
  48.5 0.0 collective-permute-done.4.refs_4_
  48.5 1.3 %collective-permute-start.23 = (bf16[320,256]{1,0:T(8,128)(2,1)S(1)}, bf16[320,256]{1,0:T(8,128)(2,1)S(1)}, u32[]{:S(2)}, u32[]{:S(2)}) collective-permute-start(bf16[320,256]{1,0:T(8,128)(2,1)S(1)} %get-tuple-element.55), channel_id=1, source_target_pairs={{8,6},{9,7},{10,4},{11,5},{12,2},{13,3},{14,0},{15,1}} | collective-permute-start | bytes 491528 | tf_op jit(solution)/shard_map/ppermute | solution.py:332
  49.8 1.5 %shard_map.117 = (bf16[320,256]{1,0:T(8,128)(2,1)S(1)}, f32[4,40,320]{2,1,0:T(8,128)S(1)}, bf16[4,40,320]{2,1,0:T(8,128)(2,1)S(1)}) custom-call(bf16[320,256]{1,0:T(8,128)(2,1)S(1)} %shard_map.110.refs_6_.grad_low, bf16[320,256]{1,0:T(8,128)(2,1)S(1)} %collective-permute-done.12.received, bf16[320,256]{1,0:T(8,128)(2,1)S(1)} %collective-permute-done.13.skip_far, ...), custom_call_target="tpu_custom_call" | custom-call | tf_op jit(solution)/shard_map/pallas_call | solution.py:32
  51.3 0.0 collective-permute-done.5.refs_5_
  51.3 0.1 collective-permute-start.27
  51.4 5.9 %collective-permute-done.14.late = bf16[320,256]{1,0:T(8,128)(2,1)S(1)} collective-permute-done((bf16[320,256]{1,0:T(8,128)(2,1)S(1)}, bf16[320,256]{1,0:T(8,128)(2,1)S(1)}, u32[]{:S(2)}, u32[]{:S(2)}) %collective-permute-start.14) | collective-permute-done | bytes 163872 | tf_op jit(solution)/shard_map/ppermute | solution.py:332
  57.4 0.0 collective-permute-start.7
  57.4 0.0 collective-permute-done.18.middle
  57.4 0.6 collective-permute-start.21
  58.0 0.0 collective-permute-done.17.late
  58.0 0.1 collective-permute-start.20
  58.1 5.2 %collective-permute-done.23.late = bf16[320,256]{1,0:T(8,128)(2,1)S(1)} collective-permute-done((bf16[320,256]{1,0:T(8,128)(2,1)S(1)}, bf16[320,256]{1,0:T(8,128)(2,1)S(1)}, u32[]{:S(2)}, u32[]{:S(2)}) %collective-permute-start.23) | collective-permute-done | bytes 163872 | tf_op jit(solution)/shard_map/ppermute | solution.py:332
  63.4 0.6 collective-permute-start.26
  64.0 0.0 collective-permute-done.7.refs_7_.normed_1
  64.0 6.5 %collective-permute-start.28 = (bf16[40,320]{1,0:T(8,128)(2,1)S(1)}, bf16[40,320]{1,0:T(8,128)(2,1)S(1)}, u32[]{:S(2)}, u32[]{:S(2)}) collective-permute-start(bf16[40,320]{1,0:T(8,128)(2,1)S(1)} %get-tuple-element.62), channel_id=1, source_target_pairs={{0,2},{1,3},{2,0},{3,1},{4,6},{5,7},{6,4},{7,5},{8,10},{9,11},{10,... | collective-permute-start | bytes 76808 | tf_op jit(solution)/shard_map/ppermute | solution.py:323
  70.5 2.4 %collective-permute-start.30 = (bf16[40,320]{1,0:T(8,128)(2,1)S(1)}, bf16[40,320]{1,0:T(8,128)(2,1)S(1)}, u32[]{:S(2)}, u32[]{:S(2)}) collective-permute-start(bf16[40,320]{1,0:T(8,128)(2,1)S(1)} %get-tuple-element.64), channel_id=1, source_target_pairs={{0,6},{1,7},{2,4},{3,5},{4,2},{5,3},{6,0},{7,1},{8,14},{9,15},{10,... | collective-permute-start | bytes 76808 | tf_op jit(solution)/shard_map/ppermute | solution.py:323
  72.9 0.1 shard_map.103
  73.0 0.8 %shard_map.106 = (bf16[160,2048]{1,0:T(8,128)(2,1)S(1)}, f32[160,2048]{1,0:T(8,128)S(1)}) custom-call(bf16[320,160]{1,0:T(8,128)(2,1)S(1)} %get-tuple-element.40.own_in, bf16[320,256]{1,0:T(8,128)(2,1)S(1)} %get-tuple-element.47.refs_0_, bf16[320,256]{1,0:T(8,128)(2,1)S(1)} %collective-permute-done.1.refs_1_, ...), custom_call_target="tpu_custom_call" | custom-call | tf_op jit(solution)/shard_map/pallas_call | solution.py:32
  73.8 0.0 collective-permute-done.22.refs_11_
  73.8 1.1 %shard_map.115 = (f32[160,320]{1,0:T(8,128)S(1)}, f32[160,320]{1,0:T(8,128)S(1)}) custom-call(bf16[320,160]{1,0:T(8,128)(2,1)S(1)} %get-tuple-element.39.own_out, bf16[160,2048]{1,0:T(8,128)(2,1)S(1)} %get-tuple-element.48.active, f32[160,2048]{1,0:T(8,128)S(1)} %get-tuple-element.49.slope, bf16[320,256]{1,0:T(8,128)(2,1)S(1)} %get-tuple-element.47.refs_0_, ...), custom_call_target="tpu_custom_call" | custom-call | tf_op jit(solution)/shard_map/pallas_call | solution.py:32
  75.0 0.5 collective-permute-done.29.piece_2
  75.5 0.7 collective-permute-done.30.piece_3
  76.2 0.0 collective-permute-done.26.low_1
  76.2 1.3 %shard_map.119 = (f32[160,320]{1,0:T(8,128)}, f32[160,320]{1,0:T(8,128)}, f32[1,12800]{1,0:T(1,128)}, bf16[2,320,128]{2,1,0:T(8,128)(2,1)}) custom-call(bf16[320,160]{1,0:T(8,128)(2,1)S(1)} %get-tuple-element.39.own_out, bf16[160,2048]{1,0:T(8,128)(2,1)S(1)} %get-tuple-element.48.active, f32[160,2048]{1,0:T(8,128)S(1)} %get-tuple-element.49.slope, ...), custom_call_target="tpu_custom_call" | custom-call | tf_op jit(solution)/shard_map/pallas_call | solution.py:32
  (18 shorter events, 0.2 us)
Async XLA Ops:
  0.6 7.6 %copy-start = (bf16[2,128,320]{1,2,0:T(8,128)(2,1)S(1)}, bf16[2,128,320]{1,2,0:T(8,128)(2,1)}, u32[]{:S(2)}) copy-start(bf16[2,128,320]{1,2,0:T(8,128)(2,1)} %param.13) | copy-start | bytes 491524
  4.1 7.5 %collective-permute-start = (bf16[320,256]{1,0:T(8,128)(2,1)S(1)}, bf16[320,256]{1,0:T(8,128)(2,1)S(1)}, u32[]{:S(2)}, u32[]{:S(2)}) collective-permute-start(bf16[320,256]{1,0:T(8,128)(2,1)S(1)} %get-tuple-element.41), channel_id=1, source_target_pairs={{0,24},{8,16},{1,25},{9,17},{2,26},{10,18},{3,27},{11,19},{4,28},{... | collective-permute-start | bytes 491528 | tf_op jit(solution)/shard_map/ppermute | solution.py:315
  8.2 7.2 %collective-permute-start.19 = (bf16[320,256]{1,0:T(8,128)(2,1)S(1)}, bf16[320,256]{1,0:T(8,128)(2,1)S(1)}, u32[]{:S(2)}, u32[]{:S(2)}) collective-permute-start(bf16[320,256]{1,0:T(8,128)(2,1)S(1)} %get-tuple-element.44.top_low), channel_id=1, source_target_pairs={{24,28},{25,29},{26,30},{27,31},{28,24},{29,25},{30,26},{31,27}} | collective-permute-start | bytes 491528 | tf_op jit(solution)/shard_map/ppermute | solution.py:341
  12.7 4.1 %collective-permute-start.8 = (bf16[320,256]{1,0:T(8,128)(2,1)S(1)}, bf16[320,256]{1,0:T(8,128)(2,1)S(1)}, u32[]{:S(2)}, u32[]{:S(2)}) collective-permute-start(bf16[320,256]{1,0:T(8,128)(2,1)S(1)} %get-tuple-element.50.chain.chain_3), channel_id=1, source_target_pairs={{24,16},{25,17},{26,18},{27,19},{28,20},{29,21},{30,22},{31,23}} | collective-permute-start | bytes 491528 | tf_op jit(solution)/shard_map/ppermute | solution.py:315
  13.4 4.8 %collective-permute-start.10 = (bf16[320,320]{1,0:T(8,128)(2,1)S(1)}, bf16[320,320]{1,0:T(8,128)(2,1)S(1)}, u32[]{:S(2)}, u32[]{:S(2)}) collective-permute-start(bf16[320,320]{1,0:T(8,128)(2,1)S(1)} %get-tuple-element.46.w_skip), channel_id=1, source_target_pairs={{16,8},{17,9},{18,10},{19,11},{20,12},{21,13},{22,14},{23,15}} | collective-permute-start | bytes 614408 | tf_op jit(solution)/shard_map/ppermute | solution.py:315
  14.1 3.4 %collective-permute-start.16 = (bf16[320,256]{1,0:T(8,128)(2,1)S(1)}, bf16[320,256]{1,0:T(8,128)(2,1)S(1)}, u32[]{:S(2)}, u32[]{:S(2)}) collective-permute-start(bf16[320,256]{1,0:T(8,128)(2,1)S(1)} %get-tuple-element.44.top_low), channel_id=1, source_target_pairs={{24,26},{25,27},{26,24},{27,25},{28,30},{29,31},{30,28},{31,29}} | collective-permute-start | bytes 491528 | tf_op jit(solution)/shard_map/ppermute | solution.py:341
  14.8 5.0 %collective-permute-start.11 = (bf16[320,256]{1,0:T(8,128)(2,1)S(1)}, bf16[320,256]{1,0:T(8,128)(2,1)S(1)}, u32[]{:S(2)}, u32[]{:S(2)}) collective-permute-start(bf16[320,256]{1,0:T(8,128)(2,1)S(1)} %shard_map.108), channel_id=1, source_target_pairs={{24,8},{25,9},{26,10},{27,11},{28,12},{29,13},{30,14},{31,15}} | collective-permute-start | bytes 491528 | tf_op jit(solution)/shard_map/ppermute | solution.py:315
  15.5 13.4 %collective-permute-start.13 = (bf16[320,256]{1,0:T(8,128)(2,1)S(1)}, bf16[320,256]{1,0:T(8,128)(2,1)S(1)}, u32[]{:S(2)}, u32[]{:S(2)}) collective-permute-start(bf16[320,256]{1,0:T(8,128)(2,1)S(1)} %shard_map.108), channel_id=1, source_target_pairs={{24,0},{25,1},{26,2},{27,3},{28,4},{29,5},{30,6},{31,7}} | collective-permute-start | bytes 491528 | tf_op jit(solution)/shard_map/ppermute | solution.py:315
  16.8 14.6 %collective-permute-start.25 = (bf16[320,256]{1,0:T(8,128)(2,1)S(1)}, bf16[320,256]{1,0:T(8,128)(2,1)S(1)}, u32[]{:S(2)}, u32[]{:S(2)}) collective-permute-start(bf16[320,256]{1,0:T(8,128)(2,1)S(1)} %collective-permute-done.19.top), channel_id=1, source_target_pairs={{24,26},{25,27},{26,24},{27,25},{28,30},{29,31},{30,28},{31,29}} | collective-permute-start | bytes 491528 | tf_op jit(solution)/shard_map/ppermute | solution.py:341
  17.5 13.9 %collective-permute-start.9 = (bf16[320,256]{1,0:T(8,128)(2,1)S(1)}, bf16[320,256]{1,0:T(8,128)(2,1)S(1)}, u32[]{:S(2)}, u32[]{:S(2)}) collective-permute-start(bf16[320,256]{1,0:T(8,128)(2,1)S(1)} %shard_map.107.chain_2), channel_id=1, source_target_pairs={{16,8},{17,9},{18,10},{19,11},{20,12},{21,13},{22,14},{23,15}} | collective-permute-start | bytes 491528 | tf_op jit(solution)/shard_map/ppermute | solution.py:315
  18.2 13.9 %collective-permute-start.1 = (bf16[320,256]{1,0:T(8,128)(2,1)S(1)}, bf16[320,256]{1,0:T(8,128)(2,1)S(1)}, u32[]{:S(2)}, u32[]{:S(2)}) collective-permute-start(bf16[320,256]{1,0:T(8,128)(2,1)S(1)} %get-tuple-element.47.refs_0_), channel_id=1, source_target_pairs={{0,2},{1,3},{2,0},{3,1},{4,6},{5,7},{6,4},{7,5},{8,10},{9,11},{10,... | collective-permute-start | bytes 491528 | tf_op jit(solution)/shard_map/ppermute | solution.py:323
  19.8 13.6 %collective-permute-start.2 = (bf16[320,256]{1,0:T(8,128)(2,1)S(1)}, bf16[320,256]{1,0:T(8,128)(2,1)S(1)}, u32[]{:S(2)}, u32[]{:S(2)}) collective-permute-start(bf16[320,256]{1,0:T(8,128)(2,1)S(1)} %get-tuple-element.47.refs_0_), channel_id=1, source_target_pairs={{0,4},{1,5},{2,6},{3,7},{4,0},{5,1},{6,2},{7,3},{8,12},{9,13},{10,... | collective-permute-start | bytes 491528 | tf_op jit(solution)/shard_map/ppermute | solution.py:323
  28.9 7.2 %collective-permute-start.6 = (bf16[320,256]{1,0:T(8,128)(2,1)S(1)}, bf16[320,256]{1,0:T(8,128)(2,1)S(1)}, u32[]{:S(2)}, u32[]{:S(2)}) collective-permute-start(bf16[320,256]{1,0:T(8,128)(2,1)S(1)} %get-tuple-element.47.refs_0_), channel_id=1, source_target_pairs={{0,6},{1,7},{2,4},{3,5},{4,2},{5,3},{6,0},{7,1},{8,14},{9,15},{10,... | collective-permute-start | bytes 491528 | tf_op jit(solution)/shard_map/ppermute | solution.py:323
  31.3 4.7 %collective-permute-start.3 = (bf16[320,256]{1,0:T(8,128)(2,1)S(1)}, bf16[320,256]{1,0:T(8,128)(2,1)S(1)}, u32[]{:S(2)}, u32[]{:S(2)}) collective-permute-start(bf16[320,256]{1,0:T(8,128)(2,1)S(1)} %get-tuple-element.47.refs_0_), channel_id=1, source_target_pairs={{0,1},{1,0},{2,3},{3,2},{4,5},{5,4},{6,7},{7,6},{8,9},{9,8},{10,11... | collective-permute-start | bytes 491528 | tf_op jit(solution)/shard_map/ppermute | solution.py:323
  31.3 5.2 %collective-permute-start.24 = (bf16[320,256]{1,0:T(8,128)(2,1)S(1)}, bf16[320,256]{1,0:T(8,128)(2,1)S(1)}, u32[]{:S(2)}, u32[]{:S(2)}) collective-permute-start(bf16[320,256]{1,0:T(8,128)(2,1)S(1)} %shard_map.111), channel_id=1, source_target_pairs={{16,14},{17,15},{18,12},{19,13},{20,10},{21,11},{22,8},{23,9},{24,... | collective-permute-start | bytes 491528 | tf_op jit(solution)/shard_map/ppermute | solution.py:332
  32.1 12.1 %collective-permute-start.12 = (bf16[320,256]{1,0:T(8,128)(2,1)S(1)}, bf16[320,256]{1,0:T(8,128)(2,1)S(1)}, u32[]{:S(2)}, u32[]{:S(2)}) collective-permute-start(bf16[320,256]{1,0:T(8,128)(2,1)S(1)} %get-tuple-element.53.chain_1), channel_id=1, source_target_pairs={{8,0},{9,1},{10,2},{11,3},{12,4},{13,5},{14,6},{15,7}} | collective-permute-start | bytes 491528 | tf_op jit(solution)/shard_map/ppermute | solution.py:315
  33.4 11.5 %collective-permute-start.15 = (bf16[320,256]{1,0:T(8,128)(2,1)S(1)}, bf16[320,256]{1,0:T(8,128)(2,1)S(1)}, u32[]{:S(2)}, u32[]{:S(2)}) collective-permute-start(bf16[320,256]{1,0:T(8,128)(2,1)S(1)} %shard_map.111), channel_id=1, source_target_pairs={{16,10},{17,11},{18,8},{19,9},{20,14},{21,15},{22,12},{23,13},{24,... | collective-permute-start | bytes 491528 | tf_op jit(solution)/shard_map/ppermute | solution.py:332
  36.1 12.5 %collective-permute-start.4 = (bf16[320,256]{1,0:T(8,128)(2,1)S(1)}, bf16[320,256]{1,0:T(8,128)(2,1)S(1)}, u32[]{:S(2)}, u32[]{:S(2)}) collective-permute-start(bf16[320,256]{1,0:T(8,128)(2,1)S(1)} %collective-permute-done.1.refs_1_), channel_id=1, source_target_pairs={{0,1},{1,0},{2,3},{3,2},{4,5},{5,4},{6,7},{7,6},{8,9},{9,8},{10,11... | collective-permute-start | bytes 491528 | tf_op jit(solution)/shard_map/ppermute | solution.py:323
  36.1 15.2 %collective-permute-start.5 = (bf16[320,256]{1,0:T(8,128)(2,1)S(1)}, bf16[320,256]{1,0:T(8,128)(2,1)S(1)}, u32[]{:S(2)}, u32[]{:S(2)}) collective-permute-start(bf16[320,256]{1,0:T(8,128)(2,1)S(1)} %collective-permute-done.2.refs_2_), channel_id=1, source_target_pairs={{0,1},{1,0},{2,3},{3,2},{4,5},{5,4},{6,7},{7,6},{8,9},{9,8},{10,11... | collective-permute-start | bytes 491528 | tf_op jit(solution)/shard_map/ppermute | solution.py:323
  36.6 20.8 %collective-permute-start.14 = (bf16[320,256]{1,0:T(8,128)(2,1)S(1)}, bf16[320,256]{1,0:T(8,128)(2,1)S(1)}, u32[]{:S(2)}, u32[]{:S(2)}) collective-permute-start(bf16[320,256]{1,0:T(8,128)(2,1)S(1)} %get-tuple-element.55), channel_id=1, source_target_pairs={{8,2},{9,3},{10,0},{11,1},{12,6},{13,7},{14,4},{15,5}} | collective-permute-start | bytes 491528 | tf_op jit(solution)/shard_map/ppermute | solution.py:332
  44.2 13.2 %collective-permute-start.18 = (bf16[320,256]{1,0:T(8,128)(2,1)S(1)}, bf16[320,256]{1,0:T(8,128)(2,1)S(1)}, u32[]{:S(2)}, u32[]{:S(2)}) collective-permute-start(bf16[320,256]{1,0:T(8,128)(2,1)S(1)} %shard_map.113), channel_id=1, source_target_pairs={{8,12},{9,13},{10,14},{11,15},{12,8},{13,9},{14,10},{15,11},{16,20... | collective-permute-start | bytes 491528 | tf_op jit(solution)/shard_map/ppermute | solution.py:341
  44.9 13.0 %collective-permute-start.17 = (bf16[320,256]{1,0:T(8,128)(2,1)S(1)}, bf16[320,256]{1,0:T(8,128)(2,1)S(1)}, u32[]{:S(2)}, u32[]{:S(2)}) collective-permute-start(bf16[320,256]{1,0:T(8,128)(2,1)S(1)} %shard_map.110.refs_6_.grad_low), channel_id=1, source_target_pairs={{0,4},{1,5},{2,6},{3,7},{4,0},{5,1},{6,2},{7,3}} | collective-permute-start | bytes 491528 | tf_op jit(solution)/shard_map/ppermute | solution.py:341
  48.5 14.8 %collective-permute-start.23 = (bf16[320,256]{1,0:T(8,128)(2,1)S(1)}, bf16[320,256]{1,0:T(8,128)(2,1)S(1)}, u32[]{:S(2)}, u32[]{:S(2)}) collective-permute-start(bf16[320,256]{1,0:T(8,128)(2,1)S(1)} %get-tuple-element.55), channel_id=1, source_target_pairs={{8,6},{9,7},{10,4},{11,5},{12,2},{13,3},{14,0},{15,1}} | collective-permute-start | bytes 491528 | tf_op jit(solution)/shard_map/ppermute | solution.py:332
  51.3 12.0 %collective-permute-start.27 = (bf16[4,40,320]{2,1,0:T(8,128)(2,1)S(1)}, bf16[4,40,320]{2,1,0:T(8,128)(2,1)S(1)}, u32[]{:S(2)}, u32[]{:S(2)}) collective-permute-start(bf16[4,40,320]{2,1,0:T(8,128)(2,1)S(1)} %get-tuple-element.60), channel_id=1, source_target_pairs={{0,1},{1,0},{2,3},{3,2},{4,5},{5,4},{6,7},{7,6},{8,9},{9,8},{10,11... | collective-permute-start | bytes 307208 | tf_op jit(solution)/shard_map/ppermute | solution.py:323
  57.4 6.6 %collective-permute-start.7 = (bf16[320,256]{1,0:T(8,128)(2,1)S(1)}, bf16[320,256]{1,0:T(8,128)(2,1)S(1)}, u32[]{:S(2)}, u32[]{:S(2)}) collective-permute-start(bf16[320,256]{1,0:T(8,128)(2,1)S(1)} %collective-permute-done.6.refs_6_.normed_0), channel_id=1, source_target_pairs={{0,1},{1,0},{2,3},{3,2},{4,5},{5,4},{6,7},{7,6},{8,9},{9,8},{10,11... | collective-permute-start | bytes 491528 | tf_op jit(solution)/shard_map/ppermute | solution.py:323
  57.4 13.1 %collective-permute-start.21 = (bf16[320,256]{1,0:T(8,128)(2,1)S(1)}, bf16[320,256]{1,0:T(8,128)(2,1)S(1)}, u32[]{:S(2)}, u32[]{:S(2)}) collective-permute-start(bf16[320,256]{1,0:T(8,128)(2,1)S(1)} %shard_map.112.refs_7_), channel_id=1, source_target_pairs={{0,1},{1,0},{2,3},{3,2},{4,5},{5,4},{6,7},{7,6},{8,9},{9,8},{10,11... | collective-permute-start | bytes 491528 | tf_op jit(solution)/shard_map/ppermute | solution.py:323
  58.0 12.5 %collective-permute-start.20 = (bf16[320,256]{1,0:T(8,128)(2,1)S(1)}, bf16[320,256]{1,0:T(8,128)(2,1)S(1)}, u32[]{:S(2)}, u32[]{:S(2)}) collective-permute-start(bf16[320,256]{1,0:T(8,128)(2,1)S(1)} %shard_map.110.refs_6_.grad_low), channel_id=1, source_target_pairs={{0,1},{1,0},{2,3},{3,2},{4,5},{5,4},{6,7},{7,6},{8,9},{9,8},{10,11... | collective-permute-start | bytes 491528 | tf_op jit(solution)/shard_map/ppermute | solution.py:323
  63.3 10.5 %collective-permute-start.22 = (bf16[320,256]{1,0:T(8,128)(2,1)S(1)}, bf16[320,256]{1,0:T(8,128)(2,1)S(1)}, u32[]{:S(2)}, u32[]{:S(2)}) collective-permute-start(bf16[320,256]{1,0:T(8,128)(2,1)S(1)} %shard_map.114.refs_8_), channel_id=1, source_target_pairs={{0,1},{1,0},{2,3},{3,2},{4,5},{5,4},{6,7},{7,6},{8,9},{9,8},{10,11... | collective-permute-start | bytes 491528 | tf_op jit(solution)/shard_map/ppermute | solution.py:323
  63.4 12.9 %collective-permute-start.26 = (bf16[320,256]{1,0:T(8,128)(2,1)S(1)}, bf16[320,256]{1,0:T(8,128)(2,1)S(1)}, u32[]{:S(2)}, u32[]{:S(2)}) collective-permute-start(bf16[320,256]{1,0:T(8,128)(2,1)S(1)} %shard_map.116.low_0), channel_id=1, source_target_pairs={{0,1},{1,0},{2,3},{3,2},{4,5},{5,4},{6,7},{7,6},{8,9},{9,8},{10,11... | collective-permute-start | bytes 491528 | tf_op jit(solution)/shard_map/ppermute | solution.py:323
  64.0 11.0 %collective-permute-start.28 = (bf16[40,320]{1,0:T(8,128)(2,1)S(1)}, bf16[40,320]{1,0:T(8,128)(2,1)S(1)}, u32[]{:S(2)}, u32[]{:S(2)}) collective-permute-start(bf16[40,320]{1,0:T(8,128)(2,1)S(1)} %get-tuple-element.62), channel_id=1, source_target_pairs={{0,2},{1,3},{2,0},{3,1},{4,6},{5,7},{6,4},{7,5},{8,10},{9,11},{10,... | collective-permute-start | bytes 76808 | tf_op jit(solution)/shard_map/ppermute | solution.py:323
  70.5 5.0 %collective-permute-start.29 = (bf16[40,320]{1,0:T(8,128)(2,1)S(1)}, bf16[40,320]{1,0:T(8,128)(2,1)S(1)}, u32[]{:S(2)}, u32[]{:S(2)}) collective-permute-start(bf16[40,320]{1,0:T(8,128)(2,1)S(1)} %get-tuple-element.63), channel_id=1, source_target_pairs={{0,4},{1,5},{2,6},{3,7},{4,0},{5,1},{6,2},{7,3},{8,12},{9,13},{10,... | collective-permute-start | bytes 76808 | tf_op jit(solution)/shard_map/ppermute | solution.py:323
  70.5 5.8 %collective-permute-start.30 = (bf16[40,320]{1,0:T(8,128)(2,1)S(1)}, bf16[40,320]{1,0:T(8,128)(2,1)S(1)}, u32[]{:S(2)}, u32[]{:S(2)}) collective-permute-start(bf16[40,320]{1,0:T(8,128)(2,1)S(1)} %get-tuple-element.64), channel_id=1, source_target_pairs={{0,6},{1,7},{2,4},{3,5},{4,2},{5,3},{6,0},{7,1},{8,14},{9,15},{10,... | collective-permute-start | bytes 76808 | tf_op jit(solution)/shard_map/ppermute | solution.py:323
